TPU v7x, 32 devices: a whole 2x2x4 slice. The times are simulated.
32 devices in a mesh: row: 8 (over y, x, core), col: 4 (over z).
Axes of the slice: x: 2, y: 2, z: 4, core: 2. Of those that a mesh axis runs over, the one named last changes fastest.
Arguments:
- constraint_tiles: float32 [768, 4, 128, 128], P('row', 'col'), may hold values from -0.375 to 0.375
- constraint_rows: int32 [768, 4], P('row', 'col'), may hold values from 0 to 191
- constraint_cols: int32 [768, 4], P('row', 'col'), may hold values from 0 to 255
- factor_tiles: float32 [384, 4, 128, 128], P('row', 'col'), may hold values from -0.3125 to 0.3125
- factor_rows: int32 [384, 4], P('row', 'col'), may hold values from 0 to 63
- factor_cols: int32 [384, 4], P('row', 'col'), may hold values from 0 to 255
- diag_cost: float32 [1024, 128], P('col'), may hold values from 0.1 to 1
- linear_cost: float32 [1024, 128], P('col'), may hold values from -6 to 6
- lower_bound: float32 [1536, 128], P('row'), may hold values from -1.5 to -0.2
- upper_bound: float32 [1536, 128], P('row'), may hold values from 0.2 to 1.5
- primal_start: float32 [1024, 128], P('col'), may hold values from -6 to 6
- slack_start: float32 [1536, 128], P('row'), may hold values from -6 to 6
- dual_start: float32 [1536, 128], P('row'), may hold values from -6 to 6
- penalty: float32 [], replicated, may hold values from 3 to 6
Outputs:
- primal_next: float32 [1024, 128], P('col')
- slack_next: float32 [1536, 128], P('row')
- dual_next: float32 [1536, 128], P('row')
- primal_res: float32 [], replicated
- dual_res: float32 [], replicated
All inputs are finite; a program needn't handle non-finite values.
Results may differ from a plain program's by a relative error of at most 0.0003.
Values sent between devices are 32-bit elements; how exact they have to be, the bound alone decides.
No kernel may reach another device: no remote copies, remote signals or barrier semaphores. Data moves between devices by JAX's collectives and lax.ppermute only.
A program may use at most 128 MiB of HBM per device.

v0:
```python
import jax
import jax.numpy as jnp
from jax import lax
from jax.sharding import PartitionSpec as P

YG = 64
CG = 6


SIGMA = 1e-06
RELAX = 1.6
HIGH = lax.Precision.HIGHEST


def add_blocks(parts, index, count):
    onehot = (jnp.arange(count, dtype=jnp.int32)[:, None] == index[None, :]).astype(jnp.float32)
    return jnp.dot(onehot, parts, precision=HIGH)


def forward_tiles(tiles, rows, cols, vec, count):
    prod = jnp.einsum("kij,kj->ki", tiles, jnp.take(vec, cols, axis=0), precision=HIGH)
    return add_blocks(prod, rows, count)


def backward_tiles(tiles, rows, cols, vec, count):
    prod = jnp.einsum("kij,ki->kj", tiles, jnp.take(vec, rows, axis=0), precision=HIGH)
    return add_blocks(prod, cols, count)


def reduce_rows(parts):
    return lax.psum(parts, "row")


def inner_sums(values):
    return lax.psum(values, "col")


def local(
    constraint_tiles,
    constraint_rows,
    constraint_cols,
    factor_tiles,
    factor_rows,
    factor_cols,
    diag_cost,
    linear_cost,
    lower_bound,
    upper_bound,
    primal_start,
    slack_start,
    dual_start,
    penalty,
):
    width = constraint_tiles.shape[2]
    ctiles = constraint_tiles.reshape(-1, width, width)
    ftiles = factor_tiles.reshape(-1, width, width)
    crow = constraint_rows.reshape(-1)
    ccol = constraint_cols.reshape(-1)
    frow = factor_rows.reshape(-1)
    fcol = factor_cols.reshape(-1)
    xcount = primal_start.shape[0]
    ycount = slack_start.shape[0]
    gcount = YG

    def products(full, with_factor):
        avec = forward_tiles(ctiles, crow, ccol, full, ycount)
        parts = (avec, forward_tiles(ftiles, frow, fcol, full, gcount)) if with_factor else (avec,)
        return lax.psum(parts, "col")

    def transposed(avec, gvec):
        return backward_tiles(ctiles, crow, ccol, avec, xcount) + backward_tiles(
            ftiles, frow, fcol, gvec, xcount
        )

    shifted = diag_cost + SIGMA

    def apply_k(share):
        avec, gvec = products(share, True)
        summed = reduce_rows((transposed(penalty * avec, gvec),))
        return shifted * share + summed[0]

    avec, gvec = products(primal_start, True)
    kx_part = transposed(penalty * avec, gvec)
    rhs_part = backward_tiles(ctiles, crow, ccol, penalty * slack_start - dual_start, xcount)
    sq_part = penalty * add_blocks(jnp.sum(ctiles * ctiles, axis=1), ccol, xcount) + add_blocks(
        jnp.sum(ftiles * ftiles, axis=1), fcol, xcount
    )
    kx_sum, rhs_sum, sq_sum = reduce_rows((kx_part, rhs_part, sq_part))
    precond = shifted + sq_sum
    rhs = SIGMA * primal_start - linear_cost + rhs_sum
    solution = primal_start
    resid = rhs - (shifted * primal_start + kx_sum)
    scaled = resid / precond
    image = apply_k(scaled)
    gamma, delta = inner_sums((jnp.sum(resid * scaled), jnp.sum(image * scaled)))
    alpha = gamma / delta
    direction = scaled
    along = image
    for step in range(CG):
        solution = solution + alpha * direction
        resid = resid - alpha * along
        if step + 1 < CG:
            scaled = resid / precond
            image = apply_k(scaled)
            gamma_new, delta = inner_sums((jnp.sum(resid * scaled), jnp.sum(image * scaled)))
            ratio = gamma_new / gamma
            alpha = gamma_new / (delta - ratio * gamma_new / alpha)
            direction = scaled + ratio * direction
            along = image + ratio * along
            gamma = gamma_new
    tilde_z = products(solution, False)[0]
    primal_next = RELAX * solution + (1.0 - RELAX) * primal_start
    relaxed = RELAX * tilde_z + (1.0 - RELAX) * slack_start
    slack_next = jnp.minimum(jnp.maximum(relaxed + dual_start / penalty, lower_bound), upper_bound)
    dual_next = dual_start + penalty * (relaxed - slack_next)
    image_next, gnext = products(primal_next, True)
    primal_local = jnp.max(jnp.abs(image_next - slack_next))
    dual_sum = reduce_rows((transposed(dual_next, gnext),))[0]
    dvec = diag_cost * primal_next + dual_sum + linear_cost
    dual_local = jnp.max(jnp.abs(dvec))
    primal_res, dual_res = lax.pmax((primal_local, dual_local), ("row", "col"))
    return (primal_next, slack_next, dual_next, primal_res, dual_res)


def solution(mesh):
    placed = (
        P("row", "col", None, None),
        P("row", "col"),
        P("row", "col"),
        P("row", "col", None, None),
        P("row", "col"),
        P("row", "col"),
        P("col", None),
        P("col", None),
        P("row", None),
        P("row", None),
        P("col", None),
        P("row", None),
        P("row", None),
        P(),
    )
    return jax.shard_map(
        local,
        mesh=mesh,
        in_specs=placed,
        out_specs=(P("col", None), P("row", None), P("row", None), P(), P()),
        check_vma=False,
    )
```

profile of v0, /device:TPU:0, one launch (start us, length us, event | category | flops | bytes accessed | tf_op | source)
XLA Modules:
  0.0 1306.8 jit_solution(9252605806084787506)
XLA Ops:
  10.2 12.0 fusion.32
  34.5 21.5 %psum.275 = f32[64,128]{1,0:T(8,128)S(1)} all-reduce(f32[64,128]{1,0:T(8,128)S(1)} %fusion.123), channel_id=1, replica_groups=mesh['row'=8,'col'=4] {'col'}, use_global_device_ids=true, to_apply=%region_2.6 | all-reduce | flops 8192 | bytes 65536 | tf_op jit(solution)/shard_map/psum | solution.py:68
  67.0 7.4 fusion.34
  74.3 7.3 fusion.30
  83.9 53.0 %all-reduce.54.cloned.1.call-done = (f32[256,128]{1,0:T(8,128)}, f32[256,128]{1,0:T(8,128)}, f32[256,128]{1,0:T(8,128)}) async-done(((f32[256,128]{1,0:T(8,128)}, f32[256,128]{1,0:T(8,128)}, f32[256,128]{1,0:T(8,128)}), (f32[256,128]{1,0:T(8,128)}, f32[256,128]{1,0:T(8,128)}, f32[256,128]{1,0:T(8,128)})) %all-reduce.54.cloned.1.call-update) | async-done | bytes 393232 | tf_op jit(solution)/shard_map/psum | solution.py:31
  146.0 19.0 %psum.280 = f32[64,128]{1,0:T(8,128)S(1)} all-reduce(f32[64,128]{1,0:T(8,128)S(1)} %fusion.122), channel_id=1, replica_groups=mesh['row'=8,'col'=4] {'col'}, use_global_device_ids=true, to_apply=%region_10.15 | all-reduce | flops 8192 | bytes 65536 | tf_op jit(solution)/shard_map/psum | solution.py:68
  167.8 11.8 fusion.28
  184.9 26.8 %all-reduce.28.cloned.1.call-done = f32[192,128]{1,0:T(8,128)} async-done(((f32[192,128]{1,0:T(8,128)}), f32[192,128]{1,0:T(8,128)}) %all-reduce.28.cloned.1.call-update) | async-done | bytes 98320 | tf_op jit(solution)/shard_map/psum | solution.py:68
  216.4 7.3 fusion.26
  224.9 53.3 %all-reduce.30.cloned.1.call-done = f32[256,128]{1,0:T(8,128)} async-done(((f32[256,128]{1,0:T(8,128)}), f32[256,128]{1,0:T(8,128)}) %all-reduce.30.cloned.1.call-update) | async-done | bytes 131088 | tf_op jit(solution)/shard_map/psum | solution.py:31
  280.4 12.3 all-reduce.7
  303.1 16.0 %psum.285 = f32[64,128]{1,0:T(8,128)S(1)} all-reduce(f32[64,128]{1,0:T(8,128)S(1)} %fusion.121), channel_id=1, replica_groups=mesh['row'=8,'col'=4] {'col'}, use_global_device_ids=true, to_apply=%region_17.22 | all-reduce | flops 8192 | bytes 65536 | tf_op jit(solution)/shard_map/psum | solution.py:68
  321.3 11.8 fusion.24
  337.4 29.2 %all-reduce.32.cloned.1.call-done = f32[192,128]{1,0:T(8,128)} async-done(((f32[192,128]{1,0:T(8,128)}), f32[192,128]{1,0:T(8,128)}) %all-reduce.32.cloned.1.call-update) | async-done | bytes 98320 | tf_op jit(solution)/shard_map/psum | solution.py:68
  369.8 7.3 fusion.22
  378.2 53.3 %all-reduce.34.cloned.1.call-done = f32[256,128]{1,0:T(8,128)} async-done(((f32[256,128]{1,0:T(8,128)}), f32[256,128]{1,0:T(8,128)}) %all-reduce.34.cloned.1.call-update) | async-done | bytes 131088 | tf_op jit(solution)/shard_map/psum | solution.py:31
  433.1 12.8 all-reduce.6
  461.4 16.9 %psum.290 = f32[64,128]{1,0:T(8,128)} all-reduce(f32[64,128]{1,0:T(8,128)} %fusion.120), channel_id=1, replica_groups=mesh['row'=8,'col'=4] {'col'}, use_global_device_ids=true, to_apply=%region_24.29 | all-reduce | flops 8192 | bytes 65536 | tf_op jit(solution)/shard_map/psum | solution.py:68
  482.6 11.8 fusion.20
  499.6 28.3 %all-reduce.36.cloned.1.call-done = f32[192,128]{1,0:T(8,128)} async-done(((f32[192,128]{1,0:T(8,128)}), f32[192,128]{1,0:T(8,128)}) %all-reduce.36.cloned.1.call-update) | async-done | bytes 98320 | tf_op jit(solution)/shard_map/psum | solution.py:68
  532.6 7.3 fusion.18
  541.1 53.3 %all-reduce.38.cloned.1.call-done = f32[256,128]{1,0:T(8,128)} async-done(((f32[256,128]{1,0:T(8,128)}), f32[256,128]{1,0:T(8,128)}) %all-reduce.38.cloned.1.call-update) | async-done | bytes 131088 | tf_op jit(solution)/shard_map/psum | solution.py:31
  596.0 12.3 all-reduce.5
  623.4 17.1 %psum.295 = f32[64,128]{1,0:T(8,128)} all-reduce(f32[64,128]{1,0:T(8,128)} %fusion.119), channel_id=1, replica_groups=mesh['row'=8,'col'=4] {'col'}, use_global_device_ids=true, to_apply=%region_31.36 | all-reduce | flops 8192 | bytes 65536 | tf_op jit(solution)/shard_map/psum | solution.py:68
  644.8 11.8 fusion.16
  661.7 28.5 %all-reduce.40.cloned.1.call-done = f32[192,128]{1,0:T(8,128)} async-done(((f32[192,128]{1,0:T(8,128)}), f32[192,128]{1,0:T(8,128)}) %all-reduce.40.cloned.1.call-update) | async-done | bytes 98320 | tf_op jit(solution)/shard_map/psum | solution.py:68
  694.8 7.3 fusion.14
  703.3 53.3 %all-reduce.42.cloned.1.call-done = f32[256,128]{1,0:T(8,128)} async-done(((f32[256,128]{1,0:T(8,128)}), f32[256,128]{1,0:T(8,128)}) %all-reduce.42.cloned.1.call-update) | async-done | bytes 131088 | tf_op jit(solution)/shard_map/psum | solution.py:31
  758.2 12.6 all-reduce.4
  787.6 16.9 %psum.300 = f32[64,128]{1,0:T(8,128)} all-reduce(f32[64,128]{1,0:T(8,128)} %fusion.118), channel_id=1, replica_groups=mesh['row'=8,'col'=4] {'col'}, use_global_device_ids=true, to_apply=%region_38.43 | all-reduce | flops 8192 | bytes 65536 | tf_op jit(solution)/shard_map/psum | solution.py:68
  808.8 11.8 fusion.12
  826.1 28.1 %all-reduce.44.cloned.1.call-done = f32[192,128]{1,0:T(8,128)} async-done(((f32[192,128]{1,0:T(8,128)}), f32[192,128]{1,0:T(8,128)}) %all-reduce.44.cloned.1.call-update) | async-done | bytes 98320 | tf_op jit(solution)/shard_map/psum | solution.py:68
  858.8 7.3 fusion.10
  867.3 53.3 %all-reduce.46.cloned.1.call-done = f32[256,128]{1,0:T(8,128)} async-done(((f32[256,128]{1,0:T(8,128)}), f32[256,128]{1,0:T(8,128)}) %all-reduce.46.cloned.1.call-update) | async-done | bytes 131088 | tf_op jit(solution)/shard_map/psum | solution.py:31
  922.3 12.3 all-reduce.3
  951.4 17.1 %psum.305 = f32[64,128]{1,0:T(8,128)} all-reduce(f32[64,128]{1,0:T(8,128)} %fusion.117), channel_id=1, replica_groups=mesh['row'=8,'col'=4] {'col'}, use_global_device_ids=true, to_apply=%region_45.50 | all-reduce | flops 8192 | bytes 65536 | tf_op jit(solution)/shard_map/psum | solution.py:68
  972.9 11.8 fusion.8
  989.7 28.5 %all-reduce.48.cloned.1.call-done = f32[192,128]{1,0:T(8,128)} async-done(((f32[192,128]{1,0:T(8,128)}), f32[192,128]{1,0:T(8,128)}) %all-reduce.48.cloned.1.call-update) | async-done | bytes 98320 | tf_op jit(solution)/shard_map/psum | solution.py:68
  1022.8 7.3 fusion.6
  1031.3 53.3 %all-reduce.50.cloned.1.call-done = f32[256,128]{1,0:T(8,128)} async-done(((f32[256,128]{1,0:T(8,128)}), f32[256,128]{1,0:T(8,128)}) %all-reduce.50.cloned.1.call-update) | async-done | bytes 131088 | tf_op jit(solution)/shard_map/psum | solution.py:31
  1086.3 12.5 all-reduce.2
  1114.9 15.8 %psum.310 = f32[64,128]{1,0:T(8,128)S(1)} all-reduce(f32[64,128]{1,0:T(8,128)S(1)} %fusion.116), channel_id=1, replica_groups=mesh['row'=8,'col'=4] {'col'}, use_global_device_ids=true, to_apply=%region_53.58 | all-reduce | flops 8192 | bytes 65536 | tf_op jit(solution)/shard_map/psum | solution.py:68
  1132.8 11.8 fusion.2
  1144.7 11.9 fusion.4
  1161.3 30.1 %all-reduce.56.cloned.1.call-done = (f32[192,128]{1,0:T(8,128)}, f32[192,128]{1,0:T(8,128)}) async-done(((f32[192,128]{1,0:T(8,128)}, f32[192,128]{1,0:T(8,128)}), (f32[192,128]{1,0:T(8,128)}, f32[192,128]{1,0:T(8,128)})) %all-reduce.56.cloned.1.call-update) | async-done | bytes 196624 | tf_op jit(solution)/shard_map/psum | solution.py:68
  1195.6 7.3 fusion
  1205.3 53.4 %all-reduce.52.cloned.1.call-done = f32[256,128]{1,0:T(8,128)} async-done(((f32[256,128]{1,0:T(8,128)}), f32[256,128]{1,0:T(8,128)}) %all-reduce.52.cloned.1.call-update) | async-done | bytes 131088 | tf_op jit(solution)/shard_map/psum | solution.py:31
  1260.3 39.5 %all-reduce = (f32[]{:T(128)}, f32[]{:T(128)}) all-reduce(f32[]{:T(128)} %get-tuple-element.40, f32[]{:T(128)} %abs_reduce_fusion), channel_id=1, replica_groups=mesh['row'=8,'col'=4] {'row','col'}, use_global_device_ids=true, to_apply=%region_52.57 | all-reduce | flops 2 | bytes 16 | tf_op jit(solution)/shard_map/pmax | solution.py:121
  (257 shorter events, 216.6 us)
Async XLA Ops:
  7.2 15.1 %copy-start.21 = (s32[96,1]{0,1:T(1,128)S(1)}, s32[96,1]{0,1:T(1,128)}, u32[]{:S(2)}) copy-start(s32[96,1]{0,1:T(1,128)} %param.23) | copy-start | bytes 1156
  7.2 16.5 %copy-start.24 = (s32[48,1]{0,1:T(1,128)S(1)}, s32[48,1]{0,1:T(1,128)}, u32[]{:S(2)}) copy-start(s32[48,1]{0,1:T(1,128)} %param.26) | copy-start | bytes 580
  7.2 16.6 %copy-start.23 = (s32[48,1]{0,1:T(1,128)S(1)}, s32[48,1]{0,1:T(1,128)}, u32[]{:S(2)}) copy-start(s32[48,1]{0,1:T(1,128)} %param.27) | copy-start | bytes 580
  7.2 56.7 %all-reduce.26.cloned.1.call-start = ((), (), s32[]{:S(2)}) async-start(), calls=%async_computation | async-start | bytes 196608 | tf_op jit(solution)/shard_map/psum | solution.py:68
  10.2 18.1 %copy-start.4 = (f32[256,128]{1,0:T(8,128)S(1)}, f32[256,128]{1,0:T(8,128)}, u32[]{:S(2)}) copy-start(f32[256,128]{1,0:T(8,128)} %param.32) | copy-start | bytes 393220
  10.2 18.7 %copy-start = (f32[48,1,128,128]{3,2,1,0:T(8,128)S(1)}, f32[48,1,128,128]{3,2,1,0:T(8,128)}, u32[]{:S(2)}) copy-start(f32[48,1,128,128]{3,2,1,0:T(8,128)} %param.25) | copy-start | bytes 9437188
  23.1 113.8 %all-reduce.54.cloned.1.call-start = ((), (), s32[]{:S(2)}) async-start(), calls=%async_computation.14 | async-start | bytes 786432 | tf_op jit(solution)/shard_map/psum | solution.py:31
  23.2 42.9 %copy-start.25 = (pred[96]{0:T(512)(128)(4,1)}, pred[96]{0:T(512)(128)(4,1)S(1)}, u32[]{:S(2)}) copy-start(pred[96]{0:T(512)(128)(4,1)S(1)} %compare_and_fusion.3) | copy-start | bytes 292
  23.7 32.9 %copy-start.27 = (pred[48]{0:T(512)(128)(4,1)}, pred[48]{0:T(512)(128)(4,1)S(1)}, u32[]{:S(2)}) copy-start(pred[48]{0:T(512)(128)(4,1)S(1)} %compare_and_fusion) | copy-start | bytes 148
  23.8 10.6 copy-start.28
  27.5 32.5 %copy-start.20 = (s32[96,1]{0,1:T(1,128)S(1)}, s32[96,1]{0,1:T(1,128)}, u32[]{:S(2)}) copy-start(s32[96,1]{0,1:T(1,128)} %param.24) | copy-start | bytes 1156
  27.6 32.7 %copy-start.9 = (f32[192,128]{1,0:T(8,128)S(1)}, f32[192,128]{1,0:T(8,128)}, u32[]{:S(2)}) copy-start(f32[192,128]{1,0:T(8,128)} %param.34) | copy-start | bytes 294916
  28.3 6.1 copy-start.33
  28.3 31.8 %copy-start.32 = (s32[1024]{0:T(1024)}, s32[1024]{0:T(1024)S(1)}, u32[]{:S(2)}) copy-start(s32[1024]{0:T(1024)S(1)} %pad_clamp_fusion) | copy-start | bytes 12292
  62.7 19.0 %copy-start.30 = (s32[1024]{0:T(1024)}, s32[1024]{0:T(1024)S(1)}, u32[]{:S(2)}) copy-start(s32[1024]{0:T(1024)S(1)} %pad_clamp_fusion.3) | copy-start | bytes 12292
  67.0 15.8 %copy-start.13 = (f32[48,1,128]{2,1,0:T(1,128)S(1)}, f32[48,1,128]{2,1,0:T(1,128)}, u32[]{:S(2)}) copy-start(f32[48,1,128]{2,1,0:T(1,128)} %fusion.65) | copy-start | bytes 73732
  67.0 69.9 %copy-start.1 = (f32[256,128]{1,0:T(8,128)S(1)}, f32[256,128]{1,0:T(8,128)}, u32[]{:S(2)}) copy-start(f32[256,128]{1,0:T(8,128)} %param.28) | copy-start | bytes 393220
  83.6 128.1 %all-reduce.28.cloned.1.call-start = ((), (), s32[]{:S(2)}) async-start(), calls=%async_computation.1 | async-start | bytes 196608 | tf_op jit(solution)/shard_map/psum | solution.py:68
  138.7 139.4 %copy-start.3 = (f32[256,128]{1,0:T(8,128)}, f32[256,128]{1,0:T(8,128)S(1)}, u32[]{:S(2)}) copy-start(f32[256,128]{1,0:T(8,128)S(1)} %get-tuple-element.56) | copy-start | bytes 393220
  179.7 114.4 %copy-start.6 = (f32[256,128]{1,0:T(8,128)S(1)}, f32[256,128]{1,0:T(8,128)}, u32[]{:S(2)}) copy-start(f32[256,128]{1,0:T(8,128)} %get-tuple-element.57) | copy-start | bytes 393220
  180.6 97.6 %all-reduce.30.cloned.1.call-start = ((), (), s32[]{:S(2)}) async-start(), calls=%async_computation.2 | async-start | bytes 262144 | tf_op jit(solution)/shard_map/psum | solution.py:31
  215.5 8.4 copy-start.14
  224.8 141.8 %all-reduce.32.cloned.1.call-start = ((), (), s32[]{:S(2)}) async-start(), calls=%async_computation.3 | async-start | bytes 196608 | tf_op jit(solution)/shard_map/psum | solution.py:68
  334.0 97.6 %all-reduce.34.cloned.1.call-start = ((), (), s32[]{:S(2)}) async-start(), calls=%async_computation.4 | async-start | bytes 262144 | tf_op jit(solution)/shard_map/psum | solution.py:31
  368.8 8.5 copy-start.15
  368.8 62.7 %copy-start.8 = (f32[256,128]{1,0:T(8,128)S(1)}, f32[256,128]{1,0:T(8,128)}, u32[]{:S(2)}) copy-start(f32[256,128]{1,0:T(8,128)} %get-tuple-element.54) | copy-start | bytes 393220
  378.2 149.8 %all-reduce.36.cloned.1.call-start = ((), (), s32[]{:S(2)}) async-start(), calls=%async_computation.5 | async-start | bytes 196608 | tf_op jit(solution)/shard_map/psum | solution.py:68
  452.2 142.3 %copy-start.2 = (f32[256,128]{1,0:T(8,128)}, f32[256,128]{1,0:T(8,128)S(1)}, u32[]{:S(2)}) copy-start(f32[256,128]{1,0:T(8,128)S(1)} %get-tuple-element.51) | copy-start | bytes 393220
  495.3 99.1 %all-reduce.38.cloned.1.call-start = ((), (), s32[]{:S(2)}) async-start(), calls=%async_computation.6 | async-start | bytes 262144 | tf_op jit(solution)/shard_map/psum | solution.py:31
  531.7 8.4 copy-start.16
  541.0 149.1 %all-reduce.40.cloned.1.call-start = ((), (), s32[]{:S(2)}) async-start(), calls=%async_computation.7 | async-start | bytes 196608 | tf_op jit(solution)/shard_map/psum | solution.py:68
  657.6 99.1 %all-reduce.42.cloned.1.call-start = ((), (), s32[]{:S(2)}) async-start(), calls=%async_computation.8 | async-start | bytes 262144 | tf_op jit(solution)/shard_map/psum | solution.py:31
  693.9 8.4 copy-start.17
  703.3 150.9 %all-reduce.44.cloned.1.call-start = ((), (), s32[]{:S(2)}) async-start(), calls=%async_computation.9 | async-start | bytes 196608 | tf_op jit(solution)/shard_map/psum | solution.py:68
  821.5 99.1 %all-reduce.46.cloned.1.call-start = ((), (), s32[]{:S(2)}) async-start(), calls=%async_computation.10 | async-start | bytes 262144 | tf_op jit(solution)/shard_map/psum | solution.py:31
  857.9 8.4 copy-start.18
  867.2 150.9 %all-reduce.48.cloned.1.call-start = ((), (), s32[]{:S(2)}) async-start(), calls=%async_computation.11 | async-start | bytes 196608 | tf_op jit(solution)/shard_map/psum | solution.py:68
  985.6 99.0 %all-reduce.50.cloned.1.call-start = ((), (), s32[]{:S(2)}) async-start(), calls=%async_computation.12 | async-start | bytes 262144 | tf_op jit(solution)/shard_map/psum | solution.py:31
  985.6 124.0 %copy-start.29 = (pred[48]{0:T(512)(128)(4,1)S(1)}, pred[48]{0:T(512)(128)(4,1)}, u32[]{:S(2)}) copy-start(pred[48]{0:T(512)(128)(4,1)} %copy-done.28) | copy-start | bytes 148
  1021.9 8.4 copy-start.19
  1031.3 160.2 %all-reduce.56.cloned.1.call-start = ((), (), s32[]{:S(2)}) async-start(), calls=%async_computation.15 | async-start | bytes 393216 | tf_op jit(solution)/shard_map/psum | solution.py:68
  1132.8 23.8 %copy-start.22 = (s32[96,1]{0,1:T(1,128)S(1)}, s32[96,1]{0,1:T(1,128)}, u32[]{:S(2)}) copy-start(s32[96,1]{0,1:T(1,128)} %param.23) | copy-start | bytes 1156
  1144.7 46.8 %copy-start.10 = (f32[192,128]{1,0:T(8,128)S(1)}, f32[192,128]{1,0:T(8,128)}, u32[]{:S(2)}) copy-start(f32[192,128]{1,0:T(8,128)} %param.34) | copy-start | bytes 294916
  1156.6 102.2 %copy-start.5 = (f32[256,128]{1,0:T(8,128)S(1)}, f32[256,128]{1,0:T(8,128)}, u32[]{:S(2)}) copy-start(f32[256,128]{1,0:T(8,128)} %get-tuple-element.42) | copy-start | bytes 393220
  1158.3 100.5 %all-reduce.52.cloned.1.call-start = ((), (), s32[]{:S(2)}) async-start(), calls=%async_computation.13 | async-start | bytes 262144 | tf_op jit(solution)/shard_map/psum | solution.py:31
  1161.3 97.4 %copy-start.11 = (f32[256,128]{1,0:T(8,128)S(1)}, f32[256,128]{1,0:T(8,128)}, u32[]{:S(2)}) copy-start(f32[256,128]{1,0:T(8,128)} %param.29) | copy-start | bytes 393220
  1193.2 106.6 %copy-start.12 = (f32[192,128]{1,0:T(8,128)}, f32[192,128]{1,0:T(8,128)S(1)}, u32[]{:S(2)}) copy-start(f32[192,128]{1,0:T(8,128)S(1)} %get-tuple-element.41) | copy-start | bytes 294916
  1194.2 105.6 %copy-start.7 = (f32[192,128]{1,0:T(8,128)}, f32[192,128]{1,0:T(8,128)S(1)}, u32[]{:S(2)}) copy-start(f32[192,128]{1,0:T(8,128)S(1)} %multiply_add_fusion.10) | copy-start | bytes 294916
  (2 other events, 3.9 us)
Sparse Core Ops, SparseCore 0:
  23.2 37.2 all-reduce.25
  83.8 53.0 all-reduce.53
  180.7 30.9 all-reduce.27
  224.9 53.1 all-reduce.29
  334.1 32.4 all-reduce.31
  378.3 53.1 all-reduce.33
  495.4 32.4 all-reduce.35
  541.2 53.1 all-reduce.37
  657.7 32.4 all-reduce.39
  703.4 53.1 all-reduce.41
  821.6 32.4 all-reduce.43
  867.4 53.1 all-reduce.45
  985.7 32.4 all-reduce.47
  1031.4 53.1 all-reduce.49
  1158.4 32.9 all-reduce.55
  1205.4 53.2 all-reduce.51
where the time goes:
time: 1320 us; the launch traced here: 1310 us
  waiting for transfers between devices  626 us (47%)
  matrix products  266 us (20%)
  blocking collectives  255 us (19%)
  other arithmetic  70.9 us (5%)
  local copies, waits for them, and re-layouts  50.8 us (4%)
  between operations  37.1 us (3%)
    psum x8, waiting for transfers between devices, reduce_rows(): return lax.psum(parts, 'row')  426 us
    psum x8, waiting for transfers between devices, products(): return lax.psum(parts, 'col')  199 us
    dot_general x17, matrix products, forward_tiles(): jnp.einsum('kij,kj->ki', tiles, jnp.take(vec, cols, axis=0), precision=HIGH)  147 us
    psum x8, blocking collectives, products(): return lax.psum(parts, 'col')  140 us
    dot_general x17, matrix products, backward_tiles(): jnp.einsum('kij,ki->kj', tiles, jnp.take(vec, rows, axis=0), precision=HIGH)  95.8 us
    psum x6, blocking collectives, inner_sums(): return lax.psum(values, 'col')  74.8 us
    pmax x1, blocking collectives, local(): primal_res, dual_res = lax.pmax((primal_local, dual_local), ('row', 'col'))  39.5 us
    gather x17, local copies, waits for them, and re-layouts, backward_tiles(): jnp.take(vec, rows, axis=0)  26.5 us
  transfers between devices with their start and end apart: 16, of which 15 were waited for; matrix products, arithmetic and copies ran while one was open for 3% of the time, Pallas kernels for 0%

commit v1 on v0

v1 whole, which is shorter than its diff:
```python
import functools

import jax
import jax.numpy as jnp
from jax import lax
from jax.experimental import pallas as pl
from jax.experimental.pallas import tpu as pltpu
from jax.sharding import PartitionSpec as P

YG = 64
CG = 6

SIGMA = 1e-06
RELAX = 1.6

F32 = jnp.float32
BF16 = jnp.bfloat16
LANES = 128
GROUP = 4
VMEM_LIMIT = 24 * 1024 * 1024


def dot(a, b):
    return lax.dot_general(a, b, (((1,), (0,)), ((), ())), preferred_element_type=F32)


def dot_t(a, b):
    return lax.dot_general(a, b, (((1,), (1,)), ((), ())), preferred_element_type=F32)


def split3(x):
    high = x.astype(BF16)
    rest = x - high.astype(F32)
    mid = rest.astype(BF16)
    low = (rest - mid.astype(F32)).astype(BF16)
    return high, mid, low


def tree(parts, op=jnp.add):
    parts = list(parts)
    while len(parts) > 1:
        parts = [op(parts[i], parts[i + 1]) for i in range(0, len(parts), 2)]
    return parts[0]


def row_sum(x):
    return jnp.sum(x, axis=0, keepdims=True)


def pad_rows(rows):
    return jnp.concatenate(list(rows) + [jnp.zeros((8 - len(rows), LANES), F32)], axis=0)


def gather(onehot_ref, x):
    return dot(onehot_ref[...], jnp.concatenate(split3(x), axis=0))


def scatter(onehot, x):
    high, mid, low = split3(x)
    return dot(onehot, high) + (dot(onehot, mid) + dot(onehot, low))


def run_tiles(w_ref, l_ref, r0_ref, r1_ref, product):
    pairs = w_ref.shape[0]
    blocks = pairs // 2
    unroll = next(n for n in (4, 3, 2, 1) if blocks % n == 0)

    def body(step, carry):
        for inner in range(unroll):
            block = step * unroll + inner
            at = pl.multiple_of(block * 16, 16)
            left = l_ref[pl.ds(at, 16), :]
            first = product(left, w_ref[2 * block])
            second = product(left, w_ref[2 * block + 1])
            r0_ref[pl.ds(at, 8), :] = first[:8, :LANES]
            r1_ref[pl.ds(at, 8), :] = first[:8, LANES:]
            r0_ref[pl.ds(pl.multiple_of(at + 8, 8), 8), :] = second[8:, :LANES]
            r1_ref[pl.ds(pl.multiple_of(at + 8, 8), 8), :] = second[8:, LANES:]
        return carry

    lax.fori_loop(0, blocks // unroll, body, 0)


def forward_parts(vec, gf_ref, w_ref, l_ref, r0_ref, r1_ref):
    picked = gather(gf_ref, vec)
    first = lax.broadcasted_iota(jnp.int32, picked.shape, 0) % (2 * GROUP) < GROUP
    zero = jnp.zeros_like(picked)
    l_ref[:, :LANES] = jnp.where(first, picked, zero).astype(BF16)
    l_ref[:, LANES:] = jnp.where(first, zero, picked).astype(BF16)
    run_tiles(w_ref, l_ref, r0_ref, r1_ref, dot_t)
    count = 2 * w_ref.shape[0]
    out = None
    for part in (2, 1, 0):
        at = pl.ds(part, count, stride=GROUP)
        term = r0_ref[at, :] + r1_ref[at, :]
        out = term if out is None else out + term
    return out


def backward_sum(vec, gb_ref, sb_ref, w_ref, l_ref, r0_ref, r1_ref):
    picked = gather(gb_ref, vec).astype(BF16)
    l_ref[:, :LANES] = picked
    l_ref[:, LANES:] = picked
    run_tiles(w_ref, l_ref, r0_ref, r1_ref, dot)
    half = w_ref.shape[0]
    even, odd = None, None
    for part in (2, 1, 0):
        one = r0_ref[pl.ds(part, half, stride=2 * GROUP), :]
        two = r1_ref[pl.ds(GROUP + part, half, stride=2 * GROUP), :]
        even = one if even is None else even + one
        odd = two if odd is None else odd + two
    return scatter(sb_ref[...], jnp.concatenate([even, odd], axis=0))


def gathered_rows(part_refs, s_ref):
    count = s_ref.shape[2]
    return tree(scatter(s_ref[j], ref[:count, :]) for j, ref in enumerate(part_refs))


def init_kernel(a_steps, a_ref, g_ref, w_ref, sq_ref):
    step = pl.program_id(0)

    def convert(ref):
        for t in range(ref.shape[0]):
            tile = ref[t]
            high = tile.astype(BF16)
            low = (tile - high.astype(F32)).astype(BF16)
            at = (t % 2) * LANES
            w_ref[t // 2, :LANES, at : at + LANES] = high
            w_ref[t // 2, LANES:, at : at + LANES] = low
            sq_ref[t : t + 1, :] = row_sum(tile * tile)

    @pl.when(step < a_steps)
    def _():
        convert(a_ref)

    @pl.when(step >= a_steps)
    def _():
        convert(g_ref)


def first_forward_kernel(v_ref, gf_ref, w_ref, out_ref, l_ref, r0_ref, r1_ref):
    count = 2 * w_ref.shape[0]
    out_ref[:count, :] = forward_parts(v_ref[...], gf_ref, w_ref, l_ref, r0_ref, r1_ref)
    out_ref[count:, :] = jnp.zeros((8, LANES), F32)


def first_backward_kernel(n_col, ycount, acount, *refs):
    rho_ref, *refs = refs
    part_refs, refs = refs[:n_col], refs[n_col:]
    s_ref, gb_ref, sb_ref, w_ref, sq_ref, slack_ref, dual_ref, z_ref, y_ref, l_ref, r0_ref, r1_ref = refs
    rho = rho_ref[0]
    full = gathered_rows(part_refs, s_ref)
    y_ref[...] = full
    top = rho * slack_ref[...] - dual_ref[...] - rho * full[:ycount]
    vec = jnp.concatenate([top, -full[ycount:]], axis=0)
    xcount = sb_ref.shape[0]
    z_ref[:xcount, :] = backward_sum(vec, gb_ref, sb_ref, w_ref, l_ref, r0_ref, r1_ref)
    half = w_ref.shape[0]
    squares = jnp.concatenate([sq_ref[pl.ds(0, half, stride=2), :], sq_ref[pl.ds(1, half, stride=2), :]], axis=0)
    place = lax.broadcasted_iota(jnp.int32, squares.shape, 0)
    place = jnp.where(place < half, 2 * place, 2 * (place - half) + 1)
    squares = jnp.where(place < acount, rho * squares, squares)
    z_ref[xcount:, :] = scatter(sb_ref[...], squares)


def finish_forward(u, p, resid, shifted, out_ref, gf_ref, w_ref, l_ref, r0_ref, r1_ref):
    count = 2 * w_ref.shape[0]
    weighted = shifted * u
    rows = [row_sum(resid * u), row_sum(weighted * u)]
    if p is not None:
        rows.append(row_sum(weighted * p))
    out_ref[count:, :] = pad_rows(rows)
    out_ref[:count, :] = forward_parts(u, gf_ref, w_ref, l_ref, r0_ref, r1_ref)


def second_forward_kernel(n_plane, *refs):
    z_refs, refs = refs[:n_plane], refs[n_plane:]
    v_ref, d_ref, c_ref, gf_ref, w_ref, r_ref, u_ref, pre_ref, out_ref, l_ref, r0_ref, r1_ref = refs
    xcount = v_ref.shape[0]
    total = tree(ref[...] for ref in z_refs)
    v, d = v_ref[...], d_ref[...]
    resid = total[:xcount] - c_ref[...] - d * v
    shifted = d + SIGMA
    pre = shifted + total[xcount:]
    u = resid / pre
    r_ref[...] = resid
    u_ref[...] = u
    pre_ref[...] = pre
    finish_forward(u, None, resid, shifted, out_ref, gf_ref, w_ref, l_ref, r0_ref, r1_ref)


def step_scalars(first, part_refs, sc_old_ref, count):
    totals = jnp.sum(tree(ref[count:, :] for ref in part_refs), axis=1, keepdims=True)
    gamma, one, two = totals[0:1], totals[1:2], totals[2:3]
    if first:
        return gamma, jnp.zeros_like(gamma), one
    old = sc_old_ref[...]
    beta = gamma / old[0:1, 0:1]
    return gamma, beta, one + beta * (2.0 * two + beta * old[2:3, 0:1])


def wide(x):
    return jnp.broadcast_to(x, (1, LANES))


def backward_kernel(n_col, ycount, first, last, *refs):
    rho_ref, *refs = refs
    part_refs, refs = refs[:n_col], refs[n_col:]
    s_ref, refs = refs[0], refs[1:]
    sc_old_ref = None
    if not first:
        (yp_old_ref, yv_old_ref, sc_old_ref, alpha_ref), refs = refs[:4], refs[4:]
    else:
        (yv_old_ref,), refs = refs[:1], refs[1:]
    if not last:
        (gb_ref, sb_ref, w_ref), refs = refs[:3], refs[3:]
    z_ref, yp_ref, yv_ref, sc_ref, *scratch = refs
    rho = rho_ref[0]
    full = gathered_rows(part_refs, s_ref)
    gamma, beta, pdp = step_scalars(first, part_refs, sc_old_ref, s_ref.shape[2])
    sc_ref[...] = pad_rows([wide(gamma), wide(beta), wide(pdp)])
    if first:
        yp = full
        yv_ref[...] = yv_old_ref[...]
    else:
        yp_old = yp_old_ref[...]
        yp = full + beta * yp_old
        yv_ref[...] = yv_old_ref[...] + alpha_ref[0:1, 0:1] * yp_old
    yp_ref[...] = yp
    scaled = jnp.concatenate([rho * yp[:ycount], yp[ycount:]], axis=0)
    norm = pad_rows([row_sum(scaled * yp)])
    if last:
        z_ref[...] = norm
    else:
        xcount = sb_ref.shape[0]
        z_ref[xcount:, :] = norm
        z_ref[:xcount, :] = backward_sum(scaled, gb_ref, sb_ref, w_ref, *scratch)


def step_alpha(extra, sc_ref):
    norm = jnp.sum(extra[0:1], axis=1, keepdims=True)
    return sc_ref[0:1, 0:1] / (sc_ref[2:3, 0:1] + norm)


def forward_kernel(n_plane, first, *refs):
    z_refs, refs = refs[:n_plane], refs[n_plane:]
    if not first:
        p_old_ref, refs = refs[0], refs[1:]
    (u_old_ref, v_old_ref, r_old_ref, d_ref, pre_ref, sc_ref, gf_ref, w_ref), refs = refs[:8], refs[8:]
    p_ref, v_ref, r_ref, u_ref, alpha_ref, out_ref, *scratch = refs
    xcount = d_ref.shape[0]
    total = tree(ref[...] for ref in z_refs)
    alpha = step_alpha(total[xcount:], sc_ref)
    p = u_old_ref[...]
    if not first:
        p = p + sc_ref[1:2, 0:1] * p_old_ref[...]
    shifted = d_ref[...] + SIGMA
    resid = r_old_ref[...] - alpha * (shifted * p + total[:xcount])
    u = resid / pre_ref[...]
    p_ref[...] = p
    v_ref[...] = v_old_ref[...] + alpha * p
    r_ref[...] = resid
    u_ref[...] = u
    alpha_ref[...] = jnp.broadcast_to(alpha, (8, LANES))
    finish_forward(u, p, resid, shifted, out_ref, gf_ref, w_ref, *scratch)


def final_kernel(n_plane, ycount, *refs):
    rho_ref, *refs = refs
    t_refs, refs = refs[:n_plane], refs[n_plane:]
    (u_ref, p_old_ref, v_ref, start_ref, sc_ref, yp_ref, yv_ref, y0_ref), refs = refs[:8], refs[8:]
    (slack_ref, dual_ref, lower_ref, upper_ref, gb_ref, sb_ref, w_ref), refs = refs[:7], refs[7:]
    primal_out, slack_out, dual_out, z_ref, *scratch = refs
    rho = rho_ref[0]
    alpha = step_alpha(tree(ref[...] for ref in t_refs), sc_ref)
    p = u_ref[...] + sc_ref[1:2, 0:1] * p_old_ref[...]
    v = v_ref[...] + alpha * p
    primal_out[...] = RELAX * v + (1.0 - RELAX) * start_ref[...]
    image = yv_ref[...] + alpha * yp_ref[...]
    image_next = RELAX * image + (1.0 - RELAX) * y0_ref[...]
    dual = dual_ref[...]
    relaxed = RELAX * image[:ycount] + (1.0 - RELAX) * slack_ref[...]
    slack_next = jnp.minimum(jnp.maximum(relaxed + dual / rho, lower_ref[...]), upper_ref[...])
    dual_next = dual + rho * (relaxed - slack_next)
    slack_out[...] = slack_next
    dual_out[...] = dual_next
    xcount = sb_ref.shape[0]
    worst = jnp.max(jnp.abs(image_next[:ycount] - slack_next), axis=0, keepdims=True)
    z_ref[xcount:, :] = jnp.broadcast_to(worst, (8, LANES))
    vec = jnp.concatenate([dual_next, image_next[ycount:]], axis=0)
    z_ref[:xcount, :] = backward_sum(vec, gb_ref, sb_ref, w_ref, *scratch)


def residual_kernel(n_plane, *refs):
    z_refs, (primal_ref, d_ref, c_ref, out_ref) = refs[:n_plane], refs[n_plane:]
    xcount = d_ref.shape[0]
    total = tree(ref[:xcount, :] for ref in z_refs)
    primal = tree((ref[xcount:, :] for ref in z_refs), jnp.maximum)
    dvec = d_ref[...] * primal_ref[...] + total + c_ref[...]
    worst = jnp.max(jnp.abs(dvec), axis=0, keepdims=True)
    out_ref[...] = jnp.concatenate([primal[:4], jnp.broadcast_to(worst, (4, LANES))], axis=0)


VMEM_SPEC = pl.BlockSpec(memory_space=pltpu.VMEM)
SMEM_SPEC = pl.BlockSpec(memory_space=pltpu.SMEM)


def call(kernel, name, outs, args, scratch=(), scalar=False):
    specs = [SMEM_SPEC if scalar and i == 0 else VMEM_SPEC for i in range(len(args))]
    shapes = tuple(jax.ShapeDtypeStruct(s, F32) for s in outs)
    return pl.pallas_call(
        kernel,
        out_shape=shapes,
        in_specs=specs,
        out_specs=tuple(VMEM_SPEC for _ in outs),
        scratch_shapes=list(scratch),
        compiler_params=pltpu.CompilerParams(vmem_limit_bytes=VMEM_LIMIT),
        name=name,
    )(*args)


def swap(x, axis, size, distance):
    return lax.ppermute(x, axis, [(i, i ^ distance) for i in range(size)])


def exchange(x, axis, size, distances):
    return [x] + [swap(x, axis, size, m) for m in distances]


def local(n_row, n_col, *args):
    (
        constraint_tiles,
        constraint_rows,
        constraint_cols,
        factor_tiles,
        factor_rows,
        factor_cols,
        diag_cost,
        linear_cost,
        lower_bound,
        upper_bound,
        primal_start,
        slack_start,
        dual_start,
        penalty,
    ) = args
    width = constraint_tiles.shape[2]
    ctiles = constraint_tiles.reshape(-1, width, width)
    ftiles = factor_tiles.reshape(-1, width, width)
    acount, fcount = ctiles.shape[0], ftiles.shape[0]
    count = acount + fcount
    pairs = count // 2
    xcount = primal_start.shape[0]
    ycount = slack_start.shape[0]
    full = ycount + YG
    rho = penalty.reshape(1)

    def over_col(x):
        return exchange(x, "col", n_col, range(1, n_col))

    def over_row(x, op=jnp.add):
        chip = op(x, swap(x, "row", n_row, 1))
        return exchange(chip, "row", n_row, range(2, n_row, 2))

    xat = jnp.concatenate([constraint_cols.reshape(-1), factor_cols.reshape(-1)])
    yat = jnp.concatenate([constraint_rows.reshape(-1), ycount + factor_rows.reshape(-1)])
    part = jnp.arange(GROUP * count, dtype=jnp.int32) % GROUP

    def pick(at, size):
        place = jnp.where(part < 3, part * size + jnp.repeat(at, GROUP), -1)
        return (place[:, None] == jnp.arange(3 * size, dtype=jnp.int32)[None, :]).astype(BF16)

    def place(at, size):
        return (jnp.arange(size, dtype=jnp.int32)[:, None] == at[None, :]).astype(BF16)

    gf = pick(xat, xcount)
    gb = pick(yat, full)
    sb = place(jnp.concatenate([xat[0::2], xat[1::2]]), xcount)
    s_all = jnp.stack([place(at, full) for at in over_col(yat)])

    block = 8
    a_steps, f_steps = acount // block, fcount // block
    tiles, squares = pl.pallas_call(
        functools.partial(init_kernel, a_steps),
        grid=(a_steps + f_steps,),
        in_specs=[
            pl.BlockSpec((block, width, width), lambda i: (jnp.minimum(i, a_steps - 1), 0, 0)),
            pl.BlockSpec((block, width, width), lambda i: (jnp.maximum(i - a_steps, 0), 0, 0)),
        ],
        out_specs=(
            pl.BlockSpec((block // 2, 2 * width, 2 * width), lambda i: (i, 0, 0)),
            pl.BlockSpec((block, width), lambda i: (i, 0)),
        ),
        out_shape=(
            jax.ShapeDtypeStruct((pairs, 2 * width, 2 * width), BF16),
            jax.ShapeDtypeStruct((count, width), F32),
        ),
        compiler_params=pltpu.CompilerParams(vmem_limit_bytes=VMEM_LIMIT),
        name="split_tiles",
    )(ctiles, ftiles)

    scratch = (
        pltpu.VMEM((GROUP * count, 2 * width), BF16),
        pltpu.VMEM((GROUP * count, width), F32),
        pltpu.VMEM((GROUP * count, width), F32),
    )
    xs, ys, small = (xcount, width), (full, width), (8, width)
    sent, summed = (count + 8, width), (xcount + 8, width)

    (parts,) = call(first_forward_kernel, "first_forward", [sent], (primal_start, gf, tiles), scratch)
    z, y0 = call(
        functools.partial(first_backward_kernel, n_col, ycount, acount),
        "first_backward",
        [(2 * xcount, width), ys],
        (rho, *over_col(parts), s_all, gb, sb, tiles, squares, slack_start, dual_start),
        scratch,
        scalar=True,
    )
    zs = over_row(z)
    resid, u, precond, parts = call(
        functools.partial(second_forward_kernel, len(zs)),
        "second_forward",
        [xs, xs, xs, sent],
        (*zs, primal_start, diag_cost, linear_cost, gf, tiles),
        scratch,
    )
    v, yv = primal_start, y0
    p = yp = sc = alpha = None
    for step in range(CG):
        first, last = step == 0, step + 1 == CG
        state = (yv,) if first else (yp, yv, sc, alpha)
        mats = () if last else (gb, sb, tiles)
        z, yp, yv, sc = call(
            functools.partial(backward_kernel, n_col, ycount, first, last),
            "last_norm" if last else "backward",
            [small if last else summed, ys, ys, small],
            (rho, *over_col(parts), s_all, *state, *mats),
            () if last else scratch,
            scalar=True,
        )
        zs = over_row(z)
        if not last:
            p, v, resid, u, alpha, parts = call(
                functools.partial(forward_kernel, len(zs), first),
                "forward",
                [xs, xs, xs, xs, small, sent],
                (*zs, *(() if first else (p,)), u, v, resid, diag_cost, precond, sc, gf, tiles),
                scratch,
            )
    primal_next, slack_next, dual_next, z = call(
        functools.partial(final_kernel, len(zs), ycount),
        "final",
        [xs, (ycount, width), (ycount, width), summed],
        (rho, *zs, u, p, v, primal_start, sc, yp, yv, y0)
        + (slack_start, dual_start, lower_bound, upper_bound, gb, sb, tiles),
        scratch,
        scalar=True,
    )

    def join(a, b):
        is_sum = lax.broadcasted_iota(jnp.int32, a.shape, 0) < xcount
        return jnp.where(is_sum, a + b, jnp.maximum(a, b))

    zs = over_row(z, join)
    (worst,) = call(
        functools.partial(residual_kernel, len(zs)),
        "residuals",
        [small],
        (*zs, primal_next, diag_cost, linear_cost),
    )
    worst = tree(over_col(worst), jnp.maximum)
    return (primal_next, slack_next, dual_next, jnp.max(worst[:4]), jnp.max(worst[4:]))


def solution(mesh):
    placed = (
        P("row", "col", None, None),
        P("row", "col"),
        P("row", "col"),
        P("row", "col", None, None),
        P("row", "col"),
        P("row", "col"),
        P("col", None),
        P("col", None),
        P("row", None),
        P("row", None),
        P("col", None),
        P("row", None),
        P("row", None),
        P(),
    )
    return jax.shard_map(
        functools.partial(local, mesh.shape["row"], mesh.shape["col"]),
        mesh=mesh,
        in_specs=placed,
        out_specs=(P("col", None), P("row", None), P("row", None), P(), P()),
        check_vma=False,
    )
```

time: 1320 us -> 241 us (0.18)
  waiting for transfers between devices: 626 us -> 97.6 us
  matrix products: 266 us -> 0 us
  blocking collectives: 255 us -> 0 us
  starting transfers between devices: 1.94 us -> 70.9 us
  other arithmetic: 70.9 us -> 2.53 us
  Pallas kernels: 0 us -> 57.7 us
  local copies, waits for them, and re-layouts: 50.8 us -> 10 us
  between operations: 37.1 us -> 1.75 us
    psum x16 -> x0, waiting for transfers between devices: 626 us -> none  [the longest x8 426 us: reduce_rows(): return lax.psum(parts, 'row')]
    dot_general x70 -> x0, matrix products: 266 us -> none  [the longest x17 147 us: forward_tiles(): jnp.einsum('kij,kj->ki', tiles, jnp.take(vec, cols, axis=0), precision=HIGH)]
    psum x14 -> x0, blocking collectives: 215 us -> none  [the longest x8 140 us: products(): return lax.psum(parts, 'col')]
    ppermute x0 -> x59, waiting for transfers between devices: none -> 97.6 us  [swap(): return lax.ppermute(x, axis, [(i, i ^ distance) for i in range(size)])]
    ppermute x0 -> x59, starting transfers between devices: none -> 70.9 us  [swap(): return lax.ppermute(x, axis, [(i, i ^ distance) for i in range(size)])]
    pallas_call x0 -> x17, Pallas kernels: none -> 57.7 us  [the longest x16 55.1 us: call(): pl.pallas_call(kernel, out_shape=shapes, in_specs=specs, out_specs=tuple(...]
    gather x34 -> x0, local copies, waits for them, and re-layouts: 50.6 us -> none  [the longest x17 26.5 us: backward_tiles(): jnp.take(vec, rows, axis=0)]
    pmax x1 -> x0, blocking collectives: 39.5 us -> none  [local(): primal_res, dual_res = lax.pmax((primal_local, dual_local), ('row', 'col'))]
  transfers between devices with their start and end apart: 16 -> 59, of which waited for: 15 -> 44; matrix products, arithmetic and copies ran while one was open for 3% -> 1% of each run, Pallas kernels for 0% -> 0%
where the time goes in v1:
time: 241 us; the launch traced here: 240 us
  waiting for transfers between devices  97.6 us (40%)
  starting transfers between devices  70.9 us (29%)
  Pallas kernels  57.7 us (24%)
  local copies, waits for them, and re-layouts  10 us (4%)
  other arithmetic  2.53 us (1%)
    ppermute x59, waiting for transfers between devices, swap(): return lax.ppermute(x, axis, [(i, i ^ distance) for i in range(size)])  97.6 us
    ppermute x59, starting transfers between devices, swap(): return lax.ppermute(x, axis, [(i, i ^ distance) for i in range(size)])  70.9 us
    pallas_call x16, Pallas kernels, call(): pl.pallas_call(kernel, out_shape=shapes, in_specs=specs, out_specs=tuple(...  55.1 us
    unnamed x34, local copies, waits for them, and re-layouts  9.31 us
  transfers between devices with their start and end apart: 59, of which 44 were waited for; matrix products, arithmetic and copies ran while one was open for 1% of the time, Pallas kernels for 0%

profile of v1, /device:TPU:0, one launch (start us, length us, event | category | flops | bytes accessed | tf_op | source)
XLA Modules:
  0.0 240.5 jit_solution(16263419607985225050)
XLA Ops:
  1.8 2.8 %copy-done.3 = f32[96,1,128,128]{3,2,1,0:T(8,128)S(1)} copy-done((f32[96,1,128,128]{3,2,1,0:T(8,128)S(1)}, f32[96,1,128,128]{3,2,1,0:T(8,128)}, u32[]{:S(2)}) %copy-start.3) | copy-done | bytes 6291480
  4.6 1.9 copy-done.4
  6.5 2.6 %split_tiles.1 = (bf16[72,256,256]{2,1,0:T(8,128)(2,1)S(1)}, f32[144,128]{1,0:T(8,128)S(1)}) custom-call(f32[96,128,128]{2,1,0:T(8,128)S(1)} %bitcast.18, f32[48,128,128]{2,1,0:T(8,128)S(1)} %bitcast.19), custom_call_target="tpu_custom_call" | custom-call | tf_op jit(solution)/shard_map/split_tiles/pallas_call | solution.py:384
  9.2 3.9 %first_forward.1.refs_1_ = f32[152,128]{1,0:T(8,128)S(1)} custom-call(f32[256,128]{1,0:T(8,128)S(1)} %copy-done.5, bf16[576,768]{1,0:T(8,128)(2,1)S(1)} %fusion.gf_ref.refs_7_.refs_10_.refs_11_, bf16[72,256,256]{2,1,0:T(8,128)(2,1)S(1)} %get-tuple-element.70.w_ref.refs_8_.refs_9_.refs_11_.refs_12_.refs_19_), custom_call_target="tpu_custom_call" | custom-call | tf_op jit(solution)/shard_map/first_forward/pallas_call | solution.py:312
  13.1 3.1 %collective-permute-start = (f32[152,128]{1,0:T(8,128)S(1)}, f32[152,128]{1,0:T(8,128)S(1)}, u32[]{:S(2)}, u32[]{:S(2)}) collective-permute-start(f32[152,128]{1,0:T(8,128)S(1)} %first_forward.1.refs_1_), channel_id=1, source_target_pairs={{0,1},{1,0},{2,3},{3,2},{4,5},{5,4},{6,7},{7,6},{8,9},{9,8},{10,11... | collective-permute-start | bytes 233480 | tf_op jit(solution)/shard_map/ppermute | solution.py:324
  16.2 2.6 %collective-permute-start.1 = (f32[152,128]{1,0:T(8,128)S(1)}, f32[152,128]{1,0:T(8,128)S(1)}, u32[]{:S(2)}, u32[]{:S(2)}) collective-permute-start(f32[152,128]{1,0:T(8,128)S(1)} %first_forward.1.refs_1_), channel_id=1, source_target_pairs={{0,2},{1,3},{2,0},{3,1},{4,6},{5,7},{6,4},{7,5},{8,10},{9,11},{10,... | collective-permute-start | bytes 233480 | tf_op jit(solution)/shard_map/ppermute | solution.py:324
  18.9 3.8 %collective-permute-start.5 = (s32[144]{0:T(256)S(1)}, s32[144]{0:T(256)S(1)}, u32[]{:S(2)}, u32[]{:S(2)}) collective-permute-start(s32[144]{0:T(256)S(1)} %pad_add_fusion.1), channel_id=1, source_target_pairs={{0,3},{1,2},{2,1},{3,0},{4,7},{5,6},{6,5},{7,4},{8,11},{9,10},{10,... | collective-permute-start | bytes 1736 | tf_op jit(solution)/shard_map/ppermute | solution.py:324
  29.0 3.7 %copy-done.1 = bf16[72,256,256]{2,1,0:T(8,128)(2,1)S(1)} copy-done((bf16[72,256,256]{2,1,0:T(8,128)(2,1)S(1)}, bf16[72,256,256]{2,1,0:T(8,128)(2,1)}, u32[]{:S(2)}) %copy-start.1) | copy-done | bytes 9437208
  32.7 4.0 %first_backward.1 = (f32[512,128]{1,0:T(8,128)S(1)}, f32[256,128]{1,0:T(8,128)S(1)}) custom-call(f32[1]{0:T(128)} %bitcast.8.refs_0_, f32[152,128]{1,0:T(8,128)S(1)} %first_forward.1.refs_1_, f32[152,128]{1,0:T(8,128)S(1)} %collective-permute-done.refs_2_, f32[152,128]{1,0:T(8,128)S(1)} %collective-permute-done.1.refs_3_, ...), custom_call_target="tpu_custom_call" | custom-call | tf_op jit(solution)/shard_map/first_backward/pallas_call | solution.py:312
  41.9 5.7 %collective-permute-done.7.refs_1_ = f32[512,128]{1,0:T(8,128)S(1)} collective-permute-done((f32[512,128]{1,0:T(8,128)S(1)}, f32[512,128]{1,0:T(8,128)S(1)}, u32[]{:S(2)}, u32[]{:S(2)}) %collective-permute-start.7) | collective-permute-done | bytes 262176 | tf_op jit(solution)/shard_map/ppermute | solution.py:324
  47.6 6.0 %collective-permute-done.8.refs_2_ = f32[512,128]{1,0:T(8,128)S(1)} collective-permute-done((f32[512,128]{1,0:T(8,128)S(1)}, f32[512,128]{1,0:T(8,128)S(1)}, u32[]{:S(2)}, u32[]{:S(2)}) %collective-permute-start.8) | collective-permute-done | bytes 262176 | tf_op jit(solution)/shard_map/ppermute | solution.py:324
  53.6 4.0 %second_forward.1 = (f32[256,128]{1,0:T(8,128)S(1)}, f32[256,128]{1,0:T(8,128)S(1)}, f32[256,128]{1,0:T(8,128)S(1)}, f32[152,128]{1,0:T(8,128)S(1)}) custom-call(f32[512,128]{1,0:T(8,128)S(1)} %add.72.refs_0_, f32[512,128]{1,0:T(8,128)S(1)} %collective-permute-done.7.refs_1_, f32[512,128]{1,0:T(8,128)S(1)} %collective-permute-done.8.refs_2_, ...), custom_call_target="tpu_custom_call" | custom-call | tf_op jit(solution)/shard_map/second_forward/pallas_call | solution.py:312
  59.1 2.0 collective-permute-start.11
  62.8 3.6 %collective-permute-done.11.refs_3_ = f32[152,128]{1,0:T(8,128)S(1)} collective-permute-done((f32[152,128]{1,0:T(8,128)S(1)}, f32[152,128]{1,0:T(8,128)S(1)}, u32[]{:S(2)}, u32[]{:S(2)}) %collective-permute-start.11) | collective-permute-done | bytes 77856 | tf_op jit(solution)/shard_map/ppermute | solution.py:324
  67.4 3.9 %backward.5 = (f32[264,128]{1,0:T(8,128)S(1)}, f32[256,128]{1,0:T(8,128)S(1)}, f32[256,128]{1,0:T(8,128)S(1)}, f32[8,128]{1,0:T(8,128)S(1)}) custom-call(f32[1]{0:T(128)} %bitcast.9.refs_0_, f32[152,128]{1,0:T(8,128)S(1)} %get-tuple-element.73.refs_1_, f32[152,128]{1,0:T(8,128)S(1)} %collective-permute-done.10.refs_2_, ...), custom_call_target="tpu_custom_call" | custom-call | tf_op jit(solution)/shard_map/backward/pallas_call | solution.py:312
  76.3 2.9 %collective-permute-done.14.refs_1_ = f32[264,128]{1,0:T(8,128)S(1)} collective-permute-done((f32[264,128]{1,0:T(8,128)S(1)}, f32[264,128]{1,0:T(8,128)S(1)}, u32[]{:S(2)}, u32[]{:S(2)}) %collective-permute-start.14) | collective-permute-done | bytes 135200 | tf_op jit(solution)/shard_map/ppermute | solution.py:324
  82.3 4.2 %forward.5 = (f32[256,128]{1,0:T(8,128)S(1)}, f32[256,128]{1,0:T(8,128)S(1)}, f32[256,128]{1,0:T(8,128)S(1)}, f32[256,128]{1,0:T(8,128)S(1)}, f32[8,128]{1,0:T(8,128)S(1)}, /*index=5*/f32[152,128]{1,0:T(8,128)S(1)}) custom-call(f32[264,128]{1,0:T(8,128)S(1)} %add.73.refs_0_, f32[264,128]{1,0:T(8,128)S(1)} %collective-permute-done.14.refs_1_, ...), custom_call_target="tpu_custom_call" | custom-call | tf_op jit(solution)/shard_map/forward/pallas_call | solution.py:312
  91.7 4.3 %collective-permute-done.18.refs_3_ = f32[152,128]{1,0:T(8,128)S(1)} collective-permute-done((f32[152,128]{1,0:T(8,128)S(1)}, f32[152,128]{1,0:T(8,128)S(1)}, u32[]{:S(2)}, u32[]{:S(2)}) %collective-permute-start.18) | collective-permute-done | bytes 77856 | tf_op jit(solution)/shard_map/ppermute | solution.py:324
  96.0 3.5 %backward.6 = (f32[264,128]{1,0:T(8,128)S(1)}, f32[256,128]{1,0:T(8,128)S(1)}, f32[256,128]{1,0:T(8,128)S(1)}, f32[8,128]{1,0:T(8,128)S(1)}) custom-call(f32[1]{0:T(128)} %bitcast.10.refs_0_, f32[152,128]{1,0:T(8,128)S(1)} %get-tuple-element.80.refs_1_, f32[152,128]{1,0:T(8,128)S(1)} %collective-permute-done.17.refs_2_, ...), custom_call_target="tpu_custom_call" | custom-call | tf_op jit(solution)/shard_map/backward/pallas_call | solution.py:312
  104.5 3.0 %collective-permute-done.21.refs_1_ = f32[264,128]{1,0:T(8,128)S(1)} collective-permute-done((f32[264,128]{1,0:T(8,128)S(1)}, f32[264,128]{1,0:T(8,128)S(1)}, u32[]{:S(2)}, u32[]{:S(2)}) %collective-permute-start.21) | collective-permute-done | bytes 135200 | tf_op jit(solution)/shard_map/ppermute | solution.py:324
  107.5 2.3 collective-permute-done.22.refs_2_
  109.8 4.2 %forward.6 = (f32[256,128]{1,0:T(8,128)S(1)}, f32[256,128]{1,0:T(8,128)S(1)}, f32[256,128]{1,0:T(8,128)S(1)}, f32[256,128]{1,0:T(8,128)S(1)}, f32[8,128]{1,0:T(8,128)S(1)}, /*index=5*/f32[152,128]{1,0:T(8,128)S(1)}) custom-call(f32[264,128]{1,0:T(8,128)S(1)} %add.74.refs_0_, f32[264,128]{1,0:T(8,128)S(1)} %collective-permute-done.21.refs_1_, ...), custom_call_target="tpu_custom_call" | custom-call | tf_op jit(solution)/shard_map/forward/pallas_call | solution.py:312
  119.1 4.4 %collective-permute-done.25.refs_3_ = f32[152,128]{1,0:T(8,128)S(1)} collective-permute-done((f32[152,128]{1,0:T(8,128)S(1)}, f32[152,128]{1,0:T(8,128)S(1)}, u32[]{:S(2)}, u32[]{:S(2)}) %collective-permute-start.25) | collective-permute-done | bytes 77856 | tf_op jit(solution)/shard_map/ppermute | solution.py:324
  123.5 3.5 %backward.7 = (f32[264,128]{1,0:T(8,128)S(1)}, f32[256,128]{1,0:T(8,128)S(1)}, f32[256,128]{1,0:T(8,128)S(1)}, f32[8,128]{1,0:T(8,128)S(1)}) custom-call(f32[1]{0:T(128)} %bitcast.11.refs_0_, f32[152,128]{1,0:T(8,128)S(1)} %get-tuple-element.90.refs_1_, f32[152,128]{1,0:T(8,128)S(1)} %collective-permute-done.24.refs_2_, ...), custom_call_target="tpu_custom_call" | custom-call | tf_op jit(solution)/shard_map/backward/pallas_call | solution.py:312
  132.0 2.7 %collective-permute-done.28.refs_1_ = f32[264,128]{1,0:T(8,128)S(1)} collective-permute-done((f32[264,128]{1,0:T(8,128)S(1)}, f32[264,128]{1,0:T(8,128)S(1)}, u32[]{:S(2)}, u32[]{:S(2)}) %collective-permute-start.28) | collective-permute-done | bytes 135200 | tf_op jit(solution)/shard_map/ppermute | solution.py:324
  134.7 3.6 %collective-permute-done.29.refs_2_ = f32[264,128]{1,0:T(8,128)S(1)} collective-permute-done((f32[264,128]{1,0:T(8,128)S(1)}, f32[264,128]{1,0:T(8,128)S(1)}, u32[]{:S(2)}, u32[]{:S(2)}) %collective-permute-start.29) | collective-permute-done | bytes 135200 | tf_op jit(solution)/shard_map/ppermute | solution.py:324
  138.3 4.2 %forward.7 = (f32[256,128]{1,0:T(8,128)S(1)}, f32[256,128]{1,0:T(8,128)S(1)}, f32[256,128]{1,0:T(8,128)S(1)}, f32[256,128]{1,0:T(8,128)S(1)}, f32[8,128]{1,0:T(8,128)S(1)}, /*index=5*/f32[152,128]{1,0:T(8,128)S(1)}) custom-call(f32[264,128]{1,0:T(8,128)S(1)} %add.75.refs_0_, f32[264,128]{1,0:T(8,128)S(1)} %collective-permute-done.28.refs_1_, ...), custom_call_target="tpu_custom_call" | custom-call | tf_op jit(solution)/shard_map/forward/pallas_call | solution.py:312
  147.7 4.4 %collective-permute-done.32.refs_3_ = f32[152,128]{1,0:T(8,128)S(1)} collective-permute-done((f32[152,128]{1,0:T(8,128)S(1)}, f32[152,128]{1,0:T(8,128)S(1)}, u32[]{:S(2)}, u32[]{:S(2)}) %collective-permute-start.32) | collective-permute-done | bytes 77856 | tf_op jit(solution)/shard_map/ppermute | solution.py:324
  152.1 3.5 %backward.8 = (f32[264,128]{1,0:T(8,128)S(1)}, f32[256,128]{1,0:T(8,128)S(1)}, f32[256,128]{1,0:T(8,128)S(1)}, f32[8,128]{1,0:T(8,128)S(1)}) custom-call(f32[1]{0:T(128)} %bitcast.12.refs_0_, f32[152,128]{1,0:T(8,128)S(1)} %get-tuple-element.100.refs_1_, f32[152,128]{1,0:T(8,128)S(1)} %collective-permute-done.31.refs_2_, ...), custom_call_target="tpu_custom_call" | custom-call | tf_op jit(solution)/shard_map/backward/pallas_call | solution.py:312
  157.3 1.7 collective-permute-start.36
  160.6 3.0 %collective-permute-done.35.refs_1_ = f32[264,128]{1,0:T(8,128)S(1)} collective-permute-done((f32[264,128]{1,0:T(8,128)S(1)}, f32[264,128]{1,0:T(8,128)S(1)}, u32[]{:S(2)}, u32[]{:S(2)}) %collective-permute-start.35) | collective-permute-done | bytes 135200 | tf_op jit(solution)/shard_map/ppermute | solution.py:324
  163.5 2.2 collective-permute-done.36.refs_2_
  165.7 4.2 %forward.8 = (f32[256,128]{1,0:T(8,128)S(1)}, f32[256,128]{1,0:T(8,128)S(1)}, f32[256,128]{1,0:T(8,128)S(1)}, f32[256,128]{1,0:T(8,128)S(1)}, f32[8,128]{1,0:T(8,128)S(1)}, /*index=5*/f32[152,128]{1,0:T(8,128)S(1)}) custom-call(f32[264,128]{1,0:T(8,128)S(1)} %add.76.refs_0_, f32[264,128]{1,0:T(8,128)S(1)} %collective-permute-done.35.refs_1_, ...), custom_call_target="tpu_custom_call" | custom-call | tf_op jit(solution)/shard_map/forward/pallas_call | solution.py:312
  175.0 4.5 %collective-permute-done.39.refs_3_ = f32[152,128]{1,0:T(8,128)S(1)} collective-permute-done((f32[152,128]{1,0:T(8,128)S(1)}, f32[152,128]{1,0:T(8,128)S(1)}, u32[]{:S(2)}, u32[]{:S(2)}) %collective-permute-start.39) | collective-permute-done | bytes 77856 | tf_op jit(solution)/shard_map/ppermute | solution.py:324
  179.5 3.5 %backward.9 = (f32[264,128]{1,0:T(8,128)S(1)}, f32[256,128]{1,0:T(8,128)S(1)}, f32[256,128]{1,0:T(8,128)S(1)}, f32[8,128]{1,0:T(8,128)S(1)}) custom-call(f32[1]{0:T(128)} %bitcast.13.refs_0_, f32[152,128]{1,0:T(8,128)S(1)} %get-tuple-element.110.refs_1_, f32[152,128]{1,0:T(8,128)S(1)} %collective-permute-done.38.refs_2_, ...), custom_call_target="tpu_custom_call" | custom-call | tf_op jit(solution)/shard_map/backward/pallas_call | solution.py:312
  186.3 1.7 collective-permute-start.44
  188.0 2.6 %collective-permute-done.42.refs_1_ = f32[264,128]{1,0:T(8,128)S(1)} collective-permute-done((f32[264,128]{1,0:T(8,128)S(1)}, f32[264,128]{1,0:T(8,128)S(1)}, u32[]{:S(2)}, u32[]{:S(2)}) %collective-permute-start.42) | collective-permute-done | bytes 135200 | tf_op jit(solution)/shard_map/ppermute | solution.py:324
  190.5 3.8 %collective-permute-done.43.refs_2_ = f32[264,128]{1,0:T(8,128)S(1)} collective-permute-done((f32[264,128]{1,0:T(8,128)S(1)}, f32[264,128]{1,0:T(8,128)S(1)}, u32[]{:S(2)}, u32[]{:S(2)}) %collective-permute-start.43) | collective-permute-done | bytes 135200 | tf_op jit(solution)/shard_map/ppermute | solution.py:324
  194.3 4.4 %forward.9 = (f32[256,128]{1,0:T(8,128)S(1)}, f32[256,128]{1,0:T(8,128)S(1)}, f32[256,128]{1,0:T(8,128)}, f32[256,128]{1,0:T(8,128)S(1)}, f32[8,128]{1,0:T(8,128)S(1)}, /*index=5*/f32[152,128]{1,0:T(8,128)S(1)}) custom-call(f32[264,128]{1,0:T(8,128)S(1)} %add.77.refs_0_, f32[264,128]{1,0:T(8,128)S(1)} %collective-permute-done.42.refs_1_, ...), custom_call_target="tpu_custom_call" | custom-call | tf_op jit(solution)/shard_map/forward/pallas_call | solution.py:312
  200.1 1.7 collective-permute-start.46
  203.9 4.3 %collective-permute-done.46.refs_3_ = f32[152,128]{1,0:T(8,128)S(1)} collective-permute-done((f32[152,128]{1,0:T(8,128)S(1)}, f32[152,128]{1,0:T(8,128)S(1)}, u32[]{:S(2)}, u32[]{:S(2)}) %collective-permute-start.46) | collective-permute-done | bytes 77856 | tf_op jit(solution)/shard_map/ppermute | solution.py:324
  210.2 1.9 collective-permute-start.50
  213.8 2.8 %collective-permute-done.51.refs_4_ = f32[8,128]{1,0:T(8,128)S(1)} collective-permute-done((f32[8,128]{1,0:T(8,128)S(1)}, f32[8,128]{1,0:T(8,128)S(1)}, u32[]{:S(2)}, u32[]{:S(2)}) %collective-permute-start.51) | collective-permute-done | bytes 4128 | tf_op jit(solution)/shard_map/ppermute | solution.py:324
  216.6 3.6 %final.1 = (f32[256,128]{1,0:T(8,128)}, f32[192,128]{1,0:T(8,128)}, f32[192,128]{1,0:T(8,128)}, f32[264,128]{1,0:T(8,128)S(1)}) custom-call(f32[1]{0:T(128)} %bitcast.15.refs_0_, f32[8,128]{1,0:T(8,128)S(1)} %add.78.refs_1_, f32[8,128]{1,0:T(8,128)S(1)} %collective-permute-done.49.refs_2_, f32[8,128]{1,0:T(8,128)S(1)} %collective-permute-done.50.refs_3_, ...), custom_call_target="tpu_custom_call" | custom-call | tf_op jit(solution)/shard_map/final/pallas_call | solution.py:312
  222.1 1.7 collective-permute-start.54
  225.3 3.0 %collective-permute-done.53.refs_1_ = f32[264,128]{1,0:T(8,128)S(1)} collective-permute-done((f32[264,128]{1,0:T(8,128)S(1)}, f32[264,128]{1,0:T(8,128)S(1)}, u32[]{:S(2)}, u32[]{:S(2)}) %collective-permute-start.53) | collective-permute-done | bytes 135200 | tf_op jit(solution)/shard_map/ppermute | solution.py:324
  228.2 2.2 collective-permute-done.54.refs_2_
  237.3 2.5 %collective-permute-done.58 = f32[8,128]{1,0:T(8,128)S(1)} collective-permute-done((f32[8,128]{1,0:T(8,128)S(1)}, f32[8,128]{1,0:T(8,128)S(1)}, u32[]{:S(2)}, u32[]{:S(2)}) %collective-permute-start.58) | collective-permute-done | bytes 4128 | tf_op jit(solution)/shard_map/ppermute | solution.py:324
  (153 shorter events, 79.6 us)
Async XLA Ops:
  13.1 15.8 %collective-permute-start = (f32[152,128]{1,0:T(8,128)S(1)}, f32[152,128]{1,0:T(8,128)S(1)}, u32[]{:S(2)}, u32[]{:S(2)}) collective-permute-start(f32[152,128]{1,0:T(8,128)S(1)} %first_forward.1.refs_1_), channel_id=1, source_target_pairs={{0,1},{1,0},{2,3},{3,2},{4,5},{5,4},{6,7},{7,6},{8,9},{9,8},{10,11... | collective-permute-start | bytes 233480 | tf_op jit(solution)/shard_map/ppermute | solution.py:324
  16.2 12.7 %collective-permute-start.1 = (f32[152,128]{1,0:T(8,128)S(1)}, f32[152,128]{1,0:T(8,128)S(1)}, u32[]{:S(2)}, u32[]{:S(2)}) collective-permute-start(f32[152,128]{1,0:T(8,128)S(1)} %first_forward.1.refs_1_), channel_id=1, source_target_pairs={{0,2},{1,3},{2,0},{3,1},{4,6},{5,7},{6,4},{7,5},{8,10},{9,11},{10,... | collective-permute-start | bytes 233480 | tf_op jit(solution)/shard_map/ppermute | solution.py:324
  18.8 10.1 %collective-permute-start.2 = (f32[152,128]{1,0:T(8,128)S(1)}, f32[152,128]{1,0:T(8,128)S(1)}, u32[]{:S(2)}, u32[]{:S(2)}) collective-permute-start(f32[152,128]{1,0:T(8,128)S(1)} %first_forward.1.refs_1_), channel_id=1, source_target_pairs={{0,3},{1,2},{2,1},{3,0},{4,7},{5,6},{6,5},{7,4},{8,11},{9,10},{10,... | collective-permute-start | bytes 233480 | tf_op jit(solution)/shard_map/ppermute | solution.py:324
  18.9 6.3 %collective-permute-start.5 = (s32[144]{0:T(256)S(1)}, s32[144]{0:T(256)S(1)}, u32[]{:S(2)}, u32[]{:S(2)}) collective-permute-start(s32[144]{0:T(256)S(1)} %pad_add_fusion.1), channel_id=1, source_target_pairs={{0,3},{1,2},{2,1},{3,0},{4,7},{5,6},{6,5},{7,4},{8,11},{9,10},{10,... | collective-permute-start | bytes 1736 | tf_op jit(solution)/shard_map/ppermute | solution.py:324
  22.7 4.5 %collective-permute-start.4 = (s32[144]{0:T(256)S(1)}, s32[144]{0:T(256)S(1)}, u32[]{:S(2)}, u32[]{:S(2)}) collective-permute-start(s32[144]{0:T(256)S(1)} %pad_add_fusion.1), channel_id=1, source_target_pairs={{0,2},{1,3},{2,0},{3,1},{4,6},{5,7},{6,4},{7,5},{8,10},{9,11},{10,... | collective-permute-start | bytes 1736 | tf_op jit(solution)/shard_map/ppermute | solution.py:324
  38.3 9.2 %collective-permute-start.7 = (f32[512,128]{1,0:T(8,128)S(1)}, f32[512,128]{1,0:T(8,128)S(1)}, u32[]{:S(2)}, u32[]{:S(2)}) collective-permute-start(f32[512,128]{1,0:T(8,128)S(1)} %add.72.refs_0_), channel_id=1, source_target_pairs={{0,8},{4,12},{8,0},{12,4},{16,24},{20,28},{24,16},{28,20},{1,9},{5... | collective-permute-start | bytes 786440 | tf_op jit(solution)/shard_map/ppermute | solution.py:324
  39.9 13.7 %collective-permute-start.8 = (f32[512,128]{1,0:T(8,128)S(1)}, f32[512,128]{1,0:T(8,128)S(1)}, u32[]{:S(2)}, u32[]{:S(2)}) collective-permute-start(f32[512,128]{1,0:T(8,128)S(1)} %add.72.refs_0_), channel_id=1, source_target_pairs={{0,16},{4,20},{8,24},{12,28},{16,0},{20,4},{24,8},{28,12},{1,17},{... | collective-permute-start | bytes 786440 | tf_op jit(solution)/shard_map/ppermute | solution.py:324
  41.4 12.2 %collective-permute-start.9 = (f32[512,128]{1,0:T(8,128)S(1)}, f32[512,128]{1,0:T(8,128)S(1)}, u32[]{:S(2)}, u32[]{:S(2)}) collective-permute-start(f32[512,128]{1,0:T(8,128)S(1)} %add.72.refs_0_), channel_id=1, source_target_pairs={{0,24},{4,28},{8,16},{12,20},{16,8},{20,12},{24,0},{28,4},{1,25},{... | collective-permute-start | bytes 786440 | tf_op jit(solution)/shard_map/ppermute | solution.py:324
  57.6 5.2 %collective-permute-start.10 = (f32[152,128]{1,0:T(8,128)S(1)}, f32[152,128]{1,0:T(8,128)S(1)}, u32[]{:S(2)}, u32[]{:S(2)}) collective-permute-start(f32[152,128]{1,0:T(8,128)S(1)} %get-tuple-element.73.refs_1_), channel_id=1, source_target_pairs={{0,1},{1,0},{2,3},{3,2},{4,5},{5,4},{6,7},{7,6},{8,9},{9,8},{10,11... | collective-permute-start | bytes 233480 | tf_op jit(solution)/shard_map/ppermute | solution.py:324
  59.1 7.3 %collective-permute-start.11 = (f32[152,128]{1,0:T(8,128)S(1)}, f32[152,128]{1,0:T(8,128)S(1)}, u32[]{:S(2)}, u32[]{:S(2)}) collective-permute-start(f32[152,128]{1,0:T(8,128)S(1)} %get-tuple-element.73.refs_1_), channel_id=1, source_target_pairs={{0,2},{1,3},{2,0},{3,1},{4,6},{5,7},{6,4},{7,5},{8,10},{9,11},{10,... | collective-permute-start | bytes 233480 | tf_op jit(solution)/shard_map/ppermute | solution.py:324
  61.1 6.3 %collective-permute-start.12 = (f32[152,128]{1,0:T(8,128)S(1)}, f32[152,128]{1,0:T(8,128)S(1)}, u32[]{:S(2)}, u32[]{:S(2)}) collective-permute-start(f32[152,128]{1,0:T(8,128)S(1)} %get-tuple-element.73.refs_1_), channel_id=1, source_target_pairs={{0,3},{1,2},{2,1},{3,0},{4,7},{5,6},{6,5},{7,4},{8,11},{9,10},{10,... | collective-permute-start | bytes 233480 | tf_op jit(solution)/shard_map/ppermute | solution.py:324
  72.8 6.5 %collective-permute-start.14 = (f32[264,128]{1,0:T(8,128)S(1)}, f32[264,128]{1,0:T(8,128)S(1)}, u32[]{:S(2)}, u32[]{:S(2)}) collective-permute-start(f32[264,128]{1,0:T(8,128)S(1)} %add.73.refs_0_), channel_id=1, source_target_pairs={{0,8},{4,12},{8,0},{12,4},{16,24},{20,28},{24,16},{28,20},{1,9},{5... | collective-permute-start | bytes 405512 | tf_op jit(solution)/shard_map/ppermute | solution.py:324
  74.0 6.6 %collective-permute-start.15 = (f32[264,128]{1,0:T(8,128)S(1)}, f32[264,128]{1,0:T(8,128)S(1)}, u32[]{:S(2)}, u32[]{:S(2)}) collective-permute-start(f32[264,128]{1,0:T(8,128)S(1)} %add.73.refs_0_), channel_id=1, source_target_pairs={{0,16},{4,20},{8,24},{12,28},{16,0},{20,4},{24,8},{28,12},{1,17},{... | collective-permute-start | bytes 405512 | tf_op jit(solution)/shard_map/ppermute | solution.py:324
  74.9 7.4 %collective-permute-start.16 = (f32[264,128]{1,0:T(8,128)S(1)}, f32[264,128]{1,0:T(8,128)S(1)}, u32[]{:S(2)}, u32[]{:S(2)}) collective-permute-start(f32[264,128]{1,0:T(8,128)S(1)} %add.73.refs_0_), channel_id=1, source_target_pairs={{0,24},{4,28},{8,16},{12,20},{16,8},{20,12},{24,0},{28,4},{1,25},{... | collective-permute-start | bytes 405512 | tf_op jit(solution)/shard_map/ppermute | solution.py:324
  86.5 5.2 %collective-permute-start.17 = (f32[152,128]{1,0:T(8,128)S(1)}, f32[152,128]{1,0:T(8,128)S(1)}, u32[]{:S(2)}, u32[]{:S(2)}) collective-permute-start(f32[152,128]{1,0:T(8,128)S(1)} %get-tuple-element.80.refs_1_), channel_id=1, source_target_pairs={{0,1},{1,0},{2,3},{3,2},{4,5},{5,4},{6,7},{7,6},{8,9},{9,8},{10,11... | collective-permute-start | bytes 233480 | tf_op jit(solution)/shard_map/ppermute | solution.py:324
  87.9 8.1 %collective-permute-start.18 = (f32[152,128]{1,0:T(8,128)S(1)}, f32[152,128]{1,0:T(8,128)S(1)}, u32[]{:S(2)}, u32[]{:S(2)}) collective-permute-start(f32[152,128]{1,0:T(8,128)S(1)} %get-tuple-element.80.refs_1_), channel_id=1, source_target_pairs={{0,2},{1,3},{2,0},{3,1},{4,6},{5,7},{6,4},{7,5},{8,10},{9,11},{10,... | collective-permute-start | bytes 233480 | tf_op jit(solution)/shard_map/ppermute | solution.py:324
  89.6 6.5 %collective-permute-start.19 = (f32[152,128]{1,0:T(8,128)S(1)}, f32[152,128]{1,0:T(8,128)S(1)}, u32[]{:S(2)}, u32[]{:S(2)}) collective-permute-start(f32[152,128]{1,0:T(8,128)S(1)} %get-tuple-element.80.refs_1_), channel_id=1, source_target_pairs={{0,3},{1,2},{2,1},{3,0},{4,7},{5,6},{6,5},{7,4},{8,11},{9,10},{10,... | collective-permute-start | bytes 233480 | tf_op jit(solution)/shard_map/ppermute | solution.py:324
  101.0 6.5 %collective-permute-start.21 = (f32[264,128]{1,0:T(8,128)S(1)}, f32[264,128]{1,0:T(8,128)S(1)}, u32[]{:S(2)}, u32[]{:S(2)}) collective-permute-start(f32[264,128]{1,0:T(8,128)S(1)} %add.74.refs_0_), channel_id=1, source_target_pairs={{0,8},{4,12},{8,0},{12,4},{16,24},{20,28},{24,16},{28,20},{1,9},{5... | collective-permute-start | bytes 405512 | tf_op jit(solution)/shard_map/ppermute | solution.py:324
  101.5 8.3 %collective-permute-start.22 = (f32[264,128]{1,0:T(8,128)S(1)}, f32[264,128]{1,0:T(8,128)S(1)}, u32[]{:S(2)}, u32[]{:S(2)}) collective-permute-start(f32[264,128]{1,0:T(8,128)S(1)} %add.74.refs_0_), channel_id=1, source_target_pairs={{0,16},{4,20},{8,24},{12,28},{16,0},{20,4},{24,8},{28,12},{1,17},{... | collective-permute-start | bytes 405512 | tf_op jit(solution)/shard_map/ppermute | solution.py:324
  103.0 6.7 %collective-permute-start.23 = (f32[264,128]{1,0:T(8,128)S(1)}, f32[264,128]{1,0:T(8,128)S(1)}, u32[]{:S(2)}, u32[]{:S(2)}) collective-permute-start(f32[264,128]{1,0:T(8,128)S(1)} %add.74.refs_0_), channel_id=1, source_target_pairs={{0,24},{4,28},{8,16},{12,20},{16,8},{20,12},{24,0},{28,4},{1,25},{... | collective-permute-start | bytes 405512 | tf_op jit(solution)/shard_map/ppermute | solution.py:324
  113.9 5.2 %collective-permute-start.24 = (f32[152,128]{1,0:T(8,128)S(1)}, f32[152,128]{1,0:T(8,128)S(1)}, u32[]{:S(2)}, u32[]{:S(2)}) collective-permute-start(f32[152,128]{1,0:T(8,128)S(1)} %get-tuple-element.90.refs_1_), channel_id=1, source_target_pairs={{0,1},{1,0},{2,3},{3,2},{4,5},{5,4},{6,7},{7,6},{8,9},{9,8},{10,11... | collective-permute-start | bytes 233480 | tf_op jit(solution)/shard_map/ppermute | solution.py:324
  115.4 8.2 %collective-permute-start.25 = (f32[152,128]{1,0:T(8,128)S(1)}, f32[152,128]{1,0:T(8,128)S(1)}, u32[]{:S(2)}, u32[]{:S(2)}) collective-permute-start(f32[152,128]{1,0:T(8,128)S(1)} %get-tuple-element.90.refs_1_), channel_id=1, source_target_pairs={{0,2},{1,3},{2,0},{3,1},{4,6},{5,7},{6,4},{7,5},{8,10},{9,11},{10,... | collective-permute-start | bytes 233480 | tf_op jit(solution)/shard_map/ppermute | solution.py:324
  117.0 6.5 %collective-permute-start.26 = (f32[152,128]{1,0:T(8,128)S(1)}, f32[152,128]{1,0:T(8,128)S(1)}, u32[]{:S(2)}, u32[]{:S(2)}) collective-permute-start(f32[152,128]{1,0:T(8,128)S(1)} %get-tuple-element.90.refs_1_), channel_id=1, source_target_pairs={{0,3},{1,2},{2,1},{3,0},{4,7},{5,6},{6,5},{7,4},{8,11},{9,10},{10,... | collective-permute-start | bytes 233480 | tf_op jit(solution)/shard_map/ppermute | solution.py:324
  128.5 6.2 %collective-permute-start.28 = (f32[264,128]{1,0:T(8,128)S(1)}, f32[264,128]{1,0:T(8,128)S(1)}, u32[]{:S(2)}, u32[]{:S(2)}) collective-permute-start(f32[264,128]{1,0:T(8,128)S(1)} %add.75.refs_0_), channel_id=1, source_target_pairs={{0,8},{4,12},{8,0},{12,4},{16,24},{20,28},{24,16},{28,20},{1,9},{5... | collective-permute-start | bytes 405512 | tf_op jit(solution)/shard_map/ppermute | solution.py:324
  130.0 8.3 %collective-permute-start.29 = (f32[264,128]{1,0:T(8,128)S(1)}, f32[264,128]{1,0:T(8,128)S(1)}, u32[]{:S(2)}, u32[]{:S(2)}) collective-permute-start(f32[264,128]{1,0:T(8,128)S(1)} %add.75.refs_0_), channel_id=1, source_target_pairs={{0,16},{4,20},{8,24},{12,28},{16,0},{20,4},{24,8},{28,12},{1,17},{... | collective-permute-start | bytes 405512 | tf_op jit(solution)/shard_map/ppermute | solution.py:324
  130.4 7.9 %collective-permute-start.30 = (f32[264,128]{1,0:T(8,128)S(1)}, f32[264,128]{1,0:T(8,128)S(1)}, u32[]{:S(2)}, u32[]{:S(2)}) collective-permute-start(f32[264,128]{1,0:T(8,128)S(1)} %add.75.refs_0_), channel_id=1, source_target_pairs={{0,24},{4,28},{8,16},{12,20},{16,8},{20,12},{24,0},{28,4},{1,25},{... | collective-permute-start | bytes 405512 | tf_op jit(solution)/shard_map/ppermute | solution.py:324
  142.5 5.2 %collective-permute-start.31 = (f32[152,128]{1,0:T(8,128)S(1)}, f32[152,128]{1,0:T(8,128)S(1)}, u32[]{:S(2)}, u32[]{:S(2)}) collective-permute-start(f32[152,128]{1,0:T(8,128)S(1)} %get-tuple-element.100.refs_1_), channel_id=1, source_target_pairs={{0,1},{1,0},{2,3},{3,2},{4,5},{5,4},{6,7},{7,6},{8,9},{9,8},{10,11... | collective-permute-start | bytes 233480 | tf_op jit(solution)/shard_map/ppermute | solution.py:324
  143.9 8.1 %collective-permute-start.32 = (f32[152,128]{1,0:T(8,128)S(1)}, f32[152,128]{1,0:T(8,128)S(1)}, u32[]{:S(2)}, u32[]{:S(2)}) collective-permute-start(f32[152,128]{1,0:T(8,128)S(1)} %get-tuple-element.100.refs_1_), channel_id=1, source_target_pairs={{0,2},{1,3},{2,0},{3,1},{4,6},{5,7},{6,4},{7,5},{8,10},{9,11},{10,... | collective-permute-start | bytes 233480 | tf_op jit(solution)/shard_map/ppermute | solution.py:324
  145.6 6.5 %collective-permute-start.33 = (f32[152,128]{1,0:T(8,128)S(1)}, f32[152,128]{1,0:T(8,128)S(1)}, u32[]{:S(2)}, u32[]{:S(2)}) collective-permute-start(f32[152,128]{1,0:T(8,128)S(1)} %get-tuple-element.100.refs_1_), channel_id=1, source_target_pairs={{0,3},{1,2},{2,1},{3,0},{4,7},{5,6},{6,5},{7,4},{8,11},{9,10},{10,... | collective-permute-start | bytes 233480 | tf_op jit(solution)/shard_map/ppermute | solution.py:324
  157.0 6.5 %collective-permute-start.35 = (f32[264,128]{1,0:T(8,128)S(1)}, f32[264,128]{1,0:T(8,128)S(1)}, u32[]{:S(2)}, u32[]{:S(2)}) collective-permute-start(f32[264,128]{1,0:T(8,128)S(1)} %add.76.refs_0_), channel_id=1, source_target_pairs={{0,8},{4,12},{8,0},{12,4},{16,24},{20,28},{24,16},{28,20},{1,9},{5... | collective-permute-start | bytes 405512 | tf_op jit(solution)/shard_map/ppermute | solution.py:324
  157.3 8.3 %collective-permute-start.36 = (f32[264,128]{1,0:T(8,128)S(1)}, f32[264,128]{1,0:T(8,128)S(1)}, u32[]{:S(2)}, u32[]{:S(2)}) collective-permute-start(f32[264,128]{1,0:T(8,128)S(1)} %add.76.refs_0_), channel_id=1, source_target_pairs={{0,16},{4,20},{8,24},{12,28},{16,0},{20,4},{24,8},{28,12},{1,17},{... | collective-permute-start | bytes 405512 | tf_op jit(solution)/shard_map/ppermute | solution.py:324
  159.1 6.6 %collective-permute-start.37 = (f32[264,128]{1,0:T(8,128)S(1)}, f32[264,128]{1,0:T(8,128)S(1)}, u32[]{:S(2)}, u32[]{:S(2)}) collective-permute-start(f32[264,128]{1,0:T(8,128)S(1)} %add.76.refs_0_), channel_id=1, source_target_pairs={{0,24},{4,28},{8,16},{12,20},{16,8},{20,12},{24,0},{28,4},{1,25},{... | collective-permute-start | bytes 405512 | tf_op jit(solution)/shard_map/ppermute | solution.py:324
  169.8 5.1 %collective-permute-start.38 = (f32[152,128]{1,0:T(8,128)S(1)}, f32[152,128]{1,0:T(8,128)S(1)}, u32[]{:S(2)}, u32[]{:S(2)}) collective-permute-start(f32[152,128]{1,0:T(8,128)S(1)} %get-tuple-element.110.refs_1_), channel_id=1, source_target_pairs={{0,1},{1,0},{2,3},{3,2},{4,5},{5,4},{6,7},{7,6},{8,9},{9,8},{10,11... | collective-permute-start | bytes 233480 | tf_op jit(solution)/shard_map/ppermute | solution.py:324
  171.3 8.2 %collective-permute-start.39 = (f32[152,128]{1,0:T(8,128)S(1)}, f32[152,128]{1,0:T(8,128)S(1)}, u32[]{:S(2)}, u32[]{:S(2)}) collective-permute-start(f32[152,128]{1,0:T(8,128)S(1)} %get-tuple-element.110.refs_1_), channel_id=1, source_target_pairs={{0,2},{1,3},{2,0},{3,1},{4,6},{5,7},{6,4},{7,5},{8,10},{9,11},{10,... | collective-permute-start | bytes 233480 | tf_op jit(solution)/shard_map/ppermute | solution.py:324
  172.9 6.5 %collective-permute-start.40 = (f32[152,128]{1,0:T(8,128)S(1)}, f32[152,128]{1,0:T(8,128)S(1)}, u32[]{:S(2)}, u32[]{:S(2)}) collective-permute-start(f32[152,128]{1,0:T(8,128)S(1)} %get-tuple-element.110.refs_1_), channel_id=1, source_target_pairs={{0,3},{1,2},{2,1},{3,0},{4,7},{5,6},{6,5},{7,4},{8,11},{9,10},{10,... | collective-permute-start | bytes 233480 | tf_op jit(solution)/shard_map/ppermute | solution.py:324
  184.4 6.1 %collective-permute-start.42 = (f32[264,128]{1,0:T(8,128)S(1)}, f32[264,128]{1,0:T(8,128)S(1)}, u32[]{:S(2)}, u32[]{:S(2)}) collective-permute-start(f32[264,128]{1,0:T(8,128)S(1)} %add.77.refs_0_), channel_id=1, source_target_pairs={{0,8},{4,12},{8,0},{12,4},{16,24},{20,28},{24,16},{28,20},{1,9},{5... | collective-permute-start | bytes 405512 | tf_op jit(solution)/shard_map/ppermute | solution.py:324
  186.1 8.3 %collective-permute-start.43 = (f32[264,128]{1,0:T(8,128)S(1)}, f32[264,128]{1,0:T(8,128)S(1)}, u32[]{:S(2)}, u32[]{:S(2)}) collective-permute-start(f32[264,128]{1,0:T(8,128)S(1)} %add.77.refs_0_), channel_id=1, source_target_pairs={{0,16},{4,20},{8,24},{12,28},{16,0},{20,4},{24,8},{28,12},{1,17},{... | collective-permute-start | bytes 405512 | tf_op jit(solution)/shard_map/ppermute | solution.py:324
  186.3 8.0 %collective-permute-start.44 = (f32[264,128]{1,0:T(8,128)S(1)}, f32[264,128]{1,0:T(8,128)S(1)}, u32[]{:S(2)}, u32[]{:S(2)}) collective-permute-start(f32[264,128]{1,0:T(8,128)S(1)} %add.77.refs_0_), channel_id=1, source_target_pairs={{0,24},{4,28},{8,16},{12,20},{16,8},{20,12},{24,0},{28,4},{1,25},{... | collective-permute-start | bytes 405512 | tf_op jit(solution)/shard_map/ppermute | solution.py:324
  198.7 5.2 %collective-permute-start.45 = (f32[152,128]{1,0:T(8,128)S(1)}, f32[152,128]{1,0:T(8,128)S(1)}, u32[]{:S(2)}, u32[]{:S(2)}) collective-permute-start(f32[152,128]{1,0:T(8,128)S(1)} %get-tuple-element.120.refs_1_), channel_id=1, source_target_pairs={{0,1},{1,0},{2,3},{3,2},{4,5},{5,4},{6,7},{7,6},{8,9},{9,8},{10,11... | collective-permute-start | bytes 233480 | tf_op jit(solution)/shard_map/ppermute | solution.py:324
  200.1 8.1 %collective-permute-start.46 = (f32[152,128]{1,0:T(8,128)S(1)}, f32[152,128]{1,0:T(8,128)S(1)}, u32[]{:S(2)}, u32[]{:S(2)}) collective-permute-start(f32[152,128]{1,0:T(8,128)S(1)} %get-tuple-element.120.refs_1_), channel_id=1, source_target_pairs={{0,2},{1,3},{2,0},{3,1},{4,6},{5,7},{6,4},{7,5},{8,10},{9,11},{10,... | collective-permute-start | bytes 233480 | tf_op jit(solution)/shard_map/ppermute | solution.py:324
  201.8 6.4 %collective-permute-start.47 = (f32[152,128]{1,0:T(8,128)S(1)}, f32[152,128]{1,0:T(8,128)S(1)}, u32[]{:S(2)}, u32[]{:S(2)}) collective-permute-start(f32[152,128]{1,0:T(8,128)S(1)} %get-tuple-element.120.refs_1_), channel_id=1, source_target_pairs={{0,3},{1,2},{2,1},{3,0},{4,7},{5,6},{6,5},{7,4},{8,11},{9,10},{10,... | collective-permute-start | bytes 233480 | tf_op jit(solution)/shard_map/ppermute | solution.py:324
  212.1 4.5 %collective-permute-start.51 = (f32[8,128]{1,0:T(8,128)S(1)}, f32[8,128]{1,0:T(8,128)S(1)}, u32[]{:S(2)}, u32[]{:S(2)}) collective-permute-start(f32[8,128]{1,0:T(8,128)S(1)} %add.78.refs_1_), channel_id=1, source_target_pairs={{0,24},{4,28},{8,16},{12,20},{16,8},{20,12},{24,0},{28,4},{1,25},{... | collective-permute-start | bytes 12296 | tf_op jit(solution)/shard_map/ppermute | solution.py:324
  221.7 6.5 %collective-permute-start.53 = (f32[264,128]{1,0:T(8,128)S(1)}, f32[264,128]{1,0:T(8,128)S(1)}, u32[]{:S(2)}, u32[]{:S(2)}) collective-permute-start(f32[264,128]{1,0:T(8,128)S(1)} %maximum_select_fusion.refs_0_), channel_id=1, source_target_pairs={{0,8},{4,12},{8,0},{12,4},{16,24},{20,28},{24,16},{28,20},{1,9},{5... | collective-permute-start | bytes 405512 | tf_op jit(solution)/shard_map/ppermute | solution.py:324
  222.1 8.3 %collective-permute-start.54 = (f32[264,128]{1,0:T(8,128)S(1)}, f32[264,128]{1,0:T(8,128)S(1)}, u32[]{:S(2)}, u32[]{:S(2)}) collective-permute-start(f32[264,128]{1,0:T(8,128)S(1)} %maximum_select_fusion.refs_0_), channel_id=1, source_target_pairs={{0,16},{4,20},{8,24},{12,28},{16,0},{20,4},{24,8},{28,12},{1,17},{... | collective-permute-start | bytes 405512 | tf_op jit(solution)/shard_map/ppermute | solution.py:324
  223.8 6.6 %collective-permute-start.55 = (f32[264,128]{1,0:T(8,128)S(1)}, f32[264,128]{1,0:T(8,128)S(1)}, u32[]{:S(2)}, u32[]{:S(2)}) collective-permute-start(f32[264,128]{1,0:T(8,128)S(1)} %maximum_select_fusion.refs_0_), channel_id=1, source_target_pairs={{0,24},{4,28},{8,16},{12,20},{16,8},{20,12},{24,0},{28,4},{1,25},{... | collective-permute-start | bytes 405512 | tf_op jit(solution)/shard_map/ppermute | solution.py:324
  231.4 4.5 %collective-permute-start.56 = (f32[8,128]{1,0:T(8,128)S(1)}, f32[8,128]{1,0:T(8,128)S(1)}, u32[]{:S(2)}, u32[]{:S(2)}) collective-permute-start(f32[8,128]{1,0:T(8,128)S(1)} %residuals.1), channel_id=1, source_target_pairs={{0,1},{1,0},{2,3},{3,2},{4,5},{5,4},{6,7},{7,6},{8,9},{9,8},{10,11... | collective-permute-start | bytes 12296 | tf_op jit(solution)/shard_map/ppermute | solution.py:324
  232.8 4.5 %collective-permute-start.57 = (f32[8,128]{1,0:T(8,128)S(1)}, f32[8,128]{1,0:T(8,128)S(1)}, u32[]{:S(2)}, u32[]{:S(2)}) collective-permute-start(f32[8,128]{1,0:T(8,128)S(1)} %residuals.1), channel_id=1, source_target_pairs={{0,2},{1,3},{2,0},{3,1},{4,6},{5,7},{6,4},{7,5},{8,10},{9,11},{10,... | collective-permute-start | bytes 12296 | tf_op jit(solution)/shard_map/ppermute | solution.py:324
  234.5 5.4 %collective-permute-start.58 = (f32[8,128]{1,0:T(8,128)S(1)}, f32[8,128]{1,0:T(8,128)S(1)}, u32[]{:S(2)}, u32[]{:S(2)}) collective-permute-start(f32[8,128]{1,0:T(8,128)S(1)} %residuals.1), channel_id=1, source_target_pairs={{0,3},{1,2},{2,1},{3,0},{4,7},{5,6},{6,5},{7,4},{8,11},{9,10},{10,... | collective-permute-start | bytes 12296 | tf_op jit(solution)/shard_map/ppermute | solution.py:324
  (28 other events, 271.8 us)

commit v2 on v1

v2 whole, which is shorter than its diff:
```python
import functools

import jax
import jax.numpy as jnp
from jax import lax
from jax.experimental import pallas as pl
from jax.experimental.pallas import tpu as pltpu
from jax.sharding import PartitionSpec as P

YG = 64
CG = 6

SIGMA = 1e-06
RELAX = 1.6

F32 = jnp.float32
BF16 = jnp.bfloat16
LANES = 128
PARTS = 2
SHARED = 16 // (2 * PARTS)
VMEM_LIMIT = 24 * 1024 * 1024


def dot(a, b):
    return lax.dot_general(a, b, (((1,), (0,)), ((), ())), preferred_element_type=F32)


def split3(x):
    high = x.astype(BF16)
    rest = x - high.astype(F32)
    mid = rest.astype(BF16)
    low = (rest - mid.astype(F32)).astype(BF16)
    return high, mid, low


def split2(x):
    high = x.astype(BF16)
    return high, (x - high.astype(F32)).astype(BF16)


def tree(parts, op=jnp.add):
    parts = list(parts)
    while len(parts) > 1:
        parts = [op(parts[i], parts[i + 1]) for i in range(0, len(parts), 2)]
    return parts[0]


def row_sum(x):
    return jnp.sum(x, axis=0, keepdims=True)


def half_sum(x):
    half = x.shape[0] // 2
    return row_sum(x[:half]) + row_sum(x[half:])


def pad_rows(rows):
    return jnp.concatenate(list(rows) + [jnp.zeros((8 - len(rows), LANES), F32)], axis=0)


def gather(onehot_ref, x):
    return dot(onehot_ref[...], jnp.concatenate(split2(x), axis=0))


def scatter(onehot, x, split=split2):
    return tree(dot(onehot, part) for part in split(x)) if split is split2 else sum(dot(onehot, p) for p in split(x))


def run_tiles(w_ref, l_ref, r0_ref, r1_ref):
    blocks = w_ref.shape[0] // SHARED
    unroll = next(n for n in (6, 4, 3, 2, 1) if blocks % n == 0)
    rows = 2 * PARTS

    def body(step, carry):
        for inner in range(unroll):
            block = step * unroll + inner
            at = pl.multiple_of(block * 16, 16)
            left = l_ref[pl.ds(at, 16), :]
            for k in range(SHARED):
                out = dot(left, w_ref[SHARED * block + k])[k * rows : (k + 1) * rows]
                r0_ref[pl.ds(at + k * rows, rows), :] = out[:, :LANES]
                r1_ref[pl.ds(at + k * rows, rows), :] = out[:, LANES:]
        return carry

    lax.fori_loop(0, blocks // unroll, body, 0)


def forward_parts(vec, gf_ref, wt_ref, l_ref, r0_ref, r1_ref):
    picked = gather(gf_ref, vec)
    first = lax.broadcasted_iota(jnp.int32, picked.shape, 0) % (2 * PARTS) < PARTS
    zero = jnp.zeros_like(picked)
    l_ref[:, :LANES] = jnp.where(first, picked, zero).astype(BF16)
    l_ref[:, LANES:] = jnp.where(first, zero, picked).astype(BF16)
    run_tiles(wt_ref, l_ref, r0_ref, r1_ref)
    count = 2 * wt_ref.shape[0]
    terms = []
    for part in range(PARTS):
        at = pl.ds(part, count, stride=PARTS)
        terms.append(r0_ref[at, :] + r1_ref[at, :])
    return tree(terms)


def backward_sum(vec, gb_ref, sb_ref, w_ref, l_ref, r0_ref, r1_ref):
    picked = gather(gb_ref, vec).astype(BF16)
    l_ref[:, :LANES] = picked
    l_ref[:, LANES:] = picked
    run_tiles(w_ref, l_ref, r0_ref, r1_ref)
    half = w_ref.shape[0]
    even = tree(r0_ref[pl.ds(part, half, stride=2 * PARTS), :] for part in range(PARTS))
    odd = tree(r1_ref[pl.ds(PARTS + part, half, stride=2 * PARTS), :] for part in range(PARTS))
    return scatter(sb_ref[...], jnp.concatenate([even, odd], axis=0))


def gathered_rows(part_refs, s_ref):
    count = s_ref.shape[2]
    return tree(scatter(s_ref[j], ref[:count, :]) for j, ref in enumerate(part_refs))


def put_halves(refs, total, extra):
    half = total.shape[0] // 2
    for ref, part in zip(refs, (total[:half], total[half:])):
        ref[:half, :] = part
        ref[half:, :] = extra


def init_kernel(a_steps, a_ref, g_ref, w_ref, wt_ref, sq_ref):
    step = pl.program_id(0)

    def convert(ref):
        for t in range(ref.shape[0]):
            tile = ref[t]
            at = (t % 2) * LANES
            high, low = split2(tile)
            w_ref[t // 2, :LANES, at : at + LANES] = high
            w_ref[t // 2, LANES:, at : at + LANES] = low
            high, low = split2(tile.T)
            wt_ref[t // 2, at : at + LANES, :LANES] = high
            wt_ref[t // 2, at : at + LANES, LANES:] = low
            sq_ref[t : t + 1, :] = row_sum(tile * tile)

    @pl.when(step < a_steps)
    def _():
        convert(a_ref)

    @pl.when(step >= a_steps)
    def _():
        convert(g_ref)


def first_forward_kernel(v_ref, at_ref, gf_ref, w_ref, out_ref, l_ref, r0_ref, r1_ref):
    count = 2 * w_ref.shape[0]
    out_ref[:count, :] = forward_parts(v_ref[...], gf_ref, w_ref, l_ref, r0_ref, r1_ref)
    out_ref[count:, :] = at_ref[...]


def first_backward_kernel(n_col, ycount, acount, *refs):
    rho_ref, *refs = refs
    part_refs, refs = refs[:n_col], refs[n_col:]
    (gb_ref, sb_ref, w_ref, sq_ref, slack_ref, dual_ref), refs = refs[:6], refs[6:]
    mine_ref, theirs_ref, y_ref, s_ref, l_ref, r0_ref, r1_ref = refs
    rho = rho_ref[0]
    _, full_rows, count = s_ref.shape
    for j, ref in enumerate(part_refs):
        for row in range(pl.cdiv(count, LANES)):
            size = min(LANES, count - row * LANES)
            at = ref[count + row : count + row + 1, :size].astype(jnp.int32)
            hit = lax.broadcasted_iota(jnp.int32, (full_rows, size), 0) == at
            s_ref[j, :, row * LANES : row * LANES + size] = jnp.where(hit, 1.0, 0.0).astype(BF16)
    full = gathered_rows(part_refs, s_ref)
    y_ref[...] = full
    top = rho * slack_ref[...] - dual_ref[...] - rho * full[:ycount]
    vec = jnp.concatenate([top, -full[ycount:]], axis=0)
    total = backward_sum(vec, gb_ref, sb_ref, w_ref, l_ref, r0_ref, r1_ref)
    half = w_ref.shape[0]
    squares = jnp.concatenate([sq_ref[pl.ds(0, half, stride=2), :], sq_ref[pl.ds(1, half, stride=2), :]], axis=0)
    place = lax.broadcasted_iota(jnp.int32, squares.shape, 0)
    place = jnp.where(place < half, 2 * place, 2 * (place - half) + 1)
    squares = jnp.where(place < acount, rho * squares, squares)
    squares = scatter(sb_ref[...], squares, split3)
    half = total.shape[0] // 2
    mine_ref[:half, :] = total[:half]
    mine_ref[half:, :] = squares[:half]
    theirs_ref[:half, :] = total[half:]
    theirs_ref[half:, :] = squares[half:]


def finish_forward(u, p, resid, shifted, out_ref, gf_ref, w_ref, l_ref, r0_ref, r1_ref):
    count = 2 * w_ref.shape[0]
    weighted = shifted * u
    rows = [half_sum(resid * u), half_sum(weighted * u)]
    if p is not None:
        rows.append(half_sum(weighted * p))
    out_ref[count:, :] = pad_rows(rows)
    out_ref[:count, :] = forward_parts(u, gf_ref, w_ref, l_ref, r0_ref, r1_ref)


def second_forward_kernel(*refs):
    (mine_ref, theirs_ref), refs = refs[:2], refs[2:]
    v_ref, d_ref, c_ref, gf_ref, w_ref, r_ref, u_ref, pre_ref, out_ref, l_ref, r0_ref, r1_ref = refs
    half = v_ref.shape[0] // 2
    total = jnp.concatenate([mine_ref[:half, :], theirs_ref[:half, :]], axis=0)
    squares = jnp.concatenate([mine_ref[half:, :], theirs_ref[half:, :]], axis=0)
    v, d = v_ref[...], d_ref[...]
    resid = total - c_ref[...] - d * v
    shifted = d + SIGMA
    pre = shifted + squares
    u = resid / pre
    r_ref[...] = resid
    u_ref[...] = u
    pre_ref[...] = pre
    finish_forward(u, None, resid, shifted, out_ref, gf_ref, w_ref, l_ref, r0_ref, r1_ref)


def step_scalars(first, part_refs, sc_old_ref, count):
    totals = jnp.sum(tree(ref[count:, :] for ref in part_refs), axis=1, keepdims=True)
    gamma, one, two = totals[0:1], totals[1:2], totals[2:3]
    if first:
        return gamma, jnp.zeros_like(gamma), one
    old = sc_old_ref[...]
    beta = gamma / old[0:1, 0:1]
    return gamma, beta, one + beta * (2.0 * two + beta * old[2:3, 0:1])


def wide(x):
    return jnp.broadcast_to(x, (1, LANES))


def backward_kernel(n_col, ycount, first, last, *refs):
    rho_ref, *refs = refs
    part_refs, refs = refs[:n_col], refs[n_col:]
    s_ref, refs = refs[0], refs[1:]
    sc_old_ref = None
    if not first:
        (yp_old_ref, yv_old_ref, sc_old_ref, alpha_ref), refs = refs[:4], refs[4:]
    else:
        (yv_old_ref,), refs = refs[:1], refs[1:]
    if not last:
        (gb_ref, sb_ref, w_ref), refs = refs[:3], refs[3:]
    if last:
        z_ref, *refs = refs
    else:
        mine_ref, theirs_ref, *refs = refs
    yp_ref, yv_ref, sc_ref, *scratch = refs
    rho = rho_ref[0]
    full = gathered_rows(part_refs, s_ref)
    gamma, beta, pdp = step_scalars(first, part_refs, sc_old_ref, s_ref.shape[2])
    sc_ref[...] = pad_rows([wide(gamma), wide(beta), wide(pdp)])
    if first:
        yp = full
        yv_ref[...] = yv_old_ref[...]
    else:
        yp_old = yp_old_ref[...]
        yp = full + beta * yp_old
        yv_ref[...] = yv_old_ref[...] + alpha_ref[0:1, 0:1] * yp_old
    yp_ref[...] = yp
    scaled = jnp.concatenate([rho * yp[:ycount], yp[ycount:]], axis=0)
    norm = pad_rows([row_sum(scaled * yp)])
    if last:
        z_ref[...] = norm
    else:
        put_halves((mine_ref, theirs_ref), backward_sum(scaled, gb_ref, sb_ref, w_ref, *scratch), norm)


def step_alpha(extra, sc_ref):
    norm = jnp.sum(extra[0:1], axis=1, keepdims=True)
    return sc_ref[0:1, 0:1] / (sc_ref[2:3, 0:1] + norm)


def forward_kernel(first, *refs):
    (mine_ref, theirs_ref), refs = refs[:2], refs[2:]
    if not first:
        p_old_ref, refs = refs[0], refs[1:]
    (u_old_ref, v_old_ref, r_old_ref, d_ref, pre_ref, sc_ref, gf_ref, w_ref), refs = refs[:8], refs[8:]
    p_ref, v_ref, r_ref, u_ref, alpha_ref, out_ref, *scratch = refs
    half = d_ref.shape[0] // 2
    total = jnp.concatenate([mine_ref[:half, :], theirs_ref[:half, :]], axis=0)
    alpha = step_alpha(mine_ref[half:, :], sc_ref)
    p = u_old_ref[...]
    if not first:
        p = p + sc_ref[1:2, 0:1] * p_old_ref[...]
    shifted = d_ref[...] + SIGMA
    resid = r_old_ref[...] - alpha * (shifted * p + total)
    u = resid / pre_ref[...]
    p_ref[...] = p
    v_ref[...] = v_old_ref[...] + alpha * p
    r_ref[...] = resid
    u_ref[...] = u
    alpha_ref[...] = jnp.broadcast_to(alpha, (8, LANES))
    finish_forward(u, p, resid, shifted, out_ref, gf_ref, w_ref, *scratch)


def final_kernel(ycount, *refs):
    rho_ref, t_ref, *refs = refs
    (u_ref, p_old_ref, v_ref, start_ref, sc_ref, yp_ref, yv_ref, y0_ref), refs = refs[:8], refs[8:]
    (slack_ref, dual_ref, lower_ref, upper_ref, gb_ref, sb_ref, w_ref), refs = refs[:7], refs[7:]
    primal_out, slack_out, dual_out, mine_ref, theirs_ref, *scratch = refs
    rho = rho_ref[0]
    alpha = step_alpha(t_ref[...], sc_ref)
    p = u_ref[...] + sc_ref[1:2, 0:1] * p_old_ref[...]
    v = v_ref[...] + alpha * p
    primal_out[...] = RELAX * v + (1.0 - RELAX) * start_ref[...]
    image = yv_ref[...] + alpha * yp_ref[...]
    image_next = RELAX * image + (1.0 - RELAX) * y0_ref[...]
    dual = dual_ref[...]
    relaxed = RELAX * image[:ycount] + (1.0 - RELAX) * slack_ref[...]
    slack_next = jnp.minimum(jnp.maximum(relaxed + dual / rho, lower_ref[...]), upper_ref[...])
    dual_next = dual + rho * (relaxed - slack_next)
    slack_out[...] = slack_next
    dual_out[...] = dual_next
    worst = jnp.max(jnp.abs(image_next[:ycount] - slack_next), axis=0, keepdims=True)
    vec = jnp.concatenate([dual_next, image_next[ycount:]], axis=0)
    total = backward_sum(vec, gb_ref, sb_ref, w_ref, *scratch)
    put_halves((mine_ref, theirs_ref), total, jnp.broadcast_to(worst, (8, LANES)))


def residual_kernel(z_ref, primal_ref, d_ref, c_ref, out_ref):
    half = d_ref.shape[0] // 2
    dvec = d_ref[:half, :] * primal_ref[:half, :] + z_ref[:half, :] + c_ref[:half, :]
    worst = jnp.max(jnp.abs(dvec), axis=0, keepdims=True)
    out_ref[...] = jnp.concatenate([z_ref[half : half + 4, :], jnp.broadcast_to(worst, (4, LANES))], axis=0)


VMEM_SPEC = pl.BlockSpec(memory_space=pltpu.VMEM)
SMEM_SPEC = pl.BlockSpec(memory_space=pltpu.SMEM)


def call(kernel, name, outs, args, scratch=(), scalar=False):
    specs = [SMEM_SPEC if scalar and i == 0 else VMEM_SPEC for i in range(len(args))]
    shapes = tuple(s if isinstance(s, jax.ShapeDtypeStruct) else jax.ShapeDtypeStruct(s, F32) for s in outs)
    return pl.pallas_call(
        kernel,
        out_shape=shapes,
        in_specs=specs,
        out_specs=tuple(VMEM_SPEC for _ in outs),
        scratch_shapes=list(scratch),
        compiler_params=pltpu.CompilerParams(vmem_limit_bytes=VMEM_LIMIT),
        name=name,
    )(*args)


def swap(x, axis, size, distance):
    return lax.ppermute(x, axis, [(i, i ^ distance) for i in range(size)])


def exchange(x, axis, size, distances):
    return [x] + [swap(x, axis, size, m) for m in distances]


def local(n_row, n_col, *args):
    (
        constraint_tiles,
        constraint_rows,
        constraint_cols,
        factor_tiles,
        factor_rows,
        factor_cols,
        diag_cost,
        linear_cost,
        lower_bound,
        upper_bound,
        primal_start,
        slack_start,
        dual_start,
        penalty,
    ) = args
    width = constraint_tiles.shape[2]
    ctiles = constraint_tiles.reshape(-1, width, width)
    ftiles = factor_tiles.reshape(-1, width, width)
    acount, fcount = ctiles.shape[0], ftiles.shape[0]
    count = acount + fcount
    pairs = count // 2
    xcount = primal_start.shape[0]
    ycount = slack_start.shape[0]
    full = ycount + YG
    rho = penalty.reshape(1)

    half = xcount // 2
    odd_core = lax.axis_index("row") % 2 == 1

    def turn(x):
        return jnp.where(odd_core, jnp.concatenate([x[half:], x[:half]], axis=0), x)

    diag_cost, linear_cost, primal_start = turn(diag_cost), turn(linear_cost), turn(primal_start)

    def over_col(x):
        return exchange(x, "col", n_col, sorted(range(1, n_col), key=lambda m: (m != 2, m)))

    def over_plane(chip, op=jnp.add):
        return tree(exchange(chip, "row", n_row, range(2, n_row, 2)), op)

    def other_core(x):
        return swap(x, "row", n_row, 1)

    def over_row(mine, theirs):
        summed = over_plane(mine + other_core(theirs))
        return summed, other_core(summed)

    xat = jnp.concatenate([constraint_cols.reshape(-1), factor_cols.reshape(-1)])
    xat = (xat + jnp.where(odd_core, half, 0)) % xcount
    yat = jnp.concatenate([constraint_rows.reshape(-1), ycount + factor_rows.reshape(-1)])
    part = jnp.arange(PARTS * count, dtype=jnp.int32) % PARTS

    def pick(at, size):
        place = part * size + jnp.repeat(at, PARTS)
        return (place[:, None] == jnp.arange(PARTS * size, dtype=jnp.int32)[None, :]).astype(BF16)

    gf = pick(xat, xcount)
    gb = pick(yat, full)
    columns = jnp.concatenate([xat[0::2], xat[1::2]])
    sb = (jnp.arange(xcount, dtype=jnp.int32)[:, None] == columns[None, :]).astype(BF16)
    at_rows = jnp.pad(yat.astype(F32), (0, 8 * width - count)).reshape(8, width)

    block = 16 if acount % 16 == 0 and fcount % 16 == 0 else 8
    a_steps, f_steps = acount // block, fcount // block
    matrix = pl.BlockSpec((block // 2, 2 * width, 2 * width), lambda i: (i, 0, 0))
    matrices = jax.ShapeDtypeStruct((pairs, 2 * width, 2 * width), BF16)
    tiles, turned, squares = pl.pallas_call(
        functools.partial(init_kernel, a_steps),
        grid=(a_steps + f_steps,),
        in_specs=[
            pl.BlockSpec((block, width, width), lambda i: (jnp.minimum(i, a_steps - 1), 0, 0)),
            pl.BlockSpec((block, width, width), lambda i: (jnp.maximum(i - a_steps, 0), 0, 0)),
        ],
        out_specs=(matrix, matrix, pl.BlockSpec((block, width), lambda i: (i, 0))),
        out_shape=(matrices, matrices, jax.ShapeDtypeStruct((count, width), F32)),
        compiler_params=pltpu.CompilerParams(vmem_limit_bytes=VMEM_LIMIT),
        name="split_tiles",
    )(pltpu.with_memory_space_constraint(ctiles, pltpu.HBM), pltpu.with_memory_space_constraint(ftiles, pltpu.HBM))

    scratch = (
        pltpu.VMEM((PARTS * count, 2 * width), BF16),
        pltpu.VMEM((PARTS * count, width), F32),
        pltpu.VMEM((PARTS * count, width), F32),
    )
    xs, ys, small = (xcount, width), (full, width), (8, width)
    sent, summed = (count + 8, width), (half + 8, width)

    (parts,) = call(first_forward_kernel, "first_forward", [sent], (primal_start, at_rows, gf, turned), scratch)
    mine, theirs, y0, s_all = call(
        functools.partial(first_backward_kernel, n_col, ycount, acount),
        "first_backward",
        [xs, xs, ys, jax.ShapeDtypeStruct((n_col, full, count), BF16)],
        (rho, *over_col(parts), gb, sb, tiles, squares, slack_start, dual_start),
        scratch,
        scalar=True,
    )
    resid, u, precond, parts = call(
        second_forward_kernel,
        "second_forward",
        [xs, xs, xs, sent],
        (*over_row(mine, theirs), primal_start, diag_cost, linear_cost, gf, turned),
        scratch,
    )
    v, yv = primal_start, y0
    p = yp = sc = alpha = None
    for step in range(CG):
        first, last = step == 0, step + 1 == CG
        state = (yv,) if first else (yp, yv, sc, alpha)
        mats = () if last else (gb, sb, tiles)
        *z, yp, yv, sc = call(
            functools.partial(backward_kernel, n_col, ycount, first, last),
            "last_norm" if last else "backward",
            ([small] if last else [summed, summed]) + [ys, ys, small],
            (rho, *over_col(parts), s_all, *state, *mats),
            () if last else scratch,
            scalar=True,
        )
        if last:
            break
        p, v, resid, u, alpha, parts = call(
            functools.partial(forward_kernel, first),
            "forward",
            [xs, xs, xs, xs, small, sent],
            (*over_row(*z), *(() if first else (p,)), u, v, resid, diag_cost, precond, sc, gf, turned),
            scratch,
        )
    norm = over_plane(z[0] + other_core(z[0]))
    primal_next, slack_next, dual_next, mine, theirs = call(
        functools.partial(final_kernel, ycount),
        "final",
        [xs, (ycount, width), (ycount, width), summed, summed],
        (rho, norm, u, p, v, primal_start, sc, yp, yv, y0)
        + (slack_start, dual_start, lower_bound, upper_bound, gb, sb, tiles),
        scratch,
        scalar=True,
    )

    def join(a, b):
        is_sum = lax.broadcasted_iota(jnp.int32, a.shape, 0) < half
        return jnp.where(is_sum, a + b, jnp.maximum(a, b))

    z = over_plane(join(mine, other_core(theirs)), join)
    (worst,) = call(residual_kernel, "residuals", [small], (z, primal_next, diag_cost, linear_cost))
    worst = jnp.maximum(worst, other_core(worst))
    worst = tree(over_col(worst), jnp.maximum)
    return (turn(primal_next), slack_next, dual_next, jnp.max(worst[:4]), jnp.max(worst[4:]))


def solution(mesh):
    placed = (
        P("row", "col", None, None),
        P("row", "col"),
        P("row", "col"),
        P("row", "col", None, None),
        P("row", "col"),
        P("row", "col"),
        P("col", None),
        P("col", None),
        P("row", None),
        P("row", None),
        P("col", None),
        P("row", None),
        P("row", None),
        P(),
    )
    return jax.shard_map(
        functools.partial(local, mesh.shape["row"], mesh.shape["col"]),
        mesh=mesh,
        in_specs=placed,
        out_specs=(P("col", None), P("row", None), P("row", None), P(), P()),
        check_vma=False,
    )
```

time: 241 us -> 218 us (0.905)
  Pallas kernels: 57.7 us -> 40.6 us
  waiting for transfers between devices: 97.6 us -> 87.8 us
  local copies, waits for them, and re-layouts: 10 us -> 16.4 us
  starting transfers between devices: 70.9 us -> 66 us
  other arithmetic: 2.53 us -> 5.14 us
    pallas_call x16, Pallas kernels: 55.1 us -> 32.4 us  [call(): pl.pallas_call(kernel, out_shape=shapes, in_specs=specs, out_specs=tuple(...]
    ppermute x59 -> x63, waiting for transfers between devices: 97.6 us -> 87.8 us  [swap(): return lax.ppermute(x, axis, [(i, i ^ distance) for i in range(size)])]
    pallas_call x1, Pallas kernels: 2.64 us -> 8.19 us  [local(): pl.pallas_call(functools.partial(init_kernel, a_steps), grid=(a_steps + f...]
    unnamed x34 -> x26, local copies, waits for them, and re-layouts: 9.31 us -> 14.7 us
    ppermute x59 -> x63, starting transfers between devices: 70.9 us -> 66 us  [swap(): return lax.ppermute(x, axis, [(i, i ^ distance) for i in range(size)])]
  transfers between devices with their start and end apart: 59 -> 63, of which waited for: 44 -> 54; matrix products, arithmetic and copies ran while one was open for 1% -> 1% of each run, Pallas kernels for 0% -> 0%
where the time goes in v2:
time: 218 us
  waiting for transfers between devices  87.8 us (40%)
  starting transfers between devices  66 us (30%)
  Pallas kernels  40.6 us (19%)
  local copies, waits for them, and re-layouts  16.4 us (8%)
  other arithmetic  5.14 us (2%)
    ppermute x63, waiting for transfers between devices, swap(): return lax.ppermute(x, axis, [(i, i ^ distance) for i in range(size)])  87.8 us
    ppermute x63, starting transfers between devices, swap(): return lax.ppermute(x, axis, [(i, i ^ distance) for i in range(size)])  66 us
    pallas_call x16, Pallas kernels, call(): pl.pallas_call(kernel, out_shape=shapes, in_specs=specs, out_specs=tuple(...  32.4 us
    unnamed x26, local copies, waits for them, and re-layouts  14.7 us
    pallas_call x1, Pallas kernels, local(): pl.pallas_call(functools.partial(init_kernel, a_steps), grid=(a_steps + f...  8.19 us
  transfers between devices with their start and end apart: 63, of which 54 were waited for; matrix products, arithmetic and copies ran while one was open for 1% of the time, Pallas kernels for 0%

profile of v2, /device:TPU:0, one launch (start us, length us, event | category | flops | bytes accessed | tf_op | source)
XLA Modules:
  0.0 217.7 jit_solution(2768815983680377515)
XLA Ops:
  5.0 8.2 %split_tiles.1 = (bf16[72,256,256]{2,1,0:T(8,128)(2,1)S(1)}, bf16[72,256,256]{2,1,0:T(8,128)(2,1)S(1)}, f32[144,128]{1,0:T(8,128)S(1)}) custom-call(f32[96,128,128]{2,1,0:T(8,128)} %bitcast.20, f32[48,128,128]{2,1,0:T(8,128)} %bitcast.21), custom_call_target="tpu_custom_call" | custom-call | tf_op jit(solution)/shard_map/split_tiles/pallas_call | solution.py:417
  13.2 3.7 %copy-done = bf16[72,256,256]{2,1,0:T(8,128)(2,1)} copy-done((bf16[72,256,256]{2,1,0:T(8,128)(2,1)}, bf16[72,256,256]{2,1,0:T(8,128)(2,1)S(1)}, u32[]{:S(2)}) %copy-start) | copy-done | bytes 9437208
  16.9 1.8 first_forward.1.refs_1_
  18.7 3.6 %copy-done.2 = bf16[72,256,256]{2,1,0:T(8,128)(2,1)} copy-done((bf16[72,256,256]{2,1,0:T(8,128)(2,1)}, bf16[72,256,256]{2,1,0:T(8,128)(2,1)S(1)}, u32[]{:S(2)}) %copy-start.2) | copy-done | bytes 9437208
  22.3 4.1 %collective-permute-start = (f32[152,128]{1,0:T(8,128)S(1)}, f32[152,128]{1,0:T(8,128)S(1)}, u32[]{:S(2)}, u32[]{:S(2)}) collective-permute-start(f32[152,128]{1,0:T(8,128)S(1)} %first_forward.1.refs_1_), channel_id=1, source_target_pairs={{0,2},{1,3},{2,0},{3,1},{4,6},{5,7},{6,4},{7,5},{8,10},{9,11},{10,... | collective-permute-start | bytes 233480 | tf_op jit(solution)/shard_map/ppermute | solution.py:342
  30.8 3.3 %collective-permute-done.2.refs_4_ = f32[152,128]{1,0:T(8,128)S(1)} collective-permute-done((f32[152,128]{1,0:T(8,128)S(1)}, f32[152,128]{1,0:T(8,128)S(1)}, u32[]{:S(2)}, u32[]{:S(2)}) %collective-permute-start.2) | collective-permute-done | bytes 77856 | tf_op jit(solution)/shard_map/ppermute | solution.py:342
  34.2 3.7 %copy-done.1 = bf16[72,256,256]{2,1,0:T(8,128)(2,1)S(1)} copy-done((bf16[72,256,256]{2,1,0:T(8,128)(2,1)S(1)}, bf16[72,256,256]{2,1,0:T(8,128)(2,1)}, u32[]{:S(2)}) %copy-start.1) | copy-done | bytes 9437208
  37.8 2.7 %first_backward.1 = (f32[256,128]{1,0:T(8,128)S(1)}, f32[256,128]{1,0:T(8,128)S(1)}, f32[256,128]{1,0:T(8,128)S(1)}, bf16[4,256,144]{2,1,0:T(8,128)(2,1)S(1)}) custom-call(f32[1]{0:T(128)} %bitcast.10.refs_0_, f32[152,128]{1,0:T(8,128)S(1)} %first_forward.1.refs_1_, f32[152,128]{1,0:T(8,128)S(1)} %collective-permute-done.refs_2_, ...), custom_call_target="tpu_custom_call" | custom-call | tf_op jit(solution)/shard_map/first_backward/pallas_call | solution.py:330
  45.6 2.5 %collective-permute-done.4 = f32[256,128]{1,0:T(8,128)S(1)} collective-permute-done((f32[256,128]{1,0:T(8,128)S(1)}, f32[256,128]{1,0:T(8,128)S(1)}, u32[]{:S(2)}, u32[]{:S(2)}) %collective-permute-start.4) | collective-permute-done | bytes 131104 | tf_op jit(solution)/shard_map/ppermute | solution.py:342
  48.0 3.6 %collective-permute-done.5 = f32[256,128]{1,0:T(8,128)S(1)} collective-permute-done((f32[256,128]{1,0:T(8,128)S(1)}, f32[256,128]{1,0:T(8,128)S(1)}, u32[]{:S(2)}, u32[]{:S(2)}) %collective-permute-start.5) | collective-permute-done | bytes 131104 | tf_op jit(solution)/shard_map/ppermute | solution.py:342
  53.1 3.7 %copy-done.3 = bf16[72,256,256]{2,1,0:T(8,128)(2,1)S(1)} copy-done((bf16[72,256,256]{2,1,0:T(8,128)(2,1)S(1)}, bf16[72,256,256]{2,1,0:T(8,128)(2,1)}, u32[]{:S(2)}) %copy-start.3) | copy-done | bytes 9437208
  56.8 1.9 second_forward.1
  60.1 3.0 %collective-permute-start.9 = (f32[152,128]{1,0:T(8,128)S(1)}, f32[152,128]{1,0:T(8,128)S(1)}, u32[]{:S(2)}, u32[]{:S(2)}) collective-permute-start(f32[152,128]{1,0:T(8,128)S(1)} %get-tuple-element.84.refs_1_), channel_id=1, source_target_pairs={{0,1},{1,0},{2,3},{3,2},{4,5},{5,4},{6,7},{7,6},{8,9},{9,8},{10,11... | collective-permute-start | bytes 233480 | tf_op jit(solution)/shard_map/ppermute | solution.py:342
  63.1 2.7 %collective-permute-done.10.refs_4_ = f32[152,128]{1,0:T(8,128)S(1)} collective-permute-done((f32[152,128]{1,0:T(8,128)S(1)}, f32[152,128]{1,0:T(8,128)S(1)}, u32[]{:S(2)}, u32[]{:S(2)}) %collective-permute-start.10) | collective-permute-done | bytes 77856 | tf_op jit(solution)/shard_map/ppermute | solution.py:342
  65.8 2.4 %collective-permute-done.8.refs_2_ = f32[152,128]{1,0:T(8,128)S(1)} collective-permute-done((f32[152,128]{1,0:T(8,128)S(1)}, f32[152,128]{1,0:T(8,128)S(1)}, u32[]{:S(2)}, u32[]{:S(2)}) %collective-permute-start.8) | collective-permute-done | bytes 77856 | tf_op jit(solution)/shard_map/ppermute | solution.py:342
  68.3 2.6 %backward.5 = (f32[136,128]{1,0:T(8,128)S(1)}, f32[136,128]{1,0:T(8,128)S(1)}, f32[256,128]{1,0:T(8,128)S(1)}, f32[256,128]{1,0:T(8,128)S(1)}, f32[8,128]{1,0:T(8,128)S(1)}) custom-call(f32[1]{0:T(128)} %bitcast.11.refs_0_, f32[152,128]{1,0:T(8,128)S(1)} %get-tuple-element.84.refs_1_, f32[152,128]{1,0:T(8,128)S(1)} %collective-permute-done.8.refs_2_, ...), custom_call_target="tpu_custom_call" | custom-call | tf_op jit(solution)/shard_map/backward/pallas_call | solution.py:330
  76.6 2.0 collective-permute-done.13
  80.9 2.0 forward.5
  83.6 2.1 collective-permute-start.17
  87.4 2.2 collective-permute-done.16.refs_2_
  89.8 2.1 collective-permute-done.18.refs_4_
  91.9 2.4 %backward.6 = (f32[136,128]{1,0:T(8,128)S(1)}, f32[136,128]{1,0:T(8,128)S(1)}, f32[256,128]{1,0:T(8,128)S(1)}, f32[256,128]{1,0:T(8,128)S(1)}, f32[8,128]{1,0:T(8,128)S(1)}) custom-call(f32[1]{0:T(128)} %bitcast.12.refs_0_, f32[152,128]{1,0:T(8,128)S(1)} %get-tuple-element.93.refs_1_, f32[152,128]{1,0:T(8,128)S(1)} %collective-permute-done.16.refs_2_, ...), custom_call_target="tpu_custom_call" | custom-call | tf_op jit(solution)/shard_map/backward/pallas_call | solution.py:330
  100.0 2.2 %collective-permute-done.21 = f32[136,128]{1,0:T(8,128)S(1)} collective-permute-done((f32[136,128]{1,0:T(8,128)S(1)}, f32[136,128]{1,0:T(8,128)S(1)}, u32[]{:S(2)}, u32[]{:S(2)}) %collective-permute-start.21) | collective-permute-done | bytes 69664 | tf_op jit(solution)/shard_map/ppermute | solution.py:342
  104.3 2.0 forward.6
  106.4 2.1 collective-permute-start.24
  108.8 2.1 collective-permute-start.26
  110.8 3.6 %collective-permute-done.24.refs_2_ = f32[152,128]{1,0:T(8,128)S(1)} collective-permute-done((f32[152,128]{1,0:T(8,128)S(1)}, f32[152,128]{1,0:T(8,128)S(1)}, u32[]{:S(2)}, u32[]{:S(2)}) %collective-permute-start.24) | collective-permute-done | bytes 77856 | tf_op jit(solution)/shard_map/ppermute | solution.py:342
  116.1 2.4 %backward.7 = (f32[136,128]{1,0:T(8,128)S(1)}, f32[136,128]{1,0:T(8,128)S(1)}, f32[256,128]{1,0:T(8,128)S(1)}, f32[256,128]{1,0:T(8,128)S(1)}, f32[8,128]{1,0:T(8,128)S(1)}) custom-call(f32[1]{0:T(128)} %bitcast.13.refs_0_, f32[152,128]{1,0:T(8,128)S(1)} %get-tuple-element.104.refs_1_, f32[152,128]{1,0:T(8,128)S(1)} %collective-permute-done.24.refs_2_, ...), custom_call_target="tpu_custom_call" | custom-call | tf_op jit(solution)/shard_map/backward/pallas_call | solution.py:330
  124.2 1.9 collective-permute-done.29
  128.4 2.1 forward.7
  133.2 1.8 collective-permute-start.34
  135.0 5.1 %collective-permute-done.32.refs_2_ = f32[152,128]{1,0:T(8,128)S(1)} collective-permute-done((f32[152,128]{1,0:T(8,128)S(1)}, f32[152,128]{1,0:T(8,128)S(1)}, u32[]{:S(2)}, u32[]{:S(2)}) %collective-permute-start.32) | collective-permute-done | bytes 77856 | tf_op jit(solution)/shard_map/ppermute | solution.py:342
  140.1 2.4 %backward.8 = (f32[136,128]{1,0:T(8,128)S(1)}, f32[136,128]{1,0:T(8,128)S(1)}, f32[256,128]{1,0:T(8,128)S(1)}, f32[256,128]{1,0:T(8,128)S(1)}, f32[8,128]{1,0:T(8,128)S(1)}) custom-call(f32[1]{0:T(128)} %bitcast.14.refs_0_, f32[152,128]{1,0:T(8,128)S(1)} %get-tuple-element.115.refs_1_, f32[152,128]{1,0:T(8,128)S(1)} %collective-permute-done.32.refs_2_, ...), custom_call_target="tpu_custom_call" | custom-call | tf_op jit(solution)/shard_map/backward/pallas_call | solution.py:330
  148.2 2.2 %collective-permute-done.37 = f32[136,128]{1,0:T(8,128)S(1)} collective-permute-done((f32[136,128]{1,0:T(8,128)S(1)}, f32[136,128]{1,0:T(8,128)S(1)}, u32[]{:S(2)}, u32[]{:S(2)}) %collective-permute-start.37) | collective-permute-done | bytes 69664 | tf_op jit(solution)/shard_map/ppermute | solution.py:342
  152.6 2.0 forward.8
  154.6 2.0 collective-permute-start.40
  157.0 2.1 collective-permute-start.42
  159.1 3.9 %collective-permute-done.40.refs_2_ = f32[152,128]{1,0:T(8,128)S(1)} collective-permute-done((f32[152,128]{1,0:T(8,128)S(1)}, f32[152,128]{1,0:T(8,128)S(1)}, u32[]{:S(2)}, u32[]{:S(2)}) %collective-permute-start.40) | collective-permute-done | bytes 77856 | tf_op jit(solution)/shard_map/ppermute | solution.py:342
  164.2 2.4 %backward.9 = (f32[136,128]{1,0:T(8,128)S(1)}, f32[136,128]{1,0:T(8,128)S(1)}, f32[256,128]{1,0:T(8,128)S(1)}, f32[256,128]{1,0:T(8,128)S(1)}, f32[8,128]{1,0:T(8,128)S(1)}) custom-call(f32[1]{0:T(128)} %bitcast.15.refs_0_, f32[152,128]{1,0:T(8,128)S(1)} %get-tuple-element.126.refs_1_, f32[152,128]{1,0:T(8,128)S(1)} %collective-permute-done.40.refs_2_, ...), custom_call_target="tpu_custom_call" | custom-call | tf_op jit(solution)/shard_map/backward/pallas_call | solution.py:330
  172.4 1.9 collective-permute-done.45
  176.6 2.5 %forward.9 = (f32[256,128]{1,0:T(8,128)S(1)}, f32[256,128]{1,0:T(8,128)S(1)}, f32[256,128]{1,0:T(8,128)}, f32[256,128]{1,0:T(8,128)S(1)}, f32[8,128]{1,0:T(8,128)S(1)}, /*index=5*/f32[152,128]{1,0:T(8,128)S(1)}) custom-call(f32[136,128]{1,0:T(8,128)S(1)} %add_add_fusion.1.refs_0_, f32[136,128]{1,0:T(8,128)S(1)} %collective-permute-done.47.refs_1_, ...), custom_call_target="tpu_custom_call" | custom-call | tf_op jit(solution)/shard_map/forward/pallas_call | solution.py:330
  181.7 1.8 collective-permute-start.50
  183.5 4.2 %collective-permute-done.48.refs_2_ = f32[152,128]{1,0:T(8,128)S(1)} collective-permute-done((f32[152,128]{1,0:T(8,128)S(1)}, f32[152,128]{1,0:T(8,128)S(1)}, u32[]{:S(2)}, u32[]{:S(2)}) %collective-permute-start.48) | collective-permute-done | bytes 77856 | tf_op jit(solution)/shard_map/ppermute | solution.py:342
  196.9 2.4 %final.1 = (f32[256,128]{1,0:T(8,128)S(1)}, f32[192,128]{1,0:T(8,128)}, f32[192,128]{1,0:T(8,128)}, f32[136,128]{1,0:T(8,128)S(1)}, f32[136,128]{1,0:T(8,128)S(1)}) custom-call(f32[1]{0:T(128)} %bitcast.17.refs_0_, f32[8,128]{1,0:T(8,128)S(1)} %add_add_fusion.6.refs_1_, f32[256,128]{1,0:T(8,128)S(1)} %get-tuple-element.142.refs_2_, ...), custom_call_target="tpu_custom_call" | custom-call | tf_op jit(solution)/shard_map/final/pallas_call | solution.py:330
  205.0 1.9 collective-permute-done.57
  209.3 2.0 collective-permute-start.60
  211.7 1.9 collective-permute-start.62
  214.8 2.3 %collective-permute-done.62 = f32[8,128]{1,0:T(8,128)S(1)} collective-permute-done((f32[8,128]{1,0:T(8,128)S(1)}, f32[8,128]{1,0:T(8,128)S(1)}, u32[]{:S(2)}, u32[]{:S(2)}) %collective-permute-start.62) | collective-permute-done | bytes 4128 | tf_op jit(solution)/shard_map/ppermute | solution.py:342
  (165 shorter events, 86.4 us)
Async XLA Ops:
  22.3 7.1 %collective-permute-start = (f32[152,128]{1,0:T(8,128)S(1)}, f32[152,128]{1,0:T(8,128)S(1)}, u32[]{:S(2)}, u32[]{:S(2)}) collective-permute-start(f32[152,128]{1,0:T(8,128)S(1)} %first_forward.1.refs_1_), channel_id=1, source_target_pairs={{0,2},{1,3},{2,0},{3,1},{4,6},{5,7},{6,4},{7,5},{8,10},{9,11},{10,... | collective-permute-start | bytes 233480 | tf_op jit(solution)/shard_map/ppermute | solution.py:342
  26.4 4.4 %collective-permute-start.1 = (f32[152,128]{1,0:T(8,128)S(1)}, f32[152,128]{1,0:T(8,128)S(1)}, u32[]{:S(2)}, u32[]{:S(2)}) collective-permute-start(f32[152,128]{1,0:T(8,128)S(1)} %first_forward.1.refs_1_), channel_id=1, source_target_pairs={{0,1},{1,0},{2,3},{3,2},{4,5},{5,4},{6,7},{7,6},{8,9},{9,8},{10,11... | collective-permute-start | bytes 233480 | tf_op jit(solution)/shard_map/ppermute | solution.py:342
  28.0 6.2 %collective-permute-start.2 = (f32[152,128]{1,0:T(8,128)S(1)}, f32[152,128]{1,0:T(8,128)S(1)}, u32[]{:S(2)}, u32[]{:S(2)}) collective-permute-start(f32[152,128]{1,0:T(8,128)S(1)} %first_forward.1.refs_1_), channel_id=1, source_target_pairs={{0,3},{1,2},{2,1},{3,0},{4,7},{5,6},{6,5},{7,4},{8,11},{9,10},{10,... | collective-permute-start | bytes 233480 | tf_op jit(solution)/shard_map/ppermute | solution.py:342
  42.0 6.0 %collective-permute-start.4 = (f32[256,128]{1,0:T(8,128)S(1)}, f32[256,128]{1,0:T(8,128)S(1)}, u32[]{:S(2)}, u32[]{:S(2)}) collective-permute-start(f32[256,128]{1,0:T(8,128)S(1)} %add.162), channel_id=1, source_target_pairs={{0,8},{4,12},{8,0},{12,4},{16,24},{20,28},{24,16},{28,20},{1,9},{5... | collective-permute-start | bytes 393224 | tf_op jit(solution)/shard_map/ppermute | solution.py:342
  43.6 8.1 %collective-permute-start.5 = (f32[256,128]{1,0:T(8,128)S(1)}, f32[256,128]{1,0:T(8,128)S(1)}, u32[]{:S(2)}, u32[]{:S(2)}) collective-permute-start(f32[256,128]{1,0:T(8,128)S(1)} %add.162), channel_id=1, source_target_pairs={{0,16},{4,20},{8,24},{12,28},{16,0},{20,4},{24,8},{28,12},{1,17},{... | collective-permute-start | bytes 393224 | tf_op jit(solution)/shard_map/ppermute | solution.py:342
  45.1 6.6 %collective-permute-start.6 = (f32[256,128]{1,0:T(8,128)S(1)}, f32[256,128]{1,0:T(8,128)S(1)}, u32[]{:S(2)}, u32[]{:S(2)}) collective-permute-start(f32[256,128]{1,0:T(8,128)S(1)} %add.162), channel_id=1, source_target_pairs={{0,24},{4,28},{8,16},{12,20},{16,8},{20,12},{24,0},{28,4},{1,25},{... | collective-permute-start | bytes 393224 | tf_op jit(solution)/shard_map/ppermute | solution.py:342
  58.7 7.2 %collective-permute-start.10 = (f32[152,128]{1,0:T(8,128)S(1)}, f32[152,128]{1,0:T(8,128)S(1)}, u32[]{:S(2)}, u32[]{:S(2)}) collective-permute-start(f32[152,128]{1,0:T(8,128)S(1)} %get-tuple-element.84.refs_1_), channel_id=1, source_target_pairs={{0,3},{1,2},{2,1},{3,0},{4,7},{5,6},{6,5},{7,4},{8,11},{9,10},{10,... | collective-permute-start | bytes 233480 | tf_op jit(solution)/shard_map/ppermute | solution.py:342
  60.1 8.1 %collective-permute-start.8 = (f32[152,128]{1,0:T(8,128)S(1)}, f32[152,128]{1,0:T(8,128)S(1)}, u32[]{:S(2)}, u32[]{:S(2)}) collective-permute-start(f32[152,128]{1,0:T(8,128)S(1)} %get-tuple-element.84.refs_1_), channel_id=1, source_target_pairs={{0,2},{1,3},{2,0},{3,1},{4,6},{5,7},{6,4},{7,5},{8,10},{9,11},{10,... | collective-permute-start | bytes 233480 | tf_op jit(solution)/shard_map/ppermute | solution.py:342
  60.1 8.1 %collective-permute-start.9 = (f32[152,128]{1,0:T(8,128)S(1)}, f32[152,128]{1,0:T(8,128)S(1)}, u32[]{:S(2)}, u32[]{:S(2)}) collective-permute-start(f32[152,128]{1,0:T(8,128)S(1)} %get-tuple-element.84.refs_1_), channel_id=1, source_target_pairs={{0,1},{1,0},{2,3},{3,2},{4,5},{5,4},{6,7},{7,6},{8,9},{9,8},{10,11... | collective-permute-start | bytes 233480 | tf_op jit(solution)/shard_map/ppermute | solution.py:342
  72.2 4.4 %collective-permute-start.12 = (f32[136,128]{1,0:T(8,128)S(1)}, f32[136,128]{1,0:T(8,128)S(1)}, u32[]{:S(2)}, u32[]{:S(2)}) collective-permute-start(f32[136,128]{1,0:T(8,128)S(1)} %add.166), channel_id=1, source_target_pairs={{0,8},{4,12},{8,0},{12,4},{16,24},{20,28},{24,16},{28,20},{1,9},{5... | collective-permute-start | bytes 208904 | tf_op jit(solution)/shard_map/ppermute | solution.py:342
  73.5 5.1 %collective-permute-start.13 = (f32[136,128]{1,0:T(8,128)S(1)}, f32[136,128]{1,0:T(8,128)S(1)}, u32[]{:S(2)}, u32[]{:S(2)}) collective-permute-start(f32[136,128]{1,0:T(8,128)S(1)} %add.166), channel_id=1, source_target_pairs={{0,16},{4,20},{8,24},{12,28},{16,0},{20,4},{24,8},{28,12},{1,17},{... | collective-permute-start | bytes 208904 | tf_op jit(solution)/shard_map/ppermute | solution.py:342
  74.3 5.2 %collective-permute-start.14 = (f32[136,128]{1,0:T(8,128)S(1)}, f32[136,128]{1,0:T(8,128)S(1)}, u32[]{:S(2)}, u32[]{:S(2)}) collective-permute-start(f32[136,128]{1,0:T(8,128)S(1)} %add.166), channel_id=1, source_target_pairs={{0,24},{4,28},{8,16},{12,20},{16,8},{20,12},{24,0},{28,4},{1,25},{... | collective-permute-start | bytes 208904 | tf_op jit(solution)/shard_map/ppermute | solution.py:342
  83.0 6.6 %collective-permute-start.16 = (f32[152,128]{1,0:T(8,128)S(1)}, f32[152,128]{1,0:T(8,128)S(1)}, u32[]{:S(2)}, u32[]{:S(2)}) collective-permute-start(f32[152,128]{1,0:T(8,128)S(1)} %get-tuple-element.93.refs_1_), channel_id=1, source_target_pairs={{0,2},{1,3},{2,0},{3,1},{4,6},{5,7},{6,4},{7,5},{8,10},{9,11},{10,... | collective-permute-start | bytes 233480 | tf_op jit(solution)/shard_map/ppermute | solution.py:342
  83.6 6.2 %collective-permute-start.17 = (f32[152,128]{1,0:T(8,128)S(1)}, f32[152,128]{1,0:T(8,128)S(1)}, u32[]{:S(2)}, u32[]{:S(2)}) collective-permute-start(f32[152,128]{1,0:T(8,128)S(1)} %get-tuple-element.93.refs_1_), channel_id=1, source_target_pairs={{0,1},{1,0},{2,3},{3,2},{4,5},{5,4},{6,7},{7,6},{8,9},{9,8},{10,11... | collective-permute-start | bytes 233480 | tf_op jit(solution)/shard_map/ppermute | solution.py:342
  85.7 6.2 %collective-permute-start.18 = (f32[152,128]{1,0:T(8,128)S(1)}, f32[152,128]{1,0:T(8,128)S(1)}, u32[]{:S(2)}, u32[]{:S(2)}) collective-permute-start(f32[152,128]{1,0:T(8,128)S(1)} %get-tuple-element.93.refs_1_), channel_id=1, source_target_pairs={{0,3},{1,2},{2,1},{3,0},{4,7},{5,6},{6,5},{7,4},{8,11},{9,10},{10,... | collective-permute-start | bytes 233480 | tf_op jit(solution)/shard_map/ppermute | solution.py:342
  95.6 4.4 %collective-permute-start.20 = (f32[136,128]{1,0:T(8,128)S(1)}, f32[136,128]{1,0:T(8,128)S(1)}, u32[]{:S(2)}, u32[]{:S(2)}) collective-permute-start(f32[136,128]{1,0:T(8,128)S(1)} %add.170), channel_id=1, source_target_pairs={{0,8},{4,12},{8,0},{12,4},{16,24},{20,28},{24,16},{28,20},{1,9},{5... | collective-permute-start | bytes 208904 | tf_op jit(solution)/shard_map/ppermute | solution.py:342
  97.2 5.1 %collective-permute-start.21 = (f32[136,128]{1,0:T(8,128)S(1)}, f32[136,128]{1,0:T(8,128)S(1)}, u32[]{:S(2)}, u32[]{:S(2)}) collective-permute-start(f32[136,128]{1,0:T(8,128)S(1)} %add.170), channel_id=1, source_target_pairs={{0,16},{4,20},{8,24},{12,28},{16,0},{20,4},{24,8},{28,12},{1,17},{... | collective-permute-start | bytes 208904 | tf_op jit(solution)/shard_map/ppermute | solution.py:342
  97.8 5.2 %collective-permute-start.22 = (f32[136,128]{1,0:T(8,128)S(1)}, f32[136,128]{1,0:T(8,128)S(1)}, u32[]{:S(2)}, u32[]{:S(2)}) collective-permute-start(f32[136,128]{1,0:T(8,128)S(1)} %add.170), channel_id=1, source_target_pairs={{0,24},{4,28},{8,16},{12,20},{16,8},{20,12},{24,0},{28,4},{1,25},{... | collective-permute-start | bytes 208904 | tf_op jit(solution)/shard_map/ppermute | solution.py:342
  106.4 8.0 %collective-permute-start.24 = (f32[152,128]{1,0:T(8,128)S(1)}, f32[152,128]{1,0:T(8,128)S(1)}, u32[]{:S(2)}, u32[]{:S(2)}) collective-permute-start(f32[152,128]{1,0:T(8,128)S(1)} %get-tuple-element.104.refs_1_), channel_id=1, source_target_pairs={{0,2},{1,3},{2,0},{3,1},{4,6},{5,7},{6,4},{7,5},{8,10},{9,11},{10,... | collective-permute-start | bytes 233480 | tf_op jit(solution)/shard_map/ppermute | solution.py:342
  108.5 5.9 %collective-permute-start.25 = (f32[152,128]{1,0:T(8,128)S(1)}, f32[152,128]{1,0:T(8,128)S(1)}, u32[]{:S(2)}, u32[]{:S(2)}) collective-permute-start(f32[152,128]{1,0:T(8,128)S(1)} %get-tuple-element.104.refs_1_), channel_id=1, source_target_pairs={{0,1},{1,0},{2,3},{3,2},{4,5},{5,4},{6,7},{7,6},{8,9},{9,8},{10,11... | collective-permute-start | bytes 233480 | tf_op jit(solution)/shard_map/ppermute | solution.py:342
  108.8 7.3 %collective-permute-start.26 = (f32[152,128]{1,0:T(8,128)S(1)}, f32[152,128]{1,0:T(8,128)S(1)}, u32[]{:S(2)}, u32[]{:S(2)}) collective-permute-start(f32[152,128]{1,0:T(8,128)S(1)} %get-tuple-element.104.refs_1_), channel_id=1, source_target_pairs={{0,3},{1,2},{2,1},{3,0},{4,7},{5,6},{6,5},{7,4},{8,11},{9,10},{10,... | collective-permute-start | bytes 233480 | tf_op jit(solution)/shard_map/ppermute | solution.py:342
  119.8 4.4 %collective-permute-start.28 = (f32[136,128]{1,0:T(8,128)S(1)}, f32[136,128]{1,0:T(8,128)S(1)}, u32[]{:S(2)}, u32[]{:S(2)}) collective-permute-start(f32[136,128]{1,0:T(8,128)S(1)} %add.174), channel_id=1, source_target_pairs={{0,8},{4,12},{8,0},{12,4},{16,24},{20,28},{24,16},{28,20},{1,9},{5... | collective-permute-start | bytes 208904 | tf_op jit(solution)/shard_map/ppermute | solution.py:342
  121.1 5.1 %collective-permute-start.29 = (f32[136,128]{1,0:T(8,128)S(1)}, f32[136,128]{1,0:T(8,128)S(1)}, u32[]{:S(2)}, u32[]{:S(2)}) collective-permute-start(f32[136,128]{1,0:T(8,128)S(1)} %add.174), channel_id=1, source_target_pairs={{0,16},{4,20},{8,24},{12,28},{16,0},{20,4},{24,8},{28,12},{1,17},{... | collective-permute-start | bytes 208904 | tf_op jit(solution)/shard_map/ppermute | solution.py:342
  121.9 5.2 %collective-permute-start.30 = (f32[136,128]{1,0:T(8,128)S(1)}, f32[136,128]{1,0:T(8,128)S(1)}, u32[]{:S(2)}, u32[]{:S(2)}) collective-permute-start(f32[136,128]{1,0:T(8,128)S(1)} %add.174), channel_id=1, source_target_pairs={{0,24},{4,28},{8,16},{12,20},{16,8},{20,12},{24,0},{28,4},{1,25},{... | collective-permute-start | bytes 208904 | tf_op jit(solution)/shard_map/ppermute | solution.py:342
  130.6 9.5 %collective-permute-start.32 = (f32[152,128]{1,0:T(8,128)S(1)}, f32[152,128]{1,0:T(8,128)S(1)}, u32[]{:S(2)}, u32[]{:S(2)}) collective-permute-start(f32[152,128]{1,0:T(8,128)S(1)} %get-tuple-element.115.refs_1_), channel_id=1, source_target_pairs={{0,2},{1,3},{2,0},{3,1},{4,6},{5,7},{6,4},{7,5},{8,10},{9,11},{10,... | collective-permute-start | bytes 233480 | tf_op jit(solution)/shard_map/ppermute | solution.py:342
  132.2 7.9 %collective-permute-start.33 = (f32[152,128]{1,0:T(8,128)S(1)}, f32[152,128]{1,0:T(8,128)S(1)}, u32[]{:S(2)}, u32[]{:S(2)}) collective-permute-start(f32[152,128]{1,0:T(8,128)S(1)} %get-tuple-element.115.refs_1_), channel_id=1, source_target_pairs={{0,1},{1,0},{2,3},{3,2},{4,5},{5,4},{6,7},{7,6},{8,9},{9,8},{10,11... | collective-permute-start | bytes 233480 | tf_op jit(solution)/shard_map/ppermute | solution.py:342
  133.2 6.9 %collective-permute-start.34 = (f32[152,128]{1,0:T(8,128)S(1)}, f32[152,128]{1,0:T(8,128)S(1)}, u32[]{:S(2)}, u32[]{:S(2)}) collective-permute-start(f32[152,128]{1,0:T(8,128)S(1)} %get-tuple-element.115.refs_1_), channel_id=1, source_target_pairs={{0,3},{1,2},{2,1},{3,0},{4,7},{5,6},{6,5},{7,4},{8,11},{9,10},{10,... | collective-permute-start | bytes 233480 | tf_op jit(solution)/shard_map/ppermute | solution.py:342
  143.9 4.4 %collective-permute-start.36 = (f32[136,128]{1,0:T(8,128)S(1)}, f32[136,128]{1,0:T(8,128)S(1)}, u32[]{:S(2)}, u32[]{:S(2)}) collective-permute-start(f32[136,128]{1,0:T(8,128)S(1)} %add.178), channel_id=1, source_target_pairs={{0,8},{4,12},{8,0},{12,4},{16,24},{20,28},{24,16},{28,20},{1,9},{5... | collective-permute-start | bytes 208904 | tf_op jit(solution)/shard_map/ppermute | solution.py:342
  145.4 5.1 %collective-permute-start.37 = (f32[136,128]{1,0:T(8,128)S(1)}, f32[136,128]{1,0:T(8,128)S(1)}, u32[]{:S(2)}, u32[]{:S(2)}) collective-permute-start(f32[136,128]{1,0:T(8,128)S(1)} %add.178), channel_id=1, source_target_pairs={{0,16},{4,20},{8,24},{12,28},{16,0},{20,4},{24,8},{28,12},{1,17},{... | collective-permute-start | bytes 208904 | tf_op jit(solution)/shard_map/ppermute | solution.py:342
  146.0 5.2 %collective-permute-start.38 = (f32[136,128]{1,0:T(8,128)S(1)}, f32[136,128]{1,0:T(8,128)S(1)}, u32[]{:S(2)}, u32[]{:S(2)}) collective-permute-start(f32[136,128]{1,0:T(8,128)S(1)} %add.178), channel_id=1, source_target_pairs={{0,24},{4,28},{8,16},{12,20},{16,8},{20,12},{24,0},{28,4},{1,25},{... | collective-permute-start | bytes 208904 | tf_op jit(solution)/shard_map/ppermute | solution.py:342
  154.6 8.4 %collective-permute-start.40 = (f32[152,128]{1,0:T(8,128)S(1)}, f32[152,128]{1,0:T(8,128)S(1)}, u32[]{:S(2)}, u32[]{:S(2)}) collective-permute-start(f32[152,128]{1,0:T(8,128)S(1)} %get-tuple-element.126.refs_1_), channel_id=1, source_target_pairs={{0,2},{1,3},{2,0},{3,1},{4,6},{5,7},{6,4},{7,5},{8,10},{9,11},{10,... | collective-permute-start | bytes 233480 | tf_op jit(solution)/shard_map/ppermute | solution.py:342
  156.7 6.3 %collective-permute-start.41 = (f32[152,128]{1,0:T(8,128)S(1)}, f32[152,128]{1,0:T(8,128)S(1)}, u32[]{:S(2)}, u32[]{:S(2)}) collective-permute-start(f32[152,128]{1,0:T(8,128)S(1)} %get-tuple-element.126.refs_1_), channel_id=1, source_target_pairs={{0,1},{1,0},{2,3},{3,2},{4,5},{5,4},{6,7},{7,6},{8,9},{9,8},{10,11... | collective-permute-start | bytes 233480 | tf_op jit(solution)/shard_map/ppermute | solution.py:342
  157.0 7.2 %collective-permute-start.42 = (f32[152,128]{1,0:T(8,128)S(1)}, f32[152,128]{1,0:T(8,128)S(1)}, u32[]{:S(2)}, u32[]{:S(2)}) collective-permute-start(f32[152,128]{1,0:T(8,128)S(1)} %get-tuple-element.126.refs_1_), channel_id=1, source_target_pairs={{0,3},{1,2},{2,1},{3,0},{4,7},{5,6},{6,5},{7,4},{8,11},{9,10},{10,... | collective-permute-start | bytes 233480 | tf_op jit(solution)/shard_map/ppermute | solution.py:342
  168.0 4.4 %collective-permute-start.44 = (f32[136,128]{1,0:T(8,128)S(1)}, f32[136,128]{1,0:T(8,128)S(1)}, u32[]{:S(2)}, u32[]{:S(2)}) collective-permute-start(f32[136,128]{1,0:T(8,128)S(1)} %add.182), channel_id=1, source_target_pairs={{0,8},{4,12},{8,0},{12,4},{16,24},{20,28},{24,16},{28,20},{1,9},{5... | collective-permute-start | bytes 208904 | tf_op jit(solution)/shard_map/ppermute | solution.py:342
  169.2 5.1 %collective-permute-start.45 = (f32[136,128]{1,0:T(8,128)S(1)}, f32[136,128]{1,0:T(8,128)S(1)}, u32[]{:S(2)}, u32[]{:S(2)}) collective-permute-start(f32[136,128]{1,0:T(8,128)S(1)} %add.182), channel_id=1, source_target_pairs={{0,16},{4,20},{8,24},{12,28},{16,0},{20,4},{24,8},{28,12},{1,17},{... | collective-permute-start | bytes 208904 | tf_op jit(solution)/shard_map/ppermute | solution.py:342
  170.0 5.2 %collective-permute-start.46 = (f32[136,128]{1,0:T(8,128)S(1)}, f32[136,128]{1,0:T(8,128)S(1)}, u32[]{:S(2)}, u32[]{:S(2)}) collective-permute-start(f32[136,128]{1,0:T(8,128)S(1)} %add.182), channel_id=1, source_target_pairs={{0,24},{4,28},{8,16},{12,20},{16,8},{20,12},{24,0},{28,4},{1,25},{... | collective-permute-start | bytes 208904 | tf_op jit(solution)/shard_map/ppermute | solution.py:342
  179.1 8.5 %collective-permute-start.48 = (f32[152,128]{1,0:T(8,128)S(1)}, f32[152,128]{1,0:T(8,128)S(1)}, u32[]{:S(2)}, u32[]{:S(2)}) collective-permute-start(f32[152,128]{1,0:T(8,128)S(1)} %get-tuple-element.137.refs_1_), channel_id=1, source_target_pairs={{0,2},{1,3},{2,0},{3,1},{4,6},{5,7},{6,4},{7,5},{8,10},{9,11},{10,... | collective-permute-start | bytes 233480 | tf_op jit(solution)/shard_map/ppermute | solution.py:342
  180.8 6.9 %collective-permute-start.49 = (f32[152,128]{1,0:T(8,128)S(1)}, f32[152,128]{1,0:T(8,128)S(1)}, u32[]{:S(2)}, u32[]{:S(2)}) collective-permute-start(f32[152,128]{1,0:T(8,128)S(1)} %get-tuple-element.137.refs_1_), channel_id=1, source_target_pairs={{0,1},{1,0},{2,3},{3,2},{4,5},{5,4},{6,7},{7,6},{8,9},{9,8},{10,11... | collective-permute-start | bytes 233480 | tf_op jit(solution)/shard_map/ppermute | solution.py:342
  181.7 6.9 %collective-permute-start.50 = (f32[152,128]{1,0:T(8,128)S(1)}, f32[152,128]{1,0:T(8,128)S(1)}, u32[]{:S(2)}, u32[]{:S(2)}) collective-permute-start(f32[152,128]{1,0:T(8,128)S(1)} %get-tuple-element.137.refs_1_), channel_id=1, source_target_pairs={{0,3},{1,2},{2,1},{3,0},{4,7},{5,6},{6,5},{7,4},{8,11},{9,10},{10,... | collective-permute-start | bytes 233480 | tf_op jit(solution)/shard_map/ppermute | solution.py:342
  190.2 3.6 %collective-permute-start.52 = (f32[8,128]{1,0:T(8,128)S(1)}, f32[8,128]{1,0:T(8,128)S(1)}, u32[]{:S(2)}, u32[]{:S(2)}) collective-permute-start(f32[8,128]{1,0:T(8,128)S(1)} %add.186), channel_id=1, source_target_pairs={{0,8},{4,12},{8,0},{12,4},{16,24},{20,28},{24,16},{28,20},{1,9},{5... | collective-permute-start | bytes 12296 | tf_op jit(solution)/shard_map/ppermute | solution.py:342
  191.7 3.6 %collective-permute-start.53 = (f32[8,128]{1,0:T(8,128)S(1)}, f32[8,128]{1,0:T(8,128)S(1)}, u32[]{:S(2)}, u32[]{:S(2)}) collective-permute-start(f32[8,128]{1,0:T(8,128)S(1)} %add.186), channel_id=1, source_target_pairs={{0,16},{4,20},{8,24},{12,28},{16,0},{20,4},{24,8},{28,12},{1,17},{... | collective-permute-start | bytes 12296 | tf_op jit(solution)/shard_map/ppermute | solution.py:342
  192.3 4.5 %collective-permute-start.54 = (f32[8,128]{1,0:T(8,128)S(1)}, f32[8,128]{1,0:T(8,128)S(1)}, u32[]{:S(2)}, u32[]{:S(2)}) collective-permute-start(f32[8,128]{1,0:T(8,128)S(1)} %add.186), channel_id=1, source_target_pairs={{0,24},{4,28},{8,16},{12,20},{16,8},{20,12},{24,0},{28,4},{1,25},{... | collective-permute-start | bytes 12296 | tf_op jit(solution)/shard_map/ppermute | solution.py:342
  200.7 4.4 %collective-permute-start.56 = (f32[136,128]{1,0:T(8,128)S(1)}, f32[136,128]{1,0:T(8,128)S(1)}, u32[]{:S(2)}, u32[]{:S(2)}) collective-permute-start(f32[136,128]{1,0:T(8,128)S(1)} %maximum_select_fusion.5), channel_id=1, source_target_pairs={{0,8},{4,12},{8,0},{12,4},{16,24},{20,28},{24,16},{28,20},{1,9},{5... | collective-permute-start | bytes 208904 | tf_op jit(solution)/shard_map/ppermute | solution.py:342
  201.9 5.1 %collective-permute-start.57 = (f32[136,128]{1,0:T(8,128)S(1)}, f32[136,128]{1,0:T(8,128)S(1)}, u32[]{:S(2)}, u32[]{:S(2)}) collective-permute-start(f32[136,128]{1,0:T(8,128)S(1)} %maximum_select_fusion.5), channel_id=1, source_target_pairs={{0,16},{4,20},{8,24},{12,28},{16,0},{20,4},{24,8},{28,12},{1,17},{... | collective-permute-start | bytes 208904 | tf_op jit(solution)/shard_map/ppermute | solution.py:342
  202.7 5.2 %collective-permute-start.58 = (f32[136,128]{1,0:T(8,128)S(1)}, f32[136,128]{1,0:T(8,128)S(1)}, u32[]{:S(2)}, u32[]{:S(2)}) collective-permute-start(f32[136,128]{1,0:T(8,128)S(1)} %maximum_select_fusion.5), channel_id=1, source_target_pairs={{0,24},{4,28},{8,16},{12,20},{16,8},{20,12},{24,0},{28,4},{1,25},{... | collective-permute-start | bytes 208904 | tf_op jit(solution)/shard_map/ppermute | solution.py:342
  209.3 5.1 %collective-permute-start.60 = (f32[8,128]{1,0:T(8,128)S(1)}, f32[8,128]{1,0:T(8,128)S(1)}, u32[]{:S(2)}, u32[]{:S(2)}) collective-permute-start(f32[8,128]{1,0:T(8,128)S(1)} %max.28), channel_id=1, source_target_pairs={{0,2},{1,3},{2,0},{3,1},{4,6},{5,7},{6,4},{7,5},{8,10},{9,11},{10,... | collective-permute-start | bytes 12296 | tf_op jit(solution)/shard_map/ppermute | solution.py:342
  211.2 3.6 %collective-permute-start.61 = (f32[8,128]{1,0:T(8,128)S(1)}, f32[8,128]{1,0:T(8,128)S(1)}, u32[]{:S(2)}, u32[]{:S(2)}) collective-permute-start(f32[8,128]{1,0:T(8,128)S(1)} %max.28), channel_id=1, source_target_pairs={{0,1},{1,0},{2,3},{3,2},{4,5},{5,4},{6,7},{7,6},{8,9},{9,8},{10,11... | collective-permute-start | bytes 12296 | tf_op jit(solution)/shard_map/ppermute | solution.py:342
  211.7 5.4 %collective-permute-start.62 = (f32[8,128]{1,0:T(8,128)S(1)}, f32[8,128]{1,0:T(8,128)S(1)}, u32[]{:S(2)}, u32[]{:S(2)}) collective-permute-start(f32[8,128]{1,0:T(8,128)S(1)} %max.28), channel_id=1, source_target_pairs={{0,3},{1,2},{2,1},{3,0},{4,7},{5,6},{6,5},{7,4},{8,11},{9,10},{10,... | collective-permute-start | bytes 12296 | tf_op jit(solution)/shard_map/ppermute | solution.py:342
  (28 other events, 282.9 us)

commit v3 on v2

v3 whole, which is shorter than its diff:
```python
import functools

import jax
import jax.numpy as jnp
from jax import lax
from jax.experimental import pallas as pl
from jax.experimental.pallas import tpu as pltpu
from jax.sharding import PartitionSpec as P

YG = 64
CG = 6

SIGMA = 1e-06
RELAX = 1.6

F32 = jnp.float32
BF16 = jnp.bfloat16
LANES = 128
UNROLL = 6
LANES = 128
TILES = 8
VMEM_LIMIT = 24 * 1024 * 1024


def dot(a, b):
    return lax.dot_general(a, b, (((1,), (0,)), ((), ())), preferred_element_type=F32)


def split2(x):
    high = x.astype(BF16)
    return high, (x - high.astype(F32)).astype(BF16)


def split3(x):
    high = x.astype(BF16)
    return (high, *split2(x - high.astype(F32)))


def tree(parts, op=jnp.add):
    parts = list(parts)
    while len(parts) > 1:
        parts = [op(parts[i], parts[i + 1]) for i in range(0, len(parts), 2)]
    return parts[0]


def row_sum(x):
    return jnp.sum(x, axis=0, keepdims=True)


def half_sum(x):
    half = x.shape[0] // 2
    return row_sum(x[:half]) + row_sum(x[half:])


def turn(odd, x):
    half = x.shape[0] // 2
    return jnp.where(odd, jnp.concatenate([x[half:], x[:half]], axis=0), x)


def pad_rows(rows):
    return jnp.concatenate(list(rows) + [jnp.zeros((8 - len(rows), LANES), F32)], axis=0)


def gather(onehot_ref, x):
    both = dot(onehot_ref[...], jnp.concatenate(split2(x), axis=1))
    high, low = both[:, :LANES], both[:, LANES:]
    blocks = high.shape[0] // TILES
    shape = (blocks, TILES, LANES)
    return jnp.concatenate([high.reshape(shape), low.reshape(shape)], axis=1).reshape(2 * TILES * blocks, LANES)


def scatter(onehot, x):
    both = dot(onehot, jnp.concatenate(split2(x), axis=1))
    return both[:, :LANES] + both[:, LANES:]


def run_tiles(w_ref, l_ref, finish):
    pairs = TILES // 2
    blocks = w_ref.shape[0] // pairs
    unroll = next(n for n in (UNROLL, 6, 4, 3, 2, 1) if blocks % n == 0)
    of_pair = lax.broadcasted_iota(jnp.int32, (2 * TILES, 2 * LANES), 0) % TILES // 2

    def body(step, carry):
        for inner in range(unroll):
            block = step * unroll + inner
            left = l_ref[pl.ds(pl.multiple_of(block * 2 * TILES, 2 * TILES), 2 * TILES), :]
            out = dot(left, w_ref[pairs * block])
            for k in range(1, pairs):
                out = jnp.where(of_pair == k, dot(left, w_ref[pairs * block + k]), out)
            finish(pl.multiple_of(block * TILES, TILES), out[:TILES] + out[TILES:])
        return carry

    lax.fori_loop(0, blocks // unroll, body, 0)


def forward_parts(vec, gf_ref, wt_ref, out_ref, l_ref):
    picked = gather(gf_ref, vec)
    first = lax.broadcasted_iota(jnp.int32, picked.shape, 0) % 2 == 0
    zero = jnp.zeros_like(picked)
    l_ref[:, :LANES] = jnp.where(first, picked, zero).astype(BF16)
    l_ref[:, LANES:] = jnp.where(first, zero, picked).astype(BF16)

    def finish(at, out):
        out_ref[pl.ds(at, TILES), :] = out[:, :LANES] + out[:, LANES:]

    run_tiles(wt_ref, l_ref, finish)


def backward_sum(vec, gb_ref, sb_ref, w_ref, l_ref, rows_ref):
    picked = gather(gb_ref, vec).astype(BF16)
    l_ref[:, :LANES] = picked
    l_ref[:, LANES:] = picked
    first = lax.broadcasted_iota(jnp.int32, (TILES, LANES), 0) % 2 == 0

    def finish(at, out):
        rows_ref[pl.ds(at, TILES), :] = jnp.where(first, out[:, :LANES], out[:, LANES:])

    run_tiles(w_ref, l_ref, finish)
    return scatter(sb_ref[...], rows_ref[...])


def gathered_rows(part_refs, s_ref):
    count = s_ref.shape[2]
    return tree(scatter(s_ref[j], ref[:count, :]) for j, ref in enumerate(part_refs))


def put_halves(refs, total, extra):
    half = total.shape[0] // 2
    for ref, part in zip(refs, (total[:half], total[half:])):
        ref[:half, :] = part
        ref[half:, :] = extra


def select_columns(ref, rows):
    size, count = ref.shape
    for row in range(pl.cdiv(count, LANES)):
        width = min(LANES, count - row * LANES)
        hit = lax.broadcasted_iota(jnp.int32, (size, width), 0) == rows[row : row + 1, :width].astype(jnp.int32)
        ref[:, row * LANES : row * LANES + width] = jnp.where(hit, 1.0, 0.0).astype(BF16)


def select_rows(ref, rows):
    count, size = ref.shape
    across = rows.T.astype(jnp.int32)
    for row in range(pl.cdiv(count, LANES)):
        width = min(LANES, count - row * LANES)
        hit = lax.broadcasted_iota(jnp.int32, (width, size), 1) == across[:width, row : row + 1]
        ref[row * LANES : row * LANES + width, :] = jnp.where(hit, 1.0, 0.0).astype(BF16)


def both_kinds(a_steps, a_ref, g_ref, convert):
    step = pl.program_id(0)

    @pl.when(step < a_steps)
    def _():
        convert(a_ref)

    @pl.when(step >= a_steps)
    def _():
        convert(g_ref)


def split_transposed_kernel(a_steps, rho_ref, a_ref, g_ref, wt_ref):
    def convert(ref):
        for t in range(ref.shape[0]):
            at = (t % 2) * LANES
            high, low = split2(ref[t].T)
            wt_ref[t // 2, at : at + LANES, :LANES] = high
            wt_ref[t // 2, at : at + LANES, LANES:] = low

    both_kinds(a_steps, a_ref, g_ref, convert)


def split_kernel(a_steps, rho_ref, a_ref, g_ref, w_ref, sq_ref):
    def convert(ref):
        for t in range(ref.shape[0]):
            at = (t % 2) * LANES
            tile = ref[t]
            high, low = split2(tile)
            w_ref[t // 2, :LANES, at : at + LANES] = high
            w_ref[t // 2, LANES:, at : at + LANES] = low
            sq_ref[t : t + 1, :] = row_sum(tile * tile)

    both_kinds(a_steps, a_ref, g_ref, convert)


def turned_places(odd, places, xcount):
    half = xcount // 2
    moved = jnp.where(places >= half, places - half, places + half)
    return jnp.where(odd, moved, places)


def first_forward_kernel(odd_ref, v_in_ref, at_ref, wt_ref, out_ref, v_ref, gf_ref, l_ref):
    odd = odd_ref[0] == 1
    count = 2 * wt_ref.shape[0]
    v = turn(odd, v_in_ref[...])
    v_ref[...] = v
    out_ref[count:, :] = at_ref[...]
    xrows = jnp.concatenate([at_ref[4:], at_ref[:4]], axis=0)
    select_rows(gf_ref, turned_places(odd, xrows, v.shape[0]))
    forward_parts(v, gf_ref, wt_ref, out_ref, l_ref)


def first_backward_kernel(n_col, ycount, acount, *refs):
    rho_ref, odd_ref, *refs = refs
    part_refs, refs = refs[:n_col], refs[n_col:]
    (w_ref, sq_ref, slack_ref, dual_ref), refs = refs[:4], refs[4:]
    mine_ref, theirs_ref, y_ref, s_ref, gb_ref, sb_ref, l_ref, rows_ref = refs
    rho, odd = rho_ref[0], odd_ref[0] == 1
    count = s_ref.shape[2]
    for j, ref in enumerate(part_refs):
        select_columns(s_ref.at[j], ref[count:, :])
    places = part_refs[0][count:, :]
    select_rows(gb_ref, places)
    select_columns(sb_ref, turned_places(odd, places[4:], sb_ref.shape[0]))
    full = gathered_rows(part_refs, s_ref)
    y_ref[...] = full
    top = rho * slack_ref[...] - dual_ref[...] - rho * full[:ycount]
    vec = jnp.concatenate([top, -full[ycount:]], axis=0)
    total = backward_sum(vec, gb_ref, sb_ref, w_ref, l_ref, rows_ref)
    squares = sq_ref[...]
    is_a = lax.broadcasted_iota(jnp.int32, squares.shape, 0) < acount
    parts = split3(jnp.where(is_a, rho * squares, squares))
    squares = sum(dot(sb_ref[...], part) for part in parts)
    half = total.shape[0] // 2
    mine_ref[:half, :] = total[:half]
    mine_ref[half:, :] = squares[:half]
    theirs_ref[:half, :] = total[half:]
    theirs_ref[half:, :] = squares[half:]


def finish_forward(u, p, resid, shifted, out_ref, gf_ref, w_ref, l_ref):
    count = 2 * w_ref.shape[0]
    weighted = shifted * u
    rows = [half_sum(resid * u), half_sum(weighted * u)]
    if p is not None:
        rows.append(half_sum(weighted * p))
    out_ref[count:, :] = pad_rows(rows)
    forward_parts(u, gf_ref, w_ref, out_ref, l_ref)


def second_forward_kernel(odd_ref, mine_ref, theirs_ref, v_ref, d_in_ref, c_in_ref, gf_ref, w_ref, *refs):
    r_ref, u_ref, pre_ref, d_ref, c_ref, out_ref, l_ref = refs
    odd = odd_ref[0] == 1
    half = v_ref.shape[0] // 2
    total = jnp.concatenate([mine_ref[:half, :], theirs_ref[:half, :]], axis=0)
    squares = jnp.concatenate([mine_ref[half:, :], theirs_ref[half:, :]], axis=0)
    v, d, c = v_ref[...], turn(odd, d_in_ref[...]), turn(odd, c_in_ref[...])
    d_ref[...] = d
    c_ref[...] = c
    resid = total - c - d * v
    shifted = d + SIGMA
    pre = shifted + squares
    u = resid / pre
    r_ref[...] = resid
    u_ref[...] = u
    pre_ref[...] = pre
    finish_forward(u, None, resid, shifted, out_ref, gf_ref, w_ref, l_ref)


def step_scalars(first, part_refs, sc_old_ref, count):
    totals = jnp.sum(tree(ref[count:, :] for ref in part_refs), axis=1, keepdims=True)
    gamma, one, two = totals[0:1], totals[1:2], totals[2:3]
    if first:
        return gamma, jnp.zeros_like(gamma), one
    old = sc_old_ref[...]
    beta = gamma / old[0:1, 0:1]
    return gamma, beta, one + beta * (2.0 * two + beta * old[2:3, 0:1])


def wide(x):
    return jnp.broadcast_to(x, (1, LANES))


def backward_kernel(n_col, ycount, first, last, *refs):
    rho_ref, *refs = refs
    part_refs, refs = refs[:n_col], refs[n_col:]
    s_ref, refs = refs[0], refs[1:]
    sc_old_ref = None
    if not first:
        (yp_old_ref, yv_old_ref, sc_old_ref, alpha_ref), refs = refs[:4], refs[4:]
    else:
        (yv_old_ref,), refs = refs[:1], refs[1:]
    if not last:
        (gb_ref, sb_ref, w_ref), refs = refs[:3], refs[3:]
    if last:
        z_ref, *refs = refs
    else:
        mine_ref, theirs_ref, *refs = refs
    yp_ref, yv_ref, sc_ref, *scratch = refs
    rho = rho_ref[0]
    full = gathered_rows(part_refs, s_ref)
    gamma, beta, pdp = step_scalars(first, part_refs, sc_old_ref, s_ref.shape[2])
    sc_ref[...] = pad_rows([wide(gamma), wide(beta), wide(pdp)])
    if first:
        yp = full
        yv_ref[...] = yv_old_ref[...]
    else:
        yp_old = yp_old_ref[...]
        yp = full + beta * yp_old
        yv_ref[...] = yv_old_ref[...] + alpha_ref[0:1, 0:1] * yp_old
    yp_ref[...] = yp
    scaled = jnp.concatenate([rho * yp[:ycount], yp[ycount:]], axis=0)
    norm = pad_rows([row_sum(scaled * yp)])
    if last:
        z_ref[...] = norm
    else:
        put_halves((mine_ref, theirs_ref), backward_sum(scaled, gb_ref, sb_ref, w_ref, *scratch), norm)


def step_alpha(extra, sc_ref):
    norm = jnp.sum(extra[0:1], axis=1, keepdims=True)
    return sc_ref[0:1, 0:1] / (sc_ref[2:3, 0:1] + norm)


def forward_kernel(first, *refs):
    (mine_ref, theirs_ref), refs = refs[:2], refs[2:]
    if not first:
        p_old_ref, refs = refs[0], refs[1:]
    (u_old_ref, v_old_ref, r_old_ref, d_ref, pre_ref, sc_ref, gf_ref, w_ref), refs = refs[:8], refs[8:]
    p_ref, v_ref, r_ref, u_ref, alpha_ref, out_ref, *scratch = refs
    half = d_ref.shape[0] // 2
    total = jnp.concatenate([mine_ref[:half, :], theirs_ref[:half, :]], axis=0)
    alpha = step_alpha(mine_ref[half:, :], sc_ref)
    p = u_old_ref[...]
    if not first:
        p = p + sc_ref[1:2, 0:1] * p_old_ref[...]
    shifted = d_ref[...] + SIGMA
    resid = r_old_ref[...] - alpha * (shifted * p + total)
    u = resid / pre_ref[...]
    p_ref[...] = p
    v_ref[...] = v_old_ref[...] + alpha * p
    r_ref[...] = resid
    u_ref[...] = u
    alpha_ref[...] = jnp.broadcast_to(alpha, (8, LANES))
    finish_forward(u, p, resid, shifted, out_ref, gf_ref, w_ref, *scratch)


def final_kernel(ycount, *refs):
    rho_ref, odd_ref, t_ref, *refs = refs
    (u_ref, p_old_ref, v_ref, start_ref, sc_ref, yp_ref, yv_ref, y0_ref), refs = refs[:8], refs[8:]
    (slack_ref, dual_ref, lower_ref, upper_ref, gb_ref, sb_ref, w_ref), refs = refs[:7], refs[7:]
    primal_out, half_out, slack_out, dual_out, mine_ref, theirs_ref, *scratch = refs
    rho = rho_ref[0]
    alpha = step_alpha(t_ref[...], sc_ref)
    p = u_ref[...] + sc_ref[1:2, 0:1] * p_old_ref[...]
    v = v_ref[...] + alpha * p
    primal = RELAX * v + (1.0 - RELAX) * start_ref[...]
    primal_out[...] = turn(odd_ref[0] == 1, primal)
    half_out[...] = primal[: primal.shape[0] // 2]
    image = yv_ref[...] + alpha * yp_ref[...]
    image_next = RELAX * image + (1.0 - RELAX) * y0_ref[...]
    dual = dual_ref[...]
    relaxed = RELAX * image[:ycount] + (1.0 - RELAX) * slack_ref[...]
    slack_next = jnp.minimum(jnp.maximum(relaxed + dual / rho, lower_ref[...]), upper_ref[...])
    dual_next = dual + rho * (relaxed - slack_next)
    slack_out[...] = slack_next
    dual_out[...] = dual_next
    worst = jnp.max(jnp.abs(image_next[:ycount] - slack_next), axis=0, keepdims=True)
    vec = jnp.concatenate([dual_next, image_next[ycount:]], axis=0)
    total = backward_sum(vec, gb_ref, sb_ref, w_ref, *scratch)
    put_halves((mine_ref, theirs_ref), total, jnp.broadcast_to(worst, (8, LANES)))


def residual_kernel(z_ref, primal_ref, d_ref, c_ref, out_ref):
    half = d_ref.shape[0] // 2
    dvec = d_ref[:half, :] * primal_ref[...] + z_ref[:half, :] + c_ref[:half, :]
    worst = jnp.max(jnp.abs(dvec), axis=0, keepdims=True)
    out_ref[...] = jnp.concatenate([z_ref[half : half + 4, :], jnp.broadcast_to(worst, (4, LANES))], axis=0)


VMEM_SPEC = pl.BlockSpec(memory_space=pltpu.VMEM)
SMEM_SPEC = pl.BlockSpec(memory_space=pltpu.SMEM)


def call(kernel, name, outs, args, scratch=(), scalars=0):
    specs = [SMEM_SPEC if i < scalars else VMEM_SPEC for i in range(len(args))]
    shapes = tuple(s if isinstance(s, jax.ShapeDtypeStruct) else jax.ShapeDtypeStruct(s, F32) for s in outs)
    return pl.pallas_call(
        kernel,
        out_shape=shapes,
        in_specs=specs,
        out_specs=tuple(VMEM_SPEC for _ in outs),
        scratch_shapes=list(scratch),
        compiler_params=pltpu.CompilerParams(vmem_limit_bytes=VMEM_LIMIT),
        name=name,
    )(*args)


def swap(x, axis, size, distance):
    return lax.ppermute(x, axis, [(i, i ^ distance) for i in range(size)])


def exchange(x, axis, size, distances):
    return [x] + [swap(x, axis, size, m) for m in distances]


def local(n_row, n_col, *args):
    (
        constraint_tiles,
        constraint_rows,
        constraint_cols,
        factor_tiles,
        factor_rows,
        factor_cols,
        diag_cost,
        linear_cost,
        lower_bound,
        upper_bound,
        primal_start,
        slack_start,
        dual_start,
        penalty,
    ) = args
    width = constraint_tiles.shape[2]
    ctiles = constraint_tiles.reshape(-1, width, width)
    ftiles = factor_tiles.reshape(-1, width, width)
    acount, fcount = ctiles.shape[0], ftiles.shape[0]
    count = acount + fcount
    pairs = count // 2
    xcount = primal_start.shape[0]
    ycount = slack_start.shape[0]
    full = ycount + YG
    half = xcount // 2

    def over_col(x):
        return exchange(x, "col", n_col, sorted(range(1, n_col), key=lambda m: (m != 2, m)))

    def over_plane(chip, op=jnp.add):
        return tree(exchange(chip, "row", n_row, range(2, n_row, 2)), op)

    def other_core(x):
        return swap(x, "row", n_row, 1)

    def over_row(mine, theirs):
        summed = over_plane(mine + other_core(theirs))
        return summed, other_core(summed)

    def places(a, f):
        at = jnp.concatenate([a.reshape(-1), f.reshape(-1)]).astype(F32)
        return jnp.pad(at, (0, 4 * width - count)).reshape(4, width)

    at = jnp.concatenate(
        [places(constraint_rows, factor_rows + ycount), places(constraint_cols, factor_cols)], axis=0
    )
    odd = (lax.axis_index("row") % 2).astype(jnp.int32).reshape(1)
    rho = penalty.reshape(1)
    at, odd, rho, ctiles, ftiles = lax.optimization_barrier((at, odd, rho, ctiles, ftiles))

    block = 16 if acount % 16 == 0 and fcount % 16 == 0 else 8
    a_steps, f_steps = acount // block, fcount // block
    matrix = pl.BlockSpec((block // 2, 2 * width, 2 * width), lambda i: (i, 0, 0))
    matrices = jax.ShapeDtypeStruct((pairs, 2 * width, 2 * width), BF16)

    def split_tiles(kernel, name, out_specs, out_shape, ctiles, ftiles):
        return pl.pallas_call(
            functools.partial(kernel, a_steps),
            grid=(a_steps + f_steps,),
            in_specs=[
                SMEM_SPEC,
                pl.BlockSpec((block, width, width), lambda i: (jnp.minimum(i, a_steps - 1), 0, 0)),
                pl.BlockSpec((block, width, width), lambda i: (jnp.maximum(i - a_steps, 0), 0, 0)),
            ],
            out_specs=out_specs,
            out_shape=out_shape,
            compiler_params=pltpu.CompilerParams(vmem_limit_bytes=VMEM_LIMIT),
            cost_estimate=pl.CostEstimate(
                flops=8 * count * width * width, bytes_accessed=4 * count * width * width, transcendentals=0
            ),
            name=name,
        )(
            rho,
            pltpu.with_memory_space_constraint(ctiles, pltpu.HBM),
            pltpu.with_memory_space_constraint(ftiles, pltpu.HBM),
        )

    turned = split_tiles(split_transposed_kernel, "split_transposed", matrix, matrices, ctiles, ftiles)

    left = pltpu.VMEM((2 * count, 2 * width), BF16)
    rows = pltpu.VMEM((count, width), F32)
    xs, ys, small = (xcount, width), (full, width), (8, width)
    sent, summed = (count + 8, width), (half + 8, width)
    bits = functools.partial(jax.ShapeDtypeStruct, dtype=BF16)

    parts, start, gf = call(
        first_forward_kernel,
        "first_forward",
        [sent, xs, bits((count, xcount))],
        (odd, primal_start, at, turned),
        [left],
        scalars=1,
    )
    parts, ctiles, ftiles = lax.optimization_barrier((parts, ctiles, ftiles))
    all_parts = over_col(parts)
    tiles, squares = split_tiles(
        split_kernel,
        "split",
        (matrix, pl.BlockSpec((block, width), lambda i: (i, 0))),
        (matrices, jax.ShapeDtypeStruct((count, width), F32)),
        ctiles,
        ftiles,
    )
    mine, theirs, y0, s_all, gb, sb = call(
        functools.partial(first_backward_kernel, n_col, ycount, acount),
        "first_backward",
        [xs, xs, ys, bits((n_col, full, count)), bits((count, full)), bits((xcount, count))],
        (rho, odd, *all_parts, tiles, squares, slack_start, dual_start),
        [left, rows],
        scalars=2,
    )
    resid, u, precond, diag, linear, parts = call(
        second_forward_kernel,
        "second_forward",
        [xs, xs, xs, xs, xs, sent],
        (odd, *over_row(mine, theirs), start, diag_cost, linear_cost, gf, turned),
        [left],
        scalars=1,
    )
    v, yv = start, y0
    p = yp = sc = alpha = None
    for step in range(CG):
        first, last = step == 0, step + 1 == CG
        state = (yv,) if first else (yp, yv, sc, alpha)
        mats = () if last else (gb, sb, tiles)
        *z, yp, yv, sc = call(
            functools.partial(backward_kernel, n_col, ycount, first, last),
            "last_norm" if last else "backward",
            ([small] if last else [summed, summed]) + [ys, ys, small],
            (rho, *over_col(parts), s_all, *state, *mats),
            [] if last else [left, rows],
            scalars=1,
        )
        if last:
            break
        p, v, resid, u, alpha, parts = call(
            functools.partial(forward_kernel, first),
            "forward",
            [xs, xs, xs, xs, small, sent],
            (*over_row(*z), *(() if first else (p,)), u, v, resid, diag, precond, sc, gf, turned),
            [left],
        )
    norm = over_plane(z[0] + other_core(z[0]))
    primal_next, primal_half, slack_next, dual_next, mine, theirs = call(
        functools.partial(final_kernel, ycount),
        "final",
        [xs, (half, width), (ycount, width), (ycount, width), summed, summed],
        (rho, odd, norm, u, p, v, start, sc, yp, yv, y0)
        + (slack_start, dual_start, lower_bound, upper_bound, gb, sb, tiles),
        [left, rows],
        scalars=2,
    )

    def join(a, b):
        is_sum = lax.broadcasted_iota(jnp.int32, a.shape, 0) < half
        return jnp.where(is_sum, a + b, jnp.maximum(a, b))

    z = over_plane(join(mine, other_core(theirs)), join)
    (worst,) = call(residual_kernel, "residuals", [small], (z, primal_half, diag, linear))
    worst = jnp.maximum(worst, other_core(worst))
    worst = tree(over_col(worst), jnp.maximum)
    return (primal_next, slack_next, dual_next, jnp.max(worst[:4]), jnp.max(worst[4:]))


def solution(mesh):
    placed = (
        P("row", "col", None, None),
        P("row", "col"),
        P("row", "col"),
        P("row", "col", None, None),
        P("row", "col"),
        P("row", "col"),
        P("col", None),
        P("col", None),
        P("row", None),
        P("row", None),
        P("col", None),
        P("row", None),
        P("row", None),
        P(),
    )
    return jax.shard_map(
        functools.partial(local, mesh.shape["row"], mesh.shape["col"]),
        mesh=mesh,
        in_specs=placed,
        out_specs=(P("col", None), P("row", None), P("row", None), P(), P()),
        check_vma=False,
    )
```

time: 218 us -> 202 us (0.927)
  local copies, waits for them, and re-layouts: 16.4 us -> 0.04 us
  Pallas kernels: 40.6 us -> 45.8 us
  waiting for transfers between devices: 87.8 us -> 85.3 us
    unnamed x26 -> x14, local copies, waits for them, and re-layouts: 14.7 us -> 0.03 us
    pallas_call x1 -> x2, Pallas kernels: 8.19 us -> 14.9 us  [split_tiles(): pl.pallas_call(functools.partial(kernel, a_steps), grid=(a_steps + f_step...]
    ppermute x63, waiting for transfers between devices: 87.8 us -> 85.3 us  [swap(): return lax.ppermute(x, axis, [(i, i ^ distance) for i in range(size)])]
    select_n x4 -> x0, other arithmetic: 2.39 us -> none  [the longest x3 1.63 us: turn(): return jnp.where(odd_core, jnp.concatenate([x[half:], x[:half]], axis=0), x)]
  transfers between devices with their start and end apart: 63 -> 63, of which waited for: 54 -> 54; matrix products, arithmetic and copies ran while one was open for 1% -> 0% of each run, Pallas kernels for 0% -> 4%
where the time goes in v3:
time: 202 us
  waiting for transfers between devices  85.3 us (42%)
  starting transfers between devices  65.8 us (33%)
  Pallas kernels  45.8 us (23%)
  other arithmetic  3.16 us (2%)
    ppermute x63, waiting for transfers between devices, swap(): return lax.ppermute(x, axis, [(i, i ^ distance) for i in range(size)])  85.3 us
    ppermute x63, starting transfers between devices, swap(): return lax.ppermute(x, axis, [(i, i ^ distance) for i in range(size)])  65.8 us
    pallas_call x16, Pallas kernels, call(): pl.pallas_call(kernel, out_shape=shapes, in_specs=specs, out_specs=tuple(...  30.9 us
    pallas_call x2, Pallas kernels, split_tiles(): pl.pallas_call(functools.partial(kernel, a_steps), grid=(a_steps + f_step...  14.9 us
  transfers between devices with their start and end apart: 63, of which 54 were waited for; matrix products, arithmetic and copies ran while one was open for 0% of the time, Pallas kernels for 4%

profile of v3, /device:TPU:0, one launch (start us, length us, event | category | flops | bytes accessed | tf_op | source)
XLA Modules:
  0.0 201.8 jit_solution(12446345663476869409)
XLA Ops:
  3.5 7.7 %split_transposed.1.wt_ref.w_ref.refs_9_.refs_10_ = bf16[72,256,256]{2,1,0:T(8,128)(2,1)S(1)} custom-call(f32[1]{0:T(128)} %bitcast.13.rho_ref, f32[96,128,128]{2,1,0:T(8,128)} %bitcast.23, f32[48,128,128]{2,1,0:T(8,128)} %bitcast.25), custom_call_target="tpu_custom_call" | custom-call | flops 18874368 | bytes 9437184 | tf_op jit(solution)/shard_map/split_transposed/pallas_call | solution.py:456
  11.2 1.9 first_forward.1
  13.1 4.1 %collective-permute-start = (f32[152,128]{1,0:T(8,128)S(1)}, f32[152,128]{1,0:T(8,128)S(1)}, u32[]{:S(2)}, u32[]{:S(2)}) collective-permute-start(f32[152,128]{1,0:T(8,128)S(1)} %get-tuple-element.100.refs_2_), channel_id=1, source_target_pairs={{0,2},{1,3},{2,0},{3,1},{4,6},{5,7},{6,4},{7,5},{8,10},{9,11},{10,... | collective-permute-start | bytes 233480 | tf_op jit(solution)/shard_map/ppermute | solution.py:391
  17.2 1.6 collective-permute-start.1
  18.8 7.2 %split.1 = (bf16[72,256,256]{2,1,0:T(8,128)(2,1)S(1)}, f32[144,128]{1,0:T(8,128)S(1)}) custom-call(f32[1]{0:T(128)} %bitcast.14.rho_ref, f32[96,128,128]{2,1,0:T(8,128)} %bitcast.24, f32[48,128,128]{2,1,0:T(8,128)} %bitcast.26), custom_call_target="tpu_custom_call" | custom-call | flops 18874368 | bytes 9437184 | tf_op jit(solution)/shard_map/split/pallas_call | solution.py:456
  26.0 2.4 %first_backward.1 = (f32[256,128]{1,0:T(8,128)S(1)}, f32[256,128]{1,0:T(8,128)S(1)}, f32[256,128]{1,0:T(8,128)S(1)}, bf16[4,256,144]{2,1,0:T(8,128)(2,1)S(1)}, b...) custom-call(f32[1]{0:T(128)} %bitcast.15.refs_0_, s32[1]{0:T(128)} %bitcast.6.odd_ref.refs_1_, ...), custom_call_target="tpu_custom_call" | custom-call | tf_op jit(solution)/shard_map/first_backward/pallas_call | solution.py:379
  29.9 1.8 collective-permute-start.4
  33.4 2.3 %collective-permute-done.4 = f32[256,128]{1,0:T(8,128)S(1)} collective-permute-done((f32[256,128]{1,0:T(8,128)S(1)}, f32[256,128]{1,0:T(8,128)S(1)}, u32[]{:S(2)}, u32[]{:S(2)}) %collective-permute-start.4) | collective-permute-done | bytes 131104 | tf_op jit(solution)/shard_map/ppermute | solution.py:391
  35.7 4.0 %collective-permute-done.5 = f32[256,128]{1,0:T(8,128)S(1)} collective-permute-done((f32[256,128]{1,0:T(8,128)S(1)}, f32[256,128]{1,0:T(8,128)S(1)}, u32[]{:S(2)}, u32[]{:S(2)}) %collective-permute-start.5) | collective-permute-done | bytes 131104 | tf_op jit(solution)/shard_map/ppermute | solution.py:391
  41.2 1.8 second_forward.1
  43.0 3.6 %collective-permute-start.10 = (f32[152,128]{1,0:T(8,128)S(1)}, f32[152,128]{1,0:T(8,128)S(1)}, u32[]{:S(2)}, u32[]{:S(2)}) collective-permute-start(f32[152,128]{1,0:T(8,128)S(1)} %get-tuple-element.109.refs_1_), channel_id=1, source_target_pairs={{0,3},{1,2},{2,1},{3,0},{4,7},{5,6},{6,5},{7,4},{8,11},{9,10},{10,... | collective-permute-start | bytes 233480 | tf_op jit(solution)/shard_map/ppermute | solution.py:391
  47.4 2.6 %collective-permute-done.10.refs_4_ = f32[152,128]{1,0:T(8,128)S(1)} collective-permute-done((f32[152,128]{1,0:T(8,128)S(1)}, f32[152,128]{1,0:T(8,128)S(1)}, u32[]{:S(2)}, u32[]{:S(2)}) %collective-permute-start.10) | collective-permute-done | bytes 77856 | tf_op jit(solution)/shard_map/ppermute | solution.py:391
  50.1 2.6 %collective-permute-done.8.refs_2_ = f32[152,128]{1,0:T(8,128)S(1)} collective-permute-done((f32[152,128]{1,0:T(8,128)S(1)}, f32[152,128]{1,0:T(8,128)S(1)}, u32[]{:S(2)}, u32[]{:S(2)}) %collective-permute-start.8) | collective-permute-done | bytes 77856 | tf_op jit(solution)/shard_map/ppermute | solution.py:391
  52.9 2.2 %backward.5 = (f32[136,128]{1,0:T(8,128)S(1)}, f32[136,128]{1,0:T(8,128)S(1)}, f32[256,128]{1,0:T(8,128)S(1)}, f32[256,128]{1,0:T(8,128)S(1)}, f32[8,128]{1,0:T(8,128)S(1)}) custom-call(f32[1]{0:T(128)} %bitcast.16.refs_0_, f32[152,128]{1,0:T(8,128)S(1)} %get-tuple-element.109.refs_1_, f32[152,128]{1,0:T(8,128)S(1)} %collective-permute-done.8.refs_2_, ...), custom_call_target="tpu_custom_call" | custom-call | tf_op jit(solution)/shard_map/backward/pallas_call | solution.py:379
  60.9 2.0 collective-permute-done.13
  65.2 2.0 forward.5
  67.2 1.6 collective-permute-start.16
  71.6 3.7 %collective-permute-done.16.refs_2_ = f32[152,128]{1,0:T(8,128)S(1)} collective-permute-done((f32[152,128]{1,0:T(8,128)S(1)}, f32[152,128]{1,0:T(8,128)S(1)}, u32[]{:S(2)}, u32[]{:S(2)}) %collective-permute-start.16) | collective-permute-done | bytes 77856 | tf_op jit(solution)/shard_map/ppermute | solution.py:391
  76.8 2.2 %backward.6 = (f32[136,128]{1,0:T(8,128)S(1)}, f32[136,128]{1,0:T(8,128)S(1)}, f32[256,128]{1,0:T(8,128)S(1)}, f32[256,128]{1,0:T(8,128)S(1)}, f32[8,128]{1,0:T(8,128)S(1)}) custom-call(f32[1]{0:T(128)} %bitcast.17.refs_0_, f32[152,128]{1,0:T(8,128)S(1)} %get-tuple-element.121.refs_1_, f32[152,128]{1,0:T(8,128)S(1)} %collective-permute-done.16.refs_2_, ...), custom_call_target="tpu_custom_call" | custom-call | tf_op jit(solution)/shard_map/backward/pallas_call | solution.py:379
  80.4 1.6 collective-permute-start.20
  84.7 2.2 %collective-permute-done.21 = f32[136,128]{1,0:T(8,128)S(1)} collective-permute-done((f32[136,128]{1,0:T(8,128)S(1)}, f32[136,128]{1,0:T(8,128)S(1)}, u32[]{:S(2)}, u32[]{:S(2)}) %collective-permute-start.21) | collective-permute-done | bytes 69664 | tf_op jit(solution)/shard_map/ppermute | solution.py:391
  89.1 2.0 forward.6
  91.0 2.3 %collective-permute-start.24 = (f32[152,128]{1,0:T(8,128)S(1)}, f32[152,128]{1,0:T(8,128)S(1)}, u32[]{:S(2)}, u32[]{:S(2)}) collective-permute-start(f32[152,128]{1,0:T(8,128)S(1)} %get-tuple-element.132.refs_1_), channel_id=1, source_target_pairs={{0,2},{1,3},{2,0},{3,1},{4,6},{5,7},{6,4},{7,5},{8,10},{9,11},{10,... | collective-permute-start | bytes 233480 | tf_op jit(solution)/shard_map/ppermute | solution.py:391
  93.5 2.0 collective-permute-start.26
  95.5 3.9 %collective-permute-done.24.refs_2_ = f32[152,128]{1,0:T(8,128)S(1)} collective-permute-done((f32[152,128]{1,0:T(8,128)S(1)}, f32[152,128]{1,0:T(8,128)S(1)}, u32[]{:S(2)}, u32[]{:S(2)}) %collective-permute-start.24) | collective-permute-done | bytes 77856 | tf_op jit(solution)/shard_map/ppermute | solution.py:391
  100.4 2.2 %backward.7 = (f32[136,128]{1,0:T(8,128)S(1)}, f32[136,128]{1,0:T(8,128)S(1)}, f32[256,128]{1,0:T(8,128)S(1)}, f32[256,128]{1,0:T(8,128)S(1)}, f32[8,128]{1,0:T(8,128)S(1)}) custom-call(f32[1]{0:T(128)} %bitcast.18.refs_0_, f32[152,128]{1,0:T(8,128)S(1)} %get-tuple-element.132.refs_1_, f32[152,128]{1,0:T(8,128)S(1)} %collective-permute-done.24.refs_2_, ...), custom_call_target="tpu_custom_call" | custom-call | tf_op jit(solution)/shard_map/backward/pallas_call | solution.py:379
  108.4 1.9 collective-permute-done.29
  112.6 2.0 forward.7
  114.6 1.9 collective-permute-start.32
  119.0 3.7 %collective-permute-done.32.refs_2_ = f32[152,128]{1,0:T(8,128)S(1)} collective-permute-done((f32[152,128]{1,0:T(8,128)S(1)}, f32[152,128]{1,0:T(8,128)S(1)}, u32[]{:S(2)}, u32[]{:S(2)}) %collective-permute-start.32) | collective-permute-done | bytes 77856 | tf_op jit(solution)/shard_map/ppermute | solution.py:391
  124.2 2.2 %backward.8 = (f32[136,128]{1,0:T(8,128)S(1)}, f32[136,128]{1,0:T(8,128)S(1)}, f32[256,128]{1,0:T(8,128)S(1)}, f32[256,128]{1,0:T(8,128)S(1)}, f32[8,128]{1,0:T(8,128)S(1)}) custom-call(f32[1]{0:T(128)} %bitcast.19.refs_0_, f32[152,128]{1,0:T(8,128)S(1)} %get-tuple-element.143.refs_1_, f32[152,128]{1,0:T(8,128)S(1)} %collective-permute-done.32.refs_2_, ...), custom_call_target="tpu_custom_call" | custom-call | tf_op jit(solution)/shard_map/backward/pallas_call | solution.py:379
  127.8 1.6 collective-permute-start.36
  132.2 2.2 %collective-permute-done.37 = f32[136,128]{1,0:T(8,128)S(1)} collective-permute-done((f32[136,128]{1,0:T(8,128)S(1)}, f32[136,128]{1,0:T(8,128)S(1)}, u32[]{:S(2)}, u32[]{:S(2)}) %collective-permute-start.37) | collective-permute-done | bytes 69664 | tf_op jit(solution)/shard_map/ppermute | solution.py:391
  136.5 2.2 %forward.8 = (f32[256,128]{1,0:T(8,128)S(1)}, f32[256,128]{1,0:T(8,128)S(1)}, f32[256,128]{1,0:T(8,128)S(1)}, f32[256,128]{1,0:T(8,128)S(1)}, f32[8,128]{1,0:T(8,128)S(1)}, /*index=5*/f32[152,128]{1,0:T(8,128)S(1)}) custom-call(f32[136,128]{1,0:T(8,128)S(1)} %add_add_fusion.2.refs_0_, f32[136,128]{1,0:T(8,128)S(1)} %collective-permute-done.39.refs_1_, ...), custom_call_target="tpu_custom_call" | custom-call | tf_op jit(solution)/shard_map/forward/pallas_call | solution.py:379
  138.7 2.3 %collective-permute-start.40 = (f32[152,128]{1,0:T(8,128)S(1)}, f32[152,128]{1,0:T(8,128)S(1)}, u32[]{:S(2)}, u32[]{:S(2)}) collective-permute-start(f32[152,128]{1,0:T(8,128)S(1)} %get-tuple-element.154.refs_1_), channel_id=1, source_target_pairs={{0,2},{1,3},{2,0},{3,1},{4,6},{5,7},{6,4},{7,5},{8,10},{9,11},{10,... | collective-permute-start | bytes 233480 | tf_op jit(solution)/shard_map/ppermute | solution.py:391
  141.2 1.9 collective-permute-start.42
  143.1 3.9 %collective-permute-done.40.refs_2_ = f32[152,128]{1,0:T(8,128)S(1)} collective-permute-done((f32[152,128]{1,0:T(8,128)S(1)}, f32[152,128]{1,0:T(8,128)S(1)}, u32[]{:S(2)}, u32[]{:S(2)}) %collective-permute-start.40) | collective-permute-done | bytes 77856 | tf_op jit(solution)/shard_map/ppermute | solution.py:391
  148.1 2.2 %backward.9 = (f32[136,128]{1,0:T(8,128)S(1)}, f32[136,128]{1,0:T(8,128)S(1)}, f32[256,128]{1,0:T(8,128)S(1)}, f32[256,128]{1,0:T(8,128)S(1)}, f32[8,128]{1,0:T(8,128)S(1)}) custom-call(f32[1]{0:T(128)} %bitcast.20.refs_0_, f32[152,128]{1,0:T(8,128)S(1)} %get-tuple-element.154.refs_1_, f32[152,128]{1,0:T(8,128)S(1)} %collective-permute-done.40.refs_2_, ...), custom_call_target="tpu_custom_call" | custom-call | tf_op jit(solution)/shard_map/backward/pallas_call | solution.py:379
  156.0 1.9 collective-permute-done.45
  160.3 2.5 %forward.9 = (f32[256,128]{1,0:T(8,128)S(1)}, f32[256,128]{1,0:T(8,128)S(1)}, f32[256,128]{1,0:T(8,128)}, f32[256,128]{1,0:T(8,128)S(1)}, f32[8,128]{1,0:T(8,128)S(1)}, /*index=5*/f32[152,128]{1,0:T(8,128)S(1)}) custom-call(f32[136,128]{1,0:T(8,128)S(1)} %add_add_fusion.1.refs_0_, f32[136,128]{1,0:T(8,128)S(1)} %collective-permute-done.47.refs_1_, ...), custom_call_target="tpu_custom_call" | custom-call | tf_op jit(solution)/shard_map/forward/pallas_call | solution.py:379
  162.8 2.0 collective-permute-start.48
  167.2 3.7 %collective-permute-done.48.refs_2_ = f32[152,128]{1,0:T(8,128)S(1)} collective-permute-done((f32[152,128]{1,0:T(8,128)S(1)}, f32[152,128]{1,0:T(8,128)S(1)}, u32[]{:S(2)}, u32[]{:S(2)}) %collective-permute-start.48) | collective-permute-done | bytes 77856 | tf_op jit(solution)/shard_map/ppermute | solution.py:391
  180.5 2.6 %final.1 = (f32[256,128]{1,0:T(8,128)}, f32[128,128]{1,0:T(8,128)S(1)}, f32[192,128]{1,0:T(8,128)}, f32[192,128]{1,0:T(8,128)}, f32[136,128]{1,0:T(8,128)S(1)}, /*index=5*/f32[136,128]{1,0:T(8,128)S(1)}) custom-call(f32[1]{0:T(128)} %bitcast.22.refs_0_, s32[1]{0:T(128)} %bitcast.6.odd_ref.refs_1_, f32[8,128]{1,0:T(8,128)S(1)} %add_add_fusion.6.refs_2_, ...), custom_call_target="tpu_custom_call" | custom-call | tf_op jit(solution)/shard_map/final/pallas_call | solution.py:379
  186.5 1.5 collective-permute-start.58
  188.9 1.9 collective-permute-done.57
  193.1 2.3 %collective-permute-start.60 = (f32[8,128]{1,0:T(8,128)S(1)}, f32[8,128]{1,0:T(8,128)S(1)}, u32[]{:S(2)}, u32[]{:S(2)}) collective-permute-start(f32[8,128]{1,0:T(8,128)S(1)} %max.28), channel_id=1, source_target_pairs={{0,2},{1,3},{2,0},{3,1},{4,6},{5,7},{6,4},{7,5},{8,10},{9,11},{10,... | collective-permute-start | bytes 12296 | tf_op jit(solution)/shard_map/ppermute | solution.py:391
  195.7 1.8 collective-permute-start.62
  199.0 2.1 %collective-permute-done.62 = f32[8,128]{1,0:T(8,128)S(1)} collective-permute-done((f32[8,128]{1,0:T(8,128)S(1)}, f32[8,128]{1,0:T(8,128)S(1)}, u32[]{:S(2)}, u32[]{:S(2)}) %collective-permute-start.62) | collective-permute-done | bytes 4128 | tf_op jit(solution)/shard_map/ppermute | solution.py:391
  (135 shorter events, 76.3 us)
Async XLA Ops:
  13.1 12.9 %collective-permute-start = (f32[152,128]{1,0:T(8,128)S(1)}, f32[152,128]{1,0:T(8,128)S(1)}, u32[]{:S(2)}, u32[]{:S(2)}) collective-permute-start(f32[152,128]{1,0:T(8,128)S(1)} %get-tuple-element.100.refs_2_), channel_id=1, source_target_pairs={{0,2},{1,3},{2,0},{3,1},{4,6},{5,7},{6,4},{7,5},{8,10},{9,11},{10,... | collective-permute-start | bytes 233480 | tf_op jit(solution)/shard_map/ppermute | solution.py:391
  17.2 8.8 %collective-permute-start.1 = (f32[152,128]{1,0:T(8,128)S(1)}, f32[152,128]{1,0:T(8,128)S(1)}, u32[]{:S(2)}, u32[]{:S(2)}) collective-permute-start(f32[152,128]{1,0:T(8,128)S(1)} %get-tuple-element.100.refs_2_), channel_id=1, source_target_pairs={{0,1},{1,0},{2,3},{3,2},{4,5},{5,4},{6,7},{7,6},{8,9},{9,8},{10,11... | collective-permute-start | bytes 233480 | tf_op jit(solution)/shard_map/ppermute | solution.py:391
  18.7 7.2 %collective-permute-start.2 = (f32[152,128]{1,0:T(8,128)S(1)}, f32[152,128]{1,0:T(8,128)S(1)}, u32[]{:S(2)}, u32[]{:S(2)}) collective-permute-start(f32[152,128]{1,0:T(8,128)S(1)} %get-tuple-element.100.refs_2_), channel_id=1, source_target_pairs={{0,3},{1,2},{2,1},{3,0},{4,7},{5,6},{6,5},{7,4},{8,11},{9,10},{10,... | collective-permute-start | bytes 233480 | tf_op jit(solution)/shard_map/ppermute | solution.py:391
  29.9 5.8 %collective-permute-start.4 = (f32[256,128]{1,0:T(8,128)S(1)}, f32[256,128]{1,0:T(8,128)S(1)}, u32[]{:S(2)}, u32[]{:S(2)}) collective-permute-start(f32[256,128]{1,0:T(8,128)S(1)} %add.113), channel_id=1, source_target_pairs={{0,8},{4,12},{8,0},{12,4},{16,24},{20,28},{24,16},{28,20},{1,9},{5... | collective-permute-start | bytes 393224 | tf_op jit(solution)/shard_map/ppermute | solution.py:391
  31.7 8.1 %collective-permute-start.5 = (f32[256,128]{1,0:T(8,128)S(1)}, f32[256,128]{1,0:T(8,128)S(1)}, u32[]{:S(2)}, u32[]{:S(2)}) collective-permute-start(f32[256,128]{1,0:T(8,128)S(1)} %add.113), channel_id=1, source_target_pairs={{0,16},{4,20},{8,24},{12,28},{16,0},{20,4},{24,8},{28,12},{1,17},{... | collective-permute-start | bytes 393224 | tf_op jit(solution)/shard_map/ppermute | solution.py:391
  33.2 6.6 %collective-permute-start.6 = (f32[256,128]{1,0:T(8,128)S(1)}, f32[256,128]{1,0:T(8,128)S(1)}, u32[]{:S(2)}, u32[]{:S(2)}) collective-permute-start(f32[256,128]{1,0:T(8,128)S(1)} %add.113), channel_id=1, source_target_pairs={{0,24},{4,28},{8,16},{12,20},{16,8},{20,12},{24,0},{28,4},{1,25},{... | collective-permute-start | bytes 393224 | tf_op jit(solution)/shard_map/ppermute | solution.py:391
  43.0 7.0 %collective-permute-start.10 = (f32[152,128]{1,0:T(8,128)S(1)}, f32[152,128]{1,0:T(8,128)S(1)}, u32[]{:S(2)}, u32[]{:S(2)}) collective-permute-start(f32[152,128]{1,0:T(8,128)S(1)} %get-tuple-element.109.refs_1_), channel_id=1, source_target_pairs={{0,3},{1,2},{2,1},{3,0},{4,7},{5,6},{6,5},{7,4},{8,11},{9,10},{10,... | collective-permute-start | bytes 233480 | tf_op jit(solution)/shard_map/ppermute | solution.py:391
  46.6 6.0 %collective-permute-start.8 = (f32[152,128]{1,0:T(8,128)S(1)}, f32[152,128]{1,0:T(8,128)S(1)}, u32[]{:S(2)}, u32[]{:S(2)}) collective-permute-start(f32[152,128]{1,0:T(8,128)S(1)} %get-tuple-element.109.refs_1_), channel_id=1, source_target_pairs={{0,2},{1,3},{2,0},{3,1},{4,6},{5,7},{6,4},{7,5},{8,10},{9,11},{10,... | collective-permute-start | bytes 233480 | tf_op jit(solution)/shard_map/ppermute | solution.py:391
  46.6 6.3 %collective-permute-start.9 = (f32[152,128]{1,0:T(8,128)S(1)}, f32[152,128]{1,0:T(8,128)S(1)}, u32[]{:S(2)}, u32[]{:S(2)}) collective-permute-start(f32[152,128]{1,0:T(8,128)S(1)} %get-tuple-element.109.refs_1_), channel_id=1, source_target_pairs={{0,1},{1,0},{2,3},{3,2},{4,5},{5,4},{6,7},{7,6},{8,9},{9,8},{10,11... | collective-permute-start | bytes 233480 | tf_op jit(solution)/shard_map/ppermute | solution.py:391
  56.5 4.4 %collective-permute-start.12 = (f32[136,128]{1,0:T(8,128)S(1)}, f32[136,128]{1,0:T(8,128)S(1)}, u32[]{:S(2)}, u32[]{:S(2)}) collective-permute-start(f32[136,128]{1,0:T(8,128)S(1)} %add.117), channel_id=1, source_target_pairs={{0,8},{4,12},{8,0},{12,4},{16,24},{20,28},{24,16},{28,20},{1,9},{5... | collective-permute-start | bytes 208904 | tf_op jit(solution)/shard_map/ppermute | solution.py:391
  57.8 5.1 %collective-permute-start.13 = (f32[136,128]{1,0:T(8,128)S(1)}, f32[136,128]{1,0:T(8,128)S(1)}, u32[]{:S(2)}, u32[]{:S(2)}) collective-permute-start(f32[136,128]{1,0:T(8,128)S(1)} %add.117), channel_id=1, source_target_pairs={{0,16},{4,20},{8,24},{12,28},{16,0},{20,4},{24,8},{28,12},{1,17},{... | collective-permute-start | bytes 208904 | tf_op jit(solution)/shard_map/ppermute | solution.py:391
  58.6 5.2 %collective-permute-start.14 = (f32[136,128]{1,0:T(8,128)S(1)}, f32[136,128]{1,0:T(8,128)S(1)}, u32[]{:S(2)}, u32[]{:S(2)}) collective-permute-start(f32[136,128]{1,0:T(8,128)S(1)} %add.117), channel_id=1, source_target_pairs={{0,24},{4,28},{8,16},{12,20},{16,8},{20,12},{24,0},{28,4},{1,25},{... | collective-permute-start | bytes 208904 | tf_op jit(solution)/shard_map/ppermute | solution.py:391
  67.2 8.1 %collective-permute-start.16 = (f32[152,128]{1,0:T(8,128)S(1)}, f32[152,128]{1,0:T(8,128)S(1)}, u32[]{:S(2)}, u32[]{:S(2)}) collective-permute-start(f32[152,128]{1,0:T(8,128)S(1)} %get-tuple-element.121.refs_1_), channel_id=1, source_target_pairs={{0,2},{1,3},{2,0},{3,1},{4,6},{5,7},{6,4},{7,5},{8,10},{9,11},{10,... | collective-permute-start | bytes 233480 | tf_op jit(solution)/shard_map/ppermute | solution.py:391
  68.7 6.5 %collective-permute-start.17 = (f32[152,128]{1,0:T(8,128)S(1)}, f32[152,128]{1,0:T(8,128)S(1)}, u32[]{:S(2)}, u32[]{:S(2)}) collective-permute-start(f32[152,128]{1,0:T(8,128)S(1)} %get-tuple-element.121.refs_1_), channel_id=1, source_target_pairs={{0,1},{1,0},{2,3},{3,2},{4,5},{5,4},{6,7},{7,6},{8,9},{9,8},{10,11... | collective-permute-start | bytes 233480 | tf_op jit(solution)/shard_map/ppermute | solution.py:391
  70.2 6.6 %collective-permute-start.18 = (f32[152,128]{1,0:T(8,128)S(1)}, f32[152,128]{1,0:T(8,128)S(1)}, u32[]{:S(2)}, u32[]{:S(2)}) collective-permute-start(f32[152,128]{1,0:T(8,128)S(1)} %get-tuple-element.121.refs_1_), channel_id=1, source_target_pairs={{0,3},{1,2},{2,1},{3,0},{4,7},{5,6},{6,5},{7,4},{8,11},{9,10},{10,... | collective-permute-start | bytes 233480 | tf_op jit(solution)/shard_map/ppermute | solution.py:391
  80.4 4.4 %collective-permute-start.20 = (f32[136,128]{1,0:T(8,128)S(1)}, f32[136,128]{1,0:T(8,128)S(1)}, u32[]{:S(2)}, u32[]{:S(2)}) collective-permute-start(f32[136,128]{1,0:T(8,128)S(1)} %add.121), channel_id=1, source_target_pairs={{0,8},{4,12},{8,0},{12,4},{16,24},{20,28},{24,16},{28,20},{1,9},{5... | collective-permute-start | bytes 208904 | tf_op jit(solution)/shard_map/ppermute | solution.py:391
  81.9 5.1 %collective-permute-start.21 = (f32[136,128]{1,0:T(8,128)S(1)}, f32[136,128]{1,0:T(8,128)S(1)}, u32[]{:S(2)}, u32[]{:S(2)}) collective-permute-start(f32[136,128]{1,0:T(8,128)S(1)} %add.121), channel_id=1, source_target_pairs={{0,16},{4,20},{8,24},{12,28},{16,0},{20,4},{24,8},{28,12},{1,17},{... | collective-permute-start | bytes 208904 | tf_op jit(solution)/shard_map/ppermute | solution.py:391
  82.5 5.2 %collective-permute-start.22 = (f32[136,128]{1,0:T(8,128)S(1)}, f32[136,128]{1,0:T(8,128)S(1)}, u32[]{:S(2)}, u32[]{:S(2)}) collective-permute-start(f32[136,128]{1,0:T(8,128)S(1)} %add.121), channel_id=1, source_target_pairs={{0,24},{4,28},{8,16},{12,20},{16,8},{20,12},{24,0},{28,4},{1,25},{... | collective-permute-start | bytes 208904 | tf_op jit(solution)/shard_map/ppermute | solution.py:391
  91.0 8.3 %collective-permute-start.24 = (f32[152,128]{1,0:T(8,128)S(1)}, f32[152,128]{1,0:T(8,128)S(1)}, u32[]{:S(2)}, u32[]{:S(2)}) collective-permute-start(f32[152,128]{1,0:T(8,128)S(1)} %get-tuple-element.132.refs_1_), channel_id=1, source_target_pairs={{0,2},{1,3},{2,0},{3,1},{4,6},{5,7},{6,4},{7,5},{8,10},{9,11},{10,... | collective-permute-start | bytes 233480 | tf_op jit(solution)/shard_map/ppermute | solution.py:391
  93.4 5.9 %collective-permute-start.25 = (f32[152,128]{1,0:T(8,128)S(1)}, f32[152,128]{1,0:T(8,128)S(1)}, u32[]{:S(2)}, u32[]{:S(2)}) collective-permute-start(f32[152,128]{1,0:T(8,128)S(1)} %get-tuple-element.132.refs_1_), channel_id=1, source_target_pairs={{0,1},{1,0},{2,3},{3,2},{4,5},{5,4},{6,7},{7,6},{8,9},{9,8},{10,11... | collective-permute-start | bytes 233480 | tf_op jit(solution)/shard_map/ppermute | solution.py:391
  93.5 6.9 %collective-permute-start.26 = (f32[152,128]{1,0:T(8,128)S(1)}, f32[152,128]{1,0:T(8,128)S(1)}, u32[]{:S(2)}, u32[]{:S(2)}) collective-permute-start(f32[152,128]{1,0:T(8,128)S(1)} %get-tuple-element.132.refs_1_), channel_id=1, source_target_pairs={{0,3},{1,2},{2,1},{3,0},{4,7},{5,6},{6,5},{7,4},{8,11},{9,10},{10,... | collective-permute-start | bytes 233480 | tf_op jit(solution)/shard_map/ppermute | solution.py:391
  104.0 4.4 %collective-permute-start.28 = (f32[136,128]{1,0:T(8,128)S(1)}, f32[136,128]{1,0:T(8,128)S(1)}, u32[]{:S(2)}, u32[]{:S(2)}) collective-permute-start(f32[136,128]{1,0:T(8,128)S(1)} %add.125), channel_id=1, source_target_pairs={{0,8},{4,12},{8,0},{12,4},{16,24},{20,28},{24,16},{28,20},{1,9},{5... | collective-permute-start | bytes 208904 | tf_op jit(solution)/shard_map/ppermute | solution.py:391
  105.2 5.1 %collective-permute-start.29 = (f32[136,128]{1,0:T(8,128)S(1)}, f32[136,128]{1,0:T(8,128)S(1)}, u32[]{:S(2)}, u32[]{:S(2)}) collective-permute-start(f32[136,128]{1,0:T(8,128)S(1)} %add.125), channel_id=1, source_target_pairs={{0,16},{4,20},{8,24},{12,28},{16,0},{20,4},{24,8},{28,12},{1,17},{... | collective-permute-start | bytes 208904 | tf_op jit(solution)/shard_map/ppermute | solution.py:391
  106.1 5.2 %collective-permute-start.30 = (f32[136,128]{1,0:T(8,128)S(1)}, f32[136,128]{1,0:T(8,128)S(1)}, u32[]{:S(2)}, u32[]{:S(2)}) collective-permute-start(f32[136,128]{1,0:T(8,128)S(1)} %add.125), channel_id=1, source_target_pairs={{0,24},{4,28},{8,16},{12,20},{16,8},{20,12},{24,0},{28,4},{1,25},{... | collective-permute-start | bytes 208904 | tf_op jit(solution)/shard_map/ppermute | solution.py:391
  114.6 8.1 %collective-permute-start.32 = (f32[152,128]{1,0:T(8,128)S(1)}, f32[152,128]{1,0:T(8,128)S(1)}, u32[]{:S(2)}, u32[]{:S(2)}) collective-permute-start(f32[152,128]{1,0:T(8,128)S(1)} %get-tuple-element.143.refs_1_), channel_id=1, source_target_pairs={{0,2},{1,3},{2,0},{3,1},{4,6},{5,7},{6,4},{7,5},{8,10},{9,11},{10,... | collective-permute-start | bytes 233480 | tf_op jit(solution)/shard_map/ppermute | solution.py:391
  116.5 6.2 %collective-permute-start.33 = (f32[152,128]{1,0:T(8,128)S(1)}, f32[152,128]{1,0:T(8,128)S(1)}, u32[]{:S(2)}, u32[]{:S(2)}) collective-permute-start(f32[152,128]{1,0:T(8,128)S(1)} %get-tuple-element.143.refs_1_), channel_id=1, source_target_pairs={{0,1},{1,0},{2,3},{3,2},{4,5},{5,4},{6,7},{7,6},{8,9},{9,8},{10,11... | collective-permute-start | bytes 233480 | tf_op jit(solution)/shard_map/ppermute | solution.py:391
  117.7 6.5 %collective-permute-start.34 = (f32[152,128]{1,0:T(8,128)S(1)}, f32[152,128]{1,0:T(8,128)S(1)}, u32[]{:S(2)}, u32[]{:S(2)}) collective-permute-start(f32[152,128]{1,0:T(8,128)S(1)} %get-tuple-element.143.refs_1_), channel_id=1, source_target_pairs={{0,3},{1,2},{2,1},{3,0},{4,7},{5,6},{6,5},{7,4},{8,11},{9,10},{10,... | collective-permute-start | bytes 233480 | tf_op jit(solution)/shard_map/ppermute | solution.py:391
  127.8 4.4 %collective-permute-start.36 = (f32[136,128]{1,0:T(8,128)S(1)}, f32[136,128]{1,0:T(8,128)S(1)}, u32[]{:S(2)}, u32[]{:S(2)}) collective-permute-start(f32[136,128]{1,0:T(8,128)S(1)} %add.129), channel_id=1, source_target_pairs={{0,8},{4,12},{8,0},{12,4},{16,24},{20,28},{24,16},{28,20},{1,9},{5... | collective-permute-start | bytes 208904 | tf_op jit(solution)/shard_map/ppermute | solution.py:391
  129.4 5.1 %collective-permute-start.37 = (f32[136,128]{1,0:T(8,128)S(1)}, f32[136,128]{1,0:T(8,128)S(1)}, u32[]{:S(2)}, u32[]{:S(2)}) collective-permute-start(f32[136,128]{1,0:T(8,128)S(1)} %add.129), channel_id=1, source_target_pairs={{0,16},{4,20},{8,24},{12,28},{16,0},{20,4},{24,8},{28,12},{1,17},{... | collective-permute-start | bytes 208904 | tf_op jit(solution)/shard_map/ppermute | solution.py:391
  130.0 5.2 %collective-permute-start.38 = (f32[136,128]{1,0:T(8,128)S(1)}, f32[136,128]{1,0:T(8,128)S(1)}, u32[]{:S(2)}, u32[]{:S(2)}) collective-permute-start(f32[136,128]{1,0:T(8,128)S(1)} %add.129), channel_id=1, source_target_pairs={{0,24},{4,28},{8,16},{12,20},{16,8},{20,12},{24,0},{28,4},{1,25},{... | collective-permute-start | bytes 208904 | tf_op jit(solution)/shard_map/ppermute | solution.py:391
  138.7 8.3 %collective-permute-start.40 = (f32[152,128]{1,0:T(8,128)S(1)}, f32[152,128]{1,0:T(8,128)S(1)}, u32[]{:S(2)}, u32[]{:S(2)}) collective-permute-start(f32[152,128]{1,0:T(8,128)S(1)} %get-tuple-element.154.refs_1_), channel_id=1, source_target_pairs={{0,2},{1,3},{2,0},{3,1},{4,6},{5,7},{6,4},{7,5},{8,10},{9,11},{10,... | collective-permute-start | bytes 233480 | tf_op jit(solution)/shard_map/ppermute | solution.py:391
  141.0 5.9 %collective-permute-start.41 = (f32[152,128]{1,0:T(8,128)S(1)}, f32[152,128]{1,0:T(8,128)S(1)}, u32[]{:S(2)}, u32[]{:S(2)}) collective-permute-start(f32[152,128]{1,0:T(8,128)S(1)} %get-tuple-element.154.refs_1_), channel_id=1, source_target_pairs={{0,1},{1,0},{2,3},{3,2},{4,5},{5,4},{6,7},{7,6},{8,9},{9,8},{10,11... | collective-permute-start | bytes 233480 | tf_op jit(solution)/shard_map/ppermute | solution.py:391
  141.2 6.8 %collective-permute-start.42 = (f32[152,128]{1,0:T(8,128)S(1)}, f32[152,128]{1,0:T(8,128)S(1)}, u32[]{:S(2)}, u32[]{:S(2)}) collective-permute-start(f32[152,128]{1,0:T(8,128)S(1)} %get-tuple-element.154.refs_1_), channel_id=1, source_target_pairs={{0,3},{1,2},{2,1},{3,0},{4,7},{5,6},{6,5},{7,4},{8,11},{9,10},{10,... | collective-permute-start | bytes 233480 | tf_op jit(solution)/shard_map/ppermute | solution.py:391
  151.7 4.4 %collective-permute-start.44 = (f32[136,128]{1,0:T(8,128)S(1)}, f32[136,128]{1,0:T(8,128)S(1)}, u32[]{:S(2)}, u32[]{:S(2)}) collective-permute-start(f32[136,128]{1,0:T(8,128)S(1)} %add.133), channel_id=1, source_target_pairs={{0,8},{4,12},{8,0},{12,4},{16,24},{20,28},{24,16},{28,20},{1,9},{5... | collective-permute-start | bytes 208904 | tf_op jit(solution)/shard_map/ppermute | solution.py:391
  152.9 5.1 %collective-permute-start.45 = (f32[136,128]{1,0:T(8,128)S(1)}, f32[136,128]{1,0:T(8,128)S(1)}, u32[]{:S(2)}, u32[]{:S(2)}) collective-permute-start(f32[136,128]{1,0:T(8,128)S(1)} %add.133), channel_id=1, source_target_pairs={{0,16},{4,20},{8,24},{12,28},{16,0},{20,4},{24,8},{28,12},{1,17},{... | collective-permute-start | bytes 208904 | tf_op jit(solution)/shard_map/ppermute | solution.py:391
  153.7 5.2 %collective-permute-start.46 = (f32[136,128]{1,0:T(8,128)S(1)}, f32[136,128]{1,0:T(8,128)S(1)}, u32[]{:S(2)}, u32[]{:S(2)}) collective-permute-start(f32[136,128]{1,0:T(8,128)S(1)} %add.133), channel_id=1, source_target_pairs={{0,24},{4,28},{8,16},{12,20},{16,8},{20,12},{24,0},{28,4},{1,25},{... | collective-permute-start | bytes 208904 | tf_op jit(solution)/shard_map/ppermute | solution.py:391
  162.8 8.1 %collective-permute-start.48 = (f32[152,128]{1,0:T(8,128)S(1)}, f32[152,128]{1,0:T(8,128)S(1)}, u32[]{:S(2)}, u32[]{:S(2)}) collective-permute-start(f32[152,128]{1,0:T(8,128)S(1)} %get-tuple-element.165.refs_1_), channel_id=1, source_target_pairs={{0,2},{1,3},{2,0},{3,1},{4,6},{5,7},{6,4},{7,5},{8,10},{9,11},{10,... | collective-permute-start | bytes 233480 | tf_op jit(solution)/shard_map/ppermute | solution.py:391
  164.8 6.1 %collective-permute-start.49 = (f32[152,128]{1,0:T(8,128)S(1)}, f32[152,128]{1,0:T(8,128)S(1)}, u32[]{:S(2)}, u32[]{:S(2)}) collective-permute-start(f32[152,128]{1,0:T(8,128)S(1)} %get-tuple-element.165.refs_1_), channel_id=1, source_target_pairs={{0,1},{1,0},{2,3},{3,2},{4,5},{5,4},{6,7},{7,6},{8,9},{9,8},{10,11... | collective-permute-start | bytes 233480 | tf_op jit(solution)/shard_map/ppermute | solution.py:391
  165.8 6.5 %collective-permute-start.50 = (f32[152,128]{1,0:T(8,128)S(1)}, f32[152,128]{1,0:T(8,128)S(1)}, u32[]{:S(2)}, u32[]{:S(2)}) collective-permute-start(f32[152,128]{1,0:T(8,128)S(1)} %get-tuple-element.165.refs_1_), channel_id=1, source_target_pairs={{0,3},{1,2},{2,1},{3,0},{4,7},{5,6},{6,5},{7,4},{8,11},{9,10},{10,... | collective-permute-start | bytes 233480 | tf_op jit(solution)/shard_map/ppermute | solution.py:391
  173.9 3.6 %collective-permute-start.52 = (f32[8,128]{1,0:T(8,128)S(1)}, f32[8,128]{1,0:T(8,128)S(1)}, u32[]{:S(2)}, u32[]{:S(2)}) collective-permute-start(f32[8,128]{1,0:T(8,128)S(1)} %add.137), channel_id=1, source_target_pairs={{0,8},{4,12},{8,0},{12,4},{16,24},{20,28},{24,16},{28,20},{1,9},{5... | collective-permute-start | bytes 12296 | tf_op jit(solution)/shard_map/ppermute | solution.py:391
  175.4 3.6 %collective-permute-start.53 = (f32[8,128]{1,0:T(8,128)S(1)}, f32[8,128]{1,0:T(8,128)S(1)}, u32[]{:S(2)}, u32[]{:S(2)}) collective-permute-start(f32[8,128]{1,0:T(8,128)S(1)} %add.137), channel_id=1, source_target_pairs={{0,16},{4,20},{8,24},{12,28},{16,0},{20,4},{24,8},{28,12},{1,17},{... | collective-permute-start | bytes 12296 | tf_op jit(solution)/shard_map/ppermute | solution.py:391
  176.0 4.5 %collective-permute-start.54 = (f32[8,128]{1,0:T(8,128)S(1)}, f32[8,128]{1,0:T(8,128)S(1)}, u32[]{:S(2)}, u32[]{:S(2)}) collective-permute-start(f32[8,128]{1,0:T(8,128)S(1)} %add.137), channel_id=1, source_target_pairs={{0,24},{4,28},{8,16},{12,20},{16,8},{20,12},{24,0},{28,4},{1,25},{... | collective-permute-start | bytes 12296 | tf_op jit(solution)/shard_map/ppermute | solution.py:391
  184.5 4.4 %collective-permute-start.56 = (f32[136,128]{1,0:T(8,128)S(1)}, f32[136,128]{1,0:T(8,128)S(1)}, u32[]{:S(2)}, u32[]{:S(2)}) collective-permute-start(f32[136,128]{1,0:T(8,128)S(1)} %maximum_select_fusion.1), channel_id=1, source_target_pairs={{0,8},{4,12},{8,0},{12,4},{16,24},{20,28},{24,16},{28,20},{1,9},{5... | collective-permute-start | bytes 208904 | tf_op jit(solution)/shard_map/ppermute | solution.py:391
  185.7 5.1 %collective-permute-start.57 = (f32[136,128]{1,0:T(8,128)S(1)}, f32[136,128]{1,0:T(8,128)S(1)}, u32[]{:S(2)}, u32[]{:S(2)}) collective-permute-start(f32[136,128]{1,0:T(8,128)S(1)} %maximum_select_fusion.1), channel_id=1, source_target_pairs={{0,16},{4,20},{8,24},{12,28},{16,0},{20,4},{24,8},{28,12},{1,17},{... | collective-permute-start | bytes 208904 | tf_op jit(solution)/shard_map/ppermute | solution.py:391
  186.5 5.2 %collective-permute-start.58 = (f32[136,128]{1,0:T(8,128)S(1)}, f32[136,128]{1,0:T(8,128)S(1)}, u32[]{:S(2)}, u32[]{:S(2)}) collective-permute-start(f32[136,128]{1,0:T(8,128)S(1)} %maximum_select_fusion.1), channel_id=1, source_target_pairs={{0,24},{4,28},{8,16},{12,20},{16,8},{20,12},{24,0},{28,4},{1,25},{... | collective-permute-start | bytes 208904 | tf_op jit(solution)/shard_map/ppermute | solution.py:391
  193.1 4.5 %collective-permute-start.60 = (f32[8,128]{1,0:T(8,128)S(1)}, f32[8,128]{1,0:T(8,128)S(1)}, u32[]{:S(2)}, u32[]{:S(2)}) collective-permute-start(f32[8,128]{1,0:T(8,128)S(1)} %max.28), channel_id=1, source_target_pairs={{0,2},{1,3},{2,0},{3,1},{4,6},{5,7},{6,4},{7,5},{8,10},{9,11},{10,... | collective-permute-start | bytes 12296 | tf_op jit(solution)/shard_map/ppermute | solution.py:391
  195.4 3.6 %collective-permute-start.61 = (f32[8,128]{1,0:T(8,128)S(1)}, f32[8,128]{1,0:T(8,128)S(1)}, u32[]{:S(2)}, u32[]{:S(2)}) collective-permute-start(f32[8,128]{1,0:T(8,128)S(1)} %max.28), channel_id=1, source_target_pairs={{0,1},{1,0},{2,3},{3,2},{4,5},{5,4},{6,7},{7,6},{8,9},{9,8},{10,11... | collective-permute-start | bytes 12296 | tf_op jit(solution)/shard_map/ppermute | solution.py:391
  195.7 5.4 %collective-permute-start.62 = (f32[8,128]{1,0:T(8,128)S(1)}, f32[8,128]{1,0:T(8,128)S(1)}, u32[]{:S(2)}, u32[]{:S(2)}) collective-permute-start(f32[8,128]{1,0:T(8,128)S(1)} %max.28), channel_id=1, source_target_pairs={{0,3},{1,2},{2,1},{3,0},{4,7},{5,6},{6,5},{7,4},{8,11},{9,10},{10,... | collective-permute-start | bytes 12296 | tf_op jit(solution)/shard_map/ppermute | solution.py:391
  (22 other events, 166.9 us)

commit v4 on v3

--- a/solution.py
+++ b/solution.py
@@ -74,36 +74,46 @@
     return both[:, :LANES] + both[:, LANES:]
 
 
+def one_block(w_ref, l_ref, block, finish):
+    pairs = TILES // 2
+    of_pair = lax.broadcasted_iota(jnp.int32, (2 * TILES, 2 * LANES), 0) % TILES // 2
+    left = l_ref[pl.ds(pl.multiple_of(block * 2 * TILES, 2 * TILES), 2 * TILES), :]
+    out = dot(left, w_ref[pairs * block])
+    for k in range(1, pairs):
+        out = jnp.where(of_pair == k, dot(left, w_ref[pairs * block + k]), out)
+    finish(pl.multiple_of(block * TILES, TILES), out[:TILES] + out[TILES:])
+
+
 def run_tiles(w_ref, l_ref, finish):
-    pairs = TILES // 2
-    blocks = w_ref.shape[0] // pairs
+    blocks = w_ref.shape[0] // (TILES // 2)
     unroll = next(n for n in (UNROLL, 6, 4, 3, 2, 1) if blocks % n == 0)
-    of_pair = lax.broadcasted_iota(jnp.int32, (2 * TILES, 2 * LANES), 0) % TILES // 2
 
     def body(step, carry):
         for inner in range(unroll):
-            block = step * unroll + inner
-            left = l_ref[pl.ds(pl.multiple_of(block * 2 * TILES, 2 * TILES), 2 * TILES), :]
-            out = dot(left, w_ref[pairs * block])
-            for k in range(1, pairs):
-                out = jnp.where(of_pair == k, dot(left, w_ref[pairs * block + k]), out)
-            finish(pl.multiple_of(block * TILES, TILES), out[:TILES] + out[TILES:])
+            one_block(w_ref, l_ref, step * unroll + inner, finish)
         return carry
 
     lax.fori_loop(0, blocks // unroll, body, 0)
 
 
-def forward_parts(vec, gf_ref, wt_ref, out_ref, l_ref):
+def forward_left(vec, gf_ref, l_ref):
     picked = gather(gf_ref, vec)
     first = lax.broadcasted_iota(jnp.int32, picked.shape, 0) % 2 == 0
     zero = jnp.zeros_like(picked)
     l_ref[:, :LANES] = jnp.where(first, picked, zero).astype(BF16)
     l_ref[:, LANES:] = jnp.where(first, zero, picked).astype(BF16)
 
+
+def forward_finish(out_ref):
     def finish(at, out):
         out_ref[pl.ds(at, TILES), :] = out[:, :LANES] + out[:, LANES:]
 
-    run_tiles(wt_ref, l_ref, finish)
+    return finish
+
+
+def forward_parts(vec, gf_ref, wt_ref, out_ref, l_ref):
+    forward_left(vec, gf_ref, l_ref)
+    run_tiles(wt_ref, l_ref, forward_finish(out_ref))
 
 
 def backward_sum(vec, gb_ref, sb_ref, w_ref, l_ref, rows_ref):
@@ -148,40 +158,45 @@
         ref[row * LANES : row * LANES + width, :] = jnp.where(hit, 1.0, 0.0).astype(BF16)
 
 
-def both_kinds(a_steps, a_ref, g_ref, convert):
-    step = pl.program_id(0)
-
-    @pl.when(step < a_steps)
-    def _():
-        convert(a_ref)
-
-    @pl.when(step >= a_steps)
-    def _():
-        convert(g_ref)
-
-
-def split_transposed_kernel(a_steps, rho_ref, a_ref, g_ref, wt_ref):
-    def convert(ref):
-        for t in range(ref.shape[0]):
-            at = (t % 2) * LANES
-            high, low = split2(ref[t].T)
-            wt_ref[t // 2, at : at + LANES, :LANES] = high
-            wt_ref[t // 2, at : at + LANES, LANES:] = low
-
-    both_kinds(a_steps, a_ref, g_ref, convert)
-
-
-def split_kernel(a_steps, rho_ref, a_ref, g_ref, w_ref, sq_ref):
-    def convert(ref):
-        for t in range(ref.shape[0]):
-            at = (t % 2) * LANES
-            tile = ref[t]
+def tile_copies(chunk, refs, held_ref, sems):
+    copies, at = [], 0
+    for ref in refs:
+        for start in range(0, ref.shape[0], chunk):
+            copies.append(
+                pltpu.make_async_copy(
+                    ref.at[pl.ds(start, chunk)], held_ref.at[pl.ds(at, chunk)], sems.at[len(copies)]
+                )
+            )
+            at += chunk
+    return copies
+
+
+def wait_chunk(step, chunk, a_ref, held_ref, sems):
+    at = pl.multiple_of(step * chunk, chunk)
+    pltpu.make_async_copy(a_ref.at[pl.ds(0, chunk)], held_ref.at[pl.ds(at, chunk)], sems.at[step]).wait()
+
+
+def odd_core():
+    return lax.axis_index("row") % 2 == 1
+
+
+def split_kernel(chunk, a_ref, g_ref, w_ref, sq_ref, held_ref, sems):
+    copies = tile_copies(chunk, (a_ref, g_ref), held_ref, sems)
+    for copy in copies:
+        copy.start()
+
+    def body(step, carry):
+        wait_chunk(step, chunk, a_ref, held_ref, sems)
+        for t in range(chunk):
+            tile = held_ref[step * chunk + t]
+            pair, at = (step * chunk + t) // 2, (t % 2) * LANES
             high, low = split2(tile)
-            w_ref[t // 2, :LANES, at : at + LANES] = high
-            w_ref[t // 2, LANES:, at : at + LANES] = low
-            sq_ref[t : t + 1, :] = row_sum(tile * tile)
-
-    both_kinds(a_steps, a_ref, g_ref, convert)
+            w_ref[pair, :LANES, at : at + LANES] = high
+            w_ref[pair, LANES:, at : at + LANES] = low
+            sq_ref[pl.ds(step * chunk + t, 1), :] = row_sum(tile * tile)
+        return carry
+
+    lax.fori_loop(0, len(copies), body, 0)
 
 
 def turned_places(odd, places, xcount):
@@ -190,23 +205,71 @@
     return jnp.where(odd, moved, places)
 
 
-def first_forward_kernel(odd_ref, v_in_ref, at_ref, wt_ref, out_ref, v_ref, gf_ref, l_ref):
-    odd = odd_ref[0] == 1
+def joined(at_ref, a_ref, f_ref, base=0):
+    acount, fcount = a_ref.shape[1], f_ref.shape[1]
+    at_ref[...] = jnp.zeros_like(at_ref)
+    at_ref[0:1, :acount] = a_ref[...].astype(F32)
+    at_ref[1:2, :fcount] = (f_ref[...] + base).astype(F32)
+    a, f = at_ref[0:1, :], at_ref[1:2, :]
+    moved = pltpu.roll(jnp.broadcast_to(f, (8, LANES)), acount % LANES, 1)[0:1]
+    lane = lax.broadcasted_iota(jnp.int32, (1, LANES), 1)
+    return [jnp.where(lane < acount, a, moved), moved]
+
+
+def first_forward_kernel(chunk, ycount, rho_ref, *refs):
+    (a_ref, g_ref), small_refs, refs = refs[:2], refs[2:7], refs[7:]
+    (wt_ref, out_ref, v_ref, gf_ref, l_ref, at_ref), refs = refs[:6], refs[6:]
+    small_held, (small_sems, held_ref, sems) = refs[:5], refs[5:]
+    fetched = [pltpu.make_async_copy(a, b, small_sems.at[i]) for i, (a, b) in enumerate(zip(small_refs, small_held))]
+    copies = tile_copies(chunk, (a_ref, g_ref), held_ref, sems)
+    for copy in fetched + copies:
+        copy.start()
+    odd = odd_core()
+    for copy in fetched:
+        copy.wait()
+    v_in_ref, arow_ref, acol_ref, frow_ref, fcol_ref = small_held
     count = 2 * wt_ref.shape[0]
     v = turn(odd, v_in_ref[...])
     v_ref[...] = v
-    out_ref[count:, :] = at_ref[...]
-    xrows = jnp.concatenate([at_ref[4:], at_ref[:4]], axis=0)
-    select_rows(gf_ref, turned_places(odd, xrows, v.shape[0]))
-    forward_parts(v, gf_ref, wt_ref, out_ref, l_ref)
+    zero = [jnp.zeros((1, LANES), F32)] * 2
+    yrows = joined(at_ref, arow_ref, frow_ref, ycount) + zero
+    xrows = joined(at_ref, acol_ref, fcol_ref) + zero
+    out_ref[count:, :] = jnp.concatenate(yrows + xrows, axis=0)
+    places = jnp.concatenate(xrows + yrows, axis=0)
+    select_rows(gf_ref, turned_places(odd, places, v.shape[0]))
+    forward_left(v, gf_ref, l_ref)
+    finish = forward_finish(out_ref)
+    blocks = chunk // TILES
+
+    def products(step):
+        for inner in range(blocks):
+            one_block(wt_ref, l_ref, step * blocks + inner, finish)
+
+    def split(step):
+        wait_chunk(step, chunk, a_ref, held_ref, sems)
+        for t in range(chunk):
+            pair, at = (step * chunk + t) // 2, (t % 2) * LANES
+            high, low = split2(held_ref[step * chunk + t].T)
+            wt_ref[pair, at : at + LANES, :LANES] = high
+            wt_ref[pair, at : at + LANES, LANES:] = low
+
+    split(0)
+
+    def body(step, carry):
+        products(step - 1)
+        split(step)
+        return carry
+
+    lax.fori_loop(1, len(copies), body, 0)
+    products(len(copies) - 1)
 
 
 def first_backward_kernel(n_col, ycount, acount, *refs):
-    rho_ref, odd_ref, *refs = refs
+    rho_ref, *refs = refs
     part_refs, refs = refs[:n_col], refs[n_col:]
     (w_ref, sq_ref, slack_ref, dual_ref), refs = refs[:4], refs[4:]
     mine_ref, theirs_ref, y_ref, s_ref, gb_ref, sb_ref, l_ref, rows_ref = refs
-    rho, odd = rho_ref[0], odd_ref[0] == 1
+    rho, odd = rho_ref[0], odd_core()
     count = s_ref.shape[2]
     for j, ref in enumerate(part_refs):
         select_columns(s_ref.at[j], ref[count:, :])
@@ -239,9 +302,9 @@
     forward_parts(u, gf_ref, w_ref, out_ref, l_ref)
 
 
-def second_forward_kernel(odd_ref, mine_ref, theirs_ref, v_ref, d_in_ref, c_in_ref, gf_ref, w_ref, *refs):
+def second_forward_kernel(mine_ref, theirs_ref, v_ref, d_in_ref, c_in_ref, gf_ref, w_ref, *refs):
     r_ref, u_ref, pre_ref, d_ref, c_ref, out_ref, l_ref = refs
-    odd = odd_ref[0] == 1
+    odd = odd_core()
     half = v_ref.shape[0] // 2
     total = jnp.concatenate([mine_ref[:half, :], theirs_ref[:half, :]], axis=0)
     squares = jnp.concatenate([mine_ref[half:, :], theirs_ref[half:, :]], axis=0)
@@ -337,7 +400,7 @@
 
 
 def final_kernel(ycount, *refs):
-    rho_ref, odd_ref, t_ref, *refs = refs
+    rho_ref, t_ref, *refs = refs
     (u_ref, p_old_ref, v_ref, start_ref, sc_ref, yp_ref, yv_ref, y0_ref), refs = refs[:8], refs[8:]
     (slack_ref, dual_ref, lower_ref, upper_ref, gb_ref, sb_ref, w_ref), refs = refs[:7], refs[7:]
     primal_out, half_out, slack_out, dual_out, mine_ref, theirs_ref, *scratch = refs
@@ -346,7 +409,7 @@
     p = u_ref[...] + sc_ref[1:2, 0:1] * p_old_ref[...]
     v = v_ref[...] + alpha * p
     primal = RELAX * v + (1.0 - RELAX) * start_ref[...]
-    primal_out[...] = turn(odd_ref[0] == 1, primal)
+    primal_out[...] = turn(odd_core(), primal)
     half_out[...] = primal[: primal.shape[0] // 2]
     image = yv_ref[...] + alpha * yp_ref[...]
     image_next = RELAX * image + (1.0 - RELAX) * y0_ref[...]
@@ -371,10 +434,16 @@
 
 VMEM_SPEC = pl.BlockSpec(memory_space=pltpu.VMEM)
 SMEM_SPEC = pl.BlockSpec(memory_space=pltpu.SMEM)
-
-
-def call(kernel, name, outs, args, scratch=(), scalars=0):
-    specs = [SMEM_SPEC if i < scalars else VMEM_SPEC for i in range(len(args))]
+HBM_SPEC = pl.BlockSpec(memory_space=pltpu.HBM)
+
+
+def call(kernel, name, outs, args, scratch=(), scalars=0, streamed=0, cost=None):
+    kinds = [SMEM_SPEC] * scalars + [HBM_SPEC] * streamed
+    specs = kinds + [VMEM_SPEC] * (len(args) - len(kinds))
+    args = [
+        pltpu.with_memory_space_constraint(x, pltpu.HBM) if scalars <= i < scalars + streamed else x
+        for i, x in enumerate(args)
+    ]
     shapes = tuple(s if isinstance(s, jax.ShapeDtypeStruct) else jax.ShapeDtypeStruct(s, F32) for s in outs)
     return pl.pallas_call(
         kernel,
@@ -383,6 +452,7 @@
         out_specs=tuple(VMEM_SPEC for _ in outs),
         scratch_shapes=list(scratch),
         compiler_params=pltpu.CompilerParams(vmem_limit_bytes=VMEM_LIMIT),
+        cost_estimate=cost,
         name=name,
     )(*args)
 
@@ -436,45 +506,14 @@
         summed = over_plane(mine + other_core(theirs))
         return summed, other_core(summed)
 
-    def places(a, f):
-        at = jnp.concatenate([a.reshape(-1), f.reshape(-1)]).astype(F32)
-        return jnp.pad(at, (0, 4 * width - count)).reshape(4, width)
-
-    at = jnp.concatenate(
-        [places(constraint_rows, factor_rows + ycount), places(constraint_cols, factor_cols)], axis=0
-    )
-    odd = (lax.axis_index("row") % 2).astype(jnp.int32).reshape(1)
     rho = penalty.reshape(1)
-    at, odd, rho, ctiles, ftiles = lax.optimization_barrier((at, odd, rho, ctiles, ftiles))
-
-    block = 16 if acount % 16 == 0 and fcount % 16 == 0 else 8
-    a_steps, f_steps = acount // block, fcount // block
-    matrix = pl.BlockSpec((block // 2, 2 * width, 2 * width), lambda i: (i, 0, 0))
+    chunk = next(n for n in (16, 8) if acount % n == 0 and fcount % n == 0)
+    assert acount <= width and fcount <= width
     matrices = jax.ShapeDtypeStruct((pairs, 2 * width, 2 * width), BF16)
-
-    def split_tiles(kernel, name, out_specs, out_shape, ctiles, ftiles):
-        return pl.pallas_call(
-            functools.partial(kernel, a_steps),
-            grid=(a_steps + f_steps,),
-            in_specs=[
-                SMEM_SPEC,
-                pl.BlockSpec((block, width, width), lambda i: (jnp.minimum(i, a_steps - 1), 0, 0)),
-                pl.BlockSpec((block, width, width), lambda i: (jnp.maximum(i - a_steps, 0), 0, 0)),
-            ],
-            out_specs=out_specs,
-            out_shape=out_shape,
-            compiler_params=pltpu.CompilerParams(vmem_limit_bytes=VMEM_LIMIT),
-            cost_estimate=pl.CostEstimate(
-                flops=8 * count * width * width, bytes_accessed=4 * count * width * width, transcendentals=0
-            ),
-            name=name,
-        )(
-            rho,
-            pltpu.with_memory_space_constraint(ctiles, pltpu.HBM),
-            pltpu.with_memory_space_constraint(ftiles, pltpu.HBM),
-        )
-
-    turned = split_tiles(split_transposed_kernel, "split_transposed", matrix, matrices, ctiles, ftiles)
+    held = [
+        pltpu.VMEM((count, width, width), F32),
+        pltpu.SemaphoreType.DMA((count // chunk,)),
+    ]
 
     left = pltpu.VMEM((2 * count, 2 * width), BF16)
     rows = pltpu.VMEM((count, width), F32)
@@ -482,39 +521,45 @@
     sent, summed = (count + 8, width), (half + 8, width)
     bits = functools.partial(jax.ShapeDtypeStruct, dtype=BF16)
 
-    parts, start, gf = call(
-        first_forward_kernel,
+    turned, parts, start, gf = call(
+        functools.partial(first_forward_kernel, chunk, ycount),
         "first_forward",
-        [sent, xs, bits((count, xcount))],
-        (odd, primal_start, at, turned),
-        [left],
+        [matrices, sent, xs, bits((count, xcount))],
+        (rho, ctiles, ftiles, primal_start)
+        + tuple(x.reshape(1, -1) for x in (constraint_rows, constraint_cols, factor_rows, factor_cols)),
+        [left, pltpu.VMEM((8, width), F32), pltpu.VMEM(xs, F32)]
+        + [pltpu.VMEM((1, n), jnp.int32) for n in (acount, acount, fcount, fcount)]
+        + [pltpu.SemaphoreType.DMA((5,)), *held],
         scalars=1,
+        streamed=7,
     )
     parts, ctiles, ftiles = lax.optimization_barrier((parts, ctiles, ftiles))
     all_parts = over_col(parts)
-    tiles, squares = split_tiles(
-        split_kernel,
+    tiles, squares = call(
+        functools.partial(split_kernel, chunk),
         "split",
-        (matrix, pl.BlockSpec((block, width), lambda i: (i, 0))),
-        (matrices, jax.ShapeDtypeStruct((count, width), F32)),
-        ctiles,
-        ftiles,
+        [matrices, (count, width)],
+        (ctiles, ftiles),
+        held,
+        streamed=2,
+        cost=pl.CostEstimate(
+            flops=8 * count * width * width, bytes_accessed=4 * count * width * width, transcendentals=0
+        ),
     )
     mine, theirs, y0, s_all, gb, sb = call(
         functools.partial(first_backward_kernel, n_col, ycount, acount),
         "first_backward",
         [xs, xs, ys, bits((n_col, full, count)), bits((count, full)), bits((xcount, count))],
-        (rho, odd, *all_parts, tiles, squares, slack_start, dual_start),
+        (rho, *all_parts, tiles, squares, slack_start, dual_start),
         [left, rows],
-        scalars=2,
+        scalars=1,
     )
     resid, u, precond, diag, linear, parts = call(
         second_forward_kernel,
         "second_forward",
         [xs, xs, xs, xs, xs, sent],
-        (odd, *over_row(mine, theirs), start, diag_cost, linear_cost, gf, turned),
+        (*over_row(mine, theirs), start, diag_cost, linear_cost, gf, turned),
         [left],
-        scalars=1,
     )
     v, yv = start, y0
     p = yp = sc = alpha = None
@@ -544,10 +589,10 @@
         functools.partial(final_kernel, ycount),
         "final",
         [xs, (half, width), (ycount, width), (ycount, width), summed, summed],
-        (rho, odd, norm, u, p, v, start, sc, yp, yv, y0)
+        (rho, norm, u, p, v, start, sc, yp, yv, y0)
         + (slack_start, dual_start, lower_bound, upper_bound, gb, sb, tiles),
         [left, rows],
-        scalars=2,
+        scalars=1,
     )
 
     def join(a, b):
@@ -557,7 +602,7 @@
     z = over_plane(join(mine, other_core(theirs)), join)
     (worst,) = call(residual_kernel, "residuals", [small], (z, primal_half, diag, linear))
     worst = jnp.maximum(worst, other_core(worst))
-    worst = tree(over_col(worst), jnp.maximum)
+    worst = tree(exchange(worst, "col", n_col, range(1, n_col)), jnp.maximum)
     return (primal_next, slack_next, dual_next, jnp.max(worst[:4]), jnp.max(worst[4:]))
 
 

time: 202 us -> 197 us (0.975)
  Pallas kernels: 45.8 us -> 42.3 us
  other arithmetic: 3.16 us -> 1.01 us
    pallas_call x2 -> x0, Pallas kernels: 14.9 us -> none  [split_tiles(): pl.pallas_call(functools.partial(kernel, a_steps), grid=(a_steps + f_step...]
    pallas_call x16 -> x17, Pallas kernels: 30.9 us -> 42.3 us  [call(): pl.pallas_call(kernel, out_shape=shapes, in_specs=specs, out_specs=tuple(...]
  transfers between devices with their start and end apart: 63 -> 63, of which waited for: 54 -> 52; matrix products, arithmetic and copies ran while one was open for 0% -> 0% of each run, Pallas kernels for 4% -> 2%
where the time goes in v4:
time: 197 us
  waiting for transfers between devices  86.4 us (44%)
  starting transfers between devices  65.9 us (33%)
  Pallas kernels  42.3 us (21%)
    ppermute x63, waiting for transfers between devices, swap(): return lax.ppermute(x, axis, [(i, i ^ distance) for i in range(size)])  86.4 us
    ppermute x63, starting transfers between devices, swap(): return lax.ppermute(x, axis, [(i, i ^ distance) for i in range(size)])  65.9 us
    pallas_call x17, Pallas kernels, call(): pl.pallas_call(kernel, out_shape=shapes, in_specs=specs, out_specs=tuple(...  42.3 us
  transfers between devices with their start and end apart: 63, of which 52 were waited for; matrix products, arithmetic and copies ran while one was open for 0% of the time, Pallas kernels for 2%

profile of v4, /device:TPU:0, one launch (start us, length us, event | category | flops | bytes accessed | tf_op | source)
XLA Modules:
  0.0 197.3 jit_solution(16328113321264199414)
XLA Ops:
  1.3 9.2 %first_forward.1 = (bf16[72,256,256]{2,1,0:T(8,128)(2,1)S(1)}, f32[152,128]{1,0:T(8,128)S(1)}, f32[256,128]{1,0:T(8,128)S(1)}, bf16[144,256]{1,0:T(8,128)(2,1)S(1)}) custom-call(f32[1]{0:T(128)} %bitcast.7.rho_ref, f32[96,128,128]{2,1,0:T(8,128)} %bitcast.16, f32[48,128,128]{2,1,0:T(8,128)} %bitcast.18, f32[256,128]{1,0:T(8,128)} %refs_2_.1, ...), custom_call_target="tpu_custom_call" | custom-call | tf_op jit(solution)/shard_map/first_forward/pallas_call | solution.py:448
  10.5 4.1 %collective-permute-start = (f32[152,128]{1,0:T(8,128)S(1)}, f32[152,128]{1,0:T(8,128)S(1)}, u32[]{:S(2)}, u32[]{:S(2)}) collective-permute-start(f32[152,128]{1,0:T(8,128)S(1)} %get-tuple-element.91.refs_1_), channel_id=1, source_target_pairs={{0,2},{1,3},{2,0},{3,1},{4,6},{5,7},{6,4},{7,5},{8,10},{9,11},{10,... | collective-permute-start | bytes 233480 | tf_op jit(solution)/shard_map/ppermute | solution.py:461
  14.7 1.6 collective-permute-start.1
  16.2 4.1 %split.1 = (bf16[72,256,256]{2,1,0:T(8,128)(2,1)S(1)}, f32[144,128]{1,0:T(8,128)S(1)}) custom-call(f32[96,128,128]{2,1,0:T(8,128)} %bitcast.17, f32[48,128,128]{2,1,0:T(8,128)} %bitcast.19), custom_call_target="tpu_custom_call" | custom-call | flops 18874368 | bytes 9437184 | tf_op jit(solution)/shard_map/split/pallas_call | solution.py:448
  20.4 2.1 %collective-permute-done.2.refs_4_ = f32[152,128]{1,0:T(8,128)S(1)} collective-permute-done((f32[152,128]{1,0:T(8,128)S(1)}, f32[152,128]{1,0:T(8,128)S(1)}, u32[]{:S(2)}, u32[]{:S(2)}) %collective-permute-start.2) | collective-permute-done | bytes 77856 | tf_op jit(solution)/shard_map/ppermute | solution.py:461
  22.4 2.4 %first_backward.1 = (f32[256,128]{1,0:T(8,128)S(1)}, f32[256,128]{1,0:T(8,128)S(1)}, f32[256,128]{1,0:T(8,128)S(1)}, bf16[4,256,144]{2,1,0:T(8,128)(2,1)S(1)}, b...) custom-call(f32[1]{0:T(128)} %bitcast.8.refs_0_, f32[152,128]{1,0:T(8,128)S(1)} %get-tuple-element.91.refs_1_, ...), custom_call_target="tpu_custom_call" | custom-call | tf_op jit(solution)/shard_map/first_backward/pallas_call | solution.py:448
  26.3 1.6 collective-permute-start.4
  29.9 2.5 %collective-permute-done.4 = f32[256,128]{1,0:T(8,128)S(1)} collective-permute-done((f32[256,128]{1,0:T(8,128)S(1)}, f32[256,128]{1,0:T(8,128)S(1)}, u32[]{:S(2)}, u32[]{:S(2)}) %collective-permute-start.4) | collective-permute-done | bytes 131104 | tf_op jit(solution)/shard_map/ppermute | solution.py:461
  32.3 3.6 %collective-permute-done.5 = f32[256,128]{1,0:T(8,128)S(1)} collective-permute-done((f32[256,128]{1,0:T(8,128)S(1)}, f32[256,128]{1,0:T(8,128)S(1)}, u32[]{:S(2)}, u32[]{:S(2)}) %collective-permute-start.5) | collective-permute-done | bytes 131104 | tf_op jit(solution)/shard_map/ppermute | solution.py:461
  37.4 1.8 second_forward.1
  39.2 1.8 collective-permute-start.10
  41.5 2.1 %collective-permute-start.9 = (f32[152,128]{1,0:T(8,128)S(1)}, f32[152,128]{1,0:T(8,128)S(1)}, u32[]{:S(2)}, u32[]{:S(2)}) collective-permute-start(f32[152,128]{1,0:T(8,128)S(1)} %get-tuple-element.101.refs_1_), channel_id=1, source_target_pairs={{0,1},{1,0},{2,3},{3,2},{4,5},{5,4},{6,7},{7,6},{8,9},{9,8},{10,11... | collective-permute-start | bytes 233480 | tf_op jit(solution)/shard_map/ppermute | solution.py:461
  43.6 2.6 %collective-permute-done.10.refs_4_ = f32[152,128]{1,0:T(8,128)S(1)} collective-permute-done((f32[152,128]{1,0:T(8,128)S(1)}, f32[152,128]{1,0:T(8,128)S(1)}, u32[]{:S(2)}, u32[]{:S(2)}) %collective-permute-start.10) | collective-permute-done | bytes 77856 | tf_op jit(solution)/shard_map/ppermute | solution.py:461
  46.2 2.9 %collective-permute-done.8.refs_2_ = f32[152,128]{1,0:T(8,128)S(1)} collective-permute-done((f32[152,128]{1,0:T(8,128)S(1)}, f32[152,128]{1,0:T(8,128)S(1)}, u32[]{:S(2)}, u32[]{:S(2)}) %collective-permute-start.8) | collective-permute-done | bytes 77856 | tf_op jit(solution)/shard_map/ppermute | solution.py:461
  49.1 2.2 %backward.5 = (f32[136,128]{1,0:T(8,128)S(1)}, f32[136,128]{1,0:T(8,128)S(1)}, f32[256,128]{1,0:T(8,128)S(1)}, f32[256,128]{1,0:T(8,128)S(1)}, f32[8,128]{1,0:T(8,128)S(1)}) custom-call(f32[1]{0:T(128)} %bitcast.9.refs_0_, f32[152,128]{1,0:T(8,128)S(1)} %get-tuple-element.101.refs_1_, f32[152,128]{1,0:T(8,128)S(1)} %collective-permute-done.8.refs_2_, ...), custom_call_target="tpu_custom_call" | custom-call | tf_op jit(solution)/shard_map/backward/pallas_call | solution.py:448
  57.1 2.0 %collective-permute-done.13 = f32[136,128]{1,0:T(8,128)S(1)} collective-permute-done((f32[136,128]{1,0:T(8,128)S(1)}, f32[136,128]{1,0:T(8,128)S(1)}, u32[]{:S(2)}, u32[]{:S(2)}) %collective-permute-start.13) | collective-permute-done | bytes 69664 | tf_op jit(solution)/shard_map/ppermute | solution.py:461
  61.4 2.0 forward.5
  64.0 2.6 %collective-permute-start.17 = (f32[152,128]{1,0:T(8,128)S(1)}, f32[152,128]{1,0:T(8,128)S(1)}, u32[]{:S(2)}, u32[]{:S(2)}) collective-permute-start(f32[152,128]{1,0:T(8,128)S(1)} %get-tuple-element.113.refs_1_), channel_id=1, source_target_pairs={{0,1},{1,0},{2,3},{3,2},{4,5},{5,4},{6,7},{7,6},{8,9},{9,8},{10,11... | collective-permute-start | bytes 233480 | tf_op jit(solution)/shard_map/ppermute | solution.py:461
  67.8 2.7 %collective-permute-done.16.refs_2_ = f32[152,128]{1,0:T(8,128)S(1)} collective-permute-done((f32[152,128]{1,0:T(8,128)S(1)}, f32[152,128]{1,0:T(8,128)S(1)}, u32[]{:S(2)}, u32[]{:S(2)}) %collective-permute-start.16) | collective-permute-done | bytes 77856 | tf_op jit(solution)/shard_map/ppermute | solution.py:461
  70.5 2.2 %collective-permute-done.18.refs_4_ = f32[152,128]{1,0:T(8,128)S(1)} collective-permute-done((f32[152,128]{1,0:T(8,128)S(1)}, f32[152,128]{1,0:T(8,128)S(1)}, u32[]{:S(2)}, u32[]{:S(2)}) %collective-permute-start.18) | collective-permute-done | bytes 77856 | tf_op jit(solution)/shard_map/ppermute | solution.py:461
  72.8 2.2 %backward.6 = (f32[136,128]{1,0:T(8,128)S(1)}, f32[136,128]{1,0:T(8,128)S(1)}, f32[256,128]{1,0:T(8,128)S(1)}, f32[256,128]{1,0:T(8,128)S(1)}, f32[8,128]{1,0:T(8,128)S(1)}) custom-call(f32[1]{0:T(128)} %bitcast.10.refs_0_, f32[152,128]{1,0:T(8,128)S(1)} %get-tuple-element.113.refs_1_, f32[152,128]{1,0:T(8,128)S(1)} %collective-permute-done.16.refs_2_, ...), custom_call_target="tpu_custom_call" | custom-call | tf_op jit(solution)/shard_map/backward/pallas_call | solution.py:448
  76.4 1.6 collective-permute-start.20
  80.7 2.2 %collective-permute-done.21 = f32[136,128]{1,0:T(8,128)S(1)} collective-permute-done((f32[136,128]{1,0:T(8,128)S(1)}, f32[136,128]{1,0:T(8,128)S(1)}, u32[]{:S(2)}, u32[]{:S(2)}) %collective-permute-start.21) | collective-permute-done | bytes 69664 | tf_op jit(solution)/shard_map/ppermute | solution.py:461
  85.1 2.0 %forward.6 = (f32[256,128]{1,0:T(8,128)S(1)}, f32[256,128]{1,0:T(8,128)S(1)}, f32[256,128]{1,0:T(8,128)S(1)}, f32[256,128]{1,0:T(8,128)S(1)}, f32[8,128]{1,0:T(8,128)S(1)}, /*index=5*/f32[152,128]{1,0:T(8,128)S(1)}) custom-call(f32[136,128]{1,0:T(8,128)S(1)} %add_add_fusion.4.refs_0_, f32[136,128]{1,0:T(8,128)S(1)} %collective-permute-done.23.refs_1_, ...), custom_call_target="tpu_custom_call" | custom-call | tf_op jit(solution)/shard_map/forward/pallas_call | solution.py:448
  87.0 1.6 collective-permute-start.24
  89.1 2.3 %collective-permute-start.26 = (f32[152,128]{1,0:T(8,128)S(1)}, f32[152,128]{1,0:T(8,128)S(1)}, u32[]{:S(2)}, u32[]{:S(2)}) collective-permute-start(f32[152,128]{1,0:T(8,128)S(1)} %get-tuple-element.124.refs_1_), channel_id=1, source_target_pairs={{0,3},{1,2},{2,1},{3,0},{4,7},{5,6},{6,5},{7,4},{8,11},{9,10},{10,... | collective-permute-start | bytes 233480 | tf_op jit(solution)/shard_map/ppermute | solution.py:461
  91.5 3.7 %collective-permute-done.24.refs_2_ = f32[152,128]{1,0:T(8,128)S(1)} collective-permute-done((f32[152,128]{1,0:T(8,128)S(1)}, f32[152,128]{1,0:T(8,128)S(1)}, u32[]{:S(2)}, u32[]{:S(2)}) %collective-permute-start.24) | collective-permute-done | bytes 77856 | tf_op jit(solution)/shard_map/ppermute | solution.py:461
  95.1 1.6 collective-permute-done.26.refs_4_
  96.7 2.2 %backward.7 = (f32[136,128]{1,0:T(8,128)S(1)}, f32[136,128]{1,0:T(8,128)S(1)}, f32[256,128]{1,0:T(8,128)S(1)}, f32[256,128]{1,0:T(8,128)S(1)}, f32[8,128]{1,0:T(8,128)S(1)}) custom-call(f32[1]{0:T(128)} %bitcast.11.refs_0_, f32[152,128]{1,0:T(8,128)S(1)} %get-tuple-element.124.refs_1_, f32[152,128]{1,0:T(8,128)S(1)} %collective-permute-done.24.refs_2_, ...), custom_call_target="tpu_custom_call" | custom-call | tf_op jit(solution)/shard_map/backward/pallas_call | solution.py:448
  104.6 1.9 collective-permute-done.29
  108.9 2.0 forward.7
  112.9 2.3 %collective-permute-start.34 = (f32[152,128]{1,0:T(8,128)S(1)}, f32[152,128]{1,0:T(8,128)S(1)}, u32[]{:S(2)}, u32[]{:S(2)}) collective-permute-start(f32[152,128]{1,0:T(8,128)S(1)} %get-tuple-element.135.refs_1_), channel_id=1, source_target_pairs={{0,3},{1,2},{2,1},{3,0},{4,7},{5,6},{6,5},{7,4},{8,11},{9,10},{10,... | collective-permute-start | bytes 233480 | tf_op jit(solution)/shard_map/ppermute | solution.py:461
  115.2 5.1 %collective-permute-done.32.refs_2_ = f32[152,128]{1,0:T(8,128)S(1)} collective-permute-done((f32[152,128]{1,0:T(8,128)S(1)}, f32[152,128]{1,0:T(8,128)S(1)}, u32[]{:S(2)}, u32[]{:S(2)}) %collective-permute-start.32) | collective-permute-done | bytes 77856 | tf_op jit(solution)/shard_map/ppermute | solution.py:461
  120.3 2.2 %backward.8 = (f32[136,128]{1,0:T(8,128)S(1)}, f32[136,128]{1,0:T(8,128)S(1)}, f32[256,128]{1,0:T(8,128)S(1)}, f32[256,128]{1,0:T(8,128)S(1)}, f32[8,128]{1,0:T(8,128)S(1)}) custom-call(f32[1]{0:T(128)} %bitcast.12.refs_0_, f32[152,128]{1,0:T(8,128)S(1)} %get-tuple-element.135.refs_1_, f32[152,128]{1,0:T(8,128)S(1)} %collective-permute-done.32.refs_2_, ...), custom_call_target="tpu_custom_call" | custom-call | tf_op jit(solution)/shard_map/backward/pallas_call | solution.py:448
  123.9 1.6 collective-permute-start.36
  128.3 2.2 %collective-permute-done.37 = f32[136,128]{1,0:T(8,128)S(1)} collective-permute-done((f32[136,128]{1,0:T(8,128)S(1)}, f32[136,128]{1,0:T(8,128)S(1)}, u32[]{:S(2)}, u32[]{:S(2)}) %collective-permute-start.37) | collective-permute-done | bytes 69664 | tf_op jit(solution)/shard_map/ppermute | solution.py:461
  132.6 2.0 forward.8
  136.6 2.4 %collective-permute-start.42 = (f32[152,128]{1,0:T(8,128)S(1)}, f32[152,128]{1,0:T(8,128)S(1)}, u32[]{:S(2)}, u32[]{:S(2)}) collective-permute-start(f32[152,128]{1,0:T(8,128)S(1)} %get-tuple-element.146.refs_1_), channel_id=1, source_target_pairs={{0,3},{1,2},{2,1},{3,0},{4,7},{5,6},{6,5},{7,4},{8,11},{9,10},{10,... | collective-permute-start | bytes 233480 | tf_op jit(solution)/shard_map/ppermute | solution.py:461
  139.0 4.0 %collective-permute-done.40.refs_2_ = f32[152,128]{1,0:T(8,128)S(1)} collective-permute-done((f32[152,128]{1,0:T(8,128)S(1)}, f32[152,128]{1,0:T(8,128)S(1)}, u32[]{:S(2)}, u32[]{:S(2)}) %collective-permute-start.40) | collective-permute-done | bytes 77856 | tf_op jit(solution)/shard_map/ppermute | solution.py:461
  144.1 2.4 %backward.9 = (f32[136,128]{1,0:T(8,128)S(1)}, f32[136,128]{1,0:T(8,128)S(1)}, f32[256,128]{1,0:T(8,128)S(1)}, f32[256,128]{1,0:T(8,128)S(1)}, f32[8,128]{1,0:T(8,128)S(1)}) custom-call(f32[1]{0:T(128)} %bitcast.13.refs_0_, f32[152,128]{1,0:T(8,128)S(1)} %get-tuple-element.146.refs_1_, f32[152,128]{1,0:T(8,128)S(1)} %collective-permute-done.40.refs_2_, ...), custom_call_target="tpu_custom_call" | custom-call | tf_op jit(solution)/shard_map/backward/pallas_call | solution.py:448
  152.2 1.9 collective-permute-done.45
  156.4 2.5 %forward.9 = (f32[256,128]{1,0:T(8,128)S(1)}, f32[256,128]{1,0:T(8,128)S(1)}, f32[256,128]{1,0:T(8,128)}, f32[256,128]{1,0:T(8,128)S(1)}, f32[8,128]{1,0:T(8,128)S(1)}, /*index=5*/f32[152,128]{1,0:T(8,128)S(1)}) custom-call(f32[136,128]{1,0:T(8,128)S(1)} %add_add_fusion.1.refs_0_, f32[136,128]{1,0:T(8,128)S(1)} %collective-permute-done.47.refs_1_, ...), custom_call_target="tpu_custom_call" | custom-call | tf_op jit(solution)/shard_map/forward/pallas_call | solution.py:448
  161.0 2.3 %collective-permute-start.50 = (f32[152,128]{1,0:T(8,128)S(1)}, f32[152,128]{1,0:T(8,128)S(1)}, u32[]{:S(2)}, u32[]{:S(2)}) collective-permute-start(f32[152,128]{1,0:T(8,128)S(1)} %get-tuple-element.157.refs_1_), channel_id=1, source_target_pairs={{0,3},{1,2},{2,1},{3,0},{4,7},{5,6},{6,5},{7,4},{8,11},{9,10},{10,... | collective-permute-start | bytes 233480 | tf_op jit(solution)/shard_map/ppermute | solution.py:461
  163.3 4.1 %collective-permute-done.48.refs_2_ = f32[152,128]{1,0:T(8,128)S(1)} collective-permute-done((f32[152,128]{1,0:T(8,128)S(1)}, f32[152,128]{1,0:T(8,128)S(1)}, u32[]{:S(2)}, u32[]{:S(2)}) %collective-permute-start.48) | collective-permute-done | bytes 77856 | tf_op jit(solution)/shard_map/ppermute | solution.py:461
  176.6 2.7 %final.1 = (f32[256,128]{1,0:T(8,128)}, f32[128,128]{1,0:T(8,128)S(1)}, f32[192,128]{1,0:T(8,128)}, f32[192,128]{1,0:T(8,128)}, f32[136,128]{1,0:T(8,128)S(1)}, /*index=5*/f32[136,128]{1,0:T(8,128)S(1)}) custom-call(f32[1]{0:T(128)} %bitcast.15.refs_0_, f32[8,128]{1,0:T(8,128)S(1)} %add_add_fusion.6.refs_1_, f32[256,128]{1,0:T(8,128)S(1)} %get-tuple-element.162.refs_2_, ...), custom_call_target="tpu_custom_call" | custom-call | tf_op jit(solution)/shard_map/final/pallas_call | solution.py:448
  185.0 1.9 collective-permute-done.57
  191.2 2.4 %collective-permute-start.62 = (f32[8,128]{1,0:T(8,128)S(1)}, f32[8,128]{1,0:T(8,128)S(1)}, u32[]{:S(2)}, u32[]{:S(2)}) collective-permute-start(f32[8,128]{1,0:T(8,128)S(1)} %max.28), channel_id=1, source_target_pairs={{0,3},{1,2},{2,1},{3,0},{4,7},{5,6},{6,5},{7,4},{8,11},{9,10},{10,... | collective-permute-start | bytes 12296 | tf_op jit(solution)/shard_map/ppermute | solution.py:461
  193.6 1.6 collective-permute-done.61
  (127 shorter events, 72.9 us)
Async XLA Ops:
  10.5 9.8 %collective-permute-start = (f32[152,128]{1,0:T(8,128)S(1)}, f32[152,128]{1,0:T(8,128)S(1)}, u32[]{:S(2)}, u32[]{:S(2)}) collective-permute-start(f32[152,128]{1,0:T(8,128)S(1)} %get-tuple-element.91.refs_1_), channel_id=1, source_target_pairs={{0,2},{1,3},{2,0},{3,1},{4,6},{5,7},{6,4},{7,5},{8,10},{9,11},{10,... | collective-permute-start | bytes 233480 | tf_op jit(solution)/shard_map/ppermute | solution.py:461
  14.7 5.7 %collective-permute-start.1 = (f32[152,128]{1,0:T(8,128)S(1)}, f32[152,128]{1,0:T(8,128)S(1)}, u32[]{:S(2)}, u32[]{:S(2)}) collective-permute-start(f32[152,128]{1,0:T(8,128)S(1)} %get-tuple-element.91.refs_1_), channel_id=1, source_target_pairs={{0,1},{1,0},{2,3},{3,2},{4,5},{5,4},{6,7},{7,6},{8,9},{9,8},{10,11... | collective-permute-start | bytes 233480 | tf_op jit(solution)/shard_map/ppermute | solution.py:461
  16.2 6.2 %collective-permute-start.2 = (f32[152,128]{1,0:T(8,128)S(1)}, f32[152,128]{1,0:T(8,128)S(1)}, u32[]{:S(2)}, u32[]{:S(2)}) collective-permute-start(f32[152,128]{1,0:T(8,128)S(1)} %get-tuple-element.91.refs_1_), channel_id=1, source_target_pairs={{0,3},{1,2},{2,1},{3,0},{4,7},{5,6},{6,5},{7,4},{8,11},{9,10},{10,... | collective-permute-start | bytes 233480 | tf_op jit(solution)/shard_map/ppermute | solution.py:461
  26.3 6.0 %collective-permute-start.4 = (f32[256,128]{1,0:T(8,128)S(1)}, f32[256,128]{1,0:T(8,128)S(1)}, u32[]{:S(2)}, u32[]{:S(2)}) collective-permute-start(f32[256,128]{1,0:T(8,128)S(1)} %add.96), channel_id=1, source_target_pairs={{0,8},{4,12},{8,0},{12,4},{16,24},{20,28},{24,16},{28,20},{1,9},{5... | collective-permute-start | bytes 393224 | tf_op jit(solution)/shard_map/ppermute | solution.py:461
  27.9 8.1 %collective-permute-start.5 = (f32[256,128]{1,0:T(8,128)S(1)}, f32[256,128]{1,0:T(8,128)S(1)}, u32[]{:S(2)}, u32[]{:S(2)}) collective-permute-start(f32[256,128]{1,0:T(8,128)S(1)} %add.96), channel_id=1, source_target_pairs={{0,16},{4,20},{8,24},{12,28},{16,0},{20,4},{24,8},{28,12},{1,17},{... | collective-permute-start | bytes 393224 | tf_op jit(solution)/shard_map/ppermute | solution.py:461
  29.4 6.6 %collective-permute-start.6 = (f32[256,128]{1,0:T(8,128)S(1)}, f32[256,128]{1,0:T(8,128)S(1)}, u32[]{:S(2)}, u32[]{:S(2)}) collective-permute-start(f32[256,128]{1,0:T(8,128)S(1)} %add.96), channel_id=1, source_target_pairs={{0,24},{4,28},{8,16},{12,20},{16,8},{20,12},{24,0},{28,4},{1,25},{... | collective-permute-start | bytes 393224 | tf_op jit(solution)/shard_map/ppermute | solution.py:461
  39.2 7.0 %collective-permute-start.10 = (f32[152,128]{1,0:T(8,128)S(1)}, f32[152,128]{1,0:T(8,128)S(1)}, u32[]{:S(2)}, u32[]{:S(2)}) collective-permute-start(f32[152,128]{1,0:T(8,128)S(1)} %get-tuple-element.101.refs_1_), channel_id=1, source_target_pairs={{0,3},{1,2},{2,1},{3,0},{4,7},{5,6},{6,5},{7,4},{8,11},{9,10},{10,... | collective-permute-start | bytes 233480 | tf_op jit(solution)/shard_map/ppermute | solution.py:461
  41.0 8.1 %collective-permute-start.8 = (f32[152,128]{1,0:T(8,128)S(1)}, f32[152,128]{1,0:T(8,128)S(1)}, u32[]{:S(2)}, u32[]{:S(2)}) collective-permute-start(f32[152,128]{1,0:T(8,128)S(1)} %get-tuple-element.101.refs_1_), channel_id=1, source_target_pairs={{0,2},{1,3},{2,0},{3,1},{4,6},{5,7},{6,4},{7,5},{8,10},{9,11},{10,... | collective-permute-start | bytes 233480 | tf_op jit(solution)/shard_map/ppermute | solution.py:461
  41.5 7.6 %collective-permute-start.9 = (f32[152,128]{1,0:T(8,128)S(1)}, f32[152,128]{1,0:T(8,128)S(1)}, u32[]{:S(2)}, u32[]{:S(2)}) collective-permute-start(f32[152,128]{1,0:T(8,128)S(1)} %get-tuple-element.101.refs_1_), channel_id=1, source_target_pairs={{0,1},{1,0},{2,3},{3,2},{4,5},{5,4},{6,7},{7,6},{8,9},{9,8},{10,11... | collective-permute-start | bytes 233480 | tf_op jit(solution)/shard_map/ppermute | solution.py:461
  52.7 4.4 %collective-permute-start.12 = (f32[136,128]{1,0:T(8,128)S(1)}, f32[136,128]{1,0:T(8,128)S(1)}, u32[]{:S(2)}, u32[]{:S(2)}) collective-permute-start(f32[136,128]{1,0:T(8,128)S(1)} %add.100), channel_id=1, source_target_pairs={{0,8},{4,12},{8,0},{12,4},{16,24},{20,28},{24,16},{28,20},{1,9},{5... | collective-permute-start | bytes 208904 | tf_op jit(solution)/shard_map/ppermute | solution.py:461
  54.0 5.1 %collective-permute-start.13 = (f32[136,128]{1,0:T(8,128)S(1)}, f32[136,128]{1,0:T(8,128)S(1)}, u32[]{:S(2)}, u32[]{:S(2)}) collective-permute-start(f32[136,128]{1,0:T(8,128)S(1)} %add.100), channel_id=1, source_target_pairs={{0,16},{4,20},{8,24},{12,28},{16,0},{20,4},{24,8},{28,12},{1,17},{... | collective-permute-start | bytes 208904 | tf_op jit(solution)/shard_map/ppermute | solution.py:461
  54.8 5.2 %collective-permute-start.14 = (f32[136,128]{1,0:T(8,128)S(1)}, f32[136,128]{1,0:T(8,128)S(1)}, u32[]{:S(2)}, u32[]{:S(2)}) collective-permute-start(f32[136,128]{1,0:T(8,128)S(1)} %add.100), channel_id=1, source_target_pairs={{0,24},{4,28},{8,16},{12,20},{16,8},{20,12},{24,0},{28,4},{1,25},{... | collective-permute-start | bytes 208904 | tf_op jit(solution)/shard_map/ppermute | solution.py:461
  63.4 7.2 %collective-permute-start.16 = (f32[152,128]{1,0:T(8,128)S(1)}, f32[152,128]{1,0:T(8,128)S(1)}, u32[]{:S(2)}, u32[]{:S(2)}) collective-permute-start(f32[152,128]{1,0:T(8,128)S(1)} %get-tuple-element.113.refs_1_), channel_id=1, source_target_pairs={{0,2},{1,3},{2,0},{3,1},{4,6},{5,7},{6,4},{7,5},{8,10},{9,11},{10,... | collective-permute-start | bytes 233480 | tf_op jit(solution)/shard_map/ppermute | solution.py:461
  64.0 6.5 %collective-permute-start.17 = (f32[152,128]{1,0:T(8,128)S(1)}, f32[152,128]{1,0:T(8,128)S(1)}, u32[]{:S(2)}, u32[]{:S(2)}) collective-permute-start(f32[152,128]{1,0:T(8,128)S(1)} %get-tuple-element.113.refs_1_), channel_id=1, source_target_pairs={{0,1},{1,0},{2,3},{3,2},{4,5},{5,4},{6,7},{7,6},{8,9},{9,8},{10,11... | collective-permute-start | bytes 233480 | tf_op jit(solution)/shard_map/ppermute | solution.py:461
  66.6 6.2 %collective-permute-start.18 = (f32[152,128]{1,0:T(8,128)S(1)}, f32[152,128]{1,0:T(8,128)S(1)}, u32[]{:S(2)}, u32[]{:S(2)}) collective-permute-start(f32[152,128]{1,0:T(8,128)S(1)} %get-tuple-element.113.refs_1_), channel_id=1, source_target_pairs={{0,3},{1,2},{2,1},{3,0},{4,7},{5,6},{6,5},{7,4},{8,11},{9,10},{10,... | collective-permute-start | bytes 233480 | tf_op jit(solution)/shard_map/ppermute | solution.py:461
  76.4 4.4 %collective-permute-start.20 = (f32[136,128]{1,0:T(8,128)S(1)}, f32[136,128]{1,0:T(8,128)S(1)}, u32[]{:S(2)}, u32[]{:S(2)}) collective-permute-start(f32[136,128]{1,0:T(8,128)S(1)} %add.104), channel_id=1, source_target_pairs={{0,8},{4,12},{8,0},{12,4},{16,24},{20,28},{24,16},{28,20},{1,9},{5... | collective-permute-start | bytes 208904 | tf_op jit(solution)/shard_map/ppermute | solution.py:461
  77.9 5.1 %collective-permute-start.21 = (f32[136,128]{1,0:T(8,128)S(1)}, f32[136,128]{1,0:T(8,128)S(1)}, u32[]{:S(2)}, u32[]{:S(2)}) collective-permute-start(f32[136,128]{1,0:T(8,128)S(1)} %add.104), channel_id=1, source_target_pairs={{0,16},{4,20},{8,24},{12,28},{16,0},{20,4},{24,8},{28,12},{1,17},{... | collective-permute-start | bytes 208904 | tf_op jit(solution)/shard_map/ppermute | solution.py:461
  78.5 5.2 %collective-permute-start.22 = (f32[136,128]{1,0:T(8,128)S(1)}, f32[136,128]{1,0:T(8,128)S(1)}, u32[]{:S(2)}, u32[]{:S(2)}) collective-permute-start(f32[136,128]{1,0:T(8,128)S(1)} %add.104), channel_id=1, source_target_pairs={{0,24},{4,28},{8,16},{12,20},{16,8},{20,12},{24,0},{28,4},{1,25},{... | collective-permute-start | bytes 208904 | tf_op jit(solution)/shard_map/ppermute | solution.py:461
  87.0 8.1 %collective-permute-start.24 = (f32[152,128]{1,0:T(8,128)S(1)}, f32[152,128]{1,0:T(8,128)S(1)}, u32[]{:S(2)}, u32[]{:S(2)}) collective-permute-start(f32[152,128]{1,0:T(8,128)S(1)} %get-tuple-element.124.refs_1_), channel_id=1, source_target_pairs={{0,2},{1,3},{2,0},{3,1},{4,6},{5,7},{6,4},{7,5},{8,10},{9,11},{10,... | collective-permute-start | bytes 233480 | tf_op jit(solution)/shard_map/ppermute | solution.py:461
  88.7 6.5 %collective-permute-start.25 = (f32[152,128]{1,0:T(8,128)S(1)}, f32[152,128]{1,0:T(8,128)S(1)}, u32[]{:S(2)}, u32[]{:S(2)}) collective-permute-start(f32[152,128]{1,0:T(8,128)S(1)} %get-tuple-element.124.refs_1_), channel_id=1, source_target_pairs={{0,1},{1,0},{2,3},{3,2},{4,5},{5,4},{6,7},{7,6},{8,9},{9,8},{10,11... | collective-permute-start | bytes 233480 | tf_op jit(solution)/shard_map/ppermute | solution.py:461
  89.1 7.6 %collective-permute-start.26 = (f32[152,128]{1,0:T(8,128)S(1)}, f32[152,128]{1,0:T(8,128)S(1)}, u32[]{:S(2)}, u32[]{:S(2)}) collective-permute-start(f32[152,128]{1,0:T(8,128)S(1)} %get-tuple-element.124.refs_1_), channel_id=1, source_target_pairs={{0,3},{1,2},{2,1},{3,0},{4,7},{5,6},{6,5},{7,4},{8,11},{9,10},{10,... | collective-permute-start | bytes 233480 | tf_op jit(solution)/shard_map/ppermute | solution.py:461
  100.3 4.4 %collective-permute-start.28 = (f32[136,128]{1,0:T(8,128)S(1)}, f32[136,128]{1,0:T(8,128)S(1)}, u32[]{:S(2)}, u32[]{:S(2)}) collective-permute-start(f32[136,128]{1,0:T(8,128)S(1)} %add.108), channel_id=1, source_target_pairs={{0,8},{4,12},{8,0},{12,4},{16,24},{20,28},{24,16},{28,20},{1,9},{5... | collective-permute-start | bytes 208904 | tf_op jit(solution)/shard_map/ppermute | solution.py:461
  101.5 5.1 %collective-permute-start.29 = (f32[136,128]{1,0:T(8,128)S(1)}, f32[136,128]{1,0:T(8,128)S(1)}, u32[]{:S(2)}, u32[]{:S(2)}) collective-permute-start(f32[136,128]{1,0:T(8,128)S(1)} %add.108), channel_id=1, source_target_pairs={{0,16},{4,20},{8,24},{12,28},{16,0},{20,4},{24,8},{28,12},{1,17},{... | collective-permute-start | bytes 208904 | tf_op jit(solution)/shard_map/ppermute | solution.py:461
  102.3 5.2 %collective-permute-start.30 = (f32[136,128]{1,0:T(8,128)S(1)}, f32[136,128]{1,0:T(8,128)S(1)}, u32[]{:S(2)}, u32[]{:S(2)}) collective-permute-start(f32[136,128]{1,0:T(8,128)S(1)} %add.108), channel_id=1, source_target_pairs={{0,24},{4,28},{8,16},{12,20},{16,8},{20,12},{24,0},{28,4},{1,25},{... | collective-permute-start | bytes 208904 | tf_op jit(solution)/shard_map/ppermute | solution.py:461
  110.8 9.5 %collective-permute-start.32 = (f32[152,128]{1,0:T(8,128)S(1)}, f32[152,128]{1,0:T(8,128)S(1)}, u32[]{:S(2)}, u32[]{:S(2)}) collective-permute-start(f32[152,128]{1,0:T(8,128)S(1)} %get-tuple-element.135.refs_1_), channel_id=1, source_target_pairs={{0,2},{1,3},{2,0},{3,1},{4,6},{5,7},{6,4},{7,5},{8,10},{9,11},{10,... | collective-permute-start | bytes 233480 | tf_op jit(solution)/shard_map/ppermute | solution.py:461
  112.1 8.2 %collective-permute-start.33 = (f32[152,128]{1,0:T(8,128)S(1)}, f32[152,128]{1,0:T(8,128)S(1)}, u32[]{:S(2)}, u32[]{:S(2)}) collective-permute-start(f32[152,128]{1,0:T(8,128)S(1)} %get-tuple-element.135.refs_1_), channel_id=1, source_target_pairs={{0,1},{1,0},{2,3},{3,2},{4,5},{5,4},{6,7},{7,6},{8,9},{9,8},{10,11... | collective-permute-start | bytes 233480 | tf_op jit(solution)/shard_map/ppermute | solution.py:461
  112.9 7.3 %collective-permute-start.34 = (f32[152,128]{1,0:T(8,128)S(1)}, f32[152,128]{1,0:T(8,128)S(1)}, u32[]{:S(2)}, u32[]{:S(2)}) collective-permute-start(f32[152,128]{1,0:T(8,128)S(1)} %get-tuple-element.135.refs_1_), channel_id=1, source_target_pairs={{0,3},{1,2},{2,1},{3,0},{4,7},{5,6},{6,5},{7,4},{8,11},{9,10},{10,... | collective-permute-start | bytes 233480 | tf_op jit(solution)/shard_map/ppermute | solution.py:461
  123.9 4.4 %collective-permute-start.36 = (f32[136,128]{1,0:T(8,128)S(1)}, f32[136,128]{1,0:T(8,128)S(1)}, u32[]{:S(2)}, u32[]{:S(2)}) collective-permute-start(f32[136,128]{1,0:T(8,128)S(1)} %add.112), channel_id=1, source_target_pairs={{0,8},{4,12},{8,0},{12,4},{16,24},{20,28},{24,16},{28,20},{1,9},{5... | collective-permute-start | bytes 208904 | tf_op jit(solution)/shard_map/ppermute | solution.py:461
  125.4 5.1 %collective-permute-start.37 = (f32[136,128]{1,0:T(8,128)S(1)}, f32[136,128]{1,0:T(8,128)S(1)}, u32[]{:S(2)}, u32[]{:S(2)}) collective-permute-start(f32[136,128]{1,0:T(8,128)S(1)} %add.112), channel_id=1, source_target_pairs={{0,16},{4,20},{8,24},{12,28},{16,0},{20,4},{24,8},{28,12},{1,17},{... | collective-permute-start | bytes 208904 | tf_op jit(solution)/shard_map/ppermute | solution.py:461
  126.0 5.2 %collective-permute-start.38 = (f32[136,128]{1,0:T(8,128)S(1)}, f32[136,128]{1,0:T(8,128)S(1)}, u32[]{:S(2)}, u32[]{:S(2)}) collective-permute-start(f32[136,128]{1,0:T(8,128)S(1)} %add.112), channel_id=1, source_target_pairs={{0,24},{4,28},{8,16},{12,20},{16,8},{20,12},{24,0},{28,4},{1,25},{... | collective-permute-start | bytes 208904 | tf_op jit(solution)/shard_map/ppermute | solution.py:461
  134.6 8.4 %collective-permute-start.40 = (f32[152,128]{1,0:T(8,128)S(1)}, f32[152,128]{1,0:T(8,128)S(1)}, u32[]{:S(2)}, u32[]{:S(2)}) collective-permute-start(f32[152,128]{1,0:T(8,128)S(1)} %get-tuple-element.146.refs_1_), channel_id=1, source_target_pairs={{0,2},{1,3},{2,0},{3,1},{4,6},{5,7},{6,4},{7,5},{8,10},{9,11},{10,... | collective-permute-start | bytes 233480 | tf_op jit(solution)/shard_map/ppermute | solution.py:461
  136.1 6.9 %collective-permute-start.41 = (f32[152,128]{1,0:T(8,128)S(1)}, f32[152,128]{1,0:T(8,128)S(1)}, u32[]{:S(2)}, u32[]{:S(2)}) collective-permute-start(f32[152,128]{1,0:T(8,128)S(1)} %get-tuple-element.146.refs_1_), channel_id=1, source_target_pairs={{0,1},{1,0},{2,3},{3,2},{4,5},{5,4},{6,7},{7,6},{8,9},{9,8},{10,11... | collective-permute-start | bytes 233480 | tf_op jit(solution)/shard_map/ppermute | solution.py:461
  136.6 7.5 %collective-permute-start.42 = (f32[152,128]{1,0:T(8,128)S(1)}, f32[152,128]{1,0:T(8,128)S(1)}, u32[]{:S(2)}, u32[]{:S(2)}) collective-permute-start(f32[152,128]{1,0:T(8,128)S(1)} %get-tuple-element.146.refs_1_), channel_id=1, source_target_pairs={{0,3},{1,2},{2,1},{3,0},{4,7},{5,6},{6,5},{7,4},{8,11},{9,10},{10,... | collective-permute-start | bytes 233480 | tf_op jit(solution)/shard_map/ppermute | solution.py:461
  147.9 4.4 %collective-permute-start.44 = (f32[136,128]{1,0:T(8,128)S(1)}, f32[136,128]{1,0:T(8,128)S(1)}, u32[]{:S(2)}, u32[]{:S(2)}) collective-permute-start(f32[136,128]{1,0:T(8,128)S(1)} %add.116), channel_id=1, source_target_pairs={{0,8},{4,12},{8,0},{12,4},{16,24},{20,28},{24,16},{28,20},{1,9},{5... | collective-permute-start | bytes 208904 | tf_op jit(solution)/shard_map/ppermute | solution.py:461
  149.1 5.1 %collective-permute-start.45 = (f32[136,128]{1,0:T(8,128)S(1)}, f32[136,128]{1,0:T(8,128)S(1)}, u32[]{:S(2)}, u32[]{:S(2)}) collective-permute-start(f32[136,128]{1,0:T(8,128)S(1)} %add.116), channel_id=1, source_target_pairs={{0,16},{4,20},{8,24},{12,28},{16,0},{20,4},{24,8},{28,12},{1,17},{... | collective-permute-start | bytes 208904 | tf_op jit(solution)/shard_map/ppermute | solution.py:461
  149.9 5.2 %collective-permute-start.46 = (f32[136,128]{1,0:T(8,128)S(1)}, f32[136,128]{1,0:T(8,128)S(1)}, u32[]{:S(2)}, u32[]{:S(2)}) collective-permute-start(f32[136,128]{1,0:T(8,128)S(1)} %add.116), channel_id=1, source_target_pairs={{0,24},{4,28},{8,16},{12,20},{16,8},{20,12},{24,0},{28,4},{1,25},{... | collective-permute-start | bytes 208904 | tf_op jit(solution)/shard_map/ppermute | solution.py:461
  158.9 8.5 %collective-permute-start.48 = (f32[152,128]{1,0:T(8,128)S(1)}, f32[152,128]{1,0:T(8,128)S(1)}, u32[]{:S(2)}, u32[]{:S(2)}) collective-permute-start(f32[152,128]{1,0:T(8,128)S(1)} %get-tuple-element.157.refs_1_), channel_id=1, source_target_pairs={{0,2},{1,3},{2,0},{3,1},{4,6},{5,7},{6,4},{7,5},{8,10},{9,11},{10,... | collective-permute-start | bytes 233480 | tf_op jit(solution)/shard_map/ppermute | solution.py:461
  160.3 7.2 %collective-permute-start.49 = (f32[152,128]{1,0:T(8,128)S(1)}, f32[152,128]{1,0:T(8,128)S(1)}, u32[]{:S(2)}, u32[]{:S(2)}) collective-permute-start(f32[152,128]{1,0:T(8,128)S(1)} %get-tuple-element.157.refs_1_), channel_id=1, source_target_pairs={{0,1},{1,0},{2,3},{3,2},{4,5},{5,4},{6,7},{7,6},{8,9},{9,8},{10,11... | collective-permute-start | bytes 233480 | tf_op jit(solution)/shard_map/ppermute | solution.py:461
  161.0 7.4 %collective-permute-start.50 = (f32[152,128]{1,0:T(8,128)S(1)}, f32[152,128]{1,0:T(8,128)S(1)}, u32[]{:S(2)}, u32[]{:S(2)}) collective-permute-start(f32[152,128]{1,0:T(8,128)S(1)} %get-tuple-element.157.refs_1_), channel_id=1, source_target_pairs={{0,3},{1,2},{2,1},{3,0},{4,7},{5,6},{6,5},{7,4},{8,11},{9,10},{10,... | collective-permute-start | bytes 233480 | tf_op jit(solution)/shard_map/ppermute | solution.py:461
  169.9 3.6 %collective-permute-start.52 = (f32[8,128]{1,0:T(8,128)S(1)}, f32[8,128]{1,0:T(8,128)S(1)}, u32[]{:S(2)}, u32[]{:S(2)}) collective-permute-start(f32[8,128]{1,0:T(8,128)S(1)} %add.120), channel_id=1, source_target_pairs={{0,8},{4,12},{8,0},{12,4},{16,24},{20,28},{24,16},{28,20},{1,9},{5... | collective-permute-start | bytes 12296 | tf_op jit(solution)/shard_map/ppermute | solution.py:461
  171.4 3.6 %collective-permute-start.53 = (f32[8,128]{1,0:T(8,128)S(1)}, f32[8,128]{1,0:T(8,128)S(1)}, u32[]{:S(2)}, u32[]{:S(2)}) collective-permute-start(f32[8,128]{1,0:T(8,128)S(1)} %add.120), channel_id=1, source_target_pairs={{0,16},{4,20},{8,24},{12,28},{16,0},{20,4},{24,8},{28,12},{1,17},{... | collective-permute-start | bytes 12296 | tf_op jit(solution)/shard_map/ppermute | solution.py:461
  172.0 4.5 %collective-permute-start.54 = (f32[8,128]{1,0:T(8,128)S(1)}, f32[8,128]{1,0:T(8,128)S(1)}, u32[]{:S(2)}, u32[]{:S(2)}) collective-permute-start(f32[8,128]{1,0:T(8,128)S(1)} %add.120), channel_id=1, source_target_pairs={{0,24},{4,28},{8,16},{12,20},{16,8},{20,12},{24,0},{28,4},{1,25},{... | collective-permute-start | bytes 12296 | tf_op jit(solution)/shard_map/ppermute | solution.py:461
  180.6 4.4 %collective-permute-start.56 = (f32[136,128]{1,0:T(8,128)S(1)}, f32[136,128]{1,0:T(8,128)S(1)}, u32[]{:S(2)}, u32[]{:S(2)}) collective-permute-start(f32[136,128]{1,0:T(8,128)S(1)} %maximum_select_fusion.1), channel_id=1, source_target_pairs={{0,8},{4,12},{8,0},{12,4},{16,24},{20,28},{24,16},{28,20},{1,9},{5... | collective-permute-start | bytes 208904 | tf_op jit(solution)/shard_map/ppermute | solution.py:461
  181.8 5.1 %collective-permute-start.57 = (f32[136,128]{1,0:T(8,128)S(1)}, f32[136,128]{1,0:T(8,128)S(1)}, u32[]{:S(2)}, u32[]{:S(2)}) collective-permute-start(f32[136,128]{1,0:T(8,128)S(1)} %maximum_select_fusion.1), channel_id=1, source_target_pairs={{0,16},{4,20},{8,24},{12,28},{16,0},{20,4},{24,8},{28,12},{1,17},{... | collective-permute-start | bytes 208904 | tf_op jit(solution)/shard_map/ppermute | solution.py:461
  182.6 5.2 %collective-permute-start.58 = (f32[136,128]{1,0:T(8,128)S(1)}, f32[136,128]{1,0:T(8,128)S(1)}, u32[]{:S(2)}, u32[]{:S(2)}) collective-permute-start(f32[136,128]{1,0:T(8,128)S(1)} %maximum_select_fusion.1), channel_id=1, source_target_pairs={{0,24},{4,28},{8,16},{12,20},{16,8},{20,12},{24,0},{28,4},{1,25},{... | collective-permute-start | bytes 208904 | tf_op jit(solution)/shard_map/ppermute | solution.py:461
  189.2 4.4 %collective-permute-start.60 = (f32[8,128]{1,0:T(8,128)S(1)}, f32[8,128]{1,0:T(8,128)S(1)}, u32[]{:S(2)}, u32[]{:S(2)}) collective-permute-start(f32[8,128]{1,0:T(8,128)S(1)} %max.28), channel_id=1, source_target_pairs={{0,1},{1,0},{2,3},{3,2},{4,5},{5,4},{6,7},{7,6},{8,9},{9,8},{10,11... | collective-permute-start | bytes 12296 | tf_op jit(solution)/shard_map/ppermute | solution.py:461
  190.6 4.5 %collective-permute-start.61 = (f32[8,128]{1,0:T(8,128)S(1)}, f32[8,128]{1,0:T(8,128)S(1)}, u32[]{:S(2)}, u32[]{:S(2)}) collective-permute-start(f32[8,128]{1,0:T(8,128)S(1)} %max.28), channel_id=1, source_target_pairs={{0,2},{1,3},{2,0},{3,1},{4,6},{5,7},{6,4},{7,5},{8,10},{9,11},{10,... | collective-permute-start | bytes 12296 | tf_op jit(solution)/shard_map/ppermute | solution.py:461
  191.2 5.4 %collective-permute-start.62 = (f32[8,128]{1,0:T(8,128)S(1)}, f32[8,128]{1,0:T(8,128)S(1)}, u32[]{:S(2)}, u32[]{:S(2)}) collective-permute-start(f32[8,128]{1,0:T(8,128)S(1)} %max.28), channel_id=1, source_target_pairs={{0,3},{1,2},{2,1},{3,0},{4,7},{5,6},{6,5},{7,4},{8,11},{9,10},{10,... | collective-permute-start | bytes 12296 | tf_op jit(solution)/shard_map/ppermute | solution.py:461
  (21 other events, 180.8 us)

commit v5 on v4

--- a/solution.py
+++ b/solution.py
@@ -16,7 +16,8 @@
 F32 = jnp.float32
 BF16 = jnp.bfloat16
 LANES = 128
-UNROLL = 6
+UNROLL = 18
+IN_FLIGHT = 2
 LANES = 128
 TILES = 8
 VMEM_LIMIT = 24 * 1024 * 1024
@@ -84,9 +85,9 @@
     finish(pl.multiple_of(block * TILES, TILES), out[:TILES] + out[TILES:])
 
 
-def run_tiles(w_ref, l_ref, finish):
+def run_tiles(w_ref, l_ref, most, finish):
     blocks = w_ref.shape[0] // (TILES // 2)
-    unroll = next(n for n in (UNROLL, 6, 4, 3, 2, 1) if blocks % n == 0)
+    unroll = next(n for n in (most, 6, 4, 3, 2, 1) if blocks % n == 0)
 
     def body(step, carry):
         for inner in range(unroll):
@@ -113,7 +114,7 @@
 
 def forward_parts(vec, gf_ref, wt_ref, out_ref, l_ref):
     forward_left(vec, gf_ref, l_ref)
-    run_tiles(wt_ref, l_ref, forward_finish(out_ref))
+    run_tiles(wt_ref, l_ref, UNROLL, forward_finish(out_ref))
 
 
 def backward_sum(vec, gb_ref, sb_ref, w_ref, l_ref, rows_ref):
@@ -125,7 +126,7 @@
     def finish(at, out):
         rows_ref[pl.ds(at, TILES), :] = jnp.where(first, out[:, :LANES], out[:, LANES:])
 
-    run_tiles(w_ref, l_ref, finish)
+    run_tiles(w_ref, l_ref, UNROLL, finish)
     return scatter(sb_ref[...], rows_ref[...])
 
 
@@ -171,7 +172,9 @@
     return copies
 
 
-def wait_chunk(step, chunk, a_ref, held_ref, sems):
+def wait_chunk(step, chunk, copies, a_ref, held_ref, sems):
+    for later in range(IN_FLIGHT, len(copies)):
+        pl.when(step + IN_FLIGHT == later)(copies[later].start)
     at = pl.multiple_of(step * chunk, chunk)
     pltpu.make_async_copy(a_ref.at[pl.ds(0, chunk)], held_ref.at[pl.ds(at, chunk)], sems.at[step]).wait()
 
@@ -186,7 +189,7 @@
         copy.start()
 
     def body(step, carry):
-        wait_chunk(step, chunk, a_ref, held_ref, sems)
+        wait_chunk(step, chunk, (), a_ref, held_ref, sems)
         for t in range(chunk):
             tile = held_ref[step * chunk + t]
             pair, at = (step * chunk + t) // 2, (t % 2) * LANES
@@ -222,7 +225,7 @@
     small_held, (small_sems, held_ref, sems) = refs[:5], refs[5:]
     fetched = [pltpu.make_async_copy(a, b, small_sems.at[i]) for i, (a, b) in enumerate(zip(small_refs, small_held))]
     copies = tile_copies(chunk, (a_ref, g_ref), held_ref, sems)
-    for copy in fetched + copies:
+    for copy in fetched + copies[:IN_FLIGHT]:
         copy.start()
     odd = odd_core()
     for copy in fetched:
@@ -246,7 +249,7 @@
             one_block(wt_ref, l_ref, step * blocks + inner, finish)
 
     def split(step):
-        wait_chunk(step, chunk, a_ref, held_ref, sems)
+        wait_chunk(step, chunk, copies, a_ref, held_ref, sems)
         for t in range(chunk):
             pair, at = (step * chunk + t) // 2, (t % 2) * LANES
             high, low = split2(held_ref[step * chunk + t].T)
@@ -507,7 +510,7 @@
         return summed, other_core(summed)
 
     rho = penalty.reshape(1)
-    chunk = next(n for n in (16, 8) if acount % n == 0 and fcount % n == 0)
+    chunk = next(n for n in (24, 16, 8) if acount % n == 0 and fcount % n == 0)
     assert acount <= width and fcount <= width
     matrices = jax.ShapeDtypeStruct((pairs, 2 * width, 2 * width), BF16)
     held = [

time: 197 us -> 191 us (0.970)
  Pallas kernels: 42.3 us -> 36 us
    pallas_call x17, Pallas kernels: 42.3 us -> 36 us  [call(): pl.pallas_call(kernel, out_shape=shapes, in_specs=specs, out_specs=tuple(...]
  transfers between devices with their start and end apart: 63 -> 63, of which waited for: 52 -> 53; matrix products, arithmetic and copies ran while one was open for 0% -> 0% of each run, Pallas kernels for 2% -> 2%
where the time goes in v5:
time: 191 us
  waiting for transfers between devices  86.3 us (45%)
  starting transfers between devices  65.9 us (35%)
  Pallas kernels  36 us (19%)
    ppermute x63, waiting for transfers between devices, swap(): return lax.ppermute(x, axis, [(i, i ^ distance) for i in range(size)])  86.3 us
    ppermute x63, starting transfers between devices, swap(): return lax.ppermute(x, axis, [(i, i ^ distance) for i in range(size)])  65.9 us
    pallas_call x17, Pallas kernels, call(): pl.pallas_call(kernel, out_shape=shapes, in_specs=specs, out_specs=tuple(...  36 us
  transfers between devices with their start and end apart: 63, of which 53 were waited for; matrix products, arithmetic and copies ran while one was open for 0% of the time, Pallas kernels for 2%

profile of v5, /device:TPU:0, one launch (start us, length us, event | category | flops | bytes accessed | tf_op | source)
XLA Modules:
  0.0 190.8 jit_solution(5906731379459453045)
XLA Ops:
  1.3 6.6 %first_forward.1 = (bf16[72,256,256]{2,1,0:T(8,128)(2,1)S(1)}, f32[152,128]{1,0:T(8,128)S(1)}, f32[256,128]{1,0:T(8,128)S(1)}, bf16[144,256]{1,0:T(8,128)(2,1)S(1)}) custom-call(f32[1]{0:T(128)} %bitcast.7.rho_ref, f32[96,128,128]{2,1,0:T(8,128)} %bitcast.16, f32[48,128,128]{2,1,0:T(8,128)} %bitcast.18, f32[256,128]{1,0:T(8,128)} %refs_2_.1, ...), custom_call_target="tpu_custom_call" | custom-call | tf_op jit(solution)/shard_map/first_forward/pallas_call | solution.py:451
  8.0 4.1 %collective-permute-start = (f32[152,128]{1,0:T(8,128)S(1)}, f32[152,128]{1,0:T(8,128)S(1)}, u32[]{:S(2)}, u32[]{:S(2)}) collective-permute-start(f32[152,128]{1,0:T(8,128)S(1)} %get-tuple-element.91.refs_1_), channel_id=1, source_target_pairs={{0,2},{1,3},{2,0},{3,1},{4,6},{5,7},{6,4},{7,5},{8,10},{9,11},{10,... | collective-permute-start | bytes 233480 | tf_op jit(solution)/shard_map/ppermute | solution.py:464
  12.1 1.6 collective-permute-start.1
  13.7 4.4 %split.1 = (bf16[72,256,256]{2,1,0:T(8,128)(2,1)S(1)}, f32[144,128]{1,0:T(8,128)S(1)}) custom-call(f32[96,128,128]{2,1,0:T(8,128)} %bitcast.17, f32[48,128,128]{2,1,0:T(8,128)} %bitcast.19), custom_call_target="tpu_custom_call" | custom-call | flops 18874368 | bytes 9437184 | tf_op jit(solution)/shard_map/split/pallas_call | solution.py:451
  18.1 1.8 collective-permute-done.2.refs_4_
  19.9 2.1 %first_backward.1 = (f32[256,128]{1,0:T(8,128)S(1)}, f32[256,128]{1,0:T(8,128)S(1)}, f32[256,128]{1,0:T(8,128)S(1)}, bf16[4,256,144]{2,1,0:T(8,128)(2,1)S(1)}, b...) custom-call(f32[1]{0:T(128)} %bitcast.8.refs_0_, f32[152,128]{1,0:T(8,128)S(1)} %get-tuple-element.91.refs_1_, ...), custom_call_target="tpu_custom_call" | custom-call | tf_op jit(solution)/shard_map/first_backward/pallas_call | solution.py:451
  23.4 1.6 collective-permute-start.4
  26.9 2.5 %collective-permute-done.4 = f32[256,128]{1,0:T(8,128)S(1)} collective-permute-done((f32[256,128]{1,0:T(8,128)S(1)}, f32[256,128]{1,0:T(8,128)S(1)}, u32[]{:S(2)}, u32[]{:S(2)}) %collective-permute-start.4) | collective-permute-done | bytes 131104 | tf_op jit(solution)/shard_map/ppermute | solution.py:464
  29.4 3.6 %collective-permute-done.5 = f32[256,128]{1,0:T(8,128)S(1)} collective-permute-done((f32[256,128]{1,0:T(8,128)S(1)}, f32[256,128]{1,0:T(8,128)S(1)}, u32[]{:S(2)}, u32[]{:S(2)}) %collective-permute-start.5) | collective-permute-done | bytes 131104 | tf_op jit(solution)/shard_map/ppermute | solution.py:464
  34.5 1.6 second_forward.1
  36.0 2.1 %collective-permute-start.10 = (f32[152,128]{1,0:T(8,128)S(1)}, f32[152,128]{1,0:T(8,128)S(1)}, u32[]{:S(2)}, u32[]{:S(2)}) collective-permute-start(f32[152,128]{1,0:T(8,128)S(1)} %get-tuple-element.101.refs_1_), channel_id=1, source_target_pairs={{0,3},{1,2},{2,1},{3,0},{4,7},{5,6},{6,5},{7,4},{8,11},{9,10},{10,... | collective-permute-start | bytes 233480 | tf_op jit(solution)/shard_map/ppermute | solution.py:464
  38.3 2.1 %collective-permute-start.9 = (f32[152,128]{1,0:T(8,128)S(1)}, f32[152,128]{1,0:T(8,128)S(1)}, u32[]{:S(2)}, u32[]{:S(2)}) collective-permute-start(f32[152,128]{1,0:T(8,128)S(1)} %get-tuple-element.101.refs_1_), channel_id=1, source_target_pairs={{0,1},{1,0},{2,3},{3,2},{4,5},{5,4},{6,7},{7,6},{8,9},{9,8},{10,11... | collective-permute-start | bytes 233480 | tf_op jit(solution)/shard_map/ppermute | solution.py:464
  40.4 2.6 %collective-permute-done.10.refs_4_ = f32[152,128]{1,0:T(8,128)S(1)} collective-permute-done((f32[152,128]{1,0:T(8,128)S(1)}, f32[152,128]{1,0:T(8,128)S(1)}, u32[]{:S(2)}, u32[]{:S(2)}) %collective-permute-start.10) | collective-permute-done | bytes 77856 | tf_op jit(solution)/shard_map/ppermute | solution.py:464
  43.0 2.9 %collective-permute-done.8.refs_2_ = f32[152,128]{1,0:T(8,128)S(1)} collective-permute-done((f32[152,128]{1,0:T(8,128)S(1)}, f32[152,128]{1,0:T(8,128)S(1)}, u32[]{:S(2)}, u32[]{:S(2)}) %collective-permute-start.8) | collective-permute-done | bytes 77856 | tf_op jit(solution)/shard_map/ppermute | solution.py:464
  45.9 2.0 %backward.5 = (f32[136,128]{1,0:T(8,128)S(1)}, f32[136,128]{1,0:T(8,128)S(1)}, f32[256,128]{1,0:T(8,128)S(1)}, f32[256,128]{1,0:T(8,128)S(1)}, f32[8,128]{1,0:T(8,128)S(1)}) custom-call(f32[1]{0:T(128)} %bitcast.9.refs_0_, f32[152,128]{1,0:T(8,128)S(1)} %get-tuple-element.101.refs_1_, f32[152,128]{1,0:T(8,128)S(1)} %collective-permute-done.8.refs_2_, ...), custom_call_target="tpu_custom_call" | custom-call | tf_op jit(solution)/shard_map/backward/pallas_call | solution.py:451
  53.7 2.0 %collective-permute-done.13 = f32[136,128]{1,0:T(8,128)S(1)} collective-permute-done((f32[136,128]{1,0:T(8,128)S(1)}, f32[136,128]{1,0:T(8,128)S(1)}, u32[]{:S(2)}, u32[]{:S(2)}) %collective-permute-start.13) | collective-permute-done | bytes 69664 | tf_op jit(solution)/shard_map/ppermute | solution.py:464
  58.0 1.7 forward.5
  60.6 2.3 %collective-permute-start.17 = (f32[152,128]{1,0:T(8,128)S(1)}, f32[152,128]{1,0:T(8,128)S(1)}, u32[]{:S(2)}, u32[]{:S(2)}) collective-permute-start(f32[152,128]{1,0:T(8,128)S(1)} %get-tuple-element.113.refs_1_), channel_id=1, source_target_pairs={{0,1},{1,0},{2,3},{3,2},{4,5},{5,4},{6,7},{7,6},{8,9},{9,8},{10,11... | collective-permute-start | bytes 233480 | tf_op jit(solution)/shard_map/ppermute | solution.py:464
  64.1 2.7 %collective-permute-done.16.refs_2_ = f32[152,128]{1,0:T(8,128)S(1)} collective-permute-done((f32[152,128]{1,0:T(8,128)S(1)}, f32[152,128]{1,0:T(8,128)S(1)}, u32[]{:S(2)}, u32[]{:S(2)}) %collective-permute-start.16) | collective-permute-done | bytes 77856 | tf_op jit(solution)/shard_map/ppermute | solution.py:464
  66.9 2.1 %collective-permute-done.18.refs_4_ = f32[152,128]{1,0:T(8,128)S(1)} collective-permute-done((f32[152,128]{1,0:T(8,128)S(1)}, f32[152,128]{1,0:T(8,128)S(1)}, u32[]{:S(2)}, u32[]{:S(2)}) %collective-permute-start.18) | collective-permute-done | bytes 77856 | tf_op jit(solution)/shard_map/ppermute | solution.py:464
  69.1 2.0 %backward.6 = (f32[136,128]{1,0:T(8,128)S(1)}, f32[136,128]{1,0:T(8,128)S(1)}, f32[256,128]{1,0:T(8,128)S(1)}, f32[256,128]{1,0:T(8,128)S(1)}, f32[8,128]{1,0:T(8,128)S(1)}) custom-call(f32[1]{0:T(128)} %bitcast.10.refs_0_, f32[152,128]{1,0:T(8,128)S(1)} %get-tuple-element.113.refs_1_, f32[152,128]{1,0:T(8,128)S(1)} %collective-permute-done.16.refs_2_, ...), custom_call_target="tpu_custom_call" | custom-call | tf_op jit(solution)/shard_map/backward/pallas_call | solution.py:451
  76.8 2.2 %collective-permute-done.21 = f32[136,128]{1,0:T(8,128)S(1)} collective-permute-done((f32[136,128]{1,0:T(8,128)S(1)}, f32[136,128]{1,0:T(8,128)S(1)}, u32[]{:S(2)}, u32[]{:S(2)}) %collective-permute-start.21) | collective-permute-done | bytes 69664 | tf_op jit(solution)/shard_map/ppermute | solution.py:464
  81.1 1.7 forward.6
  82.9 1.8 collective-permute-start.24
  84.9 2.3 %collective-permute-start.26 = (f32[152,128]{1,0:T(8,128)S(1)}, f32[152,128]{1,0:T(8,128)S(1)}, u32[]{:S(2)}, u32[]{:S(2)}) collective-permute-start(f32[152,128]{1,0:T(8,128)S(1)} %get-tuple-element.124.refs_1_), channel_id=1, source_target_pairs={{0,3},{1,2},{2,1},{3,0},{4,7},{5,6},{6,5},{7,4},{8,11},{9,10},{10,... | collective-permute-start | bytes 233480 | tf_op jit(solution)/shard_map/ppermute | solution.py:464
  87.3 3.6 %collective-permute-done.24.refs_2_ = f32[152,128]{1,0:T(8,128)S(1)} collective-permute-done((f32[152,128]{1,0:T(8,128)S(1)}, f32[152,128]{1,0:T(8,128)S(1)}, u32[]{:S(2)}, u32[]{:S(2)}) %collective-permute-start.24) | collective-permute-done | bytes 77856 | tf_op jit(solution)/shard_map/ppermute | solution.py:464
  90.9 1.6 collective-permute-done.26.refs_4_
  92.5 2.2 %backward.7 = (f32[136,128]{1,0:T(8,128)S(1)}, f32[136,128]{1,0:T(8,128)S(1)}, f32[256,128]{1,0:T(8,128)S(1)}, f32[256,128]{1,0:T(8,128)S(1)}, f32[8,128]{1,0:T(8,128)S(1)}) custom-call(f32[1]{0:T(128)} %bitcast.11.refs_0_, f32[152,128]{1,0:T(8,128)S(1)} %get-tuple-element.124.refs_1_, f32[152,128]{1,0:T(8,128)S(1)} %collective-permute-done.24.refs_2_, ...), custom_call_target="tpu_custom_call" | custom-call | tf_op jit(solution)/shard_map/backward/pallas_call | solution.py:451
  100.4 1.9 collective-permute-done.29
  104.6 1.7 forward.7
  108.7 2.1 %collective-permute-start.34 = (f32[152,128]{1,0:T(8,128)S(1)}, f32[152,128]{1,0:T(8,128)S(1)}, u32[]{:S(2)}, u32[]{:S(2)}) collective-permute-start(f32[152,128]{1,0:T(8,128)S(1)} %get-tuple-element.135.refs_1_), channel_id=1, source_target_pairs={{0,3},{1,2},{2,1},{3,0},{4,7},{5,6},{6,5},{7,4},{8,11},{9,10},{10,... | collective-permute-start | bytes 233480 | tf_op jit(solution)/shard_map/ppermute | solution.py:464
  110.8 5.1 %collective-permute-done.32.refs_2_ = f32[152,128]{1,0:T(8,128)S(1)} collective-permute-done((f32[152,128]{1,0:T(8,128)S(1)}, f32[152,128]{1,0:T(8,128)S(1)}, u32[]{:S(2)}, u32[]{:S(2)}) %collective-permute-start.32) | collective-permute-done | bytes 77856 | tf_op jit(solution)/shard_map/ppermute | solution.py:464
  115.8 2.0 %backward.8 = (f32[136,128]{1,0:T(8,128)S(1)}, f32[136,128]{1,0:T(8,128)S(1)}, f32[256,128]{1,0:T(8,128)S(1)}, f32[256,128]{1,0:T(8,128)S(1)}, f32[8,128]{1,0:T(8,128)S(1)}) custom-call(f32[1]{0:T(128)} %bitcast.12.refs_0_, f32[152,128]{1,0:T(8,128)S(1)} %get-tuple-element.135.refs_1_, f32[152,128]{1,0:T(8,128)S(1)} %collective-permute-done.32.refs_2_, ...), custom_call_target="tpu_custom_call" | custom-call | tf_op jit(solution)/shard_map/backward/pallas_call | solution.py:451
  119.2 1.6 collective-permute-start.36
  123.5 2.2 %collective-permute-done.37 = f32[136,128]{1,0:T(8,128)S(1)} collective-permute-done((f32[136,128]{1,0:T(8,128)S(1)}, f32[136,128]{1,0:T(8,128)S(1)}, u32[]{:S(2)}, u32[]{:S(2)}) %collective-permute-start.37) | collective-permute-done | bytes 69664 | tf_op jit(solution)/shard_map/ppermute | solution.py:464
  127.9 1.7 forward.8
  129.6 1.7 collective-permute-start.40
  131.7 2.3 %collective-permute-start.42 = (f32[152,128]{1,0:T(8,128)S(1)}, f32[152,128]{1,0:T(8,128)S(1)}, u32[]{:S(2)}, u32[]{:S(2)}) collective-permute-start(f32[152,128]{1,0:T(8,128)S(1)} %get-tuple-element.146.refs_1_), channel_id=1, source_target_pairs={{0,3},{1,2},{2,1},{3,0},{4,7},{5,6},{6,5},{7,4},{8,11},{9,10},{10,... | collective-permute-start | bytes 233480 | tf_op jit(solution)/shard_map/ppermute | solution.py:464
  134.0 3.9 %collective-permute-done.40.refs_2_ = f32[152,128]{1,0:T(8,128)S(1)} collective-permute-done((f32[152,128]{1,0:T(8,128)S(1)}, f32[152,128]{1,0:T(8,128)S(1)}, u32[]{:S(2)}, u32[]{:S(2)}) %collective-permute-start.40) | collective-permute-done | bytes 77856 | tf_op jit(solution)/shard_map/ppermute | solution.py:464
  139.1 2.0 %backward.9 = (f32[136,128]{1,0:T(8,128)S(1)}, f32[136,128]{1,0:T(8,128)S(1)}, f32[256,128]{1,0:T(8,128)S(1)}, f32[256,128]{1,0:T(8,128)S(1)}, f32[8,128]{1,0:T(8,128)S(1)}) custom-call(f32[1]{0:T(128)} %bitcast.13.refs_0_, f32[152,128]{1,0:T(8,128)S(1)} %get-tuple-element.146.refs_1_, f32[152,128]{1,0:T(8,128)S(1)} %collective-permute-done.40.refs_2_, ...), custom_call_target="tpu_custom_call" | custom-call | tf_op jit(solution)/shard_map/backward/pallas_call | solution.py:451
  146.9 1.9 collective-permute-done.45
  151.1 1.7 forward.9
  155.1 2.1 %collective-permute-start.50 = (f32[152,128]{1,0:T(8,128)S(1)}, f32[152,128]{1,0:T(8,128)S(1)}, u32[]{:S(2)}, u32[]{:S(2)}) collective-permute-start(f32[152,128]{1,0:T(8,128)S(1)} %get-tuple-element.157.refs_1_), channel_id=1, source_target_pairs={{0,3},{1,2},{2,1},{3,0},{4,7},{5,6},{6,5},{7,4},{8,11},{9,10},{10,... | collective-permute-start | bytes 233480 | tf_op jit(solution)/shard_map/ppermute | solution.py:464
  157.2 4.1 %collective-permute-done.48.refs_2_ = f32[152,128]{1,0:T(8,128)S(1)} collective-permute-done((f32[152,128]{1,0:T(8,128)S(1)}, f32[152,128]{1,0:T(8,128)S(1)}, u32[]{:S(2)}, u32[]{:S(2)}) %collective-permute-start.48) | collective-permute-done | bytes 77856 | tf_op jit(solution)/shard_map/ppermute | solution.py:464
  170.4 2.3 %final.1 = (f32[256,128]{1,0:T(8,128)}, f32[128,128]{1,0:T(8,128)S(1)}, f32[192,128]{1,0:T(8,128)}, f32[192,128]{1,0:T(8,128)}, f32[136,128]{1,0:T(8,128)S(1)}, /*index=5*/f32[136,128]{1,0:T(8,128)S(1)}) custom-call(f32[1]{0:T(128)} %bitcast.15.refs_0_, f32[8,128]{1,0:T(8,128)S(1)} %add_add_fusion.6.refs_1_, f32[256,128]{1,0:T(8,128)S(1)} %get-tuple-element.162.refs_2_, ...), custom_call_target="tpu_custom_call" | custom-call | tf_op jit(solution)/shard_map/final/pallas_call | solution.py:451
  178.4 1.9 collective-permute-done.57
  184.8 2.2 %collective-permute-start.62 = (f32[8,128]{1,0:T(8,128)S(1)}, f32[8,128]{1,0:T(8,128)S(1)}, u32[]{:S(2)}, u32[]{:S(2)}) collective-permute-start(f32[8,128]{1,0:T(8,128)S(1)} %max.28), channel_id=1, source_target_pairs={{0,3},{1,2},{2,1},{3,0},{4,7},{5,6},{6,5},{7,4},{8,11},{9,10},{10,... | collective-permute-start | bytes 12296 | tf_op jit(solution)/shard_map/ppermute | solution.py:464
  188.6 1.6 collective-permute-done.62
  (127 shorter events, 73.3 us)
Async XLA Ops:
  8.0 10.1 %collective-permute-start = (f32[152,128]{1,0:T(8,128)S(1)}, f32[152,128]{1,0:T(8,128)S(1)}, u32[]{:S(2)}, u32[]{:S(2)}) collective-permute-start(f32[152,128]{1,0:T(8,128)S(1)} %get-tuple-element.91.refs_1_), channel_id=1, source_target_pairs={{0,2},{1,3},{2,0},{3,1},{4,6},{5,7},{6,4},{7,5},{8,10},{9,11},{10,... | collective-permute-start | bytes 233480 | tf_op jit(solution)/shard_map/ppermute | solution.py:464
  12.1 6.0 %collective-permute-start.1 = (f32[152,128]{1,0:T(8,128)S(1)}, f32[152,128]{1,0:T(8,128)S(1)}, u32[]{:S(2)}, u32[]{:S(2)}) collective-permute-start(f32[152,128]{1,0:T(8,128)S(1)} %get-tuple-element.91.refs_1_), channel_id=1, source_target_pairs={{0,1},{1,0},{2,3},{3,2},{4,5},{5,4},{6,7},{7,6},{8,9},{9,8},{10,11... | collective-permute-start | bytes 233480 | tf_op jit(solution)/shard_map/ppermute | solution.py:464
  13.7 6.2 %collective-permute-start.2 = (f32[152,128]{1,0:T(8,128)S(1)}, f32[152,128]{1,0:T(8,128)S(1)}, u32[]{:S(2)}, u32[]{:S(2)}) collective-permute-start(f32[152,128]{1,0:T(8,128)S(1)} %get-tuple-element.91.refs_1_), channel_id=1, source_target_pairs={{0,3},{1,2},{2,1},{3,0},{4,7},{5,6},{6,5},{7,4},{8,11},{9,10},{10,... | collective-permute-start | bytes 233480 | tf_op jit(solution)/shard_map/ppermute | solution.py:464
  23.4 6.0 %collective-permute-start.4 = (f32[256,128]{1,0:T(8,128)S(1)}, f32[256,128]{1,0:T(8,128)S(1)}, u32[]{:S(2)}, u32[]{:S(2)}) collective-permute-start(f32[256,128]{1,0:T(8,128)S(1)} %add.96), channel_id=1, source_target_pairs={{0,8},{4,12},{8,0},{12,4},{16,24},{20,28},{24,16},{28,20},{1,9},{5... | collective-permute-start | bytes 393224 | tf_op jit(solution)/shard_map/ppermute | solution.py:464
  24.9 8.1 %collective-permute-start.5 = (f32[256,128]{1,0:T(8,128)S(1)}, f32[256,128]{1,0:T(8,128)S(1)}, u32[]{:S(2)}, u32[]{:S(2)}) collective-permute-start(f32[256,128]{1,0:T(8,128)S(1)} %add.96), channel_id=1, source_target_pairs={{0,16},{4,20},{8,24},{12,28},{16,0},{20,4},{24,8},{28,12},{1,17},{... | collective-permute-start | bytes 393224 | tf_op jit(solution)/shard_map/ppermute | solution.py:464
  26.4 6.6 %collective-permute-start.6 = (f32[256,128]{1,0:T(8,128)S(1)}, f32[256,128]{1,0:T(8,128)S(1)}, u32[]{:S(2)}, u32[]{:S(2)}) collective-permute-start(f32[256,128]{1,0:T(8,128)S(1)} %add.96), channel_id=1, source_target_pairs={{0,24},{4,28},{8,16},{12,20},{16,8},{20,12},{24,0},{28,4},{1,25},{... | collective-permute-start | bytes 393224 | tf_op jit(solution)/shard_map/ppermute | solution.py:464
  36.0 7.0 %collective-permute-start.10 = (f32[152,128]{1,0:T(8,128)S(1)}, f32[152,128]{1,0:T(8,128)S(1)}, u32[]{:S(2)}, u32[]{:S(2)}) collective-permute-start(f32[152,128]{1,0:T(8,128)S(1)} %get-tuple-element.101.refs_1_), channel_id=1, source_target_pairs={{0,3},{1,2},{2,1},{3,0},{4,7},{5,6},{6,5},{7,4},{8,11},{9,10},{10,... | collective-permute-start | bytes 233480 | tf_op jit(solution)/shard_map/ppermute | solution.py:464
  38.1 7.8 %collective-permute-start.8 = (f32[152,128]{1,0:T(8,128)S(1)}, f32[152,128]{1,0:T(8,128)S(1)}, u32[]{:S(2)}, u32[]{:S(2)}) collective-permute-start(f32[152,128]{1,0:T(8,128)S(1)} %get-tuple-element.101.refs_1_), channel_id=1, source_target_pairs={{0,2},{1,3},{2,0},{3,1},{4,6},{5,7},{6,4},{7,5},{8,10},{9,11},{10,... | collective-permute-start | bytes 233480 | tf_op jit(solution)/shard_map/ppermute | solution.py:464
  38.3 7.6 %collective-permute-start.9 = (f32[152,128]{1,0:T(8,128)S(1)}, f32[152,128]{1,0:T(8,128)S(1)}, u32[]{:S(2)}, u32[]{:S(2)}) collective-permute-start(f32[152,128]{1,0:T(8,128)S(1)} %get-tuple-element.101.refs_1_), channel_id=1, source_target_pairs={{0,1},{1,0},{2,3},{3,2},{4,5},{5,4},{6,7},{7,6},{8,9},{9,8},{10,11... | collective-permute-start | bytes 233480 | tf_op jit(solution)/shard_map/ppermute | solution.py:464
  49.3 4.4 %collective-permute-start.12 = (f32[136,128]{1,0:T(8,128)S(1)}, f32[136,128]{1,0:T(8,128)S(1)}, u32[]{:S(2)}, u32[]{:S(2)}) collective-permute-start(f32[136,128]{1,0:T(8,128)S(1)} %add.100), channel_id=1, source_target_pairs={{0,8},{4,12},{8,0},{12,4},{16,24},{20,28},{24,16},{28,20},{1,9},{5... | collective-permute-start | bytes 208904 | tf_op jit(solution)/shard_map/ppermute | solution.py:464
  50.6 5.1 %collective-permute-start.13 = (f32[136,128]{1,0:T(8,128)S(1)}, f32[136,128]{1,0:T(8,128)S(1)}, u32[]{:S(2)}, u32[]{:S(2)}) collective-permute-start(f32[136,128]{1,0:T(8,128)S(1)} %add.100), channel_id=1, source_target_pairs={{0,16},{4,20},{8,24},{12,28},{16,0},{20,4},{24,8},{28,12},{1,17},{... | collective-permute-start | bytes 208904 | tf_op jit(solution)/shard_map/ppermute | solution.py:464
  51.4 5.2 %collective-permute-start.14 = (f32[136,128]{1,0:T(8,128)S(1)}, f32[136,128]{1,0:T(8,128)S(1)}, u32[]{:S(2)}, u32[]{:S(2)}) collective-permute-start(f32[136,128]{1,0:T(8,128)S(1)} %add.100), channel_id=1, source_target_pairs={{0,24},{4,28},{8,16},{12,20},{16,8},{20,12},{24,0},{28,4},{1,25},{... | collective-permute-start | bytes 208904 | tf_op jit(solution)/shard_map/ppermute | solution.py:464
  59.7 7.1 %collective-permute-start.16 = (f32[152,128]{1,0:T(8,128)S(1)}, f32[152,128]{1,0:T(8,128)S(1)}, u32[]{:S(2)}, u32[]{:S(2)}) collective-permute-start(f32[152,128]{1,0:T(8,128)S(1)} %get-tuple-element.113.refs_1_), channel_id=1, source_target_pairs={{0,2},{1,3},{2,0},{3,1},{4,6},{5,7},{6,4},{7,5},{8,10},{9,11},{10,... | collective-permute-start | bytes 233480 | tf_op jit(solution)/shard_map/ppermute | solution.py:464
  60.6 6.4 %collective-permute-start.17 = (f32[152,128]{1,0:T(8,128)S(1)}, f32[152,128]{1,0:T(8,128)S(1)}, u32[]{:S(2)}, u32[]{:S(2)}) collective-permute-start(f32[152,128]{1,0:T(8,128)S(1)} %get-tuple-element.113.refs_1_), channel_id=1, source_target_pairs={{0,1},{1,0},{2,3},{3,2},{4,5},{5,4},{6,7},{7,6},{8,9},{9,8},{10,11... | collective-permute-start | bytes 233480 | tf_op jit(solution)/shard_map/ppermute | solution.py:464
  62.9 6.2 %collective-permute-start.18 = (f32[152,128]{1,0:T(8,128)S(1)}, f32[152,128]{1,0:T(8,128)S(1)}, u32[]{:S(2)}, u32[]{:S(2)}) collective-permute-start(f32[152,128]{1,0:T(8,128)S(1)} %get-tuple-element.113.refs_1_), channel_id=1, source_target_pairs={{0,3},{1,2},{2,1},{3,0},{4,7},{5,6},{6,5},{7,4},{8,11},{9,10},{10,... | collective-permute-start | bytes 233480 | tf_op jit(solution)/shard_map/ppermute | solution.py:464
  72.4 4.4 %collective-permute-start.20 = (f32[136,128]{1,0:T(8,128)S(1)}, f32[136,128]{1,0:T(8,128)S(1)}, u32[]{:S(2)}, u32[]{:S(2)}) collective-permute-start(f32[136,128]{1,0:T(8,128)S(1)} %add.104), channel_id=1, source_target_pairs={{0,8},{4,12},{8,0},{12,4},{16,24},{20,28},{24,16},{28,20},{1,9},{5... | collective-permute-start | bytes 208904 | tf_op jit(solution)/shard_map/ppermute | solution.py:464
  74.0 5.1 %collective-permute-start.21 = (f32[136,128]{1,0:T(8,128)S(1)}, f32[136,128]{1,0:T(8,128)S(1)}, u32[]{:S(2)}, u32[]{:S(2)}) collective-permute-start(f32[136,128]{1,0:T(8,128)S(1)} %add.104), channel_id=1, source_target_pairs={{0,16},{4,20},{8,24},{12,28},{16,0},{20,4},{24,8},{28,12},{1,17},{... | collective-permute-start | bytes 208904 | tf_op jit(solution)/shard_map/ppermute | solution.py:464
  74.6 5.2 %collective-permute-start.22 = (f32[136,128]{1,0:T(8,128)S(1)}, f32[136,128]{1,0:T(8,128)S(1)}, u32[]{:S(2)}, u32[]{:S(2)}) collective-permute-start(f32[136,128]{1,0:T(8,128)S(1)} %add.104), channel_id=1, source_target_pairs={{0,24},{4,28},{8,16},{12,20},{16,8},{20,12},{24,0},{28,4},{1,25},{... | collective-permute-start | bytes 208904 | tf_op jit(solution)/shard_map/ppermute | solution.py:464
  82.9 8.1 %collective-permute-start.24 = (f32[152,128]{1,0:T(8,128)S(1)}, f32[152,128]{1,0:T(8,128)S(1)}, u32[]{:S(2)}, u32[]{:S(2)}) collective-permute-start(f32[152,128]{1,0:T(8,128)S(1)} %get-tuple-element.124.refs_1_), channel_id=1, source_target_pairs={{0,2},{1,3},{2,0},{3,1},{4,6},{5,7},{6,4},{7,5},{8,10},{9,11},{10,... | collective-permute-start | bytes 233480 | tf_op jit(solution)/shard_map/ppermute | solution.py:464
  84.7 6.2 %collective-permute-start.25 = (f32[152,128]{1,0:T(8,128)S(1)}, f32[152,128]{1,0:T(8,128)S(1)}, u32[]{:S(2)}, u32[]{:S(2)}) collective-permute-start(f32[152,128]{1,0:T(8,128)S(1)} %get-tuple-element.124.refs_1_), channel_id=1, source_target_pairs={{0,1},{1,0},{2,3},{3,2},{4,5},{5,4},{6,7},{7,6},{8,9},{9,8},{10,11... | collective-permute-start | bytes 233480 | tf_op jit(solution)/shard_map/ppermute | solution.py:464
  84.9 7.6 %collective-permute-start.26 = (f32[152,128]{1,0:T(8,128)S(1)}, f32[152,128]{1,0:T(8,128)S(1)}, u32[]{:S(2)}, u32[]{:S(2)}) collective-permute-start(f32[152,128]{1,0:T(8,128)S(1)} %get-tuple-element.124.refs_1_), channel_id=1, source_target_pairs={{0,3},{1,2},{2,1},{3,0},{4,7},{5,6},{6,5},{7,4},{8,11},{9,10},{10,... | collective-permute-start | bytes 233480 | tf_op jit(solution)/shard_map/ppermute | solution.py:464
  96.0 4.4 %collective-permute-start.28 = (f32[136,128]{1,0:T(8,128)S(1)}, f32[136,128]{1,0:T(8,128)S(1)}, u32[]{:S(2)}, u32[]{:S(2)}) collective-permute-start(f32[136,128]{1,0:T(8,128)S(1)} %add.108), channel_id=1, source_target_pairs={{0,8},{4,12},{8,0},{12,4},{16,24},{20,28},{24,16},{28,20},{1,9},{5... | collective-permute-start | bytes 208904 | tf_op jit(solution)/shard_map/ppermute | solution.py:464
  97.3 5.1 %collective-permute-start.29 = (f32[136,128]{1,0:T(8,128)S(1)}, f32[136,128]{1,0:T(8,128)S(1)}, u32[]{:S(2)}, u32[]{:S(2)}) collective-permute-start(f32[136,128]{1,0:T(8,128)S(1)} %add.108), channel_id=1, source_target_pairs={{0,16},{4,20},{8,24},{12,28},{16,0},{20,4},{24,8},{28,12},{1,17},{... | collective-permute-start | bytes 208904 | tf_op jit(solution)/shard_map/ppermute | solution.py:464
  98.1 5.2 %collective-permute-start.30 = (f32[136,128]{1,0:T(8,128)S(1)}, f32[136,128]{1,0:T(8,128)S(1)}, u32[]{:S(2)}, u32[]{:S(2)}) collective-permute-start(f32[136,128]{1,0:T(8,128)S(1)} %add.108), channel_id=1, source_target_pairs={{0,24},{4,28},{8,16},{12,20},{16,8},{20,12},{24,0},{28,4},{1,25},{... | collective-permute-start | bytes 208904 | tf_op jit(solution)/shard_map/ppermute | solution.py:464
  106.4 9.5 %collective-permute-start.32 = (f32[152,128]{1,0:T(8,128)S(1)}, f32[152,128]{1,0:T(8,128)S(1)}, u32[]{:S(2)}, u32[]{:S(2)}) collective-permute-start(f32[152,128]{1,0:T(8,128)S(1)} %get-tuple-element.135.refs_1_), channel_id=1, source_target_pairs={{0,2},{1,3},{2,0},{3,1},{4,6},{5,7},{6,4},{7,5},{8,10},{9,11},{10,... | collective-permute-start | bytes 233480 | tf_op jit(solution)/shard_map/ppermute | solution.py:464
  107.7 8.2 %collective-permute-start.33 = (f32[152,128]{1,0:T(8,128)S(1)}, f32[152,128]{1,0:T(8,128)S(1)}, u32[]{:S(2)}, u32[]{:S(2)}) collective-permute-start(f32[152,128]{1,0:T(8,128)S(1)} %get-tuple-element.135.refs_1_), channel_id=1, source_target_pairs={{0,1},{1,0},{2,3},{3,2},{4,5},{5,4},{6,7},{7,6},{8,9},{9,8},{10,11... | collective-permute-start | bytes 233480 | tf_op jit(solution)/shard_map/ppermute | solution.py:464
  108.7 7.2 %collective-permute-start.34 = (f32[152,128]{1,0:T(8,128)S(1)}, f32[152,128]{1,0:T(8,128)S(1)}, u32[]{:S(2)}, u32[]{:S(2)}) collective-permute-start(f32[152,128]{1,0:T(8,128)S(1)} %get-tuple-element.135.refs_1_), channel_id=1, source_target_pairs={{0,3},{1,2},{2,1},{3,0},{4,7},{5,6},{6,5},{7,4},{8,11},{9,10},{10,... | collective-permute-start | bytes 233480 | tf_op jit(solution)/shard_map/ppermute | solution.py:464
  119.2 4.4 %collective-permute-start.36 = (f32[136,128]{1,0:T(8,128)S(1)}, f32[136,128]{1,0:T(8,128)S(1)}, u32[]{:S(2)}, u32[]{:S(2)}) collective-permute-start(f32[136,128]{1,0:T(8,128)S(1)} %add.112), channel_id=1, source_target_pairs={{0,8},{4,12},{8,0},{12,4},{16,24},{20,28},{24,16},{28,20},{1,9},{5... | collective-permute-start | bytes 208904 | tf_op jit(solution)/shard_map/ppermute | solution.py:464
  120.7 5.1 %collective-permute-start.37 = (f32[136,128]{1,0:T(8,128)S(1)}, f32[136,128]{1,0:T(8,128)S(1)}, u32[]{:S(2)}, u32[]{:S(2)}) collective-permute-start(f32[136,128]{1,0:T(8,128)S(1)} %add.112), channel_id=1, source_target_pairs={{0,16},{4,20},{8,24},{12,28},{16,0},{20,4},{24,8},{28,12},{1,17},{... | collective-permute-start | bytes 208904 | tf_op jit(solution)/shard_map/ppermute | solution.py:464
  121.3 5.2 %collective-permute-start.38 = (f32[136,128]{1,0:T(8,128)S(1)}, f32[136,128]{1,0:T(8,128)S(1)}, u32[]{:S(2)}, u32[]{:S(2)}) collective-permute-start(f32[136,128]{1,0:T(8,128)S(1)} %add.112), channel_id=1, source_target_pairs={{0,24},{4,28},{8,16},{12,20},{16,8},{20,12},{24,0},{28,4},{1,25},{... | collective-permute-start | bytes 208904 | tf_op jit(solution)/shard_map/ppermute | solution.py:464
  129.6 8.4 %collective-permute-start.40 = (f32[152,128]{1,0:T(8,128)S(1)}, f32[152,128]{1,0:T(8,128)S(1)}, u32[]{:S(2)}, u32[]{:S(2)}) collective-permute-start(f32[152,128]{1,0:T(8,128)S(1)} %get-tuple-element.146.refs_1_), channel_id=1, source_target_pairs={{0,2},{1,3},{2,0},{3,1},{4,6},{5,7},{6,4},{7,5},{8,10},{9,11},{10,... | collective-permute-start | bytes 233480 | tf_op jit(solution)/shard_map/ppermute | solution.py:464
  131.3 6.6 %collective-permute-start.41 = (f32[152,128]{1,0:T(8,128)S(1)}, f32[152,128]{1,0:T(8,128)S(1)}, u32[]{:S(2)}, u32[]{:S(2)}) collective-permute-start(f32[152,128]{1,0:T(8,128)S(1)} %get-tuple-element.146.refs_1_), channel_id=1, source_target_pairs={{0,1},{1,0},{2,3},{3,2},{4,5},{5,4},{6,7},{7,6},{8,9},{9,8},{10,11... | collective-permute-start | bytes 233480 | tf_op jit(solution)/shard_map/ppermute | solution.py:464
  131.7 7.5 %collective-permute-start.42 = (f32[152,128]{1,0:T(8,128)S(1)}, f32[152,128]{1,0:T(8,128)S(1)}, u32[]{:S(2)}, u32[]{:S(2)}) collective-permute-start(f32[152,128]{1,0:T(8,128)S(1)} %get-tuple-element.146.refs_1_), channel_id=1, source_target_pairs={{0,3},{1,2},{2,1},{3,0},{4,7},{5,6},{6,5},{7,4},{8,11},{9,10},{10,... | collective-permute-start | bytes 233480 | tf_op jit(solution)/shard_map/ppermute | solution.py:464
  142.5 4.4 %collective-permute-start.44 = (f32[136,128]{1,0:T(8,128)S(1)}, f32[136,128]{1,0:T(8,128)S(1)}, u32[]{:S(2)}, u32[]{:S(2)}) collective-permute-start(f32[136,128]{1,0:T(8,128)S(1)} %add.116), channel_id=1, source_target_pairs={{0,8},{4,12},{8,0},{12,4},{16,24},{20,28},{24,16},{28,20},{1,9},{5... | collective-permute-start | bytes 208904 | tf_op jit(solution)/shard_map/ppermute | solution.py:464
  143.7 5.1 %collective-permute-start.45 = (f32[136,128]{1,0:T(8,128)S(1)}, f32[136,128]{1,0:T(8,128)S(1)}, u32[]{:S(2)}, u32[]{:S(2)}) collective-permute-start(f32[136,128]{1,0:T(8,128)S(1)} %add.116), channel_id=1, source_target_pairs={{0,16},{4,20},{8,24},{12,28},{16,0},{20,4},{24,8},{28,12},{1,17},{... | collective-permute-start | bytes 208904 | tf_op jit(solution)/shard_map/ppermute | solution.py:464
  144.5 5.2 %collective-permute-start.46 = (f32[136,128]{1,0:T(8,128)S(1)}, f32[136,128]{1,0:T(8,128)S(1)}, u32[]{:S(2)}, u32[]{:S(2)}) collective-permute-start(f32[136,128]{1,0:T(8,128)S(1)} %add.116), channel_id=1, source_target_pairs={{0,24},{4,28},{8,16},{12,20},{16,8},{20,12},{24,0},{28,4},{1,25},{... | collective-permute-start | bytes 208904 | tf_op jit(solution)/shard_map/ppermute | solution.py:464
  152.8 8.5 %collective-permute-start.48 = (f32[152,128]{1,0:T(8,128)S(1)}, f32[152,128]{1,0:T(8,128)S(1)}, u32[]{:S(2)}, u32[]{:S(2)}) collective-permute-start(f32[152,128]{1,0:T(8,128)S(1)} %get-tuple-element.157.refs_1_), channel_id=1, source_target_pairs={{0,2},{1,3},{2,0},{3,1},{4,6},{5,7},{6,4},{7,5},{8,10},{9,11},{10,... | collective-permute-start | bytes 233480 | tf_op jit(solution)/shard_map/ppermute | solution.py:464
  154.2 7.1 %collective-permute-start.49 = (f32[152,128]{1,0:T(8,128)S(1)}, f32[152,128]{1,0:T(8,128)S(1)}, u32[]{:S(2)}, u32[]{:S(2)}) collective-permute-start(f32[152,128]{1,0:T(8,128)S(1)} %get-tuple-element.157.refs_1_), channel_id=1, source_target_pairs={{0,1},{1,0},{2,3},{3,2},{4,5},{5,4},{6,7},{7,6},{8,9},{9,8},{10,11... | collective-permute-start | bytes 233480 | tf_op jit(solution)/shard_map/ppermute | solution.py:464
  155.1 7.2 %collective-permute-start.50 = (f32[152,128]{1,0:T(8,128)S(1)}, f32[152,128]{1,0:T(8,128)S(1)}, u32[]{:S(2)}, u32[]{:S(2)}) collective-permute-start(f32[152,128]{1,0:T(8,128)S(1)} %get-tuple-element.157.refs_1_), channel_id=1, source_target_pairs={{0,3},{1,2},{2,1},{3,0},{4,7},{5,6},{6,5},{7,4},{8,11},{9,10},{10,... | collective-permute-start | bytes 233480 | tf_op jit(solution)/shard_map/ppermute | solution.py:464
  163.8 3.6 %collective-permute-start.52 = (f32[8,128]{1,0:T(8,128)S(1)}, f32[8,128]{1,0:T(8,128)S(1)}, u32[]{:S(2)}, u32[]{:S(2)}) collective-permute-start(f32[8,128]{1,0:T(8,128)S(1)} %add.120), channel_id=1, source_target_pairs={{0,8},{4,12},{8,0},{12,4},{16,24},{20,28},{24,16},{28,20},{1,9},{5... | collective-permute-start | bytes 12296 | tf_op jit(solution)/shard_map/ppermute | solution.py:464
  165.3 3.6 %collective-permute-start.53 = (f32[8,128]{1,0:T(8,128)S(1)}, f32[8,128]{1,0:T(8,128)S(1)}, u32[]{:S(2)}, u32[]{:S(2)}) collective-permute-start(f32[8,128]{1,0:T(8,128)S(1)} %add.120), channel_id=1, source_target_pairs={{0,16},{4,20},{8,24},{12,28},{16,0},{20,4},{24,8},{28,12},{1,17},{... | collective-permute-start | bytes 12296 | tf_op jit(solution)/shard_map/ppermute | solution.py:464
  165.9 4.5 %collective-permute-start.54 = (f32[8,128]{1,0:T(8,128)S(1)}, f32[8,128]{1,0:T(8,128)S(1)}, u32[]{:S(2)}, u32[]{:S(2)}) collective-permute-start(f32[8,128]{1,0:T(8,128)S(1)} %add.120), channel_id=1, source_target_pairs={{0,24},{4,28},{8,16},{12,20},{16,8},{20,12},{24,0},{28,4},{1,25},{... | collective-permute-start | bytes 12296 | tf_op jit(solution)/shard_map/ppermute | solution.py:464
  174.0 4.4 %collective-permute-start.56 = (f32[136,128]{1,0:T(8,128)S(1)}, f32[136,128]{1,0:T(8,128)S(1)}, u32[]{:S(2)}, u32[]{:S(2)}) collective-permute-start(f32[136,128]{1,0:T(8,128)S(1)} %maximum_select_fusion.1), channel_id=1, source_target_pairs={{0,8},{4,12},{8,0},{12,4},{16,24},{20,28},{24,16},{28,20},{1,9},{5... | collective-permute-start | bytes 208904 | tf_op jit(solution)/shard_map/ppermute | solution.py:464
  175.3 5.1 %collective-permute-start.57 = (f32[136,128]{1,0:T(8,128)S(1)}, f32[136,128]{1,0:T(8,128)S(1)}, u32[]{:S(2)}, u32[]{:S(2)}) collective-permute-start(f32[136,128]{1,0:T(8,128)S(1)} %maximum_select_fusion.1), channel_id=1, source_target_pairs={{0,16},{4,20},{8,24},{12,28},{16,0},{20,4},{24,8},{28,12},{1,17},{... | collective-permute-start | bytes 208904 | tf_op jit(solution)/shard_map/ppermute | solution.py:464
  176.1 5.2 %collective-permute-start.58 = (f32[136,128]{1,0:T(8,128)S(1)}, f32[136,128]{1,0:T(8,128)S(1)}, u32[]{:S(2)}, u32[]{:S(2)}) collective-permute-start(f32[136,128]{1,0:T(8,128)S(1)} %maximum_select_fusion.1), channel_id=1, source_target_pairs={{0,24},{4,28},{8,16},{12,20},{16,8},{20,12},{24,0},{28,4},{1,25},{... | collective-permute-start | bytes 208904 | tf_op jit(solution)/shard_map/ppermute | solution.py:464
  182.7 4.4 %collective-permute-start.60 = (f32[8,128]{1,0:T(8,128)S(1)}, f32[8,128]{1,0:T(8,128)S(1)}, u32[]{:S(2)}, u32[]{:S(2)}) collective-permute-start(f32[8,128]{1,0:T(8,128)S(1)} %max.28), channel_id=1, source_target_pairs={{0,1},{1,0},{2,3},{3,2},{4,5},{5,4},{6,7},{7,6},{8,9},{9,8},{10,11... | collective-permute-start | bytes 12296 | tf_op jit(solution)/shard_map/ppermute | solution.py:464
  184.1 4.5 %collective-permute-start.61 = (f32[8,128]{1,0:T(8,128)S(1)}, f32[8,128]{1,0:T(8,128)S(1)}, u32[]{:S(2)}, u32[]{:S(2)}) collective-permute-start(f32[8,128]{1,0:T(8,128)S(1)} %max.28), channel_id=1, source_target_pairs={{0,2},{1,3},{2,0},{3,1},{4,6},{5,7},{6,4},{7,5},{8,10},{9,11},{10,... | collective-permute-start | bytes 12296 | tf_op jit(solution)/shard_map/ppermute | solution.py:464
  184.8 5.4 %collective-permute-start.62 = (f32[8,128]{1,0:T(8,128)S(1)}, f32[8,128]{1,0:T(8,128)S(1)}, u32[]{:S(2)}, u32[]{:S(2)}) collective-permute-start(f32[8,128]{1,0:T(8,128)S(1)} %max.28), channel_id=1, source_target_pairs={{0,3},{1,2},{2,1},{3,0},{4,7},{5,6},{6,5},{7,4},{8,11},{9,10},{10,... | collective-permute-start | bytes 12296 | tf_op jit(solution)/shard_map/ppermute | solution.py:464
  (21 other events, 172.6 us)

commit v6 on v5

--- a/solution.py
+++ b/solution.py
@@ -17,7 +17,7 @@
 BF16 = jnp.bfloat16
 LANES = 128
 UNROLL = 18
-IN_FLIGHT = 2
+IN_FLIGHT = 4
 LANES = 128
 TILES = 8
 VMEM_LIMIT = 24 * 1024 * 1024
@@ -225,11 +225,13 @@
     small_held, (small_sems, held_ref, sems) = refs[:5], refs[5:]
     fetched = [pltpu.make_async_copy(a, b, small_sems.at[i]) for i, (a, b) in enumerate(zip(small_refs, small_held))]
     copies = tile_copies(chunk, (a_ref, g_ref), held_ref, sems)
-    for copy in fetched + copies[:IN_FLIGHT]:
+    for copy in fetched + copies[:1]:
         copy.start()
     odd = odd_core()
     for copy in fetched:
         copy.wait()
+    for copy in copies[1:IN_FLIGHT]:
+        copy.start()
     v_in_ref, arow_ref, acol_ref, frow_ref, fcol_ref = small_held
     count = 2 * wt_ref.shape[0]
     v = turn(odd, v_in_ref[...])
@@ -242,11 +244,6 @@
     select_rows(gf_ref, turned_places(odd, places, v.shape[0]))
     forward_left(v, gf_ref, l_ref)
     finish = forward_finish(out_ref)
-    blocks = chunk // TILES
-
-    def products(step):
-        for inner in range(blocks):
-            one_block(wt_ref, l_ref, step * blocks + inner, finish)
 
     def split(step):
         wait_chunk(step, chunk, copies, a_ref, held_ref, sems)
@@ -256,15 +253,12 @@
             wt_ref[pair, at : at + LANES, :LANES] = high
             wt_ref[pair, at : at + LANES, LANES:] = low
 
-    split(0)
-
     def body(step, carry):
-        products(step - 1)
         split(step)
         return carry
 
-    lax.fori_loop(1, len(copies), body, 0)
-    products(len(copies) - 1)
+    lax.fori_loop(0, len(copies), body, 0)
+    run_tiles(wt_ref, l_ref, UNROLL, finish)
 
 
 def first_backward_kernel(n_col, ycount, acount, *refs):
@@ -605,7 +599,16 @@
     z = over_plane(join(mine, other_core(theirs)), join)
     (worst,) = call(residual_kernel, "residuals", [small], (z, primal_half, diag, linear))
     worst = jnp.maximum(worst, other_core(worst))
-    worst = tree(exchange(worst, "col", n_col, range(1, n_col)), jnp.maximum)
+    if n_col == 4:
+        def ask(even, odd):
+            at = [(r, c) for r in range(n_row) for c in range(n_col)]
+            pairs = [(r * n_col + c, r * n_col + (c ^ (odd if r % 2 else even))) for r, c in at]
+            return lax.ppermute(worst, ("row", "col"), pairs)
+
+        worst = tree((worst, ask(1, 2), ask(3, 3), worst), jnp.maximum)
+        worst = jnp.maximum(worst, other_core(worst))
+    else:
+        worst = tree(exchange(worst, "col", n_col, range(1, n_col)), jnp.maximum)
     return (primal_next, slack_next, dual_next, jnp.max(worst[:4]), jnp.max(worst[4:]))
 
 

time: 191 us -> 191 us (level)
    ppermute x63 -> x61, starting transfers between devices: 65.9 us -> 61.5 us  [swap(): return lax.ppermute(x, axis, [(i, i ^ distance) for i in range(size)])]
    ppermute x0 -> x2, waiting for transfers between devices: none -> 3.64 us  [ask(): return lax.ppermute(worst, ('row', 'col'), pairs)]
    ppermute x0 -> x2, starting transfers between devices: none -> 3.18 us  [ask(): return lax.ppermute(worst, ('row', 'col'), pairs)]
    ppermute x63 -> x61, waiting for transfers between devices: 86.3 us -> 84.3 us  [swap(): return lax.ppermute(x, axis, [(i, i ^ distance) for i in range(size)])]
  transfers between devices with their start and end apart: 63 -> 63, of which waited for: 53 -> 54; matrix products, arithmetic and copies ran while one was open for 0% -> 0% of each run, Pallas kernels for 2% -> 2%
where the time goes in v6:
time: 191 us
  waiting for transfers between devices  87.9 us (46%)
  starting transfers between devices  64.7 us (34%)
  Pallas kernels  35.8 us (19%)
    ppermute x61, waiting for transfers between devices, swap(): return lax.ppermute(x, axis, [(i, i ^ distance) for i in range(size)])  84.3 us
    ppermute x61, starting transfers between devices, swap(): return lax.ppermute(x, axis, [(i, i ^ distance) for i in range(size)])  61.5 us
    pallas_call x17, Pallas kernels, call(): pl.pallas_call(kernel, out_shape=shapes, in_specs=specs, out_specs=tuple(...  35.8 us
  transfers between devices with their start and end apart: 63, of which 54 were waited for; matrix products, arithmetic and copies ran while one was open for 0% of the time, Pallas kernels for 2%

profile of v6, /device:TPU:0, one launch (start us, length us, event | category | flops | bytes accessed | tf_op | source)
XLA Modules:
  0.0 191.0 jit_solution(5274515474270029176)
XLA Ops:
  1.3 6.4 %first_forward.1 = (bf16[72,256,256]{2,1,0:T(8,128)(2,1)S(1)}, f32[152,128]{1,0:T(8,128)S(1)}, f32[256,128]{1,0:T(8,128)S(1)}, bf16[144,256]{1,0:T(8,128)(2,1)S(1)}) custom-call(f32[1]{0:T(128)} %bitcast.7.rho_ref, f32[96,128,128]{2,1,0:T(8,128)} %bitcast.16, f32[48,128,128]{2,1,0:T(8,128)} %bitcast.18, f32[256,128]{1,0:T(8,128)} %refs_2_.1, ...), custom_call_target="tpu_custom_call" | custom-call | tf_op jit(solution)/shard_map/first_forward/pallas_call | solution.py:445
  7.7 4.1 %collective-permute-start = (f32[152,128]{1,0:T(8,128)S(1)}, f32[152,128]{1,0:T(8,128)S(1)}, u32[]{:S(2)}, u32[]{:S(2)}) collective-permute-start(f32[152,128]{1,0:T(8,128)S(1)} %get-tuple-element.91.refs_1_), channel_id=1, source_target_pairs={{0,2},{1,3},{2,0},{3,1},{4,6},{5,7},{6,4},{7,5},{8,10},{9,11},{10,... | collective-permute-start | bytes 233480 | tf_op jit(solution)/shard_map/ppermute | solution.py:458
  11.9 1.6 collective-permute-start.1
  13.5 4.4 %split.1 = (bf16[72,256,256]{2,1,0:T(8,128)(2,1)S(1)}, f32[144,128]{1,0:T(8,128)S(1)}) custom-call(f32[96,128,128]{2,1,0:T(8,128)} %bitcast.17, f32[48,128,128]{2,1,0:T(8,128)} %bitcast.19), custom_call_target="tpu_custom_call" | custom-call | flops 18874368 | bytes 9437184 | tf_op jit(solution)/shard_map/split/pallas_call | solution.py:445
  17.8 1.8 collective-permute-done.2.refs_4_
  19.6 2.1 %first_backward.1 = (f32[256,128]{1,0:T(8,128)S(1)}, f32[256,128]{1,0:T(8,128)S(1)}, f32[256,128]{1,0:T(8,128)S(1)}, bf16[4,256,144]{2,1,0:T(8,128)(2,1)S(1)}, b...) custom-call(f32[1]{0:T(128)} %bitcast.8.refs_0_, f32[152,128]{1,0:T(8,128)S(1)} %get-tuple-element.91.refs_1_, ...), custom_call_target="tpu_custom_call" | custom-call | tf_op jit(solution)/shard_map/first_backward/pallas_call | solution.py:445
  26.7 2.5 %collective-permute-done.4 = f32[256,128]{1,0:T(8,128)S(1)} collective-permute-done((f32[256,128]{1,0:T(8,128)S(1)}, f32[256,128]{1,0:T(8,128)S(1)}, u32[]{:S(2)}, u32[]{:S(2)}) %collective-permute-start.4) | collective-permute-done | bytes 131104 | tf_op jit(solution)/shard_map/ppermute | solution.py:458
  29.2 3.6 %collective-permute-done.5 = f32[256,128]{1,0:T(8,128)S(1)} collective-permute-done((f32[256,128]{1,0:T(8,128)S(1)}, f32[256,128]{1,0:T(8,128)S(1)}, u32[]{:S(2)}, u32[]{:S(2)}) %collective-permute-start.5) | collective-permute-done | bytes 131104 | tf_op jit(solution)/shard_map/ppermute | solution.py:458
  34.2 1.6 second_forward.1
  35.8 2.1 %collective-permute-start.10 = (f32[152,128]{1,0:T(8,128)S(1)}, f32[152,128]{1,0:T(8,128)S(1)}, u32[]{:S(2)}, u32[]{:S(2)}) collective-permute-start(f32[152,128]{1,0:T(8,128)S(1)} %get-tuple-element.101.refs_1_), channel_id=1, source_target_pairs={{0,3},{1,2},{2,1},{3,0},{4,7},{5,6},{6,5},{7,4},{8,11},{9,10},{10,... | collective-permute-start | bytes 233480 | tf_op jit(solution)/shard_map/ppermute | solution.py:458
  38.1 2.1 %collective-permute-start.9 = (f32[152,128]{1,0:T(8,128)S(1)}, f32[152,128]{1,0:T(8,128)S(1)}, u32[]{:S(2)}, u32[]{:S(2)}) collective-permute-start(f32[152,128]{1,0:T(8,128)S(1)} %get-tuple-element.101.refs_1_), channel_id=1, source_target_pairs={{0,1},{1,0},{2,3},{3,2},{4,5},{5,4},{6,7},{7,6},{8,9},{9,8},{10,11... | collective-permute-start | bytes 233480 | tf_op jit(solution)/shard_map/ppermute | solution.py:458
  40.2 2.6 %collective-permute-done.10.refs_4_ = f32[152,128]{1,0:T(8,128)S(1)} collective-permute-done((f32[152,128]{1,0:T(8,128)S(1)}, f32[152,128]{1,0:T(8,128)S(1)}, u32[]{:S(2)}, u32[]{:S(2)}) %collective-permute-start.10) | collective-permute-done | bytes 77856 | tf_op jit(solution)/shard_map/ppermute | solution.py:458
  42.8 2.9 %collective-permute-done.8.refs_2_ = f32[152,128]{1,0:T(8,128)S(1)} collective-permute-done((f32[152,128]{1,0:T(8,128)S(1)}, f32[152,128]{1,0:T(8,128)S(1)}, u32[]{:S(2)}, u32[]{:S(2)}) %collective-permute-start.8) | collective-permute-done | bytes 77856 | tf_op jit(solution)/shard_map/ppermute | solution.py:458
  45.7 2.0 %backward.5 = (f32[136,128]{1,0:T(8,128)S(1)}, f32[136,128]{1,0:T(8,128)S(1)}, f32[256,128]{1,0:T(8,128)S(1)}, f32[256,128]{1,0:T(8,128)S(1)}, f32[8,128]{1,0:T(8,128)S(1)}) custom-call(f32[1]{0:T(128)} %bitcast.9.refs_0_, f32[152,128]{1,0:T(8,128)S(1)} %get-tuple-element.101.refs_1_, f32[152,128]{1,0:T(8,128)S(1)} %collective-permute-done.8.refs_2_, ...), custom_call_target="tpu_custom_call" | custom-call | tf_op jit(solution)/shard_map/backward/pallas_call | solution.py:445
  53.4 2.0 %collective-permute-done.13 = f32[136,128]{1,0:T(8,128)S(1)} collective-permute-done((f32[136,128]{1,0:T(8,128)S(1)}, f32[136,128]{1,0:T(8,128)S(1)}, u32[]{:S(2)}, u32[]{:S(2)}) %collective-permute-start.13) | collective-permute-done | bytes 69664 | tf_op jit(solution)/shard_map/ppermute | solution.py:458
  57.7 1.7 forward.5
  60.4 2.3 %collective-permute-start.17 = (f32[152,128]{1,0:T(8,128)S(1)}, f32[152,128]{1,0:T(8,128)S(1)}, u32[]{:S(2)}, u32[]{:S(2)}) collective-permute-start(f32[152,128]{1,0:T(8,128)S(1)} %get-tuple-element.113.refs_1_), channel_id=1, source_target_pairs={{0,1},{1,0},{2,3},{3,2},{4,5},{5,4},{6,7},{7,6},{8,9},{9,8},{10,11... | collective-permute-start | bytes 233480 | tf_op jit(solution)/shard_map/ppermute | solution.py:458
  63.9 2.7 %collective-permute-done.16.refs_2_ = f32[152,128]{1,0:T(8,128)S(1)} collective-permute-done((f32[152,128]{1,0:T(8,128)S(1)}, f32[152,128]{1,0:T(8,128)S(1)}, u32[]{:S(2)}, u32[]{:S(2)}) %collective-permute-start.16) | collective-permute-done | bytes 77856 | tf_op jit(solution)/shard_map/ppermute | solution.py:458
  66.7 2.1 %collective-permute-done.18.refs_4_ = f32[152,128]{1,0:T(8,128)S(1)} collective-permute-done((f32[152,128]{1,0:T(8,128)S(1)}, f32[152,128]{1,0:T(8,128)S(1)}, u32[]{:S(2)}, u32[]{:S(2)}) %collective-permute-start.18) | collective-permute-done | bytes 77856 | tf_op jit(solution)/shard_map/ppermute | solution.py:458
  68.9 2.0 %backward.6 = (f32[136,128]{1,0:T(8,128)S(1)}, f32[136,128]{1,0:T(8,128)S(1)}, f32[256,128]{1,0:T(8,128)S(1)}, f32[256,128]{1,0:T(8,128)S(1)}, f32[8,128]{1,0:T(8,128)S(1)}) custom-call(f32[1]{0:T(128)} %bitcast.10.refs_0_, f32[152,128]{1,0:T(8,128)S(1)} %get-tuple-element.113.refs_1_, f32[152,128]{1,0:T(8,128)S(1)} %collective-permute-done.16.refs_2_, ...), custom_call_target="tpu_custom_call" | custom-call | tf_op jit(solution)/shard_map/backward/pallas_call | solution.py:445
  72.2 1.6 collective-permute-start.20
  76.6 2.2 %collective-permute-done.21 = f32[136,128]{1,0:T(8,128)S(1)} collective-permute-done((f32[136,128]{1,0:T(8,128)S(1)}, f32[136,128]{1,0:T(8,128)S(1)}, u32[]{:S(2)}, u32[]{:S(2)}) %collective-permute-start.21) | collective-permute-done | bytes 69664 | tf_op jit(solution)/shard_map/ppermute | solution.py:458
  80.9 1.7 forward.6
  82.6 1.8 collective-permute-start.24
  84.7 2.3 %collective-permute-start.26 = (f32[152,128]{1,0:T(8,128)S(1)}, f32[152,128]{1,0:T(8,128)S(1)}, u32[]{:S(2)}, u32[]{:S(2)}) collective-permute-start(f32[152,128]{1,0:T(8,128)S(1)} %get-tuple-element.124.refs_1_), channel_id=1, source_target_pairs={{0,3},{1,2},{2,1},{3,0},{4,7},{5,6},{6,5},{7,4},{8,11},{9,10},{10,... | collective-permute-start | bytes 233480 | tf_op jit(solution)/shard_map/ppermute | solution.py:458
  87.0 3.6 %collective-permute-done.24.refs_2_ = f32[152,128]{1,0:T(8,128)S(1)} collective-permute-done((f32[152,128]{1,0:T(8,128)S(1)}, f32[152,128]{1,0:T(8,128)S(1)}, u32[]{:S(2)}, u32[]{:S(2)}) %collective-permute-start.24) | collective-permute-done | bytes 77856 | tf_op jit(solution)/shard_map/ppermute | solution.py:458
  90.7 1.6 collective-permute-done.26.refs_4_
  92.3 2.2 %backward.7 = (f32[136,128]{1,0:T(8,128)S(1)}, f32[136,128]{1,0:T(8,128)S(1)}, f32[256,128]{1,0:T(8,128)S(1)}, f32[256,128]{1,0:T(8,128)S(1)}, f32[8,128]{1,0:T(8,128)S(1)}) custom-call(f32[1]{0:T(128)} %bitcast.11.refs_0_, f32[152,128]{1,0:T(8,128)S(1)} %get-tuple-element.124.refs_1_, f32[152,128]{1,0:T(8,128)S(1)} %collective-permute-done.24.refs_2_, ...), custom_call_target="tpu_custom_call" | custom-call | tf_op jit(solution)/shard_map/backward/pallas_call | solution.py:445
  100.2 1.9 collective-permute-done.29
  104.4 1.7 forward.7
  108.5 2.1 %collective-permute-start.34 = (f32[152,128]{1,0:T(8,128)S(1)}, f32[152,128]{1,0:T(8,128)S(1)}, u32[]{:S(2)}, u32[]{:S(2)}) collective-permute-start(f32[152,128]{1,0:T(8,128)S(1)} %get-tuple-element.135.refs_1_), channel_id=1, source_target_pairs={{0,3},{1,2},{2,1},{3,0},{4,7},{5,6},{6,5},{7,4},{8,11},{9,10},{10,... | collective-permute-start | bytes 233480 | tf_op jit(solution)/shard_map/ppermute | solution.py:458
  110.5 5.1 %collective-permute-done.32.refs_2_ = f32[152,128]{1,0:T(8,128)S(1)} collective-permute-done((f32[152,128]{1,0:T(8,128)S(1)}, f32[152,128]{1,0:T(8,128)S(1)}, u32[]{:S(2)}, u32[]{:S(2)}) %collective-permute-start.32) | collective-permute-done | bytes 77856 | tf_op jit(solution)/shard_map/ppermute | solution.py:458
  115.6 2.0 %backward.8 = (f32[136,128]{1,0:T(8,128)S(1)}, f32[136,128]{1,0:T(8,128)S(1)}, f32[256,128]{1,0:T(8,128)S(1)}, f32[256,128]{1,0:T(8,128)S(1)}, f32[8,128]{1,0:T(8,128)S(1)}) custom-call(f32[1]{0:T(128)} %bitcast.12.refs_0_, f32[152,128]{1,0:T(8,128)S(1)} %get-tuple-element.135.refs_1_, f32[152,128]{1,0:T(8,128)S(1)} %collective-permute-done.32.refs_2_, ...), custom_call_target="tpu_custom_call" | custom-call | tf_op jit(solution)/shard_map/backward/pallas_call | solution.py:445
  119.0 1.6 collective-permute-start.36
  123.3 2.2 %collective-permute-done.37 = f32[136,128]{1,0:T(8,128)S(1)} collective-permute-done((f32[136,128]{1,0:T(8,128)S(1)}, f32[136,128]{1,0:T(8,128)S(1)}, u32[]{:S(2)}, u32[]{:S(2)}) %collective-permute-start.37) | collective-permute-done | bytes 69664 | tf_op jit(solution)/shard_map/ppermute | solution.py:458
  127.7 1.7 forward.8
  129.4 1.7 collective-permute-start.40
  131.4 2.3 %collective-permute-start.42 = (f32[152,128]{1,0:T(8,128)S(1)}, f32[152,128]{1,0:T(8,128)S(1)}, u32[]{:S(2)}, u32[]{:S(2)}) collective-permute-start(f32[152,128]{1,0:T(8,128)S(1)} %get-tuple-element.146.refs_1_), channel_id=1, source_target_pairs={{0,3},{1,2},{2,1},{3,0},{4,7},{5,6},{6,5},{7,4},{8,11},{9,10},{10,... | collective-permute-start | bytes 233480 | tf_op jit(solution)/shard_map/ppermute | solution.py:458
  133.8 3.9 %collective-permute-done.40.refs_2_ = f32[152,128]{1,0:T(8,128)S(1)} collective-permute-done((f32[152,128]{1,0:T(8,128)S(1)}, f32[152,128]{1,0:T(8,128)S(1)}, u32[]{:S(2)}, u32[]{:S(2)}) %collective-permute-start.40) | collective-permute-done | bytes 77856 | tf_op jit(solution)/shard_map/ppermute | solution.py:458
  138.9 2.0 %backward.9 = (f32[136,128]{1,0:T(8,128)S(1)}, f32[136,128]{1,0:T(8,128)S(1)}, f32[256,128]{1,0:T(8,128)S(1)}, f32[256,128]{1,0:T(8,128)S(1)}, f32[8,128]{1,0:T(8,128)S(1)}) custom-call(f32[1]{0:T(128)} %bitcast.13.refs_0_, f32[152,128]{1,0:T(8,128)S(1)} %get-tuple-element.146.refs_1_, f32[152,128]{1,0:T(8,128)S(1)} %collective-permute-done.40.refs_2_, ...), custom_call_target="tpu_custom_call" | custom-call | tf_op jit(solution)/shard_map/backward/pallas_call | solution.py:445
  146.6 1.9 collective-permute-done.45
  150.8 1.7 forward.9
  154.9 2.1 %collective-permute-start.50 = (f32[152,128]{1,0:T(8,128)S(1)}, f32[152,128]{1,0:T(8,128)S(1)}, u32[]{:S(2)}, u32[]{:S(2)}) collective-permute-start(f32[152,128]{1,0:T(8,128)S(1)} %get-tuple-element.157.refs_1_), channel_id=1, source_target_pairs={{0,3},{1,2},{2,1},{3,0},{4,7},{5,6},{6,5},{7,4},{8,11},{9,10},{10,... | collective-permute-start | bytes 233480 | tf_op jit(solution)/shard_map/ppermute | solution.py:458
  157.0 4.1 %collective-permute-done.48.refs_2_ = f32[152,128]{1,0:T(8,128)S(1)} collective-permute-done((f32[152,128]{1,0:T(8,128)S(1)}, f32[152,128]{1,0:T(8,128)S(1)}, u32[]{:S(2)}, u32[]{:S(2)}) %collective-permute-start.48) | collective-permute-done | bytes 77856 | tf_op jit(solution)/shard_map/ppermute | solution.py:458
  170.2 2.3 %final.1 = (f32[256,128]{1,0:T(8,128)}, f32[128,128]{1,0:T(8,128)S(1)}, f32[192,128]{1,0:T(8,128)}, f32[192,128]{1,0:T(8,128)}, f32[136,128]{1,0:T(8,128)S(1)}, /*index=5*/f32[136,128]{1,0:T(8,128)S(1)}) custom-call(f32[1]{0:T(128)} %bitcast.15.refs_0_, f32[8,128]{1,0:T(8,128)S(1)} %add_add_fusion.6.refs_1_, f32[256,128]{1,0:T(8,128)S(1)} %get-tuple-element.162.refs_2_, ...), custom_call_target="tpu_custom_call" | custom-call | tf_op jit(solution)/shard_map/final/pallas_call | solution.py:445
  178.2 1.9 collective-permute-done.57
  183.9 1.8 collective-permute-start.61
  186.0 3.2 %collective-permute-done.61 = f32[8,128]{1,0:T(8,128)S(1)} collective-permute-done((f32[8,128]{1,0:T(8,128)S(1)}, f32[8,128]{1,0:T(8,128)S(1)}, u32[]{:S(2)}, u32[]{:S(2)}) %collective-permute-start.61) | collective-permute-done | bytes 4128 | tf_op jit(solution)/shard_map/ppermute | solution.py:606
  (128 shorter events, 72.7 us)
Async XLA Ops:
  7.7 10.1 %collective-permute-start = (f32[152,128]{1,0:T(8,128)S(1)}, f32[152,128]{1,0:T(8,128)S(1)}, u32[]{:S(2)}, u32[]{:S(2)}) collective-permute-start(f32[152,128]{1,0:T(8,128)S(1)} %get-tuple-element.91.refs_1_), channel_id=1, source_target_pairs={{0,2},{1,3},{2,0},{3,1},{4,6},{5,7},{6,4},{7,5},{8,10},{9,11},{10,... | collective-permute-start | bytes 233480 | tf_op jit(solution)/shard_map/ppermute | solution.py:458
  11.9 6.0 %collective-permute-start.1 = (f32[152,128]{1,0:T(8,128)S(1)}, f32[152,128]{1,0:T(8,128)S(1)}, u32[]{:S(2)}, u32[]{:S(2)}) collective-permute-start(f32[152,128]{1,0:T(8,128)S(1)} %get-tuple-element.91.refs_1_), channel_id=1, source_target_pairs={{0,1},{1,0},{2,3},{3,2},{4,5},{5,4},{6,7},{7,6},{8,9},{9,8},{10,11... | collective-permute-start | bytes 233480 | tf_op jit(solution)/shard_map/ppermute | solution.py:458
  13.4 6.2 %collective-permute-start.2 = (f32[152,128]{1,0:T(8,128)S(1)}, f32[152,128]{1,0:T(8,128)S(1)}, u32[]{:S(2)}, u32[]{:S(2)}) collective-permute-start(f32[152,128]{1,0:T(8,128)S(1)} %get-tuple-element.91.refs_1_), channel_id=1, source_target_pairs={{0,3},{1,2},{2,1},{3,0},{4,7},{5,6},{6,5},{7,4},{8,11},{9,10},{10,... | collective-permute-start | bytes 233480 | tf_op jit(solution)/shard_map/ppermute | solution.py:458
  21.7 1.4 collective-permute-start.3
  23.1 6.0 %collective-permute-start.4 = (f32[256,128]{1,0:T(8,128)S(1)}, f32[256,128]{1,0:T(8,128)S(1)}, u32[]{:S(2)}, u32[]{:S(2)}) collective-permute-start(f32[256,128]{1,0:T(8,128)S(1)} %add.96), channel_id=1, source_target_pairs={{0,8},{4,12},{8,0},{12,4},{16,24},{20,28},{24,16},{28,20},{1,9},{5... | collective-permute-start | bytes 393224 | tf_op jit(solution)/shard_map/ppermute | solution.py:458
  24.7 8.1 %collective-permute-start.5 = (f32[256,128]{1,0:T(8,128)S(1)}, f32[256,128]{1,0:T(8,128)S(1)}, u32[]{:S(2)}, u32[]{:S(2)}) collective-permute-start(f32[256,128]{1,0:T(8,128)S(1)} %add.96), channel_id=1, source_target_pairs={{0,16},{4,20},{8,24},{12,28},{16,0},{20,4},{24,8},{28,12},{1,17},{... | collective-permute-start | bytes 393224 | tf_op jit(solution)/shard_map/ppermute | solution.py:458
  26.2 6.6 %collective-permute-start.6 = (f32[256,128]{1,0:T(8,128)S(1)}, f32[256,128]{1,0:T(8,128)S(1)}, u32[]{:S(2)}, u32[]{:S(2)}) collective-permute-start(f32[256,128]{1,0:T(8,128)S(1)} %add.96), channel_id=1, source_target_pairs={{0,24},{4,28},{8,16},{12,20},{16,8},{20,12},{24,0},{28,4},{1,25},{... | collective-permute-start | bytes 393224 | tf_op jit(solution)/shard_map/ppermute | solution.py:458
  35.8 7.0 %collective-permute-start.10 = (f32[152,128]{1,0:T(8,128)S(1)}, f32[152,128]{1,0:T(8,128)S(1)}, u32[]{:S(2)}, u32[]{:S(2)}) collective-permute-start(f32[152,128]{1,0:T(8,128)S(1)} %get-tuple-element.101.refs_1_), channel_id=1, source_target_pairs={{0,3},{1,2},{2,1},{3,0},{4,7},{5,6},{6,5},{7,4},{8,11},{9,10},{10,... | collective-permute-start | bytes 233480 | tf_op jit(solution)/shard_map/ppermute | solution.py:458
  37.9 7.8 %collective-permute-start.8 = (f32[152,128]{1,0:T(8,128)S(1)}, f32[152,128]{1,0:T(8,128)S(1)}, u32[]{:S(2)}, u32[]{:S(2)}) collective-permute-start(f32[152,128]{1,0:T(8,128)S(1)} %get-tuple-element.101.refs_1_), channel_id=1, source_target_pairs={{0,2},{1,3},{2,0},{3,1},{4,6},{5,7},{6,4},{7,5},{8,10},{9,11},{10,... | collective-permute-start | bytes 233480 | tf_op jit(solution)/shard_map/ppermute | solution.py:458
  38.1 7.6 %collective-permute-start.9 = (f32[152,128]{1,0:T(8,128)S(1)}, f32[152,128]{1,0:T(8,128)S(1)}, u32[]{:S(2)}, u32[]{:S(2)}) collective-permute-start(f32[152,128]{1,0:T(8,128)S(1)} %get-tuple-element.101.refs_1_), channel_id=1, source_target_pairs={{0,1},{1,0},{2,3},{3,2},{4,5},{5,4},{6,7},{7,6},{8,9},{9,8},{10,11... | collective-permute-start | bytes 233480 | tf_op jit(solution)/shard_map/ppermute | solution.py:458
  49.1 4.4 %collective-permute-start.12 = (f32[136,128]{1,0:T(8,128)S(1)}, f32[136,128]{1,0:T(8,128)S(1)}, u32[]{:S(2)}, u32[]{:S(2)}) collective-permute-start(f32[136,128]{1,0:T(8,128)S(1)} %add.100), channel_id=1, source_target_pairs={{0,8},{4,12},{8,0},{12,4},{16,24},{20,28},{24,16},{28,20},{1,9},{5... | collective-permute-start | bytes 208904 | tf_op jit(solution)/shard_map/ppermute | solution.py:458
  50.3 5.1 %collective-permute-start.13 = (f32[136,128]{1,0:T(8,128)S(1)}, f32[136,128]{1,0:T(8,128)S(1)}, u32[]{:S(2)}, u32[]{:S(2)}) collective-permute-start(f32[136,128]{1,0:T(8,128)S(1)} %add.100), channel_id=1, source_target_pairs={{0,16},{4,20},{8,24},{12,28},{16,0},{20,4},{24,8},{28,12},{1,17},{... | collective-permute-start | bytes 208904 | tf_op jit(solution)/shard_map/ppermute | solution.py:458
  51.2 5.2 %collective-permute-start.14 = (f32[136,128]{1,0:T(8,128)S(1)}, f32[136,128]{1,0:T(8,128)S(1)}, u32[]{:S(2)}, u32[]{:S(2)}) collective-permute-start(f32[136,128]{1,0:T(8,128)S(1)} %add.100), channel_id=1, source_target_pairs={{0,24},{4,28},{8,16},{12,20},{16,8},{20,12},{24,0},{28,4},{1,25},{... | collective-permute-start | bytes 208904 | tf_op jit(solution)/shard_map/ppermute | solution.py:458
  59.5 7.1 %collective-permute-start.16 = (f32[152,128]{1,0:T(8,128)S(1)}, f32[152,128]{1,0:T(8,128)S(1)}, u32[]{:S(2)}, u32[]{:S(2)}) collective-permute-start(f32[152,128]{1,0:T(8,128)S(1)} %get-tuple-element.113.refs_1_), channel_id=1, source_target_pairs={{0,2},{1,3},{2,0},{3,1},{4,6},{5,7},{6,4},{7,5},{8,10},{9,11},{10,... | collective-permute-start | bytes 233480 | tf_op jit(solution)/shard_map/ppermute | solution.py:458
  60.4 6.4 %collective-permute-start.17 = (f32[152,128]{1,0:T(8,128)S(1)}, f32[152,128]{1,0:T(8,128)S(1)}, u32[]{:S(2)}, u32[]{:S(2)}) collective-permute-start(f32[152,128]{1,0:T(8,128)S(1)} %get-tuple-element.113.refs_1_), channel_id=1, source_target_pairs={{0,1},{1,0},{2,3},{3,2},{4,5},{5,4},{6,7},{7,6},{8,9},{9,8},{10,11... | collective-permute-start | bytes 233480 | tf_op jit(solution)/shard_map/ppermute | solution.py:458
  62.7 6.2 %collective-permute-start.18 = (f32[152,128]{1,0:T(8,128)S(1)}, f32[152,128]{1,0:T(8,128)S(1)}, u32[]{:S(2)}, u32[]{:S(2)}) collective-permute-start(f32[152,128]{1,0:T(8,128)S(1)} %get-tuple-element.113.refs_1_), channel_id=1, source_target_pairs={{0,3},{1,2},{2,1},{3,0},{4,7},{5,6},{6,5},{7,4},{8,11},{9,10},{10,... | collective-permute-start | bytes 233480 | tf_op jit(solution)/shard_map/ppermute | solution.py:458
  72.2 4.4 %collective-permute-start.20 = (f32[136,128]{1,0:T(8,128)S(1)}, f32[136,128]{1,0:T(8,128)S(1)}, u32[]{:S(2)}, u32[]{:S(2)}) collective-permute-start(f32[136,128]{1,0:T(8,128)S(1)} %add.104), channel_id=1, source_target_pairs={{0,8},{4,12},{8,0},{12,4},{16,24},{20,28},{24,16},{28,20},{1,9},{5... | collective-permute-start | bytes 208904 | tf_op jit(solution)/shard_map/ppermute | solution.py:458
  73.8 5.1 %collective-permute-start.21 = (f32[136,128]{1,0:T(8,128)S(1)}, f32[136,128]{1,0:T(8,128)S(1)}, u32[]{:S(2)}, u32[]{:S(2)}) collective-permute-start(f32[136,128]{1,0:T(8,128)S(1)} %add.104), channel_id=1, source_target_pairs={{0,16},{4,20},{8,24},{12,28},{16,0},{20,4},{24,8},{28,12},{1,17},{... | collective-permute-start | bytes 208904 | tf_op jit(solution)/shard_map/ppermute | solution.py:458
  74.4 5.2 %collective-permute-start.22 = (f32[136,128]{1,0:T(8,128)S(1)}, f32[136,128]{1,0:T(8,128)S(1)}, u32[]{:S(2)}, u32[]{:S(2)}) collective-permute-start(f32[136,128]{1,0:T(8,128)S(1)} %add.104), channel_id=1, source_target_pairs={{0,24},{4,28},{8,16},{12,20},{16,8},{20,12},{24,0},{28,4},{1,25},{... | collective-permute-start | bytes 208904 | tf_op jit(solution)/shard_map/ppermute | solution.py:458
  82.6 8.1 %collective-permute-start.24 = (f32[152,128]{1,0:T(8,128)S(1)}, f32[152,128]{1,0:T(8,128)S(1)}, u32[]{:S(2)}, u32[]{:S(2)}) collective-permute-start(f32[152,128]{1,0:T(8,128)S(1)} %get-tuple-element.124.refs_1_), channel_id=1, source_target_pairs={{0,2},{1,3},{2,0},{3,1},{4,6},{5,7},{6,4},{7,5},{8,10},{9,11},{10,... | collective-permute-start | bytes 233480 | tf_op jit(solution)/shard_map/ppermute | solution.py:458
  84.5 6.2 %collective-permute-start.25 = (f32[152,128]{1,0:T(8,128)S(1)}, f32[152,128]{1,0:T(8,128)S(1)}, u32[]{:S(2)}, u32[]{:S(2)}) collective-permute-start(f32[152,128]{1,0:T(8,128)S(1)} %get-tuple-element.124.refs_1_), channel_id=1, source_target_pairs={{0,1},{1,0},{2,3},{3,2},{4,5},{5,4},{6,7},{7,6},{8,9},{9,8},{10,11... | collective-permute-start | bytes 233480 | tf_op jit(solution)/shard_map/ppermute | solution.py:458
  84.7 7.6 %collective-permute-start.26 = (f32[152,128]{1,0:T(8,128)S(1)}, f32[152,128]{1,0:T(8,128)S(1)}, u32[]{:S(2)}, u32[]{:S(2)}) collective-permute-start(f32[152,128]{1,0:T(8,128)S(1)} %get-tuple-element.124.refs_1_), channel_id=1, source_target_pairs={{0,3},{1,2},{2,1},{3,0},{4,7},{5,6},{6,5},{7,4},{8,11},{9,10},{10,... | collective-permute-start | bytes 233480 | tf_op jit(solution)/shard_map/ppermute | solution.py:458
  95.8 4.4 %collective-permute-start.28 = (f32[136,128]{1,0:T(8,128)S(1)}, f32[136,128]{1,0:T(8,128)S(1)}, u32[]{:S(2)}, u32[]{:S(2)}) collective-permute-start(f32[136,128]{1,0:T(8,128)S(1)} %add.108), channel_id=1, source_target_pairs={{0,8},{4,12},{8,0},{12,4},{16,24},{20,28},{24,16},{28,20},{1,9},{5... | collective-permute-start | bytes 208904 | tf_op jit(solution)/shard_map/ppermute | solution.py:458
  97.0 5.1 %collective-permute-start.29 = (f32[136,128]{1,0:T(8,128)S(1)}, f32[136,128]{1,0:T(8,128)S(1)}, u32[]{:S(2)}, u32[]{:S(2)}) collective-permute-start(f32[136,128]{1,0:T(8,128)S(1)} %add.108), channel_id=1, source_target_pairs={{0,16},{4,20},{8,24},{12,28},{16,0},{20,4},{24,8},{28,12},{1,17},{... | collective-permute-start | bytes 208904 | tf_op jit(solution)/shard_map/ppermute | solution.py:458
  97.9 5.2 %collective-permute-start.30 = (f32[136,128]{1,0:T(8,128)S(1)}, f32[136,128]{1,0:T(8,128)S(1)}, u32[]{:S(2)}, u32[]{:S(2)}) collective-permute-start(f32[136,128]{1,0:T(8,128)S(1)} %add.108), channel_id=1, source_target_pairs={{0,24},{4,28},{8,16},{12,20},{16,8},{20,12},{24,0},{28,4},{1,25},{... | collective-permute-start | bytes 208904 | tf_op jit(solution)/shard_map/ppermute | solution.py:458
  106.1 9.5 %collective-permute-start.32 = (f32[152,128]{1,0:T(8,128)S(1)}, f32[152,128]{1,0:T(8,128)S(1)}, u32[]{:S(2)}, u32[]{:S(2)}) collective-permute-start(f32[152,128]{1,0:T(8,128)S(1)} %get-tuple-element.135.refs_1_), channel_id=1, source_target_pairs={{0,2},{1,3},{2,0},{3,1},{4,6},{5,7},{6,4},{7,5},{8,10},{9,11},{10,... | collective-permute-start | bytes 233480 | tf_op jit(solution)/shard_map/ppermute | solution.py:458
  107.4 8.2 %collective-permute-start.33 = (f32[152,128]{1,0:T(8,128)S(1)}, f32[152,128]{1,0:T(8,128)S(1)}, u32[]{:S(2)}, u32[]{:S(2)}) collective-permute-start(f32[152,128]{1,0:T(8,128)S(1)} %get-tuple-element.135.refs_1_), channel_id=1, source_target_pairs={{0,1},{1,0},{2,3},{3,2},{4,5},{5,4},{6,7},{7,6},{8,9},{9,8},{10,11... | collective-permute-start | bytes 233480 | tf_op jit(solution)/shard_map/ppermute | solution.py:458
  108.5 7.1 %collective-permute-start.34 = (f32[152,128]{1,0:T(8,128)S(1)}, f32[152,128]{1,0:T(8,128)S(1)}, u32[]{:S(2)}, u32[]{:S(2)}) collective-permute-start(f32[152,128]{1,0:T(8,128)S(1)} %get-tuple-element.135.refs_1_), channel_id=1, source_target_pairs={{0,3},{1,2},{2,1},{3,0},{4,7},{5,6},{6,5},{7,4},{8,11},{9,10},{10,... | collective-permute-start | bytes 233480 | tf_op jit(solution)/shard_map/ppermute | solution.py:458
  119.0 4.4 %collective-permute-start.36 = (f32[136,128]{1,0:T(8,128)S(1)}, f32[136,128]{1,0:T(8,128)S(1)}, u32[]{:S(2)}, u32[]{:S(2)}) collective-permute-start(f32[136,128]{1,0:T(8,128)S(1)} %add.112), channel_id=1, source_target_pairs={{0,8},{4,12},{8,0},{12,4},{16,24},{20,28},{24,16},{28,20},{1,9},{5... | collective-permute-start | bytes 208904 | tf_op jit(solution)/shard_map/ppermute | solution.py:458
  120.5 5.1 %collective-permute-start.37 = (f32[136,128]{1,0:T(8,128)S(1)}, f32[136,128]{1,0:T(8,128)S(1)}, u32[]{:S(2)}, u32[]{:S(2)}) collective-permute-start(f32[136,128]{1,0:T(8,128)S(1)} %add.112), channel_id=1, source_target_pairs={{0,16},{4,20},{8,24},{12,28},{16,0},{20,4},{24,8},{28,12},{1,17},{... | collective-permute-start | bytes 208904 | tf_op jit(solution)/shard_map/ppermute | solution.py:458
  121.1 5.2 %collective-permute-start.38 = (f32[136,128]{1,0:T(8,128)S(1)}, f32[136,128]{1,0:T(8,128)S(1)}, u32[]{:S(2)}, u32[]{:S(2)}) collective-permute-start(f32[136,128]{1,0:T(8,128)S(1)} %add.112), channel_id=1, source_target_pairs={{0,24},{4,28},{8,16},{12,20},{16,8},{20,12},{24,0},{28,4},{1,25},{... | collective-permute-start | bytes 208904 | tf_op jit(solution)/shard_map/ppermute | solution.py:458
  129.4 8.4 %collective-permute-start.40 = (f32[152,128]{1,0:T(8,128)S(1)}, f32[152,128]{1,0:T(8,128)S(1)}, u32[]{:S(2)}, u32[]{:S(2)}) collective-permute-start(f32[152,128]{1,0:T(8,128)S(1)} %get-tuple-element.146.refs_1_), channel_id=1, source_target_pairs={{0,2},{1,3},{2,0},{3,1},{4,6},{5,7},{6,4},{7,5},{8,10},{9,11},{10,... | collective-permute-start | bytes 233480 | tf_op jit(solution)/shard_map/ppermute | solution.py:458
  131.1 6.6 %collective-permute-start.41 = (f32[152,128]{1,0:T(8,128)S(1)}, f32[152,128]{1,0:T(8,128)S(1)}, u32[]{:S(2)}, u32[]{:S(2)}) collective-permute-start(f32[152,128]{1,0:T(8,128)S(1)} %get-tuple-element.146.refs_1_), channel_id=1, source_target_pairs={{0,1},{1,0},{2,3},{3,2},{4,5},{5,4},{6,7},{7,6},{8,9},{9,8},{10,11... | collective-permute-start | bytes 233480 | tf_op jit(solution)/shard_map/ppermute | solution.py:458
  131.4 7.5 %collective-permute-start.42 = (f32[152,128]{1,0:T(8,128)S(1)}, f32[152,128]{1,0:T(8,128)S(1)}, u32[]{:S(2)}, u32[]{:S(2)}) collective-permute-start(f32[152,128]{1,0:T(8,128)S(1)} %get-tuple-element.146.refs_1_), channel_id=1, source_target_pairs={{0,3},{1,2},{2,1},{3,0},{4,7},{5,6},{6,5},{7,4},{8,11},{9,10},{10,... | collective-permute-start | bytes 233480 | tf_op jit(solution)/shard_map/ppermute | solution.py:458
  142.3 4.4 %collective-permute-start.44 = (f32[136,128]{1,0:T(8,128)S(1)}, f32[136,128]{1,0:T(8,128)S(1)}, u32[]{:S(2)}, u32[]{:S(2)}) collective-permute-start(f32[136,128]{1,0:T(8,128)S(1)} %add.116), channel_id=1, source_target_pairs={{0,8},{4,12},{8,0},{12,4},{16,24},{20,28},{24,16},{28,20},{1,9},{5... | collective-permute-start | bytes 208904 | tf_op jit(solution)/shard_map/ppermute | solution.py:458
  143.5 5.1 %collective-permute-start.45 = (f32[136,128]{1,0:T(8,128)S(1)}, f32[136,128]{1,0:T(8,128)S(1)}, u32[]{:S(2)}, u32[]{:S(2)}) collective-permute-start(f32[136,128]{1,0:T(8,128)S(1)} %add.116), channel_id=1, source_target_pairs={{0,16},{4,20},{8,24},{12,28},{16,0},{20,4},{24,8},{28,12},{1,17},{... | collective-permute-start | bytes 208904 | tf_op jit(solution)/shard_map/ppermute | solution.py:458
  144.3 5.2 %collective-permute-start.46 = (f32[136,128]{1,0:T(8,128)S(1)}, f32[136,128]{1,0:T(8,128)S(1)}, u32[]{:S(2)}, u32[]{:S(2)}) collective-permute-start(f32[136,128]{1,0:T(8,128)S(1)} %add.116), channel_id=1, source_target_pairs={{0,24},{4,28},{8,16},{12,20},{16,8},{20,12},{24,0},{28,4},{1,25},{... | collective-permute-start | bytes 208904 | tf_op jit(solution)/shard_map/ppermute | solution.py:458
  152.6 8.5 %collective-permute-start.48 = (f32[152,128]{1,0:T(8,128)S(1)}, f32[152,128]{1,0:T(8,128)S(1)}, u32[]{:S(2)}, u32[]{:S(2)}) collective-permute-start(f32[152,128]{1,0:T(8,128)S(1)} %get-tuple-element.157.refs_1_), channel_id=1, source_target_pairs={{0,2},{1,3},{2,0},{3,1},{4,6},{5,7},{6,4},{7,5},{8,10},{9,11},{10,... | collective-permute-start | bytes 233480 | tf_op jit(solution)/shard_map/ppermute | solution.py:458
  154.0 7.1 %collective-permute-start.49 = (f32[152,128]{1,0:T(8,128)S(1)}, f32[152,128]{1,0:T(8,128)S(1)}, u32[]{:S(2)}, u32[]{:S(2)}) collective-permute-start(f32[152,128]{1,0:T(8,128)S(1)} %get-tuple-element.157.refs_1_), channel_id=1, source_target_pairs={{0,1},{1,0},{2,3},{3,2},{4,5},{5,4},{6,7},{7,6},{8,9},{9,8},{10,11... | collective-permute-start | bytes 233480 | tf_op jit(solution)/shard_map/ppermute | solution.py:458
  154.9 7.1 %collective-permute-start.50 = (f32[152,128]{1,0:T(8,128)S(1)}, f32[152,128]{1,0:T(8,128)S(1)}, u32[]{:S(2)}, u32[]{:S(2)}) collective-permute-start(f32[152,128]{1,0:T(8,128)S(1)} %get-tuple-element.157.refs_1_), channel_id=1, source_target_pairs={{0,3},{1,2},{2,1},{3,0},{4,7},{5,6},{6,5},{7,4},{8,11},{9,10},{10,... | collective-permute-start | bytes 233480 | tf_op jit(solution)/shard_map/ppermute | solution.py:458
  163.6 3.6 %collective-permute-start.52 = (f32[8,128]{1,0:T(8,128)S(1)}, f32[8,128]{1,0:T(8,128)S(1)}, u32[]{:S(2)}, u32[]{:S(2)}) collective-permute-start(f32[8,128]{1,0:T(8,128)S(1)} %add.120), channel_id=1, source_target_pairs={{0,8},{4,12},{8,0},{12,4},{16,24},{20,28},{24,16},{28,20},{1,9},{5... | collective-permute-start | bytes 12296 | tf_op jit(solution)/shard_map/ppermute | solution.py:458
  165.1 3.6 %collective-permute-start.53 = (f32[8,128]{1,0:T(8,128)S(1)}, f32[8,128]{1,0:T(8,128)S(1)}, u32[]{:S(2)}, u32[]{:S(2)}) collective-permute-start(f32[8,128]{1,0:T(8,128)S(1)} %add.120), channel_id=1, source_target_pairs={{0,16},{4,20},{8,24},{12,28},{16,0},{20,4},{24,8},{28,12},{1,17},{... | collective-permute-start | bytes 12296 | tf_op jit(solution)/shard_map/ppermute | solution.py:458
  165.7 4.5 %collective-permute-start.54 = (f32[8,128]{1,0:T(8,128)S(1)}, f32[8,128]{1,0:T(8,128)S(1)}, u32[]{:S(2)}, u32[]{:S(2)}) collective-permute-start(f32[8,128]{1,0:T(8,128)S(1)} %add.120), channel_id=1, source_target_pairs={{0,24},{4,28},{8,16},{12,20},{16,8},{20,12},{24,0},{28,4},{1,25},{... | collective-permute-start | bytes 12296 | tf_op jit(solution)/shard_map/ppermute | solution.py:458
  173.8 4.4 %collective-permute-start.56 = (f32[136,128]{1,0:T(8,128)S(1)}, f32[136,128]{1,0:T(8,128)S(1)}, u32[]{:S(2)}, u32[]{:S(2)}) collective-permute-start(f32[136,128]{1,0:T(8,128)S(1)} %maximum_select_fusion.1), channel_id=1, source_target_pairs={{0,8},{4,12},{8,0},{12,4},{16,24},{20,28},{24,16},{28,20},{1,9},{5... | collective-permute-start | bytes 208904 | tf_op jit(solution)/shard_map/ppermute | solution.py:458
  175.0 5.1 %collective-permute-start.57 = (f32[136,128]{1,0:T(8,128)S(1)}, f32[136,128]{1,0:T(8,128)S(1)}, u32[]{:S(2)}, u32[]{:S(2)}) collective-permute-start(f32[136,128]{1,0:T(8,128)S(1)} %maximum_select_fusion.1), channel_id=1, source_target_pairs={{0,16},{4,20},{8,24},{12,28},{16,0},{20,4},{24,8},{28,12},{1,17},{... | collective-permute-start | bytes 208904 | tf_op jit(solution)/shard_map/ppermute | solution.py:458
  175.9 5.2 %collective-permute-start.58 = (f32[136,128]{1,0:T(8,128)S(1)}, f32[136,128]{1,0:T(8,128)S(1)}, u32[]{:S(2)}, u32[]{:S(2)}) collective-permute-start(f32[136,128]{1,0:T(8,128)S(1)} %maximum_select_fusion.1), channel_id=1, source_target_pairs={{0,24},{4,28},{8,16},{12,20},{16,8},{20,12},{24,0},{28,4},{1,25},{... | collective-permute-start | bytes 208904 | tf_op jit(solution)/shard_map/ppermute | solution.py:458
  182.4 3.6 %collective-permute-start.60 = (f32[8,128]{1,0:T(8,128)S(1)}, f32[8,128]{1,0:T(8,128)S(1)}, u32[]{:S(2)}, u32[]{:S(2)}) collective-permute-start(f32[8,128]{1,0:T(8,128)S(1)} %max.31), channel_id=1, source_target_pairs={{0,1},{1,0},{2,3},{3,2},{4,6},{5,7},{6,4},{7,5},{8,9},{9,8},{10,11... | collective-permute-start | bytes 12296 | tf_op jit(solution)/shard_map/ppermute | solution.py:606
  183.9 5.4 %collective-permute-start.61 = (f32[8,128]{1,0:T(8,128)S(1)}, f32[8,128]{1,0:T(8,128)S(1)}, u32[]{:S(2)}, u32[]{:S(2)}) collective-permute-start(f32[8,128]{1,0:T(8,128)S(1)} %max.31), channel_id=1, source_target_pairs={{0,3},{1,2},{2,1},{3,0},{4,7},{5,6},{6,5},{7,4},{8,11},{9,10},{10,... | collective-permute-start | bytes 12296 | tf_op jit(solution)/shard_map/ppermute | solution.py:606
  (21 other events, 171.9 us)

commit v7 on v6

--- a/solution.py
+++ b/solution.py
@@ -491,7 +491,7 @@
     half = xcount // 2
 
     def over_col(x):
-        return exchange(x, "col", n_col, sorted(range(1, n_col), key=lambda m: (m != 2, m)))
+        return exchange(x, "col", n_col, range(1, n_col))
 
     def over_plane(chip, op=jnp.add):
         return tree(exchange(chip, "row", n_row, range(2, n_row, 2)), op)
@@ -599,16 +599,7 @@
     z = over_plane(join(mine, other_core(theirs)), join)
     (worst,) = call(residual_kernel, "residuals", [small], (z, primal_half, diag, linear))
     worst = jnp.maximum(worst, other_core(worst))
-    if n_col == 4:
-        def ask(even, odd):
-            at = [(r, c) for r in range(n_row) for c in range(n_col)]
-            pairs = [(r * n_col + c, r * n_col + (c ^ (odd if r % 2 else even))) for r, c in at]
-            return lax.ppermute(worst, ("row", "col"), pairs)
-
-        worst = tree((worst, ask(1, 2), ask(3, 3), worst), jnp.maximum)
-        worst = jnp.maximum(worst, other_core(worst))
-    else:
-        worst = tree(exchange(worst, "col", n_col, range(1, n_col)), jnp.maximum)
+    worst = tree(over_col(worst), jnp.maximum)
     return (primal_next, slack_next, dual_next, jnp.max(worst[:4]), jnp.max(worst[4:]))
 
 

time: 191 us -> 196 us (1.026)
  waiting for transfers between devices: 87.9 us -> 91.6 us
    ppermute x61 -> x63, waiting for transfers between devices: 84.3 us -> 91.6 us  [swap(): return lax.ppermute(x, axis, [(i, i ^ distance) for i in range(size)])]
    ppermute x61 -> x63, starting transfers between devices: 61.5 us -> 65.9 us  [swap(): return lax.ppermute(x, axis, [(i, i ^ distance) for i in range(size)])]
    ppermute x2 -> x0, waiting for transfers between devices: 3.64 us -> none  [ask(): return lax.ppermute(worst, ('row', 'col'), pairs)]
    ppermute x2 -> x0, starting transfers between devices: 3.18 us -> none  [ask(): return lax.ppermute(worst, ('row', 'col'), pairs)]
  transfers between devices with their start and end apart: 63 -> 63, of which waited for: 54 -> 51; matrix products, arithmetic and copies ran while one was open for 0% -> 0% of each run, Pallas kernels for 2% -> 2%
where the time goes in v7:
time: 196 us
  waiting for transfers between devices  91.6 us (47%)
  starting transfers between devices  65.9 us (34%)
  Pallas kernels  35.8 us (18%)
    ppermute x63, waiting for transfers between devices, swap(): return lax.ppermute(x, axis, [(i, i ^ distance) for i in range(size)])  91.6 us
    ppermute x63, starting transfers between devices, swap(): return lax.ppermute(x, axis, [(i, i ^ distance) for i in range(size)])  65.9 us
    pallas_call x17, Pallas kernels, call(): pl.pallas_call(kernel, out_shape=shapes, in_specs=specs, out_specs=tuple(...  35.8 us
  transfers between devices with their start and end apart: 63, of which 51 were waited for; matrix products, arithmetic and copies ran while one was open for 0% of the time, Pallas kernels for 2%

profile of v7, /device:TPU:0, one launch (start us, length us, event | category | flops | bytes accessed | tf_op | source)
XLA Modules:
  0.0 195.9 jit_solution(7485090778869908067)
XLA Ops:
  1.3 6.4 %first_forward.1 = (bf16[72,256,256]{2,1,0:T(8,128)(2,1)S(1)}, f32[152,128]{1,0:T(8,128)S(1)}, f32[256,128]{1,0:T(8,128)S(1)}, bf16[144,256]{1,0:T(8,128)(2,1)S(1)}) custom-call(f32[1]{0:T(128)} %bitcast.7.rho_ref, f32[96,128,128]{2,1,0:T(8,128)} %bitcast.16, f32[48,128,128]{2,1,0:T(8,128)} %bitcast.18, f32[256,128]{1,0:T(8,128)} %refs_2_.1, ...), custom_call_target="tpu_custom_call" | custom-call | tf_op jit(solution)/shard_map/first_forward/pallas_call | solution.py:445
  7.7 3.1 %collective-permute-start = (f32[152,128]{1,0:T(8,128)S(1)}, f32[152,128]{1,0:T(8,128)S(1)}, u32[]{:S(2)}, u32[]{:S(2)}) collective-permute-start(f32[152,128]{1,0:T(8,128)S(1)} %get-tuple-element.91.refs_1_), channel_id=1, source_target_pairs={{0,1},{1,0},{2,3},{3,2},{4,5},{5,4},{6,7},{7,6},{8,9},{9,8},{10,11... | collective-permute-start | bytes 233480 | tf_op jit(solution)/shard_map/ppermute | solution.py:458
  10.9 2.6 %collective-permute-start.1 = (f32[152,128]{1,0:T(8,128)S(1)}, f32[152,128]{1,0:T(8,128)S(1)}, u32[]{:S(2)}, u32[]{:S(2)}) collective-permute-start(f32[152,128]{1,0:T(8,128)S(1)} %get-tuple-element.91.refs_1_), channel_id=1, source_target_pairs={{0,2},{1,3},{2,0},{3,1},{4,6},{5,7},{6,4},{7,5},{8,10},{9,11},{10,... | collective-permute-start | bytes 233480 | tf_op jit(solution)/shard_map/ppermute | solution.py:458
  13.5 4.4 %split.1 = (bf16[72,256,256]{2,1,0:T(8,128)(2,1)S(1)}, f32[144,128]{1,0:T(8,128)S(1)}) custom-call(f32[96,128,128]{2,1,0:T(8,128)} %bitcast.17, f32[48,128,128]{2,1,0:T(8,128)} %bitcast.19), custom_call_target="tpu_custom_call" | custom-call | flops 18874368 | bytes 9437184 | tf_op jit(solution)/shard_map/split/pallas_call | solution.py:445
  19.7 2.1 %first_backward.1 = (f32[256,128]{1,0:T(8,128)S(1)}, f32[256,128]{1,0:T(8,128)S(1)}, f32[256,128]{1,0:T(8,128)S(1)}, bf16[4,256,144]{2,1,0:T(8,128)(2,1)S(1)}, b...) custom-call(f32[1]{0:T(128)} %bitcast.8.refs_0_, f32[152,128]{1,0:T(8,128)S(1)} %get-tuple-element.91.refs_1_, ...), custom_call_target="tpu_custom_call" | custom-call | tf_op jit(solution)/shard_map/first_backward/pallas_call | solution.py:445
  23.2 1.6 collective-permute-start.4
  26.8 2.5 %collective-permute-done.4 = f32[256,128]{1,0:T(8,128)S(1)} collective-permute-done((f32[256,128]{1,0:T(8,128)S(1)}, f32[256,128]{1,0:T(8,128)S(1)}, u32[]{:S(2)}, u32[]{:S(2)}) %collective-permute-start.4) | collective-permute-done | bytes 131104 | tf_op jit(solution)/shard_map/ppermute | solution.py:458
  29.3 3.6 %collective-permute-done.5 = f32[256,128]{1,0:T(8,128)S(1)} collective-permute-done((f32[256,128]{1,0:T(8,128)S(1)}, f32[256,128]{1,0:T(8,128)S(1)}, u32[]{:S(2)}, u32[]{:S(2)}) %collective-permute-start.5) | collective-permute-done | bytes 131104 | tf_op jit(solution)/shard_map/ppermute | solution.py:458
  34.3 1.6 second_forward.1
  35.9 2.5 %collective-permute-start.10 = (f32[152,128]{1,0:T(8,128)S(1)}, f32[152,128]{1,0:T(8,128)S(1)}, u32[]{:S(2)}, u32[]{:S(2)}) collective-permute-start(f32[152,128]{1,0:T(8,128)S(1)} %get-tuple-element.101.refs_1_), channel_id=1, source_target_pairs={{0,3},{1,2},{2,1},{3,0},{4,7},{5,6},{6,5},{7,4},{8,11},{9,10},{10,... | collective-permute-start | bytes 233480 | tf_op jit(solution)/shard_map/ppermute | solution.py:458
  40.3 2.6 %collective-permute-done.10.refs_4_ = f32[152,128]{1,0:T(8,128)S(1)} collective-permute-done((f32[152,128]{1,0:T(8,128)S(1)}, f32[152,128]{1,0:T(8,128)S(1)}, u32[]{:S(2)}, u32[]{:S(2)}) %collective-permute-start.10) | collective-permute-done | bytes 77856 | tf_op jit(solution)/shard_map/ppermute | solution.py:458
  42.9 1.9 collective-permute-done.8.refs_2_
  46.2 2.0 %backward.5 = (f32[136,128]{1,0:T(8,128)S(1)}, f32[136,128]{1,0:T(8,128)S(1)}, f32[256,128]{1,0:T(8,128)S(1)}, f32[256,128]{1,0:T(8,128)S(1)}, f32[8,128]{1,0:T(8,128)S(1)}) custom-call(f32[1]{0:T(128)} %bitcast.9.refs_0_, f32[152,128]{1,0:T(8,128)S(1)} %get-tuple-element.101.refs_1_, f32[152,128]{1,0:T(8,128)S(1)} %collective-permute-done.8.refs_2_, ...), custom_call_target="tpu_custom_call" | custom-call | tf_op jit(solution)/shard_map/backward/pallas_call | solution.py:445
  53.9 2.0 %collective-permute-done.13 = f32[136,128]{1,0:T(8,128)S(1)} collective-permute-done((f32[136,128]{1,0:T(8,128)S(1)}, f32[136,128]{1,0:T(8,128)S(1)}, u32[]{:S(2)}, u32[]{:S(2)}) %collective-permute-start.13) | collective-permute-done | bytes 69664 | tf_op jit(solution)/shard_map/ppermute | solution.py:458
  58.2 1.7 forward.5
  59.9 3.0 %collective-permute-start.17 = (f32[152,128]{1,0:T(8,128)S(1)}, f32[152,128]{1,0:T(8,128)S(1)}, u32[]{:S(2)}, u32[]{:S(2)}) collective-permute-start(f32[152,128]{1,0:T(8,128)S(1)} %get-tuple-element.113.refs_1_), channel_id=1, source_target_pairs={{0,2},{1,3},{2,0},{3,1},{4,6},{5,7},{6,4},{7,5},{8,10},{9,11},{10,... | collective-permute-start | bytes 233480 | tf_op jit(solution)/shard_map/ppermute | solution.py:458
  65.6 3.7 %collective-permute-done.17.refs_3_ = f32[152,128]{1,0:T(8,128)S(1)} collective-permute-done((f32[152,128]{1,0:T(8,128)S(1)}, f32[152,128]{1,0:T(8,128)S(1)}, u32[]{:S(2)}, u32[]{:S(2)}) %collective-permute-start.17) | collective-permute-done | bytes 77856 | tf_op jit(solution)/shard_map/ppermute | solution.py:458
  69.3 2.0 %backward.6 = (f32[136,128]{1,0:T(8,128)S(1)}, f32[136,128]{1,0:T(8,128)S(1)}, f32[256,128]{1,0:T(8,128)S(1)}, f32[256,128]{1,0:T(8,128)S(1)}, f32[8,128]{1,0:T(8,128)S(1)}) custom-call(f32[1]{0:T(128)} %bitcast.10.refs_0_, f32[152,128]{1,0:T(8,128)S(1)} %get-tuple-element.113.refs_1_, f32[152,128]{1,0:T(8,128)S(1)} %collective-permute-done.16.refs_2_, ...), custom_call_target="tpu_custom_call" | custom-call | tf_op jit(solution)/shard_map/backward/pallas_call | solution.py:445
  72.6 1.6 collective-permute-start.20
  77.0 2.2 %collective-permute-done.21 = f32[136,128]{1,0:T(8,128)S(1)} collective-permute-done((f32[136,128]{1,0:T(8,128)S(1)}, f32[136,128]{1,0:T(8,128)S(1)}, u32[]{:S(2)}, u32[]{:S(2)}) %collective-permute-start.21) | collective-permute-done | bytes 69664 | tf_op jit(solution)/shard_map/ppermute | solution.py:458
  81.3 1.7 forward.6
  83.1 1.7 collective-permute-start.24
  84.7 1.5 collective-permute-start.25
  87.5 6.4 %collective-permute-done.25.refs_3_ = f32[152,128]{1,0:T(8,128)S(1)} collective-permute-done((f32[152,128]{1,0:T(8,128)S(1)}, f32[152,128]{1,0:T(8,128)S(1)}, u32[]{:S(2)}, u32[]{:S(2)}) %collective-permute-start.25) | collective-permute-done | bytes 77856 | tf_op jit(solution)/shard_map/ppermute | solution.py:458
  93.9 2.2 %backward.7 = (f32[136,128]{1,0:T(8,128)S(1)}, f32[136,128]{1,0:T(8,128)S(1)}, f32[256,128]{1,0:T(8,128)S(1)}, f32[256,128]{1,0:T(8,128)S(1)}, f32[8,128]{1,0:T(8,128)S(1)}) custom-call(f32[1]{0:T(128)} %bitcast.11.refs_0_, f32[152,128]{1,0:T(8,128)S(1)} %get-tuple-element.124.refs_1_, f32[152,128]{1,0:T(8,128)S(1)} %collective-permute-done.24.refs_2_, ...), custom_call_target="tpu_custom_call" | custom-call | tf_op jit(solution)/shard_map/backward/pallas_call | solution.py:445
  99.5 1.5 collective-permute-start.30
  101.8 1.9 collective-permute-done.29
  106.0 1.7 forward.7
  110.5 1.7 collective-permute-start.34
  112.2 6.2 %collective-permute-done.33.refs_3_ = f32[152,128]{1,0:T(8,128)S(1)} collective-permute-done((f32[152,128]{1,0:T(8,128)S(1)}, f32[152,128]{1,0:T(8,128)S(1)}, u32[]{:S(2)}, u32[]{:S(2)}) %collective-permute-start.33) | collective-permute-done | bytes 77856 | tf_op jit(solution)/shard_map/ppermute | solution.py:458
  118.4 2.0 %backward.8 = (f32[136,128]{1,0:T(8,128)S(1)}, f32[136,128]{1,0:T(8,128)S(1)}, f32[256,128]{1,0:T(8,128)S(1)}, f32[256,128]{1,0:T(8,128)S(1)}, f32[8,128]{1,0:T(8,128)S(1)}) custom-call(f32[1]{0:T(128)} %bitcast.12.refs_0_, f32[152,128]{1,0:T(8,128)S(1)} %get-tuple-element.135.refs_1_, f32[152,128]{1,0:T(8,128)S(1)} %collective-permute-done.32.refs_2_, ...), custom_call_target="tpu_custom_call" | custom-call | tf_op jit(solution)/shard_map/backward/pallas_call | solution.py:445
  121.7 1.6 collective-permute-start.36
  126.1 2.3 %collective-permute-done.37 = f32[136,128]{1,0:T(8,128)S(1)} collective-permute-done((f32[136,128]{1,0:T(8,128)S(1)}, f32[136,128]{1,0:T(8,128)S(1)}, u32[]{:S(2)}, u32[]{:S(2)}) %collective-permute-start.37) | collective-permute-done | bytes 69664 | tf_op jit(solution)/shard_map/ppermute | solution.py:458
  130.5 1.7 forward.8
  134.8 1.8 collective-permute-start.42
  136.6 6.2 %collective-permute-done.41.refs_3_ = f32[152,128]{1,0:T(8,128)S(1)} collective-permute-done((f32[152,128]{1,0:T(8,128)S(1)}, f32[152,128]{1,0:T(8,128)S(1)}, u32[]{:S(2)}, u32[]{:S(2)}) %collective-permute-start.41) | collective-permute-done | bytes 77856 | tf_op jit(solution)/shard_map/ppermute | solution.py:458
  142.8 2.0 %backward.9 = (f32[136,128]{1,0:T(8,128)S(1)}, f32[136,128]{1,0:T(8,128)S(1)}, f32[256,128]{1,0:T(8,128)S(1)}, f32[256,128]{1,0:T(8,128)S(1)}, f32[8,128]{1,0:T(8,128)S(1)}) custom-call(f32[1]{0:T(128)} %bitcast.13.refs_0_, f32[152,128]{1,0:T(8,128)S(1)} %get-tuple-element.146.refs_1_, f32[152,128]{1,0:T(8,128)S(1)} %collective-permute-done.40.refs_2_, ...), custom_call_target="tpu_custom_call" | custom-call | tf_op jit(solution)/shard_map/backward/pallas_call | solution.py:445
  148.2 1.5 collective-permute-start.46
  150.5 1.9 collective-permute-done.45
  154.7 1.7 forward.9
  159.0 1.9 collective-permute-start.50
  160.9 6.1 %collective-permute-done.49.refs_3_ = f32[152,128]{1,0:T(8,128)S(1)} collective-permute-done((f32[152,128]{1,0:T(8,128)S(1)}, f32[152,128]{1,0:T(8,128)S(1)}, u32[]{:S(2)}, u32[]{:S(2)}) %collective-permute-start.49) | collective-permute-done | bytes 77856 | tf_op jit(solution)/shard_map/ppermute | solution.py:458
  175.2 2.3 %final.1 = (f32[256,128]{1,0:T(8,128)}, f32[128,128]{1,0:T(8,128)S(1)}, f32[192,128]{1,0:T(8,128)}, f32[192,128]{1,0:T(8,128)}, f32[136,128]{1,0:T(8,128)S(1)}, /*index=5*/f32[136,128]{1,0:T(8,128)S(1)}) custom-call(f32[1]{0:T(128)} %bitcast.15.refs_0_, f32[8,128]{1,0:T(8,128)S(1)} %add_add_fusion.6.refs_1_, f32[256,128]{1,0:T(8,128)S(1)} %get-tuple-element.162.refs_2_, ...), custom_call_target="tpu_custom_call" | custom-call | tf_op jit(solution)/shard_map/final/pallas_call | solution.py:445
  180.8 1.5 collective-permute-start.58
  183.2 1.9 collective-permute-done.57
  189.9 1.9 collective-permute-start.62
  191.8 1.6 collective-permute-done.61
  193.4 1.9 collective-permute-done.62
  (127 shorter events, 73.0 us)
Async XLA Ops:
  7.7 10.1 %collective-permute-start = (f32[152,128]{1,0:T(8,128)S(1)}, f32[152,128]{1,0:T(8,128)S(1)}, u32[]{:S(2)}, u32[]{:S(2)}) collective-permute-start(f32[152,128]{1,0:T(8,128)S(1)} %get-tuple-element.91.refs_1_), channel_id=1, source_target_pairs={{0,1},{1,0},{2,3},{3,2},{4,5},{5,4},{6,7},{7,6},{8,9},{9,8},{10,11... | collective-permute-start | bytes 233480 | tf_op jit(solution)/shard_map/ppermute | solution.py:458
  10.9 8.1 %collective-permute-start.1 = (f32[152,128]{1,0:T(8,128)S(1)}, f32[152,128]{1,0:T(8,128)S(1)}, u32[]{:S(2)}, u32[]{:S(2)}) collective-permute-start(f32[152,128]{1,0:T(8,128)S(1)} %get-tuple-element.91.refs_1_), channel_id=1, source_target_pairs={{0,2},{1,3},{2,0},{3,1},{4,6},{5,7},{6,4},{7,5},{8,10},{9,11},{10,... | collective-permute-start | bytes 233480 | tf_op jit(solution)/shard_map/ppermute | solution.py:458
  13.4 6.3 %collective-permute-start.2 = (f32[152,128]{1,0:T(8,128)S(1)}, f32[152,128]{1,0:T(8,128)S(1)}, u32[]{:S(2)}, u32[]{:S(2)}) collective-permute-start(f32[152,128]{1,0:T(8,128)S(1)} %get-tuple-element.91.refs_1_), channel_id=1, source_target_pairs={{0,3},{1,2},{2,1},{3,0},{4,7},{5,6},{6,5},{7,4},{8,11},{9,10},{10,... | collective-permute-start | bytes 233480 | tf_op jit(solution)/shard_map/ppermute | solution.py:458
  23.2 6.0 %collective-permute-start.4 = (f32[256,128]{1,0:T(8,128)S(1)}, f32[256,128]{1,0:T(8,128)S(1)}, u32[]{:S(2)}, u32[]{:S(2)}) collective-permute-start(f32[256,128]{1,0:T(8,128)S(1)} %add.96), channel_id=1, source_target_pairs={{0,8},{4,12},{8,0},{12,4},{16,24},{20,28},{24,16},{28,20},{1,9},{5... | collective-permute-start | bytes 393224 | tf_op jit(solution)/shard_map/ppermute | solution.py:458
  24.8 8.1 %collective-permute-start.5 = (f32[256,128]{1,0:T(8,128)S(1)}, f32[256,128]{1,0:T(8,128)S(1)}, u32[]{:S(2)}, u32[]{:S(2)}) collective-permute-start(f32[256,128]{1,0:T(8,128)S(1)} %add.96), channel_id=1, source_target_pairs={{0,16},{4,20},{8,24},{12,28},{16,0},{20,4},{24,8},{28,12},{1,17},{... | collective-permute-start | bytes 393224 | tf_op jit(solution)/shard_map/ppermute | solution.py:458
  26.3 6.6 %collective-permute-start.6 = (f32[256,128]{1,0:T(8,128)S(1)}, f32[256,128]{1,0:T(8,128)S(1)}, u32[]{:S(2)}, u32[]{:S(2)}) collective-permute-start(f32[256,128]{1,0:T(8,128)S(1)} %add.96), channel_id=1, source_target_pairs={{0,24},{4,28},{8,16},{12,20},{16,8},{20,12},{24,0},{28,4},{1,25},{... | collective-permute-start | bytes 393224 | tf_op jit(solution)/shard_map/ppermute | solution.py:458
  35.9 7.0 %collective-permute-start.10 = (f32[152,128]{1,0:T(8,128)S(1)}, f32[152,128]{1,0:T(8,128)S(1)}, u32[]{:S(2)}, u32[]{:S(2)}) collective-permute-start(f32[152,128]{1,0:T(8,128)S(1)} %get-tuple-element.101.refs_1_), channel_id=1, source_target_pairs={{0,3},{1,2},{2,1},{3,0},{4,7},{5,6},{6,5},{7,4},{8,11},{9,10},{10,... | collective-permute-start | bytes 233480 | tf_op jit(solution)/shard_map/ppermute | solution.py:458
  38.4 6.5 %collective-permute-start.8 = (f32[152,128]{1,0:T(8,128)S(1)}, f32[152,128]{1,0:T(8,128)S(1)}, u32[]{:S(2)}, u32[]{:S(2)}) collective-permute-start(f32[152,128]{1,0:T(8,128)S(1)} %get-tuple-element.101.refs_1_), channel_id=1, source_target_pairs={{0,1},{1,0},{2,3},{3,2},{4,5},{5,4},{6,7},{7,6},{8,9},{9,8},{10,11... | collective-permute-start | bytes 233480 | tf_op jit(solution)/shard_map/ppermute | solution.py:458
  38.9 7.3 %collective-permute-start.9 = (f32[152,128]{1,0:T(8,128)S(1)}, f32[152,128]{1,0:T(8,128)S(1)}, u32[]{:S(2)}, u32[]{:S(2)}) collective-permute-start(f32[152,128]{1,0:T(8,128)S(1)} %get-tuple-element.101.refs_1_), channel_id=1, source_target_pairs={{0,2},{1,3},{2,0},{3,1},{4,6},{5,7},{6,4},{7,5},{8,10},{9,11},{10,... | collective-permute-start | bytes 233480 | tf_op jit(solution)/shard_map/ppermute | solution.py:458
  49.5 4.4 %collective-permute-start.12 = (f32[136,128]{1,0:T(8,128)S(1)}, f32[136,128]{1,0:T(8,128)S(1)}, u32[]{:S(2)}, u32[]{:S(2)}) collective-permute-start(f32[136,128]{1,0:T(8,128)S(1)} %add.100), channel_id=1, source_target_pairs={{0,8},{4,12},{8,0},{12,4},{16,24},{20,28},{24,16},{28,20},{1,9},{5... | collective-permute-start | bytes 208904 | tf_op jit(solution)/shard_map/ppermute | solution.py:458
  50.8 5.1 %collective-permute-start.13 = (f32[136,128]{1,0:T(8,128)S(1)}, f32[136,128]{1,0:T(8,128)S(1)}, u32[]{:S(2)}, u32[]{:S(2)}) collective-permute-start(f32[136,128]{1,0:T(8,128)S(1)} %add.100), channel_id=1, source_target_pairs={{0,16},{4,20},{8,24},{12,28},{16,0},{20,4},{24,8},{28,12},{1,17},{... | collective-permute-start | bytes 208904 | tf_op jit(solution)/shard_map/ppermute | solution.py:458
  51.6 5.2 %collective-permute-start.14 = (f32[136,128]{1,0:T(8,128)S(1)}, f32[136,128]{1,0:T(8,128)S(1)}, u32[]{:S(2)}, u32[]{:S(2)}) collective-permute-start(f32[136,128]{1,0:T(8,128)S(1)} %add.100), channel_id=1, source_target_pairs={{0,24},{4,28},{8,16},{12,20},{16,8},{20,12},{24,0},{28,4},{1,25},{... | collective-permute-start | bytes 208904 | tf_op jit(solution)/shard_map/ppermute | solution.py:458
  59.9 5.7 %collective-permute-start.16 = (f32[152,128]{1,0:T(8,128)S(1)}, f32[152,128]{1,0:T(8,128)S(1)}, u32[]{:S(2)}, u32[]{:S(2)}) collective-permute-start(f32[152,128]{1,0:T(8,128)S(1)} %get-tuple-element.113.refs_1_), channel_id=1, source_target_pairs={{0,1},{1,0},{2,3},{3,2},{4,5},{5,4},{6,7},{7,6},{8,9},{9,8},{10,11... | collective-permute-start | bytes 233480 | tf_op jit(solution)/shard_map/ppermute | solution.py:458
  59.9 9.3 %collective-permute-start.17 = (f32[152,128]{1,0:T(8,128)S(1)}, f32[152,128]{1,0:T(8,128)S(1)}, u32[]{:S(2)}, u32[]{:S(2)}) collective-permute-start(f32[152,128]{1,0:T(8,128)S(1)} %get-tuple-element.113.refs_1_), channel_id=1, source_target_pairs={{0,2},{1,3},{2,0},{3,1},{4,6},{5,7},{6,4},{7,5},{8,10},{9,11},{10,... | collective-permute-start | bytes 233480 | tf_op jit(solution)/shard_map/ppermute | solution.py:458
  63.0 6.3 %collective-permute-start.18 = (f32[152,128]{1,0:T(8,128)S(1)}, f32[152,128]{1,0:T(8,128)S(1)}, u32[]{:S(2)}, u32[]{:S(2)}) collective-permute-start(f32[152,128]{1,0:T(8,128)S(1)} %get-tuple-element.113.refs_1_), channel_id=1, source_target_pairs={{0,3},{1,2},{2,1},{3,0},{4,7},{5,6},{6,5},{7,4},{8,11},{9,10},{10,... | collective-permute-start | bytes 233480 | tf_op jit(solution)/shard_map/ppermute | solution.py:458
  72.6 4.4 %collective-permute-start.20 = (f32[136,128]{1,0:T(8,128)S(1)}, f32[136,128]{1,0:T(8,128)S(1)}, u32[]{:S(2)}, u32[]{:S(2)}) collective-permute-start(f32[136,128]{1,0:T(8,128)S(1)} %add.104), channel_id=1, source_target_pairs={{0,8},{4,12},{8,0},{12,4},{16,24},{20,28},{24,16},{28,20},{1,9},{5... | collective-permute-start | bytes 208904 | tf_op jit(solution)/shard_map/ppermute | solution.py:458
  74.2 5.1 %collective-permute-start.21 = (f32[136,128]{1,0:T(8,128)S(1)}, f32[136,128]{1,0:T(8,128)S(1)}, u32[]{:S(2)}, u32[]{:S(2)}) collective-permute-start(f32[136,128]{1,0:T(8,128)S(1)} %add.104), channel_id=1, source_target_pairs={{0,16},{4,20},{8,24},{12,28},{16,0},{20,4},{24,8},{28,12},{1,17},{... | collective-permute-start | bytes 208904 | tf_op jit(solution)/shard_map/ppermute | solution.py:458
  74.8 5.2 %collective-permute-start.22 = (f32[136,128]{1,0:T(8,128)S(1)}, f32[136,128]{1,0:T(8,128)S(1)}, u32[]{:S(2)}, u32[]{:S(2)}) collective-permute-start(f32[136,128]{1,0:T(8,128)S(1)} %add.104), channel_id=1, source_target_pairs={{0,24},{4,28},{8,16},{12,20},{16,8},{20,12},{24,0},{28,4},{1,25},{... | collective-permute-start | bytes 208904 | tf_op jit(solution)/shard_map/ppermute | solution.py:458
  83.1 4.4 %collective-permute-start.24 = (f32[152,128]{1,0:T(8,128)S(1)}, f32[152,128]{1,0:T(8,128)S(1)}, u32[]{:S(2)}, u32[]{:S(2)}) collective-permute-start(f32[152,128]{1,0:T(8,128)S(1)} %get-tuple-element.124.refs_1_), channel_id=1, source_target_pairs={{0,1},{1,0},{2,3},{3,2},{4,5},{5,4},{6,7},{7,6},{8,9},{9,8},{10,11... | collective-permute-start | bytes 233480 | tf_op jit(solution)/shard_map/ppermute | solution.py:458
  84.7 9.2 %collective-permute-start.25 = (f32[152,128]{1,0:T(8,128)S(1)}, f32[152,128]{1,0:T(8,128)S(1)}, u32[]{:S(2)}, u32[]{:S(2)}) collective-permute-start(f32[152,128]{1,0:T(8,128)S(1)} %get-tuple-element.124.refs_1_), channel_id=1, source_target_pairs={{0,2},{1,3},{2,0},{3,1},{4,6},{5,7},{6,4},{7,5},{8,10},{9,11},{10,... | collective-permute-start | bytes 233480 | tf_op jit(solution)/shard_map/ppermute | solution.py:458
  86.3 7.6 %collective-permute-start.26 = (f32[152,128]{1,0:T(8,128)S(1)}, f32[152,128]{1,0:T(8,128)S(1)}, u32[]{:S(2)}, u32[]{:S(2)}) collective-permute-start(f32[152,128]{1,0:T(8,128)S(1)} %get-tuple-element.124.refs_1_), channel_id=1, source_target_pairs={{0,3},{1,2},{2,1},{3,0},{4,7},{5,6},{6,5},{7,4},{8,11},{9,10},{10,... | collective-permute-start | bytes 233480 | tf_op jit(solution)/shard_map/ppermute | solution.py:458
  97.5 4.4 %collective-permute-start.28 = (f32[136,128]{1,0:T(8,128)S(1)}, f32[136,128]{1,0:T(8,128)S(1)}, u32[]{:S(2)}, u32[]{:S(2)}) collective-permute-start(f32[136,128]{1,0:T(8,128)S(1)} %add.108), channel_id=1, source_target_pairs={{0,8},{4,12},{8,0},{12,4},{16,24},{20,28},{24,16},{28,20},{1,9},{5... | collective-permute-start | bytes 208904 | tf_op jit(solution)/shard_map/ppermute | solution.py:458
  98.7 5.1 %collective-permute-start.29 = (f32[136,128]{1,0:T(8,128)S(1)}, f32[136,128]{1,0:T(8,128)S(1)}, u32[]{:S(2)}, u32[]{:S(2)}) collective-permute-start(f32[136,128]{1,0:T(8,128)S(1)} %add.108), channel_id=1, source_target_pairs={{0,16},{4,20},{8,24},{12,28},{16,0},{20,4},{24,8},{28,12},{1,17},{... | collective-permute-start | bytes 208904 | tf_op jit(solution)/shard_map/ppermute | solution.py:458
  99.5 5.2 %collective-permute-start.30 = (f32[136,128]{1,0:T(8,128)S(1)}, f32[136,128]{1,0:T(8,128)S(1)}, u32[]{:S(2)}, u32[]{:S(2)}) collective-permute-start(f32[136,128]{1,0:T(8,128)S(1)} %add.108), channel_id=1, source_target_pairs={{0,24},{4,28},{8,16},{12,20},{16,8},{20,12},{24,0},{28,4},{1,25},{... | collective-permute-start | bytes 208904 | tf_op jit(solution)/shard_map/ppermute | solution.py:458
  107.8 4.4 %collective-permute-start.32 = (f32[152,128]{1,0:T(8,128)S(1)}, f32[152,128]{1,0:T(8,128)S(1)}, u32[]{:S(2)}, u32[]{:S(2)}) collective-permute-start(f32[152,128]{1,0:T(8,128)S(1)} %get-tuple-element.135.refs_1_), channel_id=1, source_target_pairs={{0,1},{1,0},{2,3},{3,2},{4,5},{5,4},{6,7},{7,6},{8,9},{9,8},{10,11... | collective-permute-start | bytes 233480 | tf_op jit(solution)/shard_map/ppermute | solution.py:458
  109.2 9.2 %collective-permute-start.33 = (f32[152,128]{1,0:T(8,128)S(1)}, f32[152,128]{1,0:T(8,128)S(1)}, u32[]{:S(2)}, u32[]{:S(2)}) collective-permute-start(f32[152,128]{1,0:T(8,128)S(1)} %get-tuple-element.135.refs_1_), channel_id=1, source_target_pairs={{0,2},{1,3},{2,0},{3,1},{4,6},{5,7},{6,4},{7,5},{8,10},{9,11},{10,... | collective-permute-start | bytes 233480 | tf_op jit(solution)/shard_map/ppermute | solution.py:458
  110.5 7.9 %collective-permute-start.34 = (f32[152,128]{1,0:T(8,128)S(1)}, f32[152,128]{1,0:T(8,128)S(1)}, u32[]{:S(2)}, u32[]{:S(2)}) collective-permute-start(f32[152,128]{1,0:T(8,128)S(1)} %get-tuple-element.135.refs_1_), channel_id=1, source_target_pairs={{0,3},{1,2},{2,1},{3,0},{4,7},{5,6},{6,5},{7,4},{8,11},{9,10},{10,... | collective-permute-start | bytes 233480 | tf_op jit(solution)/shard_map/ppermute | solution.py:458
  121.7 4.4 %collective-permute-start.36 = (f32[136,128]{1,0:T(8,128)S(1)}, f32[136,128]{1,0:T(8,128)S(1)}, u32[]{:S(2)}, u32[]{:S(2)}) collective-permute-start(f32[136,128]{1,0:T(8,128)S(1)} %add.112), channel_id=1, source_target_pairs={{0,8},{4,12},{8,0},{12,4},{16,24},{20,28},{24,16},{28,20},{1,9},{5... | collective-permute-start | bytes 208904 | tf_op jit(solution)/shard_map/ppermute | solution.py:458
  123.3 5.1 %collective-permute-start.37 = (f32[136,128]{1,0:T(8,128)S(1)}, f32[136,128]{1,0:T(8,128)S(1)}, u32[]{:S(2)}, u32[]{:S(2)}) collective-permute-start(f32[136,128]{1,0:T(8,128)S(1)} %add.112), channel_id=1, source_target_pairs={{0,16},{4,20},{8,24},{12,28},{16,0},{20,4},{24,8},{28,12},{1,17},{... | collective-permute-start | bytes 208904 | tf_op jit(solution)/shard_map/ppermute | solution.py:458
  123.9 5.2 %collective-permute-start.38 = (f32[136,128]{1,0:T(8,128)S(1)}, f32[136,128]{1,0:T(8,128)S(1)}, u32[]{:S(2)}, u32[]{:S(2)}) collective-permute-start(f32[136,128]{1,0:T(8,128)S(1)} %add.112), channel_id=1, source_target_pairs={{0,24},{4,28},{8,16},{12,20},{16,8},{20,12},{24,0},{28,4},{1,25},{... | collective-permute-start | bytes 208904 | tf_op jit(solution)/shard_map/ppermute | solution.py:458
  132.2 4.4 %collective-permute-start.40 = (f32[152,128]{1,0:T(8,128)S(1)}, f32[152,128]{1,0:T(8,128)S(1)}, u32[]{:S(2)}, u32[]{:S(2)}) collective-permute-start(f32[152,128]{1,0:T(8,128)S(1)} %get-tuple-element.146.refs_1_), channel_id=1, source_target_pairs={{0,1},{1,0},{2,3},{3,2},{4,5},{5,4},{6,7},{7,6},{8,9},{9,8},{10,11... | collective-permute-start | bytes 233480 | tf_op jit(solution)/shard_map/ppermute | solution.py:458
  133.7 9.2 %collective-permute-start.41 = (f32[152,128]{1,0:T(8,128)S(1)}, f32[152,128]{1,0:T(8,128)S(1)}, u32[]{:S(2)}, u32[]{:S(2)}) collective-permute-start(f32[152,128]{1,0:T(8,128)S(1)} %get-tuple-element.146.refs_1_), channel_id=1, source_target_pairs={{0,2},{1,3},{2,0},{3,1},{4,6},{5,7},{6,4},{7,5},{8,10},{9,11},{10,... | collective-permute-start | bytes 233480 | tf_op jit(solution)/shard_map/ppermute | solution.py:458
  134.8 8.0 %collective-permute-start.42 = (f32[152,128]{1,0:T(8,128)S(1)}, f32[152,128]{1,0:T(8,128)S(1)}, u32[]{:S(2)}, u32[]{:S(2)}) collective-permute-start(f32[152,128]{1,0:T(8,128)S(1)} %get-tuple-element.146.refs_1_), channel_id=1, source_target_pairs={{0,3},{1,2},{2,1},{3,0},{4,7},{5,6},{6,5},{7,4},{8,11},{9,10},{10,... | collective-permute-start | bytes 233480 | tf_op jit(solution)/shard_map/ppermute | solution.py:458
  146.2 4.4 %collective-permute-start.44 = (f32[136,128]{1,0:T(8,128)S(1)}, f32[136,128]{1,0:T(8,128)S(1)}, u32[]{:S(2)}, u32[]{:S(2)}) collective-permute-start(f32[136,128]{1,0:T(8,128)S(1)} %add.116), channel_id=1, source_target_pairs={{0,8},{4,12},{8,0},{12,4},{16,24},{20,28},{24,16},{28,20},{1,9},{5... | collective-permute-start | bytes 208904 | tf_op jit(solution)/shard_map/ppermute | solution.py:458
  147.4 5.1 %collective-permute-start.45 = (f32[136,128]{1,0:T(8,128)S(1)}, f32[136,128]{1,0:T(8,128)S(1)}, u32[]{:S(2)}, u32[]{:S(2)}) collective-permute-start(f32[136,128]{1,0:T(8,128)S(1)} %add.116), channel_id=1, source_target_pairs={{0,16},{4,20},{8,24},{12,28},{16,0},{20,4},{24,8},{28,12},{1,17},{... | collective-permute-start | bytes 208904 | tf_op jit(solution)/shard_map/ppermute | solution.py:458
  148.2 5.2 %collective-permute-start.46 = (f32[136,128]{1,0:T(8,128)S(1)}, f32[136,128]{1,0:T(8,128)S(1)}, u32[]{:S(2)}, u32[]{:S(2)}) collective-permute-start(f32[136,128]{1,0:T(8,128)S(1)} %add.116), channel_id=1, source_target_pairs={{0,24},{4,28},{8,16},{12,20},{16,8},{20,12},{24,0},{28,4},{1,25},{... | collective-permute-start | bytes 208904 | tf_op jit(solution)/shard_map/ppermute | solution.py:458
  156.4 4.5 %collective-permute-start.48 = (f32[152,128]{1,0:T(8,128)S(1)}, f32[152,128]{1,0:T(8,128)S(1)}, u32[]{:S(2)}, u32[]{:S(2)}) collective-permute-start(f32[152,128]{1,0:T(8,128)S(1)} %get-tuple-element.157.refs_1_), channel_id=1, source_target_pairs={{0,1},{1,0},{2,3},{3,2},{4,5},{5,4},{6,7},{7,6},{8,9},{9,8},{10,11... | collective-permute-start | bytes 233480 | tf_op jit(solution)/shard_map/ppermute | solution.py:458
  157.9 9.1 %collective-permute-start.49 = (f32[152,128]{1,0:T(8,128)S(1)}, f32[152,128]{1,0:T(8,128)S(1)}, u32[]{:S(2)}, u32[]{:S(2)}) collective-permute-start(f32[152,128]{1,0:T(8,128)S(1)} %get-tuple-element.157.refs_1_), channel_id=1, source_target_pairs={{0,2},{1,3},{2,0},{3,1},{4,6},{5,7},{6,4},{7,5},{8,10},{9,11},{10,... | collective-permute-start | bytes 233480 | tf_op jit(solution)/shard_map/ppermute | solution.py:458
  159.0 8.1 %collective-permute-start.50 = (f32[152,128]{1,0:T(8,128)S(1)}, f32[152,128]{1,0:T(8,128)S(1)}, u32[]{:S(2)}, u32[]{:S(2)}) collective-permute-start(f32[152,128]{1,0:T(8,128)S(1)} %get-tuple-element.157.refs_1_), channel_id=1, source_target_pairs={{0,3},{1,2},{2,1},{3,0},{4,7},{5,6},{6,5},{7,4},{8,11},{9,10},{10,... | collective-permute-start | bytes 233480 | tf_op jit(solution)/shard_map/ppermute | solution.py:458
  168.6 3.6 %collective-permute-start.52 = (f32[8,128]{1,0:T(8,128)S(1)}, f32[8,128]{1,0:T(8,128)S(1)}, u32[]{:S(2)}, u32[]{:S(2)}) collective-permute-start(f32[8,128]{1,0:T(8,128)S(1)} %add.120), channel_id=1, source_target_pairs={{0,8},{4,12},{8,0},{12,4},{16,24},{20,28},{24,16},{28,20},{1,9},{5... | collective-permute-start | bytes 12296 | tf_op jit(solution)/shard_map/ppermute | solution.py:458
  170.1 3.6 %collective-permute-start.53 = (f32[8,128]{1,0:T(8,128)S(1)}, f32[8,128]{1,0:T(8,128)S(1)}, u32[]{:S(2)}, u32[]{:S(2)}) collective-permute-start(f32[8,128]{1,0:T(8,128)S(1)} %add.120), channel_id=1, source_target_pairs={{0,16},{4,20},{8,24},{12,28},{16,0},{20,4},{24,8},{28,12},{1,17},{... | collective-permute-start | bytes 12296 | tf_op jit(solution)/shard_map/ppermute | solution.py:458
  170.7 4.5 %collective-permute-start.54 = (f32[8,128]{1,0:T(8,128)S(1)}, f32[8,128]{1,0:T(8,128)S(1)}, u32[]{:S(2)}, u32[]{:S(2)}) collective-permute-start(f32[8,128]{1,0:T(8,128)S(1)} %add.120), channel_id=1, source_target_pairs={{0,24},{4,28},{8,16},{12,20},{16,8},{20,12},{24,0},{28,4},{1,25},{... | collective-permute-start | bytes 12296 | tf_op jit(solution)/shard_map/ppermute | solution.py:458
  178.8 4.4 %collective-permute-start.56 = (f32[136,128]{1,0:T(8,128)S(1)}, f32[136,128]{1,0:T(8,128)S(1)}, u32[]{:S(2)}, u32[]{:S(2)}) collective-permute-start(f32[136,128]{1,0:T(8,128)S(1)} %maximum_select_fusion.1), channel_id=1, source_target_pairs={{0,8},{4,12},{8,0},{12,4},{16,24},{20,28},{24,16},{28,20},{1,9},{5... | collective-permute-start | bytes 208904 | tf_op jit(solution)/shard_map/ppermute | solution.py:458
  180.0 5.1 %collective-permute-start.57 = (f32[136,128]{1,0:T(8,128)S(1)}, f32[136,128]{1,0:T(8,128)S(1)}, u32[]{:S(2)}, u32[]{:S(2)}) collective-permute-start(f32[136,128]{1,0:T(8,128)S(1)} %maximum_select_fusion.1), channel_id=1, source_target_pairs={{0,16},{4,20},{8,24},{12,28},{16,0},{20,4},{24,8},{28,12},{1,17},{... | collective-permute-start | bytes 208904 | tf_op jit(solution)/shard_map/ppermute | solution.py:458
  180.8 5.2 %collective-permute-start.58 = (f32[136,128]{1,0:T(8,128)S(1)}, f32[136,128]{1,0:T(8,128)S(1)}, u32[]{:S(2)}, u32[]{:S(2)}) collective-permute-start(f32[136,128]{1,0:T(8,128)S(1)} %maximum_select_fusion.1), channel_id=1, source_target_pairs={{0,24},{4,28},{8,16},{12,20},{16,8},{20,12},{24,0},{28,4},{1,25},{... | collective-permute-start | bytes 208904 | tf_op jit(solution)/shard_map/ppermute | solution.py:458
  187.4 4.4 %collective-permute-start.60 = (f32[8,128]{1,0:T(8,128)S(1)}, f32[8,128]{1,0:T(8,128)S(1)}, u32[]{:S(2)}, u32[]{:S(2)}) collective-permute-start(f32[8,128]{1,0:T(8,128)S(1)} %max.28), channel_id=1, source_target_pairs={{0,1},{1,0},{2,3},{3,2},{4,5},{5,4},{6,7},{7,6},{8,9},{9,8},{10,11... | collective-permute-start | bytes 12296 | tf_op jit(solution)/shard_map/ppermute | solution.py:458
  188.9 4.5 %collective-permute-start.61 = (f32[8,128]{1,0:T(8,128)S(1)}, f32[8,128]{1,0:T(8,128)S(1)}, u32[]{:S(2)}, u32[]{:S(2)}) collective-permute-start(f32[8,128]{1,0:T(8,128)S(1)} %max.28), channel_id=1, source_target_pairs={{0,2},{1,3},{2,0},{3,1},{4,6},{5,7},{6,4},{7,5},{8,10},{9,11},{10,... | collective-permute-start | bytes 12296 | tf_op jit(solution)/shard_map/ppermute | solution.py:458
  189.9 5.4 %collective-permute-start.62 = (f32[8,128]{1,0:T(8,128)S(1)}, f32[8,128]{1,0:T(8,128)S(1)}, u32[]{:S(2)}, u32[]{:S(2)}) collective-permute-start(f32[8,128]{1,0:T(8,128)S(1)} %max.28), channel_id=1, source_target_pairs={{0,3},{1,2},{2,1},{3,0},{4,7},{5,6},{6,5},{7,4},{8,11},{9,10},{10,... | collective-permute-start | bytes 12296 | tf_op jit(solution)/shard_map/ppermute | solution.py:458
  (21 other events, 174.7 us)
